TPU v7x, 128 devices: a whole 4x4x4 slice. The times are simulated.
128 devices in a mesh: row: 8 (over x, z_hi), col: 16 (over z_lo, y, core).
Axes of the slice: x: 4, y: 4, z: 4 (z_hi: 2, z_lo: 2; z = z_hi * 2 + z_lo), core: 2. Of those that a mesh axis runs over, the one named last changes fastest.
Arguments:
- covariance: float32 [16384, 16384], P('row', 'col'), may hold values from -1 to 560
- seed_index: int32 [128], replicated, may hold values from 0 to 16383, as said below
Outputs:
- basis: float32 [16384, 384], P('row')
- projection: float32 [384, 256], replicated
- first_pass: float32 [384, 256], replicated
Inputs may be any that keep to these rules, and one draw needn't show every extreme that they name: `seed_index`: 128 distinct column indices.
All inputs are finite; a program needn't handle non-finite values.
Results may differ from a plain program's by a relative error of at most 0.00019.
Values sent between devices are 32-bit elements; how exact they have to be, the bound alone decides.
No kernel may reach another device: no remote copies, remote signals or barrier semaphores. Data moves between devices by JAX's collectives and lax.ppermute only.
A program may use at most 128 MiB of HBM per device.

v0:
```python
import jax
import jax.numpy as jnp
from jax import lax
from jax.experimental import pallas as pl
from jax.experimental.pallas import tpu as pltpu
from jax.sharding import Mesh, PartitionSpec as P

ROWS = "row"
CHIP = "chip"
CORE = "core"
ALL = (ROWS, CHIP, CORE)
SWAP = [(0, 1), (1, 0)]
W = 128
f32 = jnp.float32
HI = lax.Precision.HIGHEST


def dot(a, b, dims):
    return lax.dot_general(a, b, (dims, ((), ())), precision=HI, preferred_element_type=f32)


def nn(a, b):
    return dot(a, b, ((1,), (0,)))


def tn(a, b):
    return dot(a, b, ((0,), (0,)))


def nt(a, b):
    return dot(a, b, ((1,), (1,)))


def product(left, right):
    return jnp.dot(left, right, precision=lax.Precision.HIGH, preferred_element_type=f32)


def factor(gram, work, upper, inverse, unroll=1):
    sub = lax.broadcasted_iota(jnp.int32, (8, W), 0)
    lane = lax.broadcasted_iota(jnp.int32, (8, W), 1)
    work[:, :W] = gram
    work[:, W:] = (lax.broadcasted_iota(jnp.int32, (W, W), 0) == lax.broadcasted_iota(jnp.int32, (W, W), 1)).astype(f32)
    def step(j, carry):
        base = pl.multiple_of(j * 8, 8)
        left = work[pl.ds(base, 8), :W]
        right = work[pl.ds(base, 8), W:]
        turned = pltpu.roll(left, (W - base) % W, 1)
        cols = [jnp.broadcast_to(turned[:, k : k + 1], (8, W)) for k in range(8)]
        scale = jnp.zeros((8, W), f32)
        for k in range(8):
            def line(v): return jnp.broadcast_to(v[k : k + 1, :], (8, W))
            pivot = line(cols[k])
            root = lax.rsqrt(pivot)
            root = root * (1.5 - 0.5 * pivot * root * root)
            weight = jnp.where(sub > k, cols[k] * (root * root), 0.0)
            scale = jnp.where(sub == k, root, scale)
            left = left - weight * line(left)
            right = right - weight * line(right)
            for m in range(k + 1, 8):
                cols[m] = cols[m] - weight * line(cols[m])
        left = jnp.where(lane >= base + sub, left * scale, 0.0)
        right = right * scale
        upper[pl.ds(base, 8), :] = left
        inverse[pl.ds(base, 8), :] = right
        panel = jnp.concatenate([left, right], axis=1)
        work[...] = work[...] - tn(left, panel)
        return carry
    lax.fori_loop(0, W // 8, step, 0, unroll=unroll)


def first_factor(g00, upper, inverse, work):
    factor(g00[...], work, upper, inverse)


def middle(g00, cee, g01, g11, inv0, first, full, upper1, comb1, image1, gram_p, g02, work, inv1):
    li0 = inv0[...]
    x0 = li0.T
    u = nt(cee[...], li0)
    side = jnp.concatenate([g00[...], g01[...]], axis=1)
    gram = jnp.concatenate([side, jnp.concatenate([g01[...].T, g11[...]], axis=1)])
    h = nn(li0, nn(side, jnp.concatenate([u, x0])))
    g00x0 = nt(gram[:, :W], li0)
    m00 = nn(li0, g00x0[:W])
    h_full = h + (h - nn(m00, h))
    first[...] = h
    full[...] = h_full
    comb = jnp.concatenate([u - nn(x0, h_full), x0])
    y = nn(gram, comb)
    factor(tn(comb, y), work, upper1, inv1)
    li1 = inv1[...]
    c1 = nt(comb, li1)
    y1 = nt(y, li1)
    comb1[...] = c1
    image1[:W, :] = nn(cee[...], c1[:W])
    image1[W:, :] = c1
    m01 = nn(li0, y1[:W])
    gram_p[:W, :W] = m00
    gram_p[:W, W:] = m01
    gram_p[W:, :W] = m01.T
    gram_p[W:, W:] = tn(c1, y1)
    g02[...] = g11[...] + tn(cee[...], g01[...])


def last(
    scale, g00, g01, g02, g11, g12, g22, inv0, first, full, upper1, comb1, image1, gram_p, mix, projection, first_pass, work, upper2, inv2
):
    li0 = inv0[...]
    c1 = comb1[...]
    i1 = image1[...]
    a01, a02, a12 = g01[...], g02[...], g12[...]
    gram = jnp.concatenate(
        [
            jnp.concatenate([g00[...], a01, a02], axis=1),
            jnp.concatenate([a01.T, g11[...], a12], axis=1),
            jnp.concatenate([a02.T, a12.T, g22[...]], axis=1),
        ]
    )
    s = nn(gram, i1)
    h = jnp.concatenate([nn(li0, s[:W]), tn(c1, s[: 2 * W])])
    h_full = h + (h - nn(gram_p[...], h))
    back = nn(c1, h_full[W:])
    comb = jnp.concatenate([i1[:W] - (back[:W] + tn(li0, h_full[:W])), i1[W : 2 * W] - back[W:], i1[2 * W :]])
    factor(tn(comb, nn(gram, comb)), work, upper2, inv2)
    zero = jnp.zeros((W, W), f32)
    mix[:W, :W] = li0.T * scale
    mix[W:, :W] = jnp.zeros((2 * W, W), f32)
    mix[: 2 * W, W : 2 * W] = c1 * scale
    mix[2 * W :, W : 2 * W] = zero
    mix[:, 2 * W :] = nt(comb, inv2[...]) * scale
    projection[:W, :W] = full[...]
    projection[W : 2 * W, :W] = upper1[...]
    projection[2 * W :, :W] = zero
    projection[: 2 * W, W:] = h_full
    projection[2 * W :, W:] = upper2[...]
    first_pass[:W, :W] = first[...]
    first_pass[W:, :W] = jnp.zeros((2 * W, W), f32)
    first_pass[: 2 * W, W:] = h
    first_pass[2 * W :, W:] = zero


def kernel(body, shapes, scratch, *args):
    return pl.pallas_call(
        body,
        out_shape=[jax.ShapeDtypeStruct(s, f32) for s in shapes],
        scratch_shapes=[pltpu.VMEM(s, f32) for s in scratch],
    )(*args)


def scattered(parts, axis):
    return jnp.sum(lax.all_to_all(parts, axis, 0, 0, tiled=True), axis=0)


def gathered(part, axis):
    copies = jnp.broadcast_to(part, (lax.axis_size(axis), *part.shape))
    return lax.all_to_all(copies, axis, 0, 0, tiled=True)


def other_core(value):
    return lax.ppermute(value, CORE, SWAP)


def turned(rows, chips, cores):
    return [
        ((r * chips + a) * cores + b, (a * chips + r) * cores + b)
        for r in range(rows)
        for a in range(chips)
        for b in range(cores)
    ]


def in_order(mine, theirs, core):
    first = core == 0
    return jnp.concatenate([jnp.where(first, mine, theirs), jnp.where(first, theirs, mine)])


def local(covariance, seed_index):
    height, breadth = covariance.shape
    width = seed_index.shape[0]
    rows, chips, cores = (lax.axis_size(a) for a in ALL)
    row, chip, core = (lax.axis_index(a) for a in ALL)
    order = height * rows
    share = breadth // rows
    half = height // cores
    cut = half // chips
    bit = width // chips
    square = (width, width)
    first = core == 0
    turn = turned(rows, chips, cores)

    def pick(a, b):
        return jnp.where(first, a, b)

    offsets = seed_index - row * height
    inside = (offsets >= 0) & (offsets < height)
    picked = jnp.take(covariance, jnp.clip(offsets, 0, height - 1), axis=0)
    picked = jnp.where(inside[:, None], picked, 0.0)
    start_piece = scattered(picked.reshape(width, rows, share).transpose(1, 0, 2), ROWS).T
    start = gathered(start_piece, ROWS).reshape(breadth, width)
    start_turned = lax.ppermute(start_piece, ALL, turn)
    lines = (chip * cores + core) * breadth + jnp.arange(breadth, dtype=jnp.int32)
    hot = lines[:, None] == seed_index[None, :]
    rest = jnp.where(jnp.any(hot, axis=1)[:, None], 0.0, start)
    g00 = dot(start, start, ((0,), (0,)))
    cee = dot(hot.astype(f32), start, ((0,), (0,)))
    partial = product(covariance, rest)
    keep = jnp.concatenate([pick(partial[:half], partial[half:]), pick(g00, cee)])
    send = jnp.concatenate([pick(partial[half:], partial[:half]), pick(cee, g00)])
    summed = keep + other_core(send)
    parts = jnp.concatenate([summed[:half].reshape(chips, cut, width), summed[half:].reshape(chips, bit, width)], axis=1)
    mine = gathered(jnp.concatenate([scattered(parts, CHIP), start_turned]), CHIP)
    theirs = other_core(mine)
    step_mine, step_theirs = (v[:, :cut].reshape(half, width) for v in (mine, theirs))
    extra_mine, extra_theirs = (v[:, cut : cut + bit].reshape(square) for v in (mine, theirs))
    start_mine, start_theirs = (v[:, cut + bit :].reshape(half, width) for v in (mine, theirs))
    g00 = pick(extra_mine, extra_theirs)
    cee = pick(extra_theirs, extra_mine)
    upper0, inv0 = kernel(first_factor, [square] * 2, [(width, 2 * width)], g00)
    step = in_order(step_mine, step_theirs, core)
    partial = dot_high(covariance, step)
    grams = [product(start_mine.T, step_mine), product(step_mine.T, step_mine)]
    parts = jnp.concatenate([partial.reshape(rows, share, width)] + [g.reshape(rows, bit, width) for g in grams], axis=1)
    piece = lax.ppermute(scattered(parts, ROWS), ALL, turn)
    mine = gathered(piece, CHIP)
    next_mine = mine[:, :share].reshape(half, width)
    g01 = mine[:, share : share + bit].reshape(square)
    g11 = mine[:, share + bit :].reshape(square)
    both = jnp.concatenate([g01, g11])
    g12, g22 = product(step_mine.T, next_mine), product(next_mine.T, next_mine)
    got = other_core(jnp.concatenate([both, pick(g22, g12)]))
    both = both + got[: 2 * width]
    total = pick(g12, g22) + got[2 * width :]
    next_theirs = other_core(next_mine)
    total = jnp.sum(gathered(total, ROWS), axis=0)
    g01, g11 = both[:width], both[width:]
    first_h, full_h, upper1, comb1, image1, gram_p, g02 = kernel(
        middle,
        [square, square, square, (2 * width, width), (3 * width, width), (2 * width, 2 * width), square],
        [(width, 2 * width), square],
        g00,
        cee,
        g01,
        g11,
        inv0,
    )
    rest_total = other_core(total)
    g12, g22 = pick(total, rest_total), pick(rest_total, total)
    scale = float(order) ** 0.5

    def last_step(*refs):
        last(f32(scale), *refs)

    mix, projection, first_pass = kernel(
        last_step,
        [(3 * width, 3 * width), (3 * width, 2 * width), (3 * width, 2 * width)],
        [(width, 2 * width), square, square],
        g00,
        g01,
        g02,
        g11,
        g12,
        g22,
        inv0,
        first_h,
        full_h,
        upper1,
        comb1,
        image1,
        gram_p,
    )
    mine = jnp.concatenate([start_mine, step_mine, next_mine], axis=1)
    theirs = jnp.concatenate([start_theirs, step_theirs, next_theirs], axis=1)
    basis = product(in_order(mine, theirs, core), mix)
    return basis, projection, first_pass


def dot_high(covariance, step):
    return product(covariance.T, step)


def solution(mesh):
    rows, cols = mesh.devices.shape
    fine = Mesh(mesh.devices.reshape(rows, cols // 2, 2), ALL)
    return jax.shard_map(
        local,
        mesh=fine,
        in_specs=(P(ROWS, (CHIP, CORE)), P()),
        out_specs=(P(ROWS, None), P(), P()),
        check_vma=False,
    )
```

profile of v0, /device:TPU:1, one launch (start us, length us, event | category | flops | bytes accessed | tf_op | source)
XLA Modules:
  0.0 216.2 jit_solution(15052820952752675811)
XLA Ops:
  0.6 0.7 compare_and_fusion
  1.3 4.4 %gather_fusion = f32[128,1024]{1,0:T(8,128)S(1)} fusion(f32[2048,1024]{1,0:T(8,128)} %param.2, s32[1024]{0:T(1024)S(1)} %pad_clamp_fusion), kind=kCustom, calls=%fused_computation | custom fusion | bytes 1049088 | tf_op jit(solution)/shard_map/jit(_take)/gather | solution.py:195
  5.7 0.1 fusion.12
  5.9 17.7 %all_to_all.35 = f32[8,128,128]{2,1,0:T(8,128)S(1)} all-to-all(f32[8,128,128]{2,1,0:T(8,128)S(1)} %fusion.12), channel_id=1, replica_groups=mesh['row'=8,'chip'=8,'core'=2] {'row'}, dimensions={0} | all-to-all | bytes 1048576 | tf_op jit(solution)/shard_map/all_to_all | solution.py:150
  23.6 0.1 copy.62
  23.7 0.8 broadcast_in_dim.59
  24.5 3.5 %all-to-all-start.1 = ((f32[8,128,128]{2,1,0:T(8,128)}), f32[8,128,128]{2,1,0:T(8,128)S(1)}, u32[]{:S(2)}, u32[]{:S(2)}) async-start(f32[8,128,128]{2,1,0:T(8,128)} %broadcast_in_dim.59), calls=%async_computation.1 | async-start | bytes 1048576 | tf_op jit(solution)/shard_map/all_to_all | solution.py:155
  28.1 0.4 compare_reduce_fusion
  28.5 8.2 %all-to-all-done.1 = f32[8,128,128]{2,1,0:T(8,128)S(1)} async-done(((f32[8,128,128]{2,1,0:T(8,128)}), f32[8,128,128]{2,1,0:T(8,128)S(1)}, u32[]{:S(2)}, u32[]{:S(2)}) %all-to-all-start.1) | async-done | bytes 524320 | tf_op jit(solution)/shard_map/all_to_all | solution.py:155
  36.6 0.7 fusion.9
  37.4 1.0 broadcast_select_fusion.6
  38.4 0.1 copy.65
  38.5 7.0 %convolution_bitcast_fusion = f32[2048,128]{0,1:T(8,128)S(1)} fusion(f32[2048,1024]{1,0:T(8,128)} %param.2, f32[1024,128]{1,0:T(8,128)S(1)} %bitcast.57, pred[1024]{0:T(1024)(128)(4,1)S(1)} %compare_reduce_fusion), kind=kOutput, calls=%fused_computation.5 | convolution fusion | flops 1610743808 | bytes 9962496 | tf_op jit(solution)/shard_map/dot_general | solution.py:35
  45.5 0.1 slice_select_fusion.1
  45.7 3.6 %collective-permute-start = (f32[1152,128]{0,1:T(8,128)S(1)}, f32[1152,128]{0,1:T(8,128)S(1)}, u32[]{:S(2)}, u32[]{:S(2)}) collective-permute-start(f32[1152,128]{0,1:T(8,128)S(1)} %pad_maximum_fusion.3), channel_id=1, source_target_pairs={{0,1},{1,0},{2,3},{3,2},{4,5},{5,4},{6,7},{7,6},{8,9},{9,8},{10,11... | collective-permute-start | bytes 1769480 | tf_op jit(solution)/shard_map/ppermute | solution.py:159
  49.3 0.1 copy.64
  49.4 1.5 collective-permute-done
  51.0 0.2 copy.85
  51.2 0.1 copy.66
  51.3 0.9 pad_maximum_fusion.4
  52.2 4.6 %all-to-all-start.2 = ((f32[8,144,128]{2,1,0:T(8,128)}), f32[8,144,128]{2,1,0:T(8,128)S(1)}, u32[]{:S(2)}, u32[]{:S(2)}) async-start(f32[8,144,128]{2,1,0:T(8,128)} %pad_maximum_fusion.4), calls=%async_computation.2 | async-start | bytes 1179648 | tf_op jit(solution)/shard_map/all_to_all | solution.py:150
  56.8 0.7 collective-permute-start.1
  57.5 0.1 copy.68
  57.6 10.2 %all-to-all-done.2 = f32[8,144,128]{2,1,0:T(8,128)S(1)} async-done(((f32[8,144,128]{2,1,0:T(8,128)}), f32[8,144,128]{2,1,0:T(8,128)S(1)}, u32[]{:S(2)}, u32[]{:S(2)}) %all-to-all-start.2) | async-done | bytes 589856 | tf_op jit(solution)/shard_map/all_to_all | solution.py:150
  67.9 21.7 %all_to_all.36 = f32[8,272,128]{2,1,0:T(8,128)S(1)} all-to-all(f32[8,272,128]{2,1,0:T(8,128)S(1)} %broadcast_in_dim.60), channel_id=1, replica_groups=mesh['row'=8,'chip'=8,'core'=2] {'chip'}, dimensions={0} | all-to-all | bytes 2228224 | tf_op jit(solution)/shard_map/all_to_all | solution.py:155
  89.7 2.2 %collective-permute-start.2 = (f32[8,272,128]{2,1,0:T(8,128)S(1)}, f32[8,272,128]{2,1,0:T(8,128)}, u32[]{:S(2)}, u32[]{:S(2)}) collective-permute-start(f32[8,272,128]{2,1,0:T(8,128)S(1)} %all_to_all.36), channel_id=1, source_target_pairs={{0,1},{1,0},{2,3},{3,2},{4,5},{5,4},{6,7},{7,6},{8,9},{9,8},{10,11... | collective-permute-start | bytes 3342344 | tf_op jit(solution)/shard_map/ppermute | solution.py:159
  91.9 0.1 fusion.25
  92.0 0.2 copy.86
  92.2 0.2 copy.97
  92.4 0.4 fusion.28
  92.8 0.4 fusion.29
  93.1 1.3 collective-permute-done.2
  94.4 2.1 fusion.24
  96.5 0.2 copy.87
  96.7 0.1 broadcast_select_fusion.1
  96.8 6.0 %convolution_bitcast_fusion.1 = f32[1024,128]{0,1:T(8,128)S(1)} fusion(f32[2048,1024]{1,0:T(8,128)} %param.2, f32[1024,128]{0,1:T(8,128)S(1)} %get-tuple-element.36, f32[1024,128]{0,1:T(8,128)S(1)} %get-tuple-element.35), kind=kOutput, calls=%fused_computation.8 | convolution fusion | flops 1610874880 | bytes 9961472 | tf_op jit(solution)/shard_map/dot_general | solution.py:35
  102.8 1.0 copy.88
  103.8 1.1 pad_maximum_fusion.2
  104.9 15.4 %all_to_all.37 = f32[8,160,128]{2,1,0:T(8,128)S(1)} all-to-all(f32[8,160,128]{2,1,0:T(8,128)S(1)} %pad_maximum_fusion.2), channel_id=1, replica_groups=mesh['row'=8,'chip'=8,'core'=2] {'row'}, dimensions={0} | all-to-all | bytes 1310720 | tf_op jit(solution)/shard_map/all_to_all | solution.py:150
  120.3 0.1 copy.94
  120.4 0.7 collective-permute-start.3
  121.1 0.1 copy.77
  121.2 0.9 broadcast_in_dim.61
  122.1 18.5 %all-to-all-start.5 = ((f32[8,160,128]{2,1,0:T(8,128)}), f32[8,160,128]{2,1,0:T(8,128)S(1)}, u32[]{:S(2)}, u32[]{:S(2)}) async-start(f32[8,160,128]{2,1,0:T(8,128)} %broadcast_in_dim.61), calls=%async_computation.5 | async-start | bytes 1310720 | tf_op jit(solution)/shard_map/all_to_all | solution.py:155
  140.6 2.1 copy.92
  142.6 8.6 %all-to-all-done.5 = f32[8,160,128]{2,1,0:T(8,128)S(1)} async-done(((f32[8,160,128]{2,1,0:T(8,128)}), f32[8,160,128]{2,1,0:T(8,128)S(1)}, u32[]{:S(2)}, u32[]{:S(2)}) %all-to-all-start.5) | async-done | bytes 655392 | tf_op jit(solution)/shard_map/all_to_all | solution.py:155
  151.2 0.6 convolution_bitcast_fusion.2
  151.8 1.2 broadcast_select_fusion.4
  153.1 0.7 pad_maximum_fusion.5
  153.8 1.8 collective-permute-start.5
  155.5 1.5 slice_select_fusion.2
  157.0 10.7 %shard_map.49 = (f32[128,128]{1,0:T(8,128)}, f32[128,128]{1,0:T(8,128)}) custom-call(f32[128,128]{1,0:T(8,128)} %bitcast.69), custom_call_target="tpu_custom_call" | custom-call | tf_op jit(solution)/shard_map/pallas_call | solution.py:142
  167.7 0.2 copy.91
  168.1 0.9 slice_add_fusion.1
  169.0 0.8 broadcast_in_dim.62
  169.8 4.0 %all-to-all-start.6 = ((f32[8,128,128]{2,1,0:T(8,128)}), f32[8,128,128]{2,1,0:T(8,128)S(1)}, u32[]{:S(2)}, u32[]{:S(2)}) async-start(f32[8,128,128]{2,1,0:T(8,128)} %broadcast_in_dim.62), calls=%async_computation.6 | async-start | bytes 1048576 | tf_op jit(solution)/shard_map/all_to_all | solution.py:155
  173.9 0.9 slice_add_fusion
  174.8 0.7 fusion.27
  175.4 14.2 %shard_map.50 = (f32[128,128]{1,0:T(8,128)}, f32[128,128]{1,0:T(8,128)}, f32[128,128]{1,0:T(8,128)}, f32[256,128]{1,0:T(8,128)}, f32[384,128]{1,0:T(8,128)}, /*index=5*/f32[256,256]{1,0:T(8,128)}, f32[128,128]{1,0:T(8,128)}) custom-call(f32[128,128]{1,0:T(8,128)} %bitcast.70, f32[128,128]{1,0:T(8,128)} %bitcast.77, ...), custom_call_target="tpu_custom_call" | custom-call | tf_op jit(solution)/shard_map/pallas_call | solution.py:142
  189.6 1.0 collective-permute-start.6
  190.6 3.0 %fusion.5 = (f32[1024,384]{0,1:T(8,128)S(1)}, f32[1024,384]{0,1:T(8,128)}) fusion(f32[1024,128]{0,1:T(8,128)} %collective-permute-done.4, f32[1024,128]{0,1:T(8,128)S(1)} %copy.87, f32[1024,128]{0,1:T(8,128)} %copy.92, f32[1024,128]{0,1:T(8,128)} %copy-done, f32[1024,128]{0,1:T(8,128)S(1)} %copy.97, f32[1024,128]{0,1:T(8,128)S(1)} %copy.86, pred[]{:T(512)S(6)} %eq.8), kind=kLoop, calls=%fused_computation.13 | loop fusion | flops 2359296 | bytes 6291457 | tf_op jit(solution)/shard_map/jit(_where)/select_n | solution.py:173
  193.6 0.7 broadcast_select_fusion.2
  194.3 15.4 %shard_map.51 = (f32[384,384]{1,0:T(8,128)}, f32[384,256]{1,0:T(8,128)}, f32[384,256]{1,0:T(8,128)}) custom-call(f32[128,128]{1,0:T(8,128)} %bitcast.71, f32[128,128]{1,0:T(8,128)} %get-tuple-element.44.g01.refs_1_, f32[128,128]{1,0:T(8,128)} %get-tuple-element.15.refs_2_, f32[128,128]{1,0:T(8,128)} %get-tuple-element.43.g11.refs_3_, ...), custom_call_target="tpu_custom_call" | custom-call | tf_op jit(solution)/shard_map/pallas_call | solution.py:142
  209.7 6.5 %fusion = f32[2048,384]{1,0:T(8,128)} fusion(f32[384,384]{1,0:T(8,128)} %get-tuple-element.22, f32[1024,384]{0,1:T(8,128)} %get-tuple-element.28, f32[1024,384]{0,1:T(8,128)S(1)} %get-tuple-element.27), kind=kOutput, calls=%fused_computation.1 | convolution fusion | flops 1812725760 | bytes 6881280 | tf_op jit(solution)/shard_map/dot_general | solution.py:35
  (27 shorter events, 0.5 us)
Async XLA Ops:
  5.9 22.2 %copy-start.2 = (s32[128]{0:T(128)S(1)}, s32[128]{0:T(128)}, u32[]{:S(2)}) copy-start(s32[128]{0:T(128)} %param.3) | copy-start | bytes 1540
  24.5 12.1 %all-to-all-start.1 = ((f32[8,128,128]{2,1,0:T(8,128)}), f32[8,128,128]{2,1,0:T(8,128)S(1)}, u32[]{:S(2)}, u32[]{:S(2)}) async-start(f32[8,128,128]{2,1,0:T(8,128)} %broadcast_in_dim.59), calls=%async_computation.1 | async-start | bytes 1048576 | tf_op jit(solution)/shard_map/all_to_all | solution.py:155
  45.7 5.2 %collective-permute-start = (f32[1152,128]{0,1:T(8,128)S(1)}, f32[1152,128]{0,1:T(8,128)S(1)}, u32[]{:S(2)}, u32[]{:S(2)}) collective-permute-start(f32[1152,128]{0,1:T(8,128)S(1)} %pad_maximum_fusion.3), channel_id=1, source_target_pairs={{0,1},{1,0},{2,3},{3,2},{4,5},{5,4},{6,7},{7,6},{8,9},{9,8},{10,11... | collective-permute-start | bytes 1769480 | tf_op jit(solution)/shard_map/ppermute | solution.py:159
  52.2 15.6 %all-to-all-start.2 = ((f32[8,144,128]{2,1,0:T(8,128)}), f32[8,144,128]{2,1,0:T(8,128)S(1)}, u32[]{:S(2)}, u32[]{:S(2)}) async-start(f32[8,144,128]{2,1,0:T(8,128)} %pad_maximum_fusion.4), calls=%async_computation.2 | async-start | bytes 1179648 | tf_op jit(solution)/shard_map/all_to_all | solution.py:150
  56.8 0.7 collective-permute-start.1
  89.7 4.7 %collective-permute-start.2 = (f32[8,272,128]{2,1,0:T(8,128)S(1)}, f32[8,272,128]{2,1,0:T(8,128)}, u32[]{:S(2)}, u32[]{:S(2)}) collective-permute-start(f32[8,272,128]{2,1,0:T(8,128)S(1)} %all_to_all.36), channel_id=1, source_target_pairs={{0,1},{1,0},{2,3},{3,2},{4,5},{5,4},{6,7},{7,6},{8,9},{9,8},{10,11... | collective-permute-start | bytes 3342344 | tf_op jit(solution)/shard_map/ppermute | solution.py:159
  120.4 0.7 collective-permute-start.3
  122.1 29.2 %all-to-all-start.5 = ((f32[8,160,128]{2,1,0:T(8,128)}), f32[8,160,128]{2,1,0:T(8,128)S(1)}, u32[]{:S(2)}, u32[]{:S(2)}) async-start(f32[8,160,128]{2,1,0:T(8,128)} %broadcast_in_dim.61), calls=%async_computation.5 | async-start | bytes 1310720 | tf_op jit(solution)/shard_map/all_to_all | solution.py:155
  153.8 14.3 %collective-permute-start.5 = (f32[384,128]{1,0:T(8,128)}, f32[384,128]{1,0:T(8,128)}, u32[]{:S(2)}, u32[]{:S(2)}) collective-permute-start(f32[384,128]{1,0:T(8,128)} %pad_maximum_fusion.5), channel_id=1, source_target_pairs={{0,1},{1,0},{2,3},{3,2},{4,5},{5,4},{6,7},{7,6},{8,9},{9,8},{10,11... | collective-permute-start | bytes 589832 | tf_op jit(solution)/shard_map/ppermute | solution.py:159
  157.0 11.0 %copy-start.1 = (f32[128,128]{1,0:T(8,128)S(1)}, f32[128,128]{1,0:T(8,128)}, u32[]{:S(2)}) copy-start(f32[128,128]{1,0:T(8,128)} %get-tuple-element.49) | copy-start | bytes 196612
  167.9 21.7 %copy-start = (f32[1024,128]{0,1:T(8,128)}, f32[1024,128]{0,1:T(8,128)S(1)}, u32[]{:S(2)}) copy-start(f32[1024,128]{0,1:T(8,128)S(1)} %copy.91) | copy-start | bytes 1572868
  168.0 22.7 %collective-permute-start.4 = (f32[1024,128]{0,1:T(8,128)S(1)}, f32[1024,128]{0,1:T(8,128)}, u32[]{:S(2)}, u32[]{:S(2)}) collective-permute-start(f32[1024,128]{0,1:T(8,128)S(1)} %copy.91), channel_id=1, source_target_pairs={{0,1},{1,0},{2,3},{3,2},{4,5},{5,4},{6,7},{7,6},{8,9},{9,8},{10,11... | collective-permute-start | bytes 1572872 | tf_op jit(solution)/shard_map/ppermute | solution.py:159
  169.8 19.8 %all-to-all-start.6 = ((f32[8,128,128]{2,1,0:T(8,128)}), f32[8,128,128]{2,1,0:T(8,128)S(1)}, u32[]{:S(2)}, u32[]{:S(2)}) async-start(f32[8,128,128]{2,1,0:T(8,128)} %broadcast_in_dim.62), calls=%async_computation.6 | async-start | bytes 1048576 | tf_op jit(solution)/shard_map/all_to_all | solution.py:155
  189.6 4.0 %collective-permute-start.6 = (f32[128,128]{1,0:T(8,128)S(1)}, f32[128,128]{1,0:T(8,128)S(1)}, u32[]{:S(2)}, u32[]{:S(2)}) collective-permute-start(f32[128,128]{1,0:T(8,128)S(1)} %reduce_sum.39), channel_id=1, source_target_pairs={{0,1},{1,0},{2,3},{3,2},{4,5},{5,4},{6,7},{7,6},{8,9},{9,8},{10,11... | collective-permute-start | bytes 196616 | tf_op jit(solution)/shard_map/ppermute | solution.py:159
where the time goes:
time: 217 us; the launch traced here: 216 us
  blocking collectives  54.8 us (25%)
  starting transfers between devices  40.6 us (19%)
  Pallas kernels  40.3 us (19%)
  waiting for transfers between devices  29.8 us (14%)
  matrix products  23.8 us (11%)
  local copies, waits for them, and re-layouts  14.7 us (7%)
  other arithmetic  11.2 us (5%)
    pallas_call x3, Pallas kernels, kernel(): pl.pallas_call(body, out_shape=[jax.ShapeDtypeStruct(s, f32) for s in sha...  40.3 us
    all_to_all x2, blocking collectives, scattered(): return jnp.sum(lax.all_to_all(parts, axis, 0, 0, tiled=True), axis=0)  33.1 us
    all_to_all x3, starting transfers between devices, gathered(): return lax.all_to_all(copies, axis, 0, 0, tiled=True)  26 us
    dot_general x7, matrix products, product(): jnp.dot(left, right, precision=lax.Precision.HIGH, preferred_element_type...  22.1 us
    all_to_all x1, blocking collectives, gathered(): return lax.all_to_all(copies, axis, 0, 0, tiled=True)  21.7 us
    all_to_all x3, waiting for transfers between devices, gathered(): return lax.all_to_all(copies, axis, 0, 0, tiled=True)  16.8 us
    all_to_all x1, waiting for transfers between devices, scattered(): return jnp.sum(lax.all_to_all(parts, axis, 0, 0, tiled=True), axis=0)  10.2 us
    ppermute x5, starting transfers between devices, other_core(): return lax.ppermute(value, CORE, SWAP)  8.65 us
  transfers between devices with their start and end apart: 11, of which 5 were waited for; matrix products, arithmetic and copies ran while one was open for 5% of the time, Pallas kernels for 11%

commit v1 on v0

v1 whole, which is shorter than its diff:
```python
import jax
import jax.numpy as jnp
from jax import lax
from jax.experimental import pallas as pl
from jax.experimental.pallas import tpu as pltpu
from jax.sharding import Mesh, PartitionSpec as P

ROWS = "row"
CHIP = "chip"
CORE = "core"
ALL = (ROWS, CHIP, CORE)
SWAP = [(0, 1), (1, 0)]
W = 128
f32 = jnp.float32
bf16 = jnp.bfloat16
HI = lax.Precision.HIGHEST


def dot(a, b, dims):
    return lax.dot_general(a, b, (dims, ((), ())), precision=HI, preferred_element_type=f32)


def nn(a, b):
    return dot(a, b, ((1,), (0,)))


def tn(a, b):
    return dot(a, b, ((0,), (0,)))


def nt(a, b):
    return dot(a, b, ((1,), (1,)))


def pieces(x):
    a = x.astype(bf16)
    rest = x - a.astype(f32)
    b = rest.astype(bf16)
    return a, b, (rest - b.astype(f32)).astype(bf16)


def outer(left, panel):
    a0, a1, a2 = pieces(left)
    b0, b1, b2 = pieces(panel)
    return lax.dot_general(
        jnp.concatenate([a0, a0, a1, a0, a2, a1]),
        jnp.concatenate([b0, b1, b0, b2, b0, b1]),
        (((0,), (0,)), ((), ())),
        preferred_element_type=f32,
    )


BAND = 16


def factor(gram, work, upper, inverse):
    sub = lax.broadcasted_iota(jnp.int32, (BAND, W), 0)
    lane = lax.broadcasted_iota(jnp.int32, (BAND, W), 1)
    work[:, :W] = gram
    work[:, W:] = (
        lax.broadcasted_iota(jnp.int32, (W, W), 0) == lax.broadcasted_iota(jnp.int32, (W, W), 1)
    ).astype(f32)

    def step(j, carry):
        base = pl.multiple_of(j * BAND, BAND)
        left = work[pl.ds(base, BAND), :W]
        right = work[pl.ds(base, BAND), W:]
        turned = pltpu.roll(left, (W - base) % W, 1)
        cols = [jnp.broadcast_to(turned[:, k : k + 1], (BAND, W)) for k in range(BAND)]
        scale = jnp.zeros((BAND, W), f32)
        for k in range(BAND):
            top = k // 8 * 8

            def line(v):
                return jnp.broadcast_to(v[k : k + 1, :], (BAND - top, W))

            def below(old, new):
                return new if top == 0 else jnp.concatenate([old[:top], new])

            root = lax.rsqrt(line(cols[k]))
            weight = jnp.where(sub[top:] > k, cols[k][top:] * (root * root), 0.0)
            scale = below(scale, jnp.where(sub[top:] == k, root, scale[top:]))
            for m in range(k + 1, BAND):
                cols[m] = below(cols[m], cols[m][top:] - weight * line(cols[m]))
            left = below(left, left[top:] - weight * line(left))
            right = below(right, right[top:] - weight * line(right))
        left = jnp.where(lane >= base + sub, left * scale, 0.0)
        right = right * scale
        upper[pl.ds(base, BAND), :] = left
        inverse[pl.ds(base, BAND), :] = right
        work[...] = work[...] - outer(left, jnp.concatenate([left, right], axis=1))
        return carry

    lax.fori_loop(0, W // BAND, step, 0)


def first_factor(g00, upper, inverse, work):
    factor(g00[...], work, upper, inverse)


def middle(g00, cee, g01, g11, inv0, pack, work, upper1, inv1):
    li0 = inv0[...]
    x0 = li0.T
    u = nt(cee[...], li0)
    side = jnp.concatenate([g00[...], g01[...]], axis=1)
    gram = jnp.concatenate([side, jnp.concatenate([g01[...].T, g11[...]], axis=1)])
    h = nn(li0, nn(side, jnp.concatenate([u, x0])))
    g00x0 = nt(gram[:, :W], li0)
    m00 = nn(li0, g00x0[:W])
    h_full = h + (h - nn(m00, h))
    comb = jnp.concatenate([u - nn(x0, h_full), x0])
    y = nn(gram, comb)
    factor(tn(comb, y), work, upper1, inv1)
    li1 = inv1[...]
    c1 = nt(comb, li1)
    y1 = nt(y, li1)
    m01 = nn(li0, y1[:W])
    blocks = (
        [h, h_full, upper1[...], nn(cee[...], c1[:W]), c1[:W], c1[W:]]
        + [m00, m01, m01.T, tn(c1, y1), g11[...] + tn(cee[...], g01[...])]
        + [g00[...], g01[...], g11[...], li0]
    )
    for i, block in enumerate(blocks):
        pack[i * W : (i + 1) * W, :] = block


PACK = 15


def last(scale, pack, g12, g22, mix, projection, first_pass, work, upper2, inv2):
    first, full, upper1, _, c1_top, c1_low, m00, m01, m10, m11, a02, a00, a01, a11, li0 = (
        pack[i * W : (i + 1) * W, :] for i in range(PACK)
    )
    i1 = pack[3 * W : 6 * W, :]
    c1 = i1[W:]
    a12 = g12[...]
    gram = jnp.concatenate(
        [
            jnp.concatenate([a00, a01, a02], axis=1),
            jnp.concatenate([a01.T, a11, a12], axis=1),
            jnp.concatenate([a02.T, a12.T, g22[...]], axis=1),
        ]
    )
    s = nn(gram, i1)
    h = jnp.concatenate([nn(li0, s[:W]), tn(c1, s[: 2 * W])])
    gram_p = jnp.concatenate([jnp.concatenate([m00, m01], axis=1), jnp.concatenate([m10, m11], axis=1)])
    h_full = h + (h - nn(gram_p, h))
    back = nn(c1, h_full[W:])
    comb = jnp.concatenate([i1[:W] - (back[:W] + tn(li0, h_full[:W])), i1[W : 2 * W] - back[W:], i1[2 * W :]])
    factor(tn(comb, nn(gram, comb)), work, upper2, inv2)
    zero = jnp.zeros((W, W), f32)
    mix[:W, :W] = li0.T * scale
    mix[W:, :W] = jnp.zeros((2 * W, W), f32)
    mix[: 2 * W, W : 2 * W] = c1 * scale
    mix[2 * W :, W : 2 * W] = zero
    mix[:, 2 * W :] = nt(comb, inv2[...]) * scale
    projection[:W, :W] = full
    projection[W : 2 * W, :W] = upper1
    projection[2 * W :, :W] = zero
    projection[: 2 * W, W:] = h_full
    projection[2 * W :, W:] = upper2[...]
    first_pass[:W, :W] = first
    first_pass[W:, :W] = jnp.zeros((2 * W, W), f32)
    first_pass[: 2 * W, W:] = h
    first_pass[2 * W :, W:] = zero


HBM = pl.BlockSpec(memory_space=pltpu.HBM)
VMEM = pl.BlockSpec(memory_space=pltpu.VMEM)
SMEM = pl.BlockSpec(memory_space=pltpu.SMEM)


def room(mib):
    return pltpu.CompilerParams(vmem_limit_bytes=mib * 2**20)


def kernel(body, shapes, scratch, *args):
    return pl.pallas_call(
        body,
        out_shape=[jax.ShapeDtypeStruct(s, f32) for s in shapes],
        in_specs=[VMEM] * len(args),
        out_specs=[VMEM] * len(shapes),
        scratch_shapes=[pltpu.VMEM(s, f32) for s in scratch],
        compiler_params=room(16),
    )(*args)


def halves(x):
    high = x.astype(bf16)
    return high, (x - high.astype(f32)).astype(bf16)


def mm(a, b):
    return lax.dot_general(a, b, (((1,), (0,)), ((), ())), preferred_element_type=f32)


def pick_rows(place, seeds, lanes, covariance, out, buffer, sem):
    count = seeds.shape[0]
    height = covariance.shape[0]
    base = place[0] * height

    def body(i, carry):
        line = jnp.clip(seeds[i] - base, 0, height - 1)
        pltpu.make_async_copy(covariance.at[pl.ds(line, 1), :], buffer.at[pl.ds(i, 1), :], sem).start()
        return carry

    lax.fori_loop(0, count, body, 0, unroll=8)
    offsets = jnp.broadcast_to(lanes[...] - base, (count, count))
    held = jnp.where((offsets >= 0) & (offsets < height), 1.0, 0.0).T > 0
    pltpu.make_async_copy(covariance.at[pl.ds(0, count), :], buffer, sem).wait()
    for p in range(out.shape[0]):
        out[p] = jnp.where(held, buffer[:, p * W : (p + 1) * W], 0.0)


def picked_rows(place, seeds, covariance, parts):
    count = seeds.shape[0]
    return pl.pallas_call(
        pick_rows,
        out_shape=jax.ShapeDtypeStruct((parts, count, W), f32),
        in_specs=[SMEM, SMEM, VMEM, HBM],
        out_specs=VMEM,
        scratch_shapes=[pltpu.VMEM((count, covariance.shape[1]), f32), pltpu.SemaphoreType.DMA],
    )(place, seeds, seeds.reshape(1, count), covariance)


CHUNKS = 8


def chunks_of(covariance, buffer, sems):
    tall = covariance.shape[0] // CHUNKS
    return [
        pltpu.make_async_copy(covariance.at[pl.ds(i * tall, tall), :], buffer.at[i], sems.at[i]) for i in range(CHUNKS)
    ]


def chunk_scratch(covariance):
    height, breadth = covariance.shape
    return [pltpu.VMEM((CHUNKS, height // CHUNKS, breadth), f32), pltpu.SemaphoreType.DMA((CHUNKS,))]


def first_product(place, lanes, covariance, start, keep, send, buffer, sems):
    height, breadth = covariance.shape
    half = height // 2
    tall = height // CHUNKS
    copies = chunks_of(covariance, buffer, sems)
    for copy in copies:
        copy.start()
    lines = lax.broadcasted_iota(jnp.int32, (breadth, W), 0) + place[2] * breadth
    hot = jnp.where(lines == lanes[...], 1.0, 0.0)
    hit = jnp.max(hot, axis=1, keepdims=True) > 0
    block = start[...]
    weights = jnp.concatenate(halves(jnp.where(hit, 0.0, block)), axis=1)
    g00 = tn(block, block)
    hot = hot.astype(bf16)
    cee = sum(lax.dot_general(hot, p, (((0,), (0,)), ((), ())), preferred_element_type=f32) for p in pieces(block))
    first = place[1] == 0
    keep[half:, :] = jnp.where(first, g00, cee)
    send[half:, :] = jnp.where(first, cee, g00)
    for i, copy in enumerate(copies):
        copy.wait()
        high, low = halves(buffer[i])
        both = mm(high, weights)
        value = both[:, :W] + both[:, W:] + mm(low, weights[:, :W])
        rows = slice(i * tall % half, i * tall % half + tall)
        mine = first if i * tall < half else jnp.logical_not(first)

        @pl.when(mine)
        def _():
            keep[rows, :] = value

        @pl.when(jnp.logical_not(mine))
        def _():
            send[rows, :] = value


def image_of_start(place, seeds, covariance, start):
    height = covariance.shape[0]
    shape = jax.ShapeDtypeStruct((height // 2 + W, W), f32)
    return pl.pallas_call(
        first_product,
        out_shape=[shape, shape],
        in_specs=[SMEM, VMEM, HBM, VMEM],
        out_specs=[VMEM] * 2,
        scratch_shapes=chunk_scratch(covariance),
    )(place, seeds.reshape(1, W), covariance, start)


def two_grams(a, b, c, out_a, out_b):
    right = halves(c[...])
    for left, out in ((a, out_a), (b, out_b)):
        high, low = halves(left[...].T)
        both = mm(high, jnp.concatenate(right, axis=1))
        out[...] = both[:, :W] + both[:, W:] + mm(low, right[0])


def grams_of(a, b, c):
    return kernel(two_grams, [(W, W)] * 2, [], a, b, c)


def second_product(place, covariance, mine, theirs, g01, g11, out, buffer, sems, total):
    height, breadth = covariance.shape
    half = height // 2
    tall = height // CHUNKS
    copies = chunks_of(covariance, buffer, sems)
    for copy in copies:
        copy.start()
    first = place[1] == 0
    parts = out.shape[0]
    bit = W // parts
    for p in range(parts):
        out[p, W : W + bit, :] = g01[p * bit : (p + 1) * bit, :]
        out[p, W + bit :, :] = g11[p * bit : (p + 1) * bit, :]
    for i, copy in enumerate(copies):
        rows = slice(i * tall % half, i * tall % half + tall)
        own, other = (mine, theirs) if i * tall < half else (theirs, mine)
        v_high, v_low = halves(jnp.where(first, own[rows, :], other[rows, :]).T)
        copy.wait()
        high, low = halves(buffer[i])
        both = mm(jnp.concatenate([v_high, v_low]), high)
        value = both[:W] + both[W:] + mm(v_high, low)
        if i == 0:
            total[...] = value
        elif i + 1 < CHUNKS:
            total[...] += value
        else:
            value += total[...]
            for p in range(parts):
                out[p, :W, :] = value[:, p * W : (p + 1) * W].T


def image_of_step(place, covariance, mine, theirs, g01, g11):
    breadth = covariance.shape[1]
    parts = breadth // W
    return pl.pallas_call(
        second_product,
        out_shape=jax.ShapeDtypeStruct((parts, W + 2 * (W // parts), W), f32),
        in_specs=[SMEM, HBM] + [VMEM] * 4,
        out_specs=VMEM,
        scratch_shapes=chunk_scratch(covariance) + [pltpu.VMEM((W, breadth), f32)],
    )(place, covariance, mine, theirs, g01, g11)


def basis_rows(core, s0, v0, k0, s1, v1, k1, mix, out, high, low):
    step = pl.program_id(0)
    count = pl.num_programs(0) // 2
    tall = out.shape[0]

    @pl.when(step == 0)
    def _():
        high[...], low[...] = halves(mix[...])

    def rows(parts, line):
        left = jnp.concatenate([p[pl.ds(line, tall), :] for p in parts], axis=1)
        l_high, l_low = halves(left)
        out[...] = mm(l_high, high[...]) + mm(l_low, high[...]) + mm(l_high, low[...])

    @pl.when(step < count)
    def _():
        rows((s0, v0, k0), pl.multiple_of(step * tall, tall))

    @pl.when(step >= count)
    def _():
        rows((s1, v1, k1), pl.multiple_of((step - count) * tall, tall))


def basis_of(core, mine, theirs, mix):
    half = mine[0].shape[0]
    count = half // 512
    return pl.pallas_call(
        basis_rows,
        out_shape=jax.ShapeDtypeStruct((2 * half, mix.shape[1]), f32),
        grid_spec=pltpu.PrefetchScalarGridSpec(
            num_scalar_prefetch=1,
            grid=(2 * count,),
            in_specs=[VMEM] * 7,
            out_specs=pl.BlockSpec(
                (512, mix.shape[1]),
                lambda i, c: (jnp.where(i < count, i + c[0] * count, i - count + (1 - c[0]) * count), 0),
            ),
            scratch_shapes=[pltpu.VMEM(mix.shape, bf16)] * 2,
        ),
        compiler_params=room(24),
    )(core, *mine, *theirs, mix)


def scattered(parts, axis):
    return jnp.sum(lax.all_to_all(parts, axis, 0, 0, tiled=True), axis=0)


def gathered(part, axis):
    copies = jnp.broadcast_to(part, (lax.axis_size(axis), *part.shape))
    return lax.all_to_all(copies, axis, 0, 0, tiled=True)


def other_core(value):
    return lax.ppermute(value, CORE, SWAP)


def turned(rows, chips, cores):
    return [
        ((r * chips + a) * cores + b, (a * chips + r) * cores + b)
        for r in range(rows)
        for a in range(chips)
        for b in range(cores)
    ]


def local(covariance, seed_index):
    height, breadth = covariance.shape
    width = seed_index.shape[0]
    rows, chips, cores = (lax.axis_size(a) for a in ALL)
    row, chip, core = (lax.axis_index(a) for a in ALL)
    order = height * rows
    share = breadth // rows
    half = height // cores
    cut = half // chips
    bit = width // chips
    square = (width, width)
    first = core == 0
    turn = turned(rows, chips, cores)

    def pick(a, b):
        return jnp.where(first, a, b)

    place = jnp.stack([row, core, chip * cores + core]).astype(jnp.int32)
    picked = picked_rows(place, seed_index, covariance, rows)
    start_piece = scattered(picked, ROWS).T
    start = gathered(start_piece, ROWS).reshape(breadth, width)
    start_turned = lax.ppermute(start_piece, ALL, turn)
    keep, send = image_of_start(place, seed_index, covariance, start)
    summed = keep + other_core(send)
    parts = jnp.concatenate([summed[:half].reshape(chips, cut, width), summed[half:].reshape(chips, bit, width)], axis=1)
    mine = gathered(jnp.concatenate([scattered(parts, CHIP), start_turned]), CHIP)
    theirs = other_core(mine)
    step_mine, step_theirs = (v[:, :cut].reshape(half, width) for v in (mine, theirs))
    extra_mine, extra_theirs = (v[:, cut : cut + bit].reshape(square) for v in (mine, theirs))
    start_mine, start_theirs = (v[:, cut + bit :].reshape(half, width) for v in (mine, theirs))
    g00 = pick(extra_mine, extra_theirs)
    cee = pick(extra_theirs, extra_mine)
    upper0, inv0 = kernel(first_factor, [square] * 2, [(width, 2 * width)], g00)
    g01, g11 = grams_of(start_mine, step_mine, step_mine)
    parts = image_of_step(place, covariance, step_mine, step_theirs, g01, g11)
    piece = lax.ppermute(scattered(parts, ROWS), ALL, turn)
    mine = gathered(piece, CHIP)
    mine, upper0, inv0 = lax.optimization_barrier((mine, upper0, inv0))
    next_mine = mine[:, :share].reshape(half, width)
    g01 = mine[:, share : share + bit].reshape(square)
    g11 = mine[:, share + bit :].reshape(square)
    both = jnp.concatenate([g01, g11])
    g12, g22 = grams_of(step_mine, next_mine, next_mine)
    got = other_core(jnp.concatenate([both, pick(g22, g12)]))
    both = both + got[: 2 * width]
    total = pick(g12, g22) + got[2 * width :]
    next_theirs = other_core(next_mine)
    totals = gathered(total, ROWS)
    g01, g11 = both[:width], both[width:]
    (pack,) = kernel(
        middle, [(PACK * width, width)], [(width, 2 * width), square, square], g00, cee, g01, g11, inv0
    )
    totals, pack = lax.optimization_barrier((totals, pack))
    total = jnp.sum(totals, axis=0)
    rest_total = other_core(total)
    g12, g22 = pick(total, rest_total), pick(rest_total, total)
    scale = float(order) ** 0.5

    def last_step(*refs):
        last(f32(scale), *refs)

    mix, projection, first_pass = kernel(
        last_step,
        [(3 * width, 3 * width), (3 * width, 2 * width), (3 * width, 2 * width)],
        [(width, 2 * width), square, square],
        pack,
        g12,
        g22,
    )
    basis = basis_of(place[1:2], (start_mine, step_mine, next_mine), (start_theirs, step_theirs, next_theirs), mix)
    return basis, projection, first_pass


def solution(mesh):
    rows, cols = mesh.devices.shape
    fine = Mesh(mesh.devices.reshape(rows, cols // 2, 2), ALL)
    return jax.shard_map(
        local,
        mesh=fine,
        in_specs=(P(ROWS, (CHIP, CORE)), P()),
        out_specs=(P(ROWS, None), P(), P()),
        check_vma=False,
    )
```

time: 217 us -> 181 us (0.83)
  matrix products: 23.8 us -> 0 us
  blocking collectives: 54.8 us -> 66.7 us
  local copies, waits for them, and re-layouts: 14.7 us -> 3.56 us
  waiting for transfers between devices: 29.8 us -> 20.8 us
  Pallas kernels: 40.3 us -> 47.5 us
  other arithmetic: 11.2 us -> 4.74 us
  starting transfers between devices: 40.6 us -> 35.4 us
    pallas_call x0 -> x4, Pallas kernels: none -> 25 us  [the longest x1 6.96 us: image_of_start(): pl.pallas_call(first_product, out_shape=[shape, shape], in_specs=[SMEM, V...]
    dot_general x9 -> x0, matrix products: 23.8 us -> none  [the longest x7 22.1 us: product(): jnp.dot(left, right, precision=lax.Precision.HIGH, preferred_element_type...]
    pallas_call x3 -> x5, Pallas kernels: 40.3 us -> 22.4 us  [kernel(): pl.pallas_call(body, out_shape=[jax.ShapeDtypeStruct(s, f32) for s in sha...]
    all_to_all x1 -> x2, blocking collectives: 21.7 us -> 34 us  [gathered(): return lax.all_to_all(copies, axis, 0, 0, tiled=True)]
    all_to_all x3 -> x2, waiting for transfers between devices: 16.8 us -> 5.13 us  [gathered(): return lax.all_to_all(copies, axis, 0, 0, tiled=True)]
    all_to_all x3 -> x2, starting transfers between devices: 26 us -> 17.5 us  [gathered(): return lax.all_to_all(copies, axis, 0, 0, tiled=True)]
    gather x1 -> x0, local copies, waits for them, and re-layouts: 4.43 us -> none  [local(): picked = jnp.take(covariance, jnp.clip(offsets, 0, height - 1), axis=0)]
    reshape x7 -> x0, local copies, waits for them, and re-layouts: 4.03 us -> none  [the longest x2 2.26 us: local(): v[:, cut + bit:].reshape(half, width)]
  transfers between devices with their start and end apart: 11 -> 10, of which waited for: 5 -> 7; matrix products, arithmetic and copies ran while one was open for 5% -> 2% of each run, Pallas kernels for 11% -> 12%
where the time goes in v1:
time: 181 us; the launch traced here: 180 us
  blocking collectives  66.7 us (37%)
  Pallas kernels  47.5 us (26%)
  starting transfers between devices  35.4 us (20%)
  waiting for transfers between devices  20.8 us (11%)
  other arithmetic  4.74 us (3%)
  local copies, waits for them, and re-layouts  3.56 us (2%)
    all_to_all x2, blocking collectives, gathered(): return lax.all_to_all(copies, axis, 0, 0, tiled=True)  34 us
    all_to_all x2, blocking collectives, scattered(): return jnp.sum(lax.all_to_all(parts, axis, 0, 0, tiled=True), axis=0)  32.7 us
    pallas_call x5, Pallas kernels, kernel(): pl.pallas_call(body, out_shape=[jax.ShapeDtypeStruct(s, f32) for s in sha...  22.4 us
    all_to_all x2, starting transfers between devices, gathered(): return lax.all_to_all(copies, axis, 0, 0, tiled=True)  17.5 us
    ppermute x5, starting transfers between devices, other_core(): return lax.ppermute(value, CORE, SWAP)  11.9 us
    all_to_all x1, waiting for transfers between devices, scattered(): return jnp.sum(lax.all_to_all(parts, axis, 0, 0, tiled=True), axis=0)  10.2 us
    pallas_call x1, Pallas kernels, image_of_start(): pl.pallas_call(first_product, out_shape=[shape, shape], in_specs=[SMEM, V...  6.96 us
    pallas_call x1, Pallas kernels, picked_rows(): pl.pallas_call(pick_rows, out_shape=jax.ShapeDtypeStruct((parts, count, W...  6.27 us
  transfers between devices with their start and end apart: 10, of which 7 were waited for; matrix products, arithmetic and copies ran while one was open for 2% of the time, Pallas kernels for 12%

profile of v1, /device:TPU:1, one launch (start us, length us, event | category | flops | bytes accessed | tf_op | source)
XLA Modules:
  0.0 179.6 jit_solution(13873505936451632169)
XLA Ops:
  0.6 0.6 pad_add_fusion.place
  1.2 6.3 %shard_map.49 = f32[8,128,128]{2,1,0:T(8,128)} custom-call(s32[3]{0:T(128)} %pad_add_fusion.place, s32[128]{0:T(128)} %seeds.1, s32[1,128]{1,0:T(1,128)} %bitcast.43, f32[2048,1024]{1,0:T(8,128)} %covariance.5), custom_call_target="tpu_custom_call" | custom-call | tf_op jit(solution)/shard_map/pallas_call | solution.py:217
  7.5 17.5 %all_to_all.35 = f32[8,128,128]{2,1,0:T(8,128)S(1)} all-to-all(f32[8,128,128]{2,1,0:T(8,128)} %shard_map.49), channel_id=1, replica_groups=mesh['row'=8,'chip'=8,'core'=2] {'row'}, dimensions={0} | all-to-all | bytes 1048576 | tf_op jit(solution)/shard_map/all_to_all | solution.py:387
  25.0 0.1 copy.5
  25.2 12.2 %all_to_all.36 = f32[8,128,128]{2,1,0:T(8,128)} all-to-all(f32[8,128,128]{2,1,0:T(8,128)S(1)} %broadcast_in_dim.12), channel_id=1, replica_groups=mesh['row'=8,'chip'=8,'core'=2] {'row'}, dimensions={0} | all-to-all | bytes 1048576 | tf_op jit(solution)/shard_map/all_to_all | solution.py:392
  37.4 7.0 %shard_map.50 = (f32[1152,128]{1,0:T(8,128)}, f32[1152,128]{1,0:T(8,128)}) custom-call(s32[3]{0:T(128)} %pad_add_fusion.place, s32[1,128]{1,0:T(1,128)} %bitcast.44, f32[2048,1024]{1,0:T(8,128)} %covariance.5, f32[1024,128]{1,0:T(8,128)} %bitcast.34), custom_call_target="tpu_custom_call" | custom-call | tf_op jit(solution)/shard_map/pallas_call | solution.py:279
  44.3 3.6 %collective-permute-start = (f32[1152,128]{1,0:T(8,128)}, f32[1152,128]{1,0:T(8,128)S(1)}, u32[]{:S(2)}, u32[]{:S(2)}) collective-permute-start(f32[1152,128]{1,0:T(8,128)} %get-tuple-element.18), channel_id=1, source_target_pairs={{0,1},{1,0},{2,3},{3,2},{4,5},{5,4},{6,7},{7,6},{8,9},{9,8},{10,11... | collective-permute-start | bytes 1769480 | tf_op jit(solution)/shard_map/ppermute | solution.py:396
  48.0 1.8 %collective-permute-done = f32[1152,128]{1,0:T(8,128)S(1)} collective-permute-done((f32[1152,128]{1,0:T(8,128)}, f32[1152,128]{1,0:T(8,128)S(1)}, u32[]{:S(2)}, u32[]{:S(2)}) %collective-permute-start) | collective-permute-done | bytes 589856 | tf_op jit(solution)/shard_map/ppermute | solution.py:396
  49.8 1.1 add.13
  51.0 0.9 pad_maximum_fusion
  51.8 4.6 %all-to-all-start.2 = ((f32[8,144,128]{2,1,0:T(8,128)}), f32[8,144,128]{2,1,0:T(8,128)S(1)}, u32[]{:S(2)}, u32[]{:S(2)}) async-start(f32[8,144,128]{2,1,0:T(8,128)} %pad_maximum_fusion), calls=%async_computation.2 | async-start | bytes 1179648 | tf_op jit(solution)/shard_map/all_to_all | solution.py:387
  56.5 0.7 collective-permute-start.1
  57.1 0.0 collective-permute-done.1
  57.2 0.1 copy.6
  57.2 10.2 %all-to-all-done.2 = f32[8,144,128]{2,1,0:T(8,128)S(1)} async-done(((f32[8,144,128]{2,1,0:T(8,128)}), f32[8,144,128]{2,1,0:T(8,128)S(1)}, u32[]{:S(2)}, u32[]{:S(2)}) %all-to-all-start.2) | async-done | bytes 589856 | tf_op jit(solution)/shard_map/all_to_all | solution.py:387
  67.5 0.1 broadcast_in_dim.13
  67.6 21.8 %all_to_all.37 = f32[8,272,128]{2,1,0:T(8,128)S(1)} all-to-all(f32[8,272,128]{2,1,0:T(8,128)S(1)} %broadcast_in_dim.13), channel_id=1, replica_groups=mesh['row'=8,'chip'=8,'core'=2] {'chip'}, dimensions={0} | all-to-all | bytes 2228224 | tf_op jit(solution)/shard_map/all_to_all | solution.py:392
  89.4 2.1 %collective-permute-start.2 = (f32[8,272,128]{2,1,0:T(8,128)S(1)}, f32[8,272,128]{2,1,0:T(8,128)S(1)}, u32[]{:S(2)}, u32[]{:S(2)}) collective-permute-start(f32[8,272,128]{2,1,0:T(8,128)S(1)} %all_to_all.37), channel_id=1, source_target_pairs={{0,1},{1,0},{2,3},{3,2},{4,5},{5,4},{6,7},{7,6},{8,9},{9,8},{10,11... | collective-permute-start | bytes 3342344 | tf_op jit(solution)/shard_map/ppermute | solution.py:396
  91.5 0.1 fusion.1
  91.6 0.0 copy-start
  91.6 0.5 shard_map.51
  92.1 0.0 copy-start.4
  92.1 0.0 copy-start.5
  92.1 1.8 collective-permute-done.2
  93.9 0.0 copy-start.6
  93.9 1.2 fusion
  95.1 0.0 copy-done
  95.1 0.1 copy-done.6
  95.2 0.0 copy-done.4
  95.2 0.0 copy-done.5
  95.2 6.0 %shard_map.52 = f32[8,160,128]{2,1,0:T(8,128)} custom-call(s32[3]{0:T(128)} %pad_add_fusion.place, f32[2048,1024]{1,0:T(8,128)} %covariance.5, f32[1024,128]{1,0:T(8,128)} %bitcast.19, f32[1024,128]{1,0:T(8,128)} %bitcast.28, f32[128,128]{1,0:T(8,128)} %copy-done.4, f32[128,128]{1,0:T(8,128)} %copy-done.5), custom_call_target="tpu_custom_call" | custom-call | tf_op jit(solution)/shard_map/pallas_call | solution.py:334
  101.3 15.2 %all_to_all.38 = f32[8,160,128]{2,1,0:T(8,128)S(1)} all-to-all(f32[8,160,128]{2,1,0:T(8,128)} %shard_map.52), channel_id=1, replica_groups=mesh['row'=8,'chip'=8,'core'=2] {'row'}, dimensions={0} | all-to-all | bytes 1310720 | tf_op jit(solution)/shard_map/all_to_all | solution.py:387
  116.5 0.7 collective-permute-start.3
  117.2 0.0 collective-permute-done.3
  117.2 0.9 broadcast_in_dim.14
  118.1 13.2 %all-to-all-start.5 = ((f32[8,160,128]{2,1,0:T(8,128)}), f32[8,160,128]{2,1,0:T(8,128)S(1)}, u32[]{:S(2)}, u32[]{:S(2)}) async-start(f32[8,160,128]{2,1,0:T(8,128)} %broadcast_in_dim.14), calls=%async_computation.5 | async-start | bytes 1310720 | tf_op jit(solution)/shard_map/all_to_all | solution.py:392
  131.3 0.0 copy-start.1
  131.3 0.9 slice_select_fusion
  132.2 5.0 %shard_map.53 = (f32[128,128]{1,0:T(8,128)}, f32[128,128]{1,0:T(8,128)S(1)}) custom-call(f32[128,128]{1,0:T(8,128)S(1)} %bitcast.31), custom_call_target="tpu_custom_call" | custom-call | tf_op jit(solution)/shard_map/pallas_call | solution.py:178
  137.2 2.5 %all-to-all-done.5 = f32[8,160,128]{2,1,0:T(8,128)S(1)} async-done(((f32[8,160,128]{2,1,0:T(8,128)}), f32[8,160,128]{2,1,0:T(8,128)S(1)}, u32[]{:S(2)}, u32[]{:S(2)}) %all-to-all-start.5) | async-done | bytes 655392 | tf_op jit(solution)/shard_map/all_to_all | solution.py:392
  139.7 0.0 copy-done.1
  139.7 0.5 shard_map.54
  140.2 4.9 %collective-permute-start.5 = (f32[384,128]{1,0:T(8,128)S(1)}, f32[384,128]{1,0:T(8,128)S(1)}, u32[]{:S(2)}, u32[]{:S(2)}) collective-permute-start(f32[384,128]{1,0:T(8,128)S(1)} %pad_maximum_fusion.1), channel_id=1, source_target_pairs={{0,1},{1,0},{2,3},{3,2},{4,5},{5,4},{6,7},{7,6},{8,9},{9,8},{10,11... | collective-permute-start | bytes 589832 | tf_op jit(solution)/shard_map/ppermute | solution.py:396
  145.1 0.1 collective-permute-start.4
  145.2 1.0 collective-permute-done.5
  146.2 0.8 broadcast_in_dim.15
  147.0 4.3 %all-to-all-start.6 = ((f32[8,128,128]{2,1,0:T(8,128)}), f32[8,128,128]{2,1,0:T(8,128)}, u32[]{:S(2)}, u32[]{:S(2)}) async-start(f32[8,128,128]{2,1,0:T(8,128)} %broadcast_in_dim.15), calls=%async_computation.6 | async-start | bytes 1048576 | tf_op jit(solution)/shard_map/all_to_all | solution.py:392
  151.4 7.6 %shard_map.55.refs_0_ = f32[1920,128]{1,0:T(8,128)S(1)} custom-call(f32[128,128]{1,0:T(8,128)S(1)} %bitcast.32, f32[128,128]{1,0:T(8,128)S(1)} %bitcast.33, f32[128,128]{1,0:T(8,128)S(1)} %get-tuple-element.42.g01, f32[128,128]{1,0:T(8,128)S(1)} %get-tuple-element.41.g11, f32[128,128]{1,0:T(8,128)S(1)} %get-tuple-element.25.inv0), custom_call_target="tpu_custom_call" | custom-call | tf_op jit(solution)/shard_map/pallas_call | solution.py:178
  159.0 0.0 copy-start.2
  159.0 2.7 %all-to-all-done.6 = f32[8,128,128]{2,1,0:T(8,128)} async-done(((f32[8,128,128]{2,1,0:T(8,128)}), f32[8,128,128]{2,1,0:T(8,128)}, u32[]{:S(2)}, u32[]{:S(2)}) %all-to-all-start.6) | async-done | bytes 524320 | tf_op jit(solution)/shard_map/all_to_all | solution.py:392
  161.7 1.1 reduce_sum.39
  162.8 0.0 copy-start.3
  162.8 1.2 collective-permute-start.6
  164.0 0.9 collective-permute-done.6
  165.0 8.8 %shard_map.56 = (f32[384,384]{1,0:T(8,128)S(1)}, f32[384,256]{1,0:T(8,128)}, f32[384,256]{1,0:T(8,128)}) custom-call(f32[1920,128]{1,0:T(8,128)S(1)} %shard_map.55.refs_0_, f32[128,128]{1,0:T(8,128)S(1)} %get-tuple-element.40.refs_1_, f32[128,128]{1,0:T(8,128)S(1)} %get-tuple-element.39.refs_2_), custom_call_target="tpu_custom_call" | custom-call | tf_op jit(solution)/shard_map/pallas_call | solution.py:178
  173.8 0.0 collective-permute-done.4.k1
  173.8 0.0 copy-done.2
  173.8 0.0 copy-done.3
  173.8 5.8 %shard_map.57 = f32[2048,384]{1,0:T(8,128)} custom-call(s32[1]{0:T(128)} %bitcast.core, f32[1024,128]{1,0:T(8,128)S(1)} %bitcast.27, f32[1024,128]{1,0:T(8,128)S(1)} %bitcast.21, f32[1024,128]{1,0:T(8,128)S(1)} %bitcast.25, f32[1024,128]{1,0:T(8,128)S(1)} %bitcast.30, f32[1024,128]{1,0:T(8,128)S(1)} %bitcast.29, f32[1024,128]{1,0:T(8,128)} %collective-permute-done.4.k1, ...), custom_call_target="tpu_custom_call" | custom-call | tf_op jit(solution)/shard_map/pallas_call | solution.py:369
  (15 shorter events, 0.3 us)
Async XLA Ops:
  44.3 5.5 %collective-permute-start = (f32[1152,128]{1,0:T(8,128)}, f32[1152,128]{1,0:T(8,128)S(1)}, u32[]{:S(2)}, u32[]{:S(2)}) collective-permute-start(f32[1152,128]{1,0:T(8,128)} %get-tuple-element.18), channel_id=1, source_target_pairs={{0,1},{1,0},{2,3},{3,2},{4,5},{5,4},{6,7},{7,6},{8,9},{9,8},{10,11... | collective-permute-start | bytes 1769480 | tf_op jit(solution)/shard_map/ppermute | solution.py:396
  51.8 15.6 %all-to-all-start.2 = ((f32[8,144,128]{2,1,0:T(8,128)}), f32[8,144,128]{2,1,0:T(8,128)S(1)}, u32[]{:S(2)}, u32[]{:S(2)}) async-start(f32[8,144,128]{2,1,0:T(8,128)} %pad_maximum_fusion), calls=%async_computation.2 | async-start | bytes 1179648 | tf_op jit(solution)/shard_map/all_to_all | solution.py:387
  56.5 0.7 collective-permute-start.1
  89.4 4.5 %collective-permute-start.2 = (f32[8,272,128]{2,1,0:T(8,128)S(1)}, f32[8,272,128]{2,1,0:T(8,128)S(1)}, u32[]{:S(2)}, u32[]{:S(2)}) collective-permute-start(f32[8,272,128]{2,1,0:T(8,128)S(1)} %all_to_all.37), channel_id=1, source_target_pairs={{0,1},{1,0},{2,3},{3,2},{4,5},{5,4},{6,7},{7,6},{8,9},{9,8},{10,11... | collective-permute-start | bytes 3342344 | tf_op jit(solution)/shard_map/ppermute | solution.py:396
  91.6 3.5 %copy-start = (f32[8,128,128]{2,1,0:T(8,128)}, f32[8,128,128]{2,1,0:T(8,128)S(1)}, u32[]{:S(2)}) copy-start(f32[8,128,128]{2,1,0:T(8,128)S(1)} %get-tuple-element.35) | copy-start | bytes 1572868
  92.1 3.1 %copy-start.4 = (f32[128,128]{1,0:T(8,128)}, f32[128,128]{1,0:T(8,128)S(1)}, u32[]{:S(2)}) copy-start(f32[128,128]{1,0:T(8,128)S(1)} %get-tuple-element.19.g01) | copy-start | bytes 196612
  92.1 3.1 %copy-start.5 = (f32[128,128]{1,0:T(8,128)}, f32[128,128]{1,0:T(8,128)S(1)}, u32[]{:S(2)}) copy-start(f32[128,128]{1,0:T(8,128)S(1)} %get-tuple-element.20.g11) | copy-start | bytes 196612
  93.9 1.3 copy-start.6
  116.5 0.7 collective-permute-start.3
  118.1 21.5 %all-to-all-start.5 = ((f32[8,160,128]{2,1,0:T(8,128)}), f32[8,160,128]{2,1,0:T(8,128)S(1)}, u32[]{:S(2)}, u32[]{:S(2)}) async-start(f32[8,160,128]{2,1,0:T(8,128)} %broadcast_in_dim.14), calls=%async_computation.5 | async-start | bytes 1310720 | tf_op jit(solution)/shard_map/all_to_all | solution.py:392
  131.3 8.4 %copy-start.1 = (f32[8,128,128]{2,1,0:T(8,128)S(1)}, f32[8,128,128]{2,1,0:T(8,128)}, u32[]{:S(2)}) copy-start(f32[8,128,128]{2,1,0:T(8,128)} %copy-done) | copy-start | bytes 1572868
  140.2 6.0 %collective-permute-start.5 = (f32[384,128]{1,0:T(8,128)S(1)}, f32[384,128]{1,0:T(8,128)S(1)}, u32[]{:S(2)}, u32[]{:S(2)}) collective-permute-start(f32[384,128]{1,0:T(8,128)S(1)} %pad_maximum_fusion.1), channel_id=1, source_target_pairs={{0,1},{1,0},{2,3},{3,2},{4,5},{5,4},{6,7},{7,6},{8,9},{9,8},{10,11... | collective-permute-start | bytes 589832 | tf_op jit(solution)/shard_map/ppermute | solution.py:396
  145.1 28.7 %collective-permute-start.4 = (f32[1024,128]{1,0:T(8,128)S(1)}, f32[1024,128]{1,0:T(8,128)}, u32[]{:S(2)}, u32[]{:S(2)}) collective-permute-start(f32[1024,128]{1,0:T(8,128)S(1)} %bitcast.24), channel_id=1, source_target_pairs={{0,1},{1,0},{2,3},{3,2},{4,5},{5,4},{6,7},{7,6},{8,9},{9,8},{10,11... | collective-permute-start | bytes 1572872 | tf_op jit(solution)/shard_map/ppermute | solution.py:396
  147.0 14.7 %all-to-all-start.6 = ((f32[8,128,128]{2,1,0:T(8,128)}), f32[8,128,128]{2,1,0:T(8,128)}, u32[]{:S(2)}, u32[]{:S(2)}) async-start(f32[8,128,128]{2,1,0:T(8,128)} %broadcast_in_dim.15), calls=%async_computation.6 | async-start | bytes 1048576 | tf_op jit(solution)/shard_map/all_to_all | solution.py:392
  159.0 14.8 %copy-start.2 = (f32[8,128,128]{2,1,0:T(8,128)S(1)}, f32[8,128,128]{2,1,0:T(8,128)}, u32[]{:S(2)}) copy-start(f32[8,128,128]{2,1,0:T(8,128)} %get-tuple-element.34) | copy-start | bytes 1572868
  162.8 11.0 %copy-start.3 = (f32[8,128,128]{2,1,0:T(8,128)S(1)}, f32[8,128,128]{2,1,0:T(8,128)}, u32[]{:S(2)}) copy-start(f32[8,128,128]{2,1,0:T(8,128)} %get-tuple-element.33) | copy-start | bytes 1572868
  162.8 2.1 %collective-permute-start.6 = (f32[128,128]{1,0:T(8,128)S(1)}, f32[128,128]{1,0:T(8,128)S(1)}, u32[]{:S(2)}, u32[]{:S(2)}) collective-permute-start(f32[128,128]{1,0:T(8,128)S(1)} %reduce_sum.39), channel_id=1, source_target_pairs={{0,1},{1,0},{2,3},{3,2},{4,5},{5,4},{6,7},{7,6},{8,9},{9,8},{10,11... | collective-permute-start | bytes 196616 | tf_op jit(solution)/shard_map/ppermute | solution.py:396

commit v2 on v1

--- a/solution.py
+++ b/solution.py
@@ -94,16 +94,28 @@
     lax.fori_loop(0, W // BAND, step, 0)
 
 
-def first_factor(g00, upper, inverse, work):
-    factor(g00[...], work, upper, inverse)
-
-
-def middle(g00, cee, g01, g11, inv0, pack, work, upper1, inv1):
-    li0 = inv0[...]
+def blocks_of(ref, start, count):
+    return ref[:, start : start + count, :].reshape(ref.shape[0] * count, W)
+
+
+def first_factor(place, mine, theirs, out, work, upper, inverse):
+    bit = W // mine.shape[0]
+    first = place[1] == 0
+    own, other = blocks_of(mine, W, bit), blocks_of(theirs, W, bit)
+    g00 = jnp.where(first, own, other)
+    factor(g00, work, upper, inverse)
+    out[:W, :] = g00
+    out[W : 2 * W, :] = jnp.where(first, other, own)
+    out[2 * W :, :] = inverse[...]
+
+
+def middle(start, keep, got, pack, work, upper1, inv1):
+    g00, cee, li0 = (start[i * W : (i + 1) * W, :] for i in range(3))
+    g01, g11 = (keep[i * W : (i + 1) * W, :] + got[i * W : (i + 1) * W, :] for i in range(2))
     x0 = li0.T
-    u = nt(cee[...], li0)
-    side = jnp.concatenate([g00[...], g01[...]], axis=1)
-    gram = jnp.concatenate([side, jnp.concatenate([g01[...].T, g11[...]], axis=1)])
+    u = nt(cee, li0)
+    side = jnp.concatenate([g00, g01], axis=1)
+    gram = jnp.concatenate([side, jnp.concatenate([g01.T, g11], axis=1)])
     h = nn(li0, nn(side, jnp.concatenate([u, x0])))
     g00x0 = nt(gram[:, :W], li0)
     m00 = nn(li0, g00x0[:W])
@@ -116,9 +128,9 @@
     y1 = nt(y, li1)
     m01 = nn(li0, y1[:W])
     blocks = (
-        [h, h_full, upper1[...], nn(cee[...], c1[:W]), c1[:W], c1[W:]]
-        + [m00, m01, m01.T, tn(c1, y1), g11[...] + tn(cee[...], g01[...])]
-        + [g00[...], g01[...], g11[...], li0]
+        [h, h_full, upper1[...], nn(cee, c1[:W]), c1[:W], c1[W:]]
+        + [m00, m01, m01.T, tn(c1, y1), g11 + tn(cee, g01)]
+        + [g00, g01, g11, li0]
     )
     for i, block in enumerate(blocks):
         pack[i * W : (i + 1) * W, :] = block
@@ -178,7 +190,7 @@
     return pl.pallas_call(
         body,
         out_shape=[jax.ShapeDtypeStruct(s, f32) for s in shapes],
-        in_specs=[VMEM] * len(args),
+        in_specs=[VMEM if a.dtype == f32 else SMEM for a in args],
         out_specs=[VMEM] * len(shapes),
         scratch_shapes=[pltpu.VMEM(s, f32) for s in scratch],
         compiler_params=room(16),
@@ -199,15 +211,28 @@
     height = covariance.shape[0]
     base = place[0] * height
 
-    def body(i, carry):
-        line = jnp.clip(seeds[i] - base, 0, height - 1)
-        pltpu.make_async_copy(covariance.at[pl.ds(line, 1), :], buffer.at[pl.ds(i, 1), :], sem).start()
-        return carry
-
-    lax.fori_loop(0, count, body, 0, unroll=8)
+    def row(line, i):
+        return pltpu.make_async_copy(covariance.at[pl.ds(line, 1), :], buffer.at[pl.ds(i, 1), :], sem)
+
+    def body(i, found):
+        line = seeds[i] - base
+        here = (line >= 0) & (line < height)
+
+        @pl.when(here)
+        def _():
+            row(line, i).start()
+
+        return found + here.astype(jnp.int32)
+
+    found = lax.fori_loop(0, count, body, 0, unroll=8)
     offsets = jnp.broadcast_to(lanes[...] - base, (count, count))
     held = jnp.where((offsets >= 0) & (offsets < height), 1.0, 0.0).T > 0
-    pltpu.make_async_copy(covariance.at[pl.ds(0, count), :], buffer, sem).wait()
+
+    def done(i, carry):
+        row(0, 0).wait()
+        return carry
+
+    lax.fori_loop(0, found, done, 0)
     for p in range(out.shape[0]):
         out[p] = jnp.where(held, buffer[:, p * W : (p + 1) * W], 0.0)
 
@@ -250,32 +275,42 @@
     hit = jnp.max(hot, axis=1, keepdims=True) > 0
     block = start[...]
     weights = jnp.concatenate(halves(jnp.where(hit, 0.0, block)), axis=1)
-    g00 = tn(block, block)
-    hot = hot.astype(bf16)
-    cee = sum(lax.dot_general(hot, p, (((0,), (0,)), ((), ())), preferred_element_type=f32) for p in pieces(block))
+    b0, b1, b2 = pieces(block)
+    hot_t, high_t, low_t = hot.T.astype(bf16), b0.astype(f32).T.astype(bf16), b1.astype(f32).T.astype(bf16)
+    both = mm(jnp.concatenate([hot_t, high_t]), jnp.concatenate([b0, b1], axis=1))
+    cee = both[:W, :W] + both[:W, W:] + mm(hot_t, b2)
+    g00 = both[W:, :W] + both[W:, W:] + mm(low_t, b0)
     first = place[1] == 0
-    keep[half:, :] = jnp.where(first, g00, cee)
-    send[half:, :] = jnp.where(first, cee, g00)
+    parts = keep.shape[0]
+    bit = W // parts
+    for p in range(parts):
+        lines = slice(p * bit, (p + 1) * bit)
+        keep[p, W:, :] = jnp.where(first, g00[lines], cee[lines])
+        send[p, W:, :] = jnp.where(first, cee[lines], g00[lines])
     for i, copy in enumerate(copies):
         copy.wait()
         high, low = halves(buffer[i])
         both = mm(high, weights)
         value = both[:, :W] + both[:, W:] + mm(low, weights[:, :W])
-        rows = slice(i * tall % half, i * tall % half + tall)
         mine = first if i * tall < half else jnp.logical_not(first)
+
+        def store(out):
+            for q in range(tall // W):
+                out[i * tall % half // W + q, :W, :] = value[q * W : (q + 1) * W, :]
 
         @pl.when(mine)
         def _():
-            keep[rows, :] = value
+            store(keep)
 
         @pl.when(jnp.logical_not(mine))
         def _():
-            send[rows, :] = value
+            store(send)
 
 
 def image_of_start(place, seeds, covariance, start):
     height = covariance.shape[0]
-    shape = jax.ShapeDtypeStruct((height // 2 + W, W), f32)
+    parts = height // 2 // W
+    shape = jax.ShapeDtypeStruct((parts, W + W // parts, W), f32)
     return pl.pallas_call(
         first_product,
         out_shape=[shape, shape],
@@ -285,19 +320,34 @@
     )(place, seeds.reshape(1, W), covariance, start)
 
 
-def two_grams(a, b, c, out_a, out_b):
-    right = halves(c[...])
-    for left, out in ((a, out_a), (b, out_b)):
-        high, low = halves(left[...].T)
-        both = mm(high, jnp.concatenate(right, axis=1))
-        out[...] = both[:, :W] + both[:, W:] + mm(low, right[0])
-
-
-def grams_of(a, b, c):
-    return kernel(two_grams, [(W, W)] * 2, [], a, b, c)
-
-
-def second_product(place, covariance, mine, theirs, g01, g11, out, buffer, sems, total):
+def cross(a, b):
+    right = halves(b)
+    high, low = halves(a.T)
+    both = mm(high, jnp.concatenate(right, axis=1))
+    return both[:, :W] + both[:, W:] + mm(low, right[0])
+
+
+def step_grams(mine, out):
+    bit = W // mine.shape[0]
+    step, start = blocks_of(mine, 0, W), blocks_of(mine, W + bit, W)
+    out[:W, :] = cross(start, step)
+    out[W:, :] = cross(step, step)
+
+
+def next_grams(place, mine, following, keep, send):
+    bit = W // mine.shape[0]
+    step, then = blocks_of(mine, 0, W), blocks_of(following, 0, W)
+    first = place[1] == 0
+    g01, g11 = blocks_of(following, W, bit), blocks_of(following, W + bit, bit)
+    g12, g22 = cross(step, then), cross(then, then)
+    for out in (keep, send):
+        out[:W, :] = g01
+        out[W : 2 * W, :] = g11
+    keep[2 * W :, :] = jnp.where(first, g12, g22)
+    send[2 * W :, :] = jnp.where(first, g22, g12)
+
+
+def second_product(place, covariance, mine, theirs, grams, out, buffer, sems, total):
     height, breadth = covariance.shape
     half = height // 2
     tall = height // CHUNKS
@@ -308,12 +358,13 @@
     parts = out.shape[0]
     bit = W // parts
     for p in range(parts):
-        out[p, W : W + bit, :] = g01[p * bit : (p + 1) * bit, :]
-        out[p, W + bit :, :] = g11[p * bit : (p + 1) * bit, :]
+        out[p, W : W + bit, :] = grams[p * bit : (p + 1) * bit, :]
+        out[p, W + bit :, :] = grams[W + p * bit : W + (p + 1) * bit, :]
     for i, copy in enumerate(copies):
-        rows = slice(i * tall % half, i * tall % half + tall)
+        lines = slice(i * tall % half // W, (i * tall % half + tall) // W)
         own, other = (mine, theirs) if i * tall < half else (theirs, mine)
-        v_high, v_low = halves(jnp.where(first, own[rows, :], other[rows, :]).T)
+        block = jnp.where(first, own[lines, :W, :], other[lines, :W, :]).reshape(tall, W)
+        v_high, v_low = halves(block.T)
         copy.wait()
         high, low = halves(buffer[i])
         both = mm(jnp.concatenate([v_high, v_low]), high)
@@ -328,59 +379,78 @@
                 out[p, :W, :] = value[:, p * W : (p + 1) * W].T
 
 
-def image_of_step(place, covariance, mine, theirs, g01, g11):
+def image_of_step(place, covariance, mine, theirs, grams):
     breadth = covariance.shape[1]
     parts = breadth // W
     return pl.pallas_call(
         second_product,
         out_shape=jax.ShapeDtypeStruct((parts, W + 2 * (W // parts), W), f32),
-        in_specs=[SMEM, HBM] + [VMEM] * 4,
+        in_specs=[SMEM, HBM] + [VMEM] * 3,
         out_specs=VMEM,
         scratch_shapes=chunk_scratch(covariance) + [pltpu.VMEM((W, breadth), f32)],
-    )(place, covariance, mine, theirs, g01, g11)
-
-
-def basis_rows(core, s0, v0, k0, s1, v1, k1, mix, out, high, low):
+    )(place, covariance, mine, theirs, grams)
+
+
+def basis_rows(core, mine, mine_next, theirs, theirs_next, mix, out, wide, tip):
     step = pl.program_id(0)
     count = pl.num_programs(0) // 2
     tall = out.shape[0]
+    parts = tall // W
+    bit = W // mine.shape[0]
 
     @pl.when(step == 0)
     def _():
-        high[...], low[...] = halves(mix[...])
-
-    def rows(parts, line):
-        left = jnp.concatenate([p[pl.ds(line, tall), :] for p in parts], axis=1)
-        l_high, l_low = halves(left)
-        out[...] = mm(l_high, high[...]) + mm(l_low, high[...]) + mm(l_high, low[...])
+        high, low = halves(mix[: 2 * W, : 2 * W])
+        wide[:, : 2 * W] = high
+        wide[:, 2 * W :] = low
+        high, low = halves(mix[:, 2 * W :])
+        tip[:, :W] = high
+        tip[:, W:] = low
+
+    def rows(pair, following, part):
+        lines = pl.ds(part, parts)
+        left = jnp.concatenate(
+            [
+                pair[lines, W + bit :, :].reshape(tall, W),
+                pair[lines, :W, :].reshape(tall, W),
+                following[lines, :W, :].reshape(tall, W),
+            ],
+            axis=1,
+        )
+        high, low = halves(left)
+        h2, l2 = high[:, : 2 * W], low[:, : 2 * W]
+        out[:, : 2 * W] = mm(h2, wide[:, : 2 * W]) + mm(h2, wide[:, 2 * W :]) + mm(l2, wide[:, : 2 * W])
+        both = mm(high, tip[...])
+        out[:, 2 * W :] = both[:, :W] + both[:, W:] + mm(low, tip[:, :W])
 
     @pl.when(step < count)
     def _():
-        rows((s0, v0, k0), pl.multiple_of(step * tall, tall))
+        rows(mine, mine_next, step * parts)
 
     @pl.when(step >= count)
     def _():
-        rows((s1, v1, k1), pl.multiple_of((step - count) * tall, tall))
-
-
-def basis_of(core, mine, theirs, mix):
-    half = mine[0].shape[0]
-    count = half // 512
+        rows(theirs, theirs_next, (step - count) * parts)
+
+
+def basis_of(core, mine, mine_next, theirs, theirs_next, mix):
+    half = mine.shape[0] * W
+    tall = 512
+    count = half // tall
     return pl.pallas_call(
         basis_rows,
         out_shape=jax.ShapeDtypeStruct((2 * half, mix.shape[1]), f32),
         grid_spec=pltpu.PrefetchScalarGridSpec(
             num_scalar_prefetch=1,
             grid=(2 * count,),
-            in_specs=[VMEM] * 7,
+            in_specs=[VMEM] * 5,
             out_specs=pl.BlockSpec(
-                (512, mix.shape[1]),
+                (tall, mix.shape[1]),
                 lambda i, c: (jnp.where(i < count, i + c[0] * count, i - count + (1 - c[0]) * count), 0),
             ),
-            scratch_shapes=[pltpu.VMEM(mix.shape, bf16)] * 2,
+            scratch_shapes=[pltpu.VMEM((2 * W, 4 * W), bf16), pltpu.VMEM((3 * W, 2 * W), bf16)],
         ),
         compiler_params=room(24),
-    )(core, *mine, *theirs, mix)
+    )(core, mine, mine_next, theirs, theirs_next, mix)
 
 
 def scattered(parts, axis):
@@ -411,56 +481,33 @@
     rows, chips, cores = (lax.axis_size(a) for a in ALL)
     row, chip, core = (lax.axis_index(a) for a in ALL)
     order = height * rows
-    share = breadth // rows
-    half = height // cores
-    cut = half // chips
-    bit = width // chips
     square = (width, width)
     first = core == 0
     turn = turned(rows, chips, cores)
-
-    def pick(a, b):
-        return jnp.where(first, a, b)
-
     place = jnp.stack([row, core, chip * cores + core]).astype(jnp.int32)
-    picked = picked_rows(place, seed_index, covariance, rows)
-    start_piece = scattered(picked, ROWS).T
+    start_piece = scattered(picked_rows(place, seed_index, covariance, rows), ROWS).T
+    start_turned = lax.ppermute(start_piece, ALL, turn)
     start = gathered(start_piece, ROWS).reshape(breadth, width)
-    start_turned = lax.ppermute(start_piece, ALL, turn)
+    start, start_turned = lax.optimization_barrier((start, start_turned))
     keep, send = image_of_start(place, seed_index, covariance, start)
-    summed = keep + other_core(send)
-    parts = jnp.concatenate([summed[:half].reshape(chips, cut, width), summed[half:].reshape(chips, bit, width)], axis=1)
-    mine = gathered(jnp.concatenate([scattered(parts, CHIP), start_turned]), CHIP)
+    mine = gathered(jnp.concatenate([scattered(keep + other_core(send), CHIP), start_turned]), CHIP)
     theirs = other_core(mine)
-    step_mine, step_theirs = (v[:, :cut].reshape(half, width) for v in (mine, theirs))
-    extra_mine, extra_theirs = (v[:, cut : cut + bit].reshape(square) for v in (mine, theirs))
-    start_mine, start_theirs = (v[:, cut + bit :].reshape(half, width) for v in (mine, theirs))
-    g00 = pick(extra_mine, extra_theirs)
-    cee = pick(extra_theirs, extra_mine)
-    upper0, inv0 = kernel(first_factor, [square] * 2, [(width, 2 * width)], g00)
-    g01, g11 = grams_of(start_mine, step_mine, step_mine)
-    parts = image_of_step(place, covariance, step_mine, step_theirs, g01, g11)
+    (grams,) = kernel(step_grams, [(2 * width, width)], [], mine)
+    parts = image_of_step(place, covariance, mine, theirs, grams)
     piece = lax.ppermute(scattered(parts, ROWS), ALL, turn)
-    mine = gathered(piece, CHIP)
-    mine, upper0, inv0 = lax.optimization_barrier((mine, upper0, inv0))
-    next_mine = mine[:, :share].reshape(half, width)
-    g01 = mine[:, share : share + bit].reshape(square)
-    g11 = mine[:, share + bit :].reshape(square)
-    both = jnp.concatenate([g01, g11])
-    g12, g22 = grams_of(step_mine, next_mine, next_mine)
-    got = other_core(jnp.concatenate([both, pick(g22, g12)]))
-    both = both + got[: 2 * width]
-    total = pick(g12, g22) + got[2 * width :]
-    next_theirs = other_core(next_mine)
-    totals = gathered(total, ROWS)
-    g01, g11 = both[:width], both[width:]
-    (pack,) = kernel(
-        middle, [(PACK * width, width)], [(width, 2 * width), square, square], g00, cee, g01, g11, inv0
-    )
+    (zero_pack,) = kernel(
+        first_factor, [(3 * width, width)], [(width, 2 * width), square, square], place, mine, theirs
+    )
+    mine_next, zero_pack = lax.optimization_barrier((gathered(piece, CHIP), zero_pack))
+    keep, send = kernel(next_grams, [(3 * width, width)] * 2, [], place, mine, mine_next)
+    got = other_core(send)
+    theirs_next = other_core(mine_next)
+    totals = gathered(keep[2 * width :] + got[2 * width :], ROWS)
+    (pack,) = kernel(middle, [(PACK * width, width)], [(width, 2 * width), square, square], zero_pack, keep, got)
     totals, pack = lax.optimization_barrier((totals, pack))
     total = jnp.sum(totals, axis=0)
     rest_total = other_core(total)
-    g12, g22 = pick(total, rest_total), pick(rest_total, total)
+    g12, g22 = jnp.where(first, total, rest_total), jnp.where(first, rest_total, total)
     scale = float(order) ** 0.5
 
     def last_step(*refs):
@@ -474,7 +521,7 @@
         g12,
         g22,
     )
-    basis = basis_of(place[1:2], (start_mine, step_mine, next_mine), (start_theirs, step_theirs, next_theirs), mix)
+    basis = basis_of(place[1:2], mine, mine_next, theirs, theirs_next, mix)
     return basis, projection, first_pass
 
 

time: 181 us -> 181 us (level)
  blocking collectives: 66.7 us -> 53.8 us
  waiting for transfers between devices: 20.8 us -> 28.5 us
  starting transfers between devices: 35.4 us -> 41.2 us
  local copies, waits for them, and re-layouts: 3.56 us -> 7.42 us
  Pallas kernels: 47.5 us -> 44.4 us
    all_to_all x2 -> x1, blocking collectives: 34 us -> 17.8 us  [gathered(): return lax.all_to_all(copies, axis, 0, 0, tiled=True)]
    all_to_all x2 -> x3, waiting for transfers between devices: 5.13 us -> 12.6 us  [gathered(): return lax.all_to_all(copies, axis, 0, 0, tiled=True)]
    unnamed x14 -> x18, local copies, waits for them, and re-layouts: 0.15 us -> 4.61 us
    all_to_all x2 -> x3, starting transfers between devices: 17.5 us -> 21.4 us  [gathered(): return lax.all_to_all(copies, axis, 0, 0, tiled=True)]
    all_to_all x2, blocking collectives: 32.7 us -> 36 us  [scattered(): return jnp.sum(lax.all_to_all(parts, axis, 0, 0, tiled=True), axis=0)]
    pallas_call x1, Pallas kernels: 6.27 us -> 3.06 us  [picked_rows(): pl.pallas_call(pick_rows, out_shape=jax.ShapeDtypeStruct((parts, count, W...]
    ppermute x5, starting transfers between devices: 11.9 us -> 14.5 us  [other_core(): return lax.ppermute(value, CORE, SWAP)]
  transfers between devices with their start and end apart: 10 -> 11, of which waited for: 7 -> 8; matrix products, arithmetic and copies ran while one was open for 2% -> 1% of each run, Pallas kernels for 12% -> 12%
where the time goes in v2:
time: 181 us; the launch traced here: 180 us
  blocking collectives  53.8 us (30%)
  Pallas kernels  44.4 us (25%)
  starting transfers between devices  41.2 us (23%)
  waiting for transfers between devices  28.5 us (16%)
  local copies, waits for them, and re-layouts  7.42 us (4%)
  other arithmetic  3.81 us (2%)
    all_to_all x2, blocking collectives, scattered(): return jnp.sum(lax.all_to_all(parts, axis, 0, 0, tiled=True), axis=0)  36 us
    pallas_call x5, Pallas kernels, kernel(): pl.pallas_call(body, out_shape=[jax.ShapeDtypeStruct(s, f32) for s in sha...  23.1 us
    all_to_all x3, starting transfers between devices, gathered(): return lax.all_to_all(copies, axis, 0, 0, tiled=True)  21.4 us
    all_to_all x1, blocking collectives, gathered(): return lax.all_to_all(copies, axis, 0, 0, tiled=True)  17.8 us
    ppermute x5, starting transfers between devices, other_core(): return lax.ppermute(value, CORE, SWAP)  14.5 us
    all_to_all x3, waiting for transfers between devices, gathered(): return lax.all_to_all(copies, axis, 0, 0, tiled=True)  12.6 us
    all_to_all x1, waiting for transfers between devices, scattered(): return jnp.sum(lax.all_to_all(parts, axis, 0, 0, tiled=True), axis=0)  10.9 us
    pallas_call x1, Pallas kernels, image_of_start(): pl.pallas_call(first_product, out_shape=[shape, shape], in_specs=[SMEM, V...  6.96 us
  transfers between devices with their start and end apart: 11, of which 8 were waited for; matrix products, arithmetic and copies ran while one was open for 1% of the time, Pallas kernels for 12%

profile of v2, /device:TPU:1, one launch (start us, length us, event | category | flops | bytes accessed | tf_op | source)
XLA Modules:
  0.0 180.0 jit_solution(14964965721423290864)
XLA Ops:
  0.6 0.7 pad_add_fusion.place
  1.3 3.1 %shard_map.49 = f32[8,128,128]{2,1,0:T(8,128)} custom-call(s32[3]{0:T(128)} %pad_add_fusion.place, s32[128]{0:T(128)} %seeds.1, s32[1,128]{1,0:T(1,128)} %bitcast.9, f32[2048,1024]{1,0:T(8,128)} %covariance.5), custom_call_target="tpu_custom_call" | custom-call | tf_op jit(solution)/shard_map/pallas_call | solution.py:242
  4.4 18.0 %all_to_all.35 = f32[8,128,128]{2,1,0:T(8,128)S(1)} all-to-all(f32[8,128,128]{2,1,0:T(8,128)} %shard_map.49), channel_id=1, replica_groups=mesh['row'=8,'chip'=8,'core'=2] {'row'}, dimensions={0} | all-to-all | bytes 1048576 | tf_op jit(solution)/shard_map/all_to_all | solution.py:457
  22.4 0.1 copy.5
  22.5 0.8 broadcast_in_dim.12
  23.4 3.5 %all-to-all-start.1 = ((f32[8,128,128]{2,1,0:T(8,128)}), f32[8,128,128]{2,1,0:T(8,128)S(1)}, u32[]{:S(2)}, u32[]{:S(2)}) async-start(f32[8,128,128]{2,1,0:T(8,128)} %broadcast_in_dim.12), calls=%async_computation.1 | async-start | bytes 1048576 | tf_op jit(solution)/shard_map/all_to_all | solution.py:462
  26.9 0.7 collective-permute-start
  27.5 0.0 collective-permute-done
  27.5 7.9 %all-to-all-done.1 = f32[8,128,128]{2,1,0:T(8,128)S(1)} async-done(((f32[8,128,128]{2,1,0:T(8,128)}), f32[8,128,128]{2,1,0:T(8,128)S(1)}, u32[]{:S(2)}, u32[]{:S(2)}) %all-to-all-start.1) | async-done | bytes 524320 | tf_op jit(solution)/shard_map/all_to_all | solution.py:462
  35.4 0.0 copy-start.8
  35.4 0.8 copy-done.8
  36.2 7.0 %shard_map.50 = (f32[8,144,128]{2,1,0:T(8,128)}, f32[8,144,128]{2,1,0:T(8,128)}) custom-call(s32[3]{0:T(128)} %pad_add_fusion.place, s32[1,128]{1,0:T(1,128)} %bitcast.10, f32[2048,1024]{1,0:T(8,128)} %covariance.5, f32[1024,128]{1,0:T(8,128)} %bitcast.6), custom_call_target="tpu_custom_call" | custom-call | tf_op jit(solution)/shard_map/pallas_call | solution.py:314
  43.2 6.4 %collective-permute-start.1 = (f32[8,144,128]{2,1,0:T(8,128)}, f32[8,144,128]{2,1,0:T(8,128)S(1)}, u32[]{:S(2)}, u32[]{:S(2)}) collective-permute-start(f32[8,144,128]{2,1,0:T(8,128)} %get-tuple-element.18), channel_id=1, source_target_pairs={{0,1},{1,0},{2,3},{3,2},{4,5},{5,4},{6,7},{7,6},{8,9},{9,8},{10,11... | collective-permute-start | bytes 1769480 | tf_op jit(solution)/shard_map/ppermute | solution.py:466
  49.6 1.8 %collective-permute-done.1 = f32[8,144,128]{2,1,0:T(8,128)S(1)} collective-permute-done((f32[8,144,128]{2,1,0:T(8,128)}, f32[8,144,128]{2,1,0:T(8,128)S(1)}, u32[]{:S(2)}, u32[]{:S(2)}) %collective-permute-start.1) | collective-permute-done | bytes 589856 | tf_op jit(solution)/shard_map/ppermute | solution.py:466
  51.4 1.9 %add.10 = f32[8,144,128]{2,1,0:T(8,128)} add(f32[8,144,128]{2,1,0:T(8,128)} %get-tuple-element.17, f32[8,144,128]{2,1,0:T(8,128)S(1)} %collective-permute-done.1) | non-fusion elementwise | flops 147456 | bytes 1769472 | tf_op jit(solution)/shard_map/add | solution.py:493
  53.4 3.9 %all-to-all-start.2 = ((f32[8,144,128]{2,1,0:T(8,128)}), f32[8,144,128]{2,1,0:T(8,128)S(1)}, u32[]{:S(2)}, u32[]{:S(2)}) async-start(f32[8,144,128]{2,1,0:T(8,128)} %add.10), calls=%async_computation.2 | async-start | bytes 1179648 | tf_op jit(solution)/shard_map/all_to_all | solution.py:457
  57.3 0.1 copy.6
  57.4 10.9 %all-to-all-done.2 = f32[8,144,128]{2,1,0:T(8,128)S(1)} async-done(((f32[8,144,128]{2,1,0:T(8,128)}), f32[8,144,128]{2,1,0:T(8,128)S(1)}, u32[]{:S(2)}, u32[]{:S(2)}) %all-to-all-start.2) | async-done | bytes 589856 | tf_op jit(solution)/shard_map/all_to_all | solution.py:457
  68.3 0.1 broadcast_in_dim.13
  68.4 17.8 %all_to_all.36.mine = f32[8,272,128]{2,1,0:T(8,128)S(1)} all-to-all(f32[8,272,128]{2,1,0:T(8,128)S(1)} %broadcast_in_dim.13), channel_id=1, replica_groups=mesh['row'=8,'chip'=8,'core'=2] {'chip'}, dimensions={0} | all-to-all | bytes 2228224 | tf_op jit(solution)/shard_map/all_to_all | solution.py:462
  86.2 0.0 copy-start
  86.2 2.1 %collective-permute-start.2 = (f32[8,272,128]{2,1,0:T(8,128)S(1)}, f32[8,272,128]{2,1,0:T(8,128)S(1)}, u32[]{:S(2)}, u32[]{:S(2)}) collective-permute-start(f32[8,272,128]{2,1,0:T(8,128)S(1)} %all_to_all.36.mine), channel_id=1, source_target_pairs={{0,1},{1,0},{2,3},{3,2},{4,5},{5,4},{6,7},{7,6},{8,9},{9,8},{10,11... | collective-permute-start | bytes 3342344 | tf_op jit(solution)/shard_map/ppermute | solution.py:466
  88.3 0.5 shard_map.51.grams
  88.8 0.0 copy-start.6
  88.9 0.6 copy-done.6
  89.5 1.2 collective-permute-done.2.theirs
  90.7 0.0 copy-done
  90.7 0.0 copy-start.2
  90.7 1.0 copy-done.2
  91.7 6.4 %shard_map.52 = f32[8,160,128]{2,1,0:T(8,128)} custom-call(s32[3]{0:T(128)} %pad_add_fusion.place, f32[2048,1024]{1,0:T(8,128)} %covariance.5, f32[8,272,128]{2,1,0:T(8,128)} %copy-done, f32[8,272,128]{2,1,0:T(8,128)} %copy-done.2, f32[256,128]{1,0:T(8,128)} %copy-done.6), custom_call_target="tpu_custom_call" | custom-call | tf_op jit(solution)/shard_map/pallas_call | solution.py:385
  98.2 18.0 %all_to_all.37 = f32[8,160,128]{2,1,0:T(8,128)S(1)} all-to-all(f32[8,160,128]{2,1,0:T(8,128)} %shard_map.52), channel_id=1, replica_groups=mesh['row'=8,'chip'=8,'core'=2] {'row'}, dimensions={0} | all-to-all | bytes 1310720 | tf_op jit(solution)/shard_map/all_to_all | solution.py:457
  116.1 0.0 copy-start.3
  116.2 0.0 copy-start.1
  116.2 0.0 copy-start.7
  116.2 0.8 collective-permute-start.3
  117.0 0.0 collective-permute-done.3
  117.0 0.9 broadcast_in_dim.14
  117.9 13.7 %all-to-all-start.5 = ((f32[8,160,128]{2,1,0:T(8,128)}), f32[8,160,128]{2,1,0:T(8,128)S(1)}, u32[]{:S(2)}, u32[]{:S(2)}) async-start(f32[8,160,128]{2,1,0:T(8,128)} %broadcast_in_dim.14), calls=%async_computation.5 | async-start | bytes 1310720 | tf_op jit(solution)/shard_map/all_to_all | solution.py:462
  131.6 0.0 copy-done.3
  131.6 0.0 copy-done.1
  131.7 0.0 copy-done.7
  131.7 5.1 %shard_map.53.start = f32[384,128]{1,0:T(8,128)S(1)} custom-call(s32[3]{0:T(128)S(1)} %copy-done.7, f32[8,272,128]{2,1,0:T(8,128)S(1)} %copy-done.1, f32[8,272,128]{2,1,0:T(8,128)S(1)} %copy-done.3), custom_call_target="tpu_custom_call" | custom-call | tf_op jit(solution)/shard_map/pallas_call | solution.py:190
  136.8 3.4 %all-to-all-done.5.following.mine_next = f32[8,160,128]{2,1,0:T(8,128)S(1)} async-done(((f32[8,160,128]{2,1,0:T(8,128)}), f32[8,160,128]{2,1,0:T(8,128)S(1)}, u32[]{:S(2)}, u32[]{:S(2)}) %all-to-all-start.5) | async-done | bytes 655392 | tf_op jit(solution)/shard_map/all_to_all | solution.py:462
  140.2 1.0 shard_map.54
  141.2 4.1 %collective-permute-start.5 = (f32[384,128]{1,0:T(8,128)S(1)}, f32[384,128]{1,0:T(8,128)S(1)}, u32[]{:S(2)}, u32[]{:S(2)}) collective-permute-start(f32[384,128]{1,0:T(8,128)S(1)} %get-tuple-element.22), channel_id=1, source_target_pairs={{0,1},{1,0},{2,3},{3,2},{4,5},{5,4},{6,7},{7,6},{8,9},{9,8},{10,11... | collective-permute-start | bytes 589832 | tf_op jit(solution)/shard_map/ppermute | solution.py:466
  145.3 1.1 collective-permute-done.5.got
  146.4 0.8 broadcast_in_dim.15
  147.2 4.2 %all-to-all-start.6 = ((f32[8,128,128]{2,1,0:T(8,128)}), f32[8,128,128]{2,1,0:T(8,128)}, u32[]{:S(2)}, u32[]{:S(2)}) async-start(f32[8,128,128]{2,1,0:T(8,128)} %broadcast_in_dim.15), calls=%async_computation.6 | async-start | bytes 1048576 | tf_op jit(solution)/shard_map/all_to_all | solution.py:462
  151.4 0.6 collective-permute-start.4
  152.0 7.7 %shard_map.55.refs_0_ = f32[1920,128]{1,0:T(8,128)S(1)} custom-call(f32[384,128]{1,0:T(8,128)S(1)} %shard_map.53.start, f32[384,128]{1,0:T(8,128)S(1)} %get-tuple-element.21.keep, f32[384,128]{1,0:T(8,128)S(1)} %collective-permute-done.5.got), custom_call_target="tpu_custom_call" | custom-call | tf_op jit(solution)/shard_map/pallas_call | solution.py:190
  159.7 0.0 copy-start.4
  159.7 0.9 copy-done.4
  160.6 1.3 all-to-all-done.6
  161.9 1.1 reduce_sum.39
  163.0 1.2 collective-permute-start.6
  164.2 0.9 collective-permute-done.6
  165.2 0.0 copy-start.5
  165.2 1.2 copy-done.5
  166.4 8.8 %shard_map.56 = (f32[384,384]{1,0:T(8,128)S(1)}, f32[384,256]{1,0:T(8,128)}, f32[384,256]{1,0:T(8,128)}) custom-call(f32[1920,128]{1,0:T(8,128)S(1)} %copy-done.5, f32[128,128]{1,0:T(8,128)S(1)} %get-tuple-element.30.refs_1_, f32[128,128]{1,0:T(8,128)S(1)} %get-tuple-element.29.refs_2_), custom_call_target="tpu_custom_call" | custom-call | tf_op jit(solution)/shard_map/pallas_call | solution.py:190
  175.2 0.0 collective-permute-done.4.theirs_next
  175.2 4.8 %shard_map.57 = f32[2048,384]{1,0:T(8,128)} custom-call(s32[1]{0:T(128)} %bitcast.core, f32[8,272,128]{2,1,0:T(8,128)S(1)} %copy-done.1, f32[8,160,128]{2,1,0:T(8,128)S(1)} %all-to-all-done.5.following.mine_next, f32[8,272,128]{2,1,0:T(8,128)S(1)} %copy-done.3, f32[8,160,128]{2,1,0:T(8,128)} %collective-permute-done.4.theirs_next, ...), custom_call_target="tpu_custom_call" | custom-call | tf_op jit(solution)/shard_map/pallas_call | solution.py:439
  (6 shorter events, 0.1 us)
Async XLA Ops:
  23.4 12.1 %all-to-all-start.1 = ((f32[8,128,128]{2,1,0:T(8,128)}), f32[8,128,128]{2,1,0:T(8,128)S(1)}, u32[]{:S(2)}, u32[]{:S(2)}) async-start(f32[8,128,128]{2,1,0:T(8,128)} %broadcast_in_dim.12), calls=%async_computation.1 | async-start | bytes 1048576 | tf_op jit(solution)/shard_map/all_to_all | solution.py:462
  26.9 0.7 collective-permute-start
  35.4 0.8 copy-start.8
  43.2 8.2 %collective-permute-start.1 = (f32[8,144,128]{2,1,0:T(8,128)}, f32[8,144,128]{2,1,0:T(8,128)S(1)}, u32[]{:S(2)}, u32[]{:S(2)}) collective-permute-start(f32[8,144,128]{2,1,0:T(8,128)} %get-tuple-element.18), channel_id=1, source_target_pairs={{0,1},{1,0},{2,3},{3,2},{4,5},{5,4},{6,7},{7,6},{8,9},{9,8},{10,11... | collective-permute-start | bytes 1769480 | tf_op jit(solution)/shard_map/ppermute | solution.py:466
  53.4 14.9 %all-to-all-start.2 = ((f32[8,144,128]{2,1,0:T(8,128)}), f32[8,144,128]{2,1,0:T(8,128)S(1)}, u32[]{:S(2)}, u32[]{:S(2)}) async-start(f32[8,144,128]{2,1,0:T(8,128)} %add.10), calls=%async_computation.2 | async-start | bytes 1179648 | tf_op jit(solution)/shard_map/all_to_all | solution.py:457
  86.2 4.5 %copy-start = (f32[8,272,128]{2,1,0:T(8,128)}, f32[8,272,128]{2,1,0:T(8,128)S(1)}, u32[]{:S(2)}) copy-start(f32[8,272,128]{2,1,0:T(8,128)S(1)} %all_to_all.36.mine) | copy-start | bytes 3342340
  86.2 4.5 %collective-permute-start.2 = (f32[8,272,128]{2,1,0:T(8,128)S(1)}, f32[8,272,128]{2,1,0:T(8,128)S(1)}, u32[]{:S(2)}, u32[]{:S(2)}) collective-permute-start(f32[8,272,128]{2,1,0:T(8,128)S(1)} %all_to_all.36.mine), channel_id=1, source_target_pairs={{0,1},{1,0},{2,3},{3,2},{4,5},{5,4},{6,7},{7,6},{8,9},{9,8},{10,11... | collective-permute-start | bytes 3342344 | tf_op jit(solution)/shard_map/ppermute | solution.py:466
  88.8 0.7 copy-start.6
  90.7 1.0 copy-start.2
  116.1 15.5 %copy-start.3 = (f32[8,272,128]{2,1,0:T(8,128)S(1)}, f32[8,272,128]{2,1,0:T(8,128)}, u32[]{:S(2)}) copy-start(f32[8,272,128]{2,1,0:T(8,128)} %copy-done.2) | copy-start | bytes 3342340
  116.2 15.5 %copy-start.1 = (f32[8,272,128]{2,1,0:T(8,128)S(1)}, f32[8,272,128]{2,1,0:T(8,128)}, u32[]{:S(2)}) copy-start(f32[8,272,128]{2,1,0:T(8,128)} %copy-done) | copy-start | bytes 3342340
  116.2 15.5 %copy-start.7 = (s32[3]{0:T(128)S(1)}, s32[3]{0:T(128)}, u32[]{:S(2)}) copy-start(s32[3]{0:T(128)} %pad_add_fusion.place) | copy-start | bytes 40
  116.2 0.8 collective-permute-start.3
  117.9 22.3 %all-to-all-start.5 = ((f32[8,160,128]{2,1,0:T(8,128)}), f32[8,160,128]{2,1,0:T(8,128)S(1)}, u32[]{:S(2)}, u32[]{:S(2)}) async-start(f32[8,160,128]{2,1,0:T(8,128)} %broadcast_in_dim.14), calls=%async_computation.5 | async-start | bytes 1310720 | tf_op jit(solution)/shard_map/all_to_all | solution.py:462
  141.2 5.2 %collective-permute-start.5 = (f32[384,128]{1,0:T(8,128)S(1)}, f32[384,128]{1,0:T(8,128)S(1)}, u32[]{:S(2)}, u32[]{:S(2)}) collective-permute-start(f32[384,128]{1,0:T(8,128)S(1)} %get-tuple-element.22), channel_id=1, source_target_pairs={{0,1},{1,0},{2,3},{3,2},{4,5},{5,4},{6,7},{7,6},{8,9},{9,8},{10,11... | collective-permute-start | bytes 589832 | tf_op jit(solution)/shard_map/ppermute | solution.py:466
  147.2 14.7 %all-to-all-start.6 = ((f32[8,128,128]{2,1,0:T(8,128)}), f32[8,128,128]{2,1,0:T(8,128)}, u32[]{:S(2)}, u32[]{:S(2)}) async-start(f32[8,128,128]{2,1,0:T(8,128)} %broadcast_in_dim.15), calls=%async_computation.6 | async-start | bytes 1048576 | tf_op jit(solution)/shard_map/all_to_all | solution.py:462
  151.4 23.8 %collective-permute-start.4 = (f32[8,160,128]{2,1,0:T(8,128)S(1)}, f32[8,160,128]{2,1,0:T(8,128)}, u32[]{:S(2)}, u32[]{:S(2)}) collective-permute-start(f32[8,160,128]{2,1,0:T(8,128)S(1)} %all-to-all-done.5.following.mine_next), channel_id=1, source_target_pairs={{0,1},{1,0},{2,3},{3,2},{4,5},{5,4},{6,7},{7,6},{8,9},{9,8},{10,11... | collective-permute-start | bytes 1966088 | tf_op jit(solution)/shard_map/ppermute | solution.py:466
  159.7 0.9 copy-start.4
  163.0 2.1 %collective-permute-start.6 = (f32[128,128]{1,0:T(8,128)S(1)}, f32[128,128]{1,0:T(8,128)S(1)}, u32[]{:S(2)}, u32[]{:S(2)}) collective-permute-start(f32[128,128]{1,0:T(8,128)S(1)} %reduce_sum.39), channel_id=1, source_target_pairs={{0,1},{1,0},{2,3},{3,2},{4,5},{5,4},{6,7},{7,6},{8,9},{9,8},{10,11... | collective-permute-start | bytes 196616 | tf_op jit(solution)/shard_map/ppermute | solution.py:466
  165.2 1.2 copy-start.5

commit v3 on v2

--- a/solution.py
+++ b/solution.py
@@ -10,6 +10,16 @@
 CORE = "core"
 ALL = (ROWS, CHIP, CORE)
 SWAP = [(0, 1), (1, 0)]
+SLOTS = (
+    (2, 6, 0, 5, 1, 4, 3, 7),
+    (7, 1, 4, 3, 5, 2, 6, 0),
+    (1, 5, 0, 4, 3, 7, 2, 6),
+    (4, 2, 5, 1, 6, 0, 7, 3),
+    (5, 0, 7, 1, 6, 2, 4, 3),
+    (1, 4, 0, 6, 3, 5, 2, 7),
+    (4, 3, 7, 2, 6, 1, 5, 0),
+    (2, 4, 3, 6, 0, 7, 1, 5),
+)
 W = 128
 f32 = jnp.float32
 bf16 = jnp.bfloat16
@@ -98,27 +108,24 @@
     return ref[:, start : start + count, :].reshape(ref.shape[0] * count, W)
 
 
-def first_factor(place, mine, theirs, out, work, upper, inverse):
-    bit = W // mine.shape[0]
-    first = place[1] == 0
-    own, other = blocks_of(mine, W, bit), blocks_of(theirs, W, bit)
-    g00 = jnp.where(first, own, other)
-    factor(g00, work, upper, inverse)
-    out[:W, :] = g00
-    out[W : 2 * W, :] = jnp.where(first, other, own)
-    out[2 * W :, :] = inverse[...]
-
-
-def middle(start, keep, got, pack, work, upper1, inv1):
-    g00, cee, li0 = (start[i * W : (i + 1) * W, :] for i in range(3))
+def turned_blocks(ref, place, start, count, parts):
+    return jnp.concatenate([ref[place[3 + p], start : start + count, :] for p in parts])
+
+
+def first_factor(g00, inverse, work, upper):
+    factor(g00[:W, :], work, upper, inverse)
+
+
+def middle(start, inv0, keep, got, pack, work, upper1, inv1):
+    g00, cee = start[:W, :], start[W:, :]
+    li0 = inv0[...]
     g01, g11 = (keep[i * W : (i + 1) * W, :] + got[i * W : (i + 1) * W, :] for i in range(2))
     x0 = li0.T
     u = nt(cee, li0)
     side = jnp.concatenate([g00, g01], axis=1)
     gram = jnp.concatenate([side, jnp.concatenate([g01.T, g11], axis=1)])
     h = nn(li0, nn(side, jnp.concatenate([u, x0])))
-    g00x0 = nt(gram[:, :W], li0)
-    m00 = nn(li0, g00x0[:W])
+    m00 = nn(li0, nt(g00, li0))
     h_full = h + (h - nn(m00, h))
     comb = jnp.concatenate([u - nn(x0, h_full), x0])
     y = nn(gram, comb)
@@ -127,20 +134,24 @@
     c1 = nt(comb, li1)
     y1 = nt(y, li1)
     m01 = nn(li0, y1[:W])
+    g02 = g11 + tn(cee, g01)
+    i1 = jnp.concatenate([nn(cee, c1[:W]), c1])
+    s0 = nn(jnp.concatenate([side, g02], axis=1), i1)
+    s1 = nn(gram[W:], i1[: 2 * W])
     blocks = (
-        [h, h_full, upper1[...], nn(cee, c1[:W]), c1[:W], c1[W:]]
-        + [m00, m01, m01.T, tn(c1, y1), g11 + tn(cee, g01)]
-        + [g00, g01, g11, li0]
+        [h, h_full, upper1[...], i1[:W], i1[W : 2 * W], i1[2 * W :]]
+        + [m00, m01, tn(c1, y1), g02, g00, g01, g11, li0]
+        + [nn(li0, s0), tn(c1[:W], s0), s1]
     )
     for i, block in enumerate(blocks):
         pack[i * W : (i + 1) * W, :] = block
 
 
-PACK = 15
+PACK = 17
 
 
 def last(scale, pack, g12, g22, mix, projection, first_pass, work, upper2, inv2):
-    first, full, upper1, _, c1_top, c1_low, m00, m01, m10, m11, a02, a00, a01, a11, li0 = (
+    first, full, upper1, _, c1_top, c1_low, m00, m01, m11, a02, a00, a01, a11, li0, first0, part1, s1 = (
         pack[i * W : (i + 1) * W, :] for i in range(PACK)
     )
     i1 = pack[3 * W : 6 * W, :]
@@ -153,18 +164,15 @@
             jnp.concatenate([a02.T, a12.T, g22[...]], axis=1),
         ]
     )
-    s = nn(gram, i1)
-    h = jnp.concatenate([nn(li0, s[:W]), tn(c1, s[: 2 * W])])
-    gram_p = jnp.concatenate([jnp.concatenate([m00, m01], axis=1), jnp.concatenate([m10, m11], axis=1)])
+    h = jnp.concatenate([first0, part1 + tn(c1_low, s1 + nn(a12, c1_low))])
+    gram_p = jnp.concatenate([jnp.concatenate([m00, m01], axis=1), jnp.concatenate([m01.T, m11], axis=1)])
     h_full = h + (h - nn(gram_p, h))
-    back = nn(c1, h_full[W:])
-    comb = jnp.concatenate([i1[:W] - (back[:W] + tn(li0, h_full[:W])), i1[W : 2 * W] - back[W:], i1[2 * W :]])
+    zero = jnp.zeros((W, W), f32)
+    places = jnp.concatenate([jnp.concatenate([li0.T, zero]), c1], axis=1)
+    comb = jnp.concatenate([i1[: 2 * W] - nn(places, h_full), i1[2 * W :]])
     factor(tn(comb, nn(gram, comb)), work, upper2, inv2)
-    zero = jnp.zeros((W, W), f32)
-    mix[:W, :W] = li0.T * scale
-    mix[W:, :W] = jnp.zeros((2 * W, W), f32)
-    mix[: 2 * W, W : 2 * W] = c1 * scale
-    mix[2 * W :, W : 2 * W] = zero
+    mix[: 2 * W, : 2 * W] = places * scale
+    mix[2 * W :, : 2 * W] = jnp.zeros((W, 2 * W), f32)
     mix[:, 2 * W :] = nt(comb, inv2[...]) * scale
     projection[:W, :W] = full
     projection[W : 2 * W, :W] = upper1
@@ -273,20 +281,8 @@
     lines = lax.broadcasted_iota(jnp.int32, (breadth, W), 0) + place[2] * breadth
     hot = jnp.where(lines == lanes[...], 1.0, 0.0)
     hit = jnp.max(hot, axis=1, keepdims=True) > 0
-    block = start[...]
-    weights = jnp.concatenate(halves(jnp.where(hit, 0.0, block)), axis=1)
-    b0, b1, b2 = pieces(block)
-    hot_t, high_t, low_t = hot.T.astype(bf16), b0.astype(f32).T.astype(bf16), b1.astype(f32).T.astype(bf16)
-    both = mm(jnp.concatenate([hot_t, high_t]), jnp.concatenate([b0, b1], axis=1))
-    cee = both[:W, :W] + both[:W, W:] + mm(hot_t, b2)
-    g00 = both[W:, :W] + both[W:, W:] + mm(low_t, b0)
+    weights = jnp.concatenate(halves(jnp.where(hit, 0.0, start[...])), axis=1)
     first = place[1] == 0
-    parts = keep.shape[0]
-    bit = W // parts
-    for p in range(parts):
-        lines = slice(p * bit, (p + 1) * bit)
-        keep[p, W:, :] = jnp.where(first, g00[lines], cee[lines])
-        send[p, W:, :] = jnp.where(first, cee[lines], g00[lines])
     for i, copy in enumerate(copies):
         copy.wait()
         high, low = halves(buffer[i])
@@ -296,7 +292,7 @@
 
         def store(out):
             for q in range(tall // W):
-                out[i * tall % half // W + q, :W, :] = value[q * W : (q + 1) * W, :]
+                out[i * tall % half // W + q] = value[q * W : (q + 1) * W, :]
 
         @pl.when(mine)
         def _():
@@ -309,15 +305,43 @@
 
 def image_of_start(place, seeds, covariance, start):
     height = covariance.shape[0]
-    parts = height // 2 // W
-    shape = jax.ShapeDtypeStruct((parts, W + W // parts, W), f32)
+    shape = jax.ShapeDtypeStruct((height // 2 // W, W, W), f32)
     return pl.pallas_call(
         first_product,
         out_shape=[shape, shape],
         in_specs=[SMEM, VMEM, HBM, VMEM],
         out_specs=[VMEM] * 2,
         scratch_shapes=chunk_scratch(covariance),
+        compiler_params=room(50),
     )(place, seeds.reshape(1, W), covariance, start)
+
+
+def start_grams(place, lanes, start, out):
+    block = start[...]
+    lines = lax.broadcasted_iota(jnp.int32, block.shape, 0) + place[2] * block.shape[0]
+    hot_t = jnp.where(lines == lanes[...], 1.0, 0.0).T.astype(bf16)
+    b0, b1, b2 = pieces(block)
+    turned_block = block.T
+    high_t, low_t = halves(turned_block)
+    both = mm(jnp.concatenate([hot_t, high_t]), jnp.concatenate([b0, b1], axis=1))
+    cee = both[:W, :W] + both[:W, W:] + mm(hot_t, b2)
+    g00 = both[W:, :W] + both[W:, W:] + mm(low_t, b0)
+    parts = out.shape[0]
+    bit = W // parts
+    for p in range(parts):
+        lines = slice(p * bit, (p + 1) * bit)
+        out[p, :bit, :] = g00[lines]
+        out[p, bit:, :] = cee[lines]
+
+
+def grams_of_start(place, seeds, start, parts):
+    return pl.pallas_call(
+        start_grams,
+        out_shape=jax.ShapeDtypeStruct((parts, 2 * W // parts, W), f32),
+        in_specs=[SMEM, VMEM, VMEM],
+        out_specs=VMEM,
+        compiler_params=room(16),
+    )(place, seeds.reshape(1, W), start)
 
 
 def cross(a, b):
@@ -327,18 +351,21 @@
     return both[:, :W] + both[:, W:] + mm(low, right[0])
 
 
-def step_grams(mine, out):
-    bit = W // mine.shape[0]
-    step, start = blocks_of(mine, 0, W), blocks_of(mine, W + bit, W)
+def step_grams(place, mine, out):
+    parts = mine.shape[0]
+    step, start = blocks_of(mine, 0, W), turned_blocks(mine, place, W + 2 * W // parts, W, range(parts))
     out[:W, :] = cross(start, step)
     out[W:, :] = cross(step, step)
 
 
 def next_grams(place, mine, following, keep, send):
-    bit = W // mine.shape[0]
-    step, then = blocks_of(mine, 0, W), blocks_of(following, 0, W)
+    parts = mine.shape[0]
+    bit = W // parts
+    step = blocks_of(mine, 0, W)
+    then, g01, g11 = (
+        turned_blocks(following, place, s, n, range(parts)) for s, n in ((0, W), (W, bit), (W + bit, bit))
+    )
     first = place[1] == 0
-    g01, g11 = blocks_of(following, W, bit), blocks_of(following, W + bit, bit)
     g12, g22 = cross(step, then), cross(then, then)
     for out in (keep, send):
         out[:W, :] = g01
@@ -347,7 +374,7 @@
     send[2 * W :, :] = jnp.where(first, g22, g12)
 
 
-def second_product(place, covariance, mine, theirs, grams, out, buffer, sems, total):
+def second_product(place, covariance, mine, theirs, grams, out, small, buffer, sems, total):
     height, breadth = covariance.shape
     half = height // 2
     tall = height // CHUNKS
@@ -360,6 +387,9 @@
     for p in range(parts):
         out[p, W : W + bit, :] = grams[p * bit : (p + 1) * bit, :]
         out[p, W + bit :, :] = grams[W + p * bit : W + (p + 1) * bit, :]
+    for i in range(2):
+        lines = W + i * bit
+        small[i * W : (i + 1) * W, :] = blocks_of(mine, lines, bit) + blocks_of(theirs, lines, bit)
     for i, copy in enumerate(copies):
         lines = slice(i * tall % half // W, (i * tall % half + tall) // W)
         own, other = (mine, theirs) if i * tall < half else (theirs, mine)
@@ -384,19 +414,23 @@
     parts = breadth // W
     return pl.pallas_call(
         second_product,
-        out_shape=jax.ShapeDtypeStruct((parts, W + 2 * (W // parts), W), f32),
+        out_shape=[
+            jax.ShapeDtypeStruct((parts, W + 2 * (W // parts), W), f32),
+            jax.ShapeDtypeStruct((2 * W, W), f32),
+        ],
         in_specs=[SMEM, HBM] + [VMEM] * 3,
-        out_specs=VMEM,
+        out_specs=[VMEM] * 2,
         scratch_shapes=chunk_scratch(covariance) + [pltpu.VMEM((W, breadth), f32)],
+        compiler_params=room(50),
     )(place, covariance, mine, theirs, grams)
 
 
-def basis_rows(core, mine, mine_next, theirs, theirs_next, mix, out, wide, tip):
+def basis_rows(place, mine, mine_next, theirs, theirs_next, mix, out, wide, tip):
     step = pl.program_id(0)
     count = pl.num_programs(0) // 2
     tall = out.shape[0]
     parts = tall // W
-    bit = W // mine.shape[0]
+    bit = 2 * W // mine.shape[0]
 
     @pl.when(step == 0)
     def _():
@@ -408,12 +442,12 @@
         tip[:, W:] = low
 
     def rows(pair, following, part):
-        lines = pl.ds(part, parts)
+        order = [part + p for p in range(parts)]
         left = jnp.concatenate(
             [
-                pair[lines, W + bit :, :].reshape(tall, W),
-                pair[lines, :W, :].reshape(tall, W),
-                following[lines, :W, :].reshape(tall, W),
+                turned_blocks(pair, place, W + bit, W, order),
+                pair[pl.ds(part, parts), :W, :].reshape(tall, W),
+                turned_blocks(following, place, 0, W, order),
             ],
             axis=1,
         )
@@ -432,7 +466,7 @@
         rows(theirs, theirs_next, (step - count) * parts)
 
 
-def basis_of(core, mine, mine_next, theirs, theirs_next, mix):
+def basis_of(place, mine, mine_next, theirs, theirs_next, mix):
     half = mine.shape[0] * W
     tall = 512
     count = half // tall
@@ -445,12 +479,12 @@
             in_specs=[VMEM] * 5,
             out_specs=pl.BlockSpec(
                 (tall, mix.shape[1]),
-                lambda i, c: (jnp.where(i < count, i + c[0] * count, i - count + (1 - c[0]) * count), 0),
+                lambda i, c: (jnp.where(i < count, i + c[1] * count, i - count + (1 - c[1]) * count), 0),
             ),
             scratch_shapes=[pltpu.VMEM((2 * W, 4 * W), bf16), pltpu.VMEM((3 * W, 2 * W), bf16)],
         ),
         compiler_params=room(24),
-    )(core, mine, mine_next, theirs, theirs_next, mix)
+    )(place, mine, mine_next, theirs, theirs_next, mix)
 
 
 def scattered(parts, axis):
@@ -468,7 +502,7 @@
 
 def turned(rows, chips, cores):
     return [
-        ((r * chips + a) * cores + b, (a * chips + r) * cores + b)
+        ((r * chips + a) * cores + b, (a * chips + SLOTS[a][r]) * cores + b)
         for r in range(rows)
         for a in range(chips)
         for b in range(cores)
@@ -484,26 +518,30 @@
     square = (width, width)
     first = core == 0
     turn = turned(rows, chips, cores)
-    place = jnp.stack([row, core, chip * cores + core]).astype(jnp.int32)
+    slots = lax.dynamic_index_in_dim(jnp.array(SLOTS, jnp.int32), row, 0, keepdims=False)
+    place = jnp.concatenate([jnp.stack([row, core, chip * cores + core]).astype(jnp.int32), slots])
     start_piece = scattered(picked_rows(place, seed_index, covariance, rows), ROWS).T
     start_turned = lax.ppermute(start_piece, ALL, turn)
     start = gathered(start_piece, ROWS).reshape(breadth, width)
     start, start_turned = lax.optimization_barrier((start, start_turned))
     keep, send = image_of_start(place, seed_index, covariance, start)
-    mine = gathered(jnp.concatenate([scattered(keep + other_core(send), CHIP), start_turned]), CHIP)
+    got = other_core(send)
+    small = grams_of_start(place, seed_index, start, chips)
+    parts = jnp.concatenate([keep + got, small], axis=1)
+    mine = gathered(jnp.concatenate([scattered(parts, CHIP), start_turned]), CHIP)
     theirs = other_core(mine)
-    (grams,) = kernel(step_grams, [(2 * width, width)], [], mine)
-    parts = image_of_step(place, covariance, mine, theirs, grams)
+    (grams,) = kernel(step_grams, [(2 * width, width)], [], place, mine)
+    parts, zero_grams = image_of_step(place, covariance, mine, theirs, grams)
     piece = lax.ppermute(scattered(parts, ROWS), ALL, turn)
-    (zero_pack,) = kernel(
-        first_factor, [(3 * width, width)], [(width, 2 * width), square, square], place, mine, theirs
-    )
-    mine_next, zero_pack = lax.optimization_barrier((gathered(piece, CHIP), zero_pack))
+    (inv0,) = kernel(first_factor, [square], [(width, 2 * width), square], zero_grams)
+    mine_next, inv0 = lax.optimization_barrier((gathered(piece, CHIP), inv0))
     keep, send = kernel(next_grams, [(3 * width, width)] * 2, [], place, mine, mine_next)
     got = other_core(send)
     theirs_next = other_core(mine_next)
     totals = gathered(keep[2 * width :] + got[2 * width :], ROWS)
-    (pack,) = kernel(middle, [(PACK * width, width)], [(width, 2 * width), square, square], zero_pack, keep, got)
+    (pack,) = kernel(
+        middle, [(PACK * width, width)], [(width, 2 * width), square, square], zero_grams, inv0, keep, got
+    )
     totals, pack = lax.optimization_barrier((totals, pack))
     total = jnp.sum(totals, axis=0)
     rest_total = other_core(total)
@@ -521,7 +559,7 @@
         g12,
         g22,
     )
-    basis = basis_of(place[1:2], mine, mine_next, theirs, theirs_next, mix)
+    basis = basis_of(place, mine, mine_next, theirs, theirs_next, mix)
     return basis, projection, first_pass
 
 

time: 181 us -> 173 us (0.956)
  waiting for transfers between devices: 28.5 us -> 24.9 us
  Pallas kernels: 44.4 us -> 42.5 us
    all_to_all x3, waiting for transfers between devices: 12.6 us -> 5.25 us  [gathered(): return lax.all_to_all(copies, axis, 0, 0, tiled=True)]
    all_to_all x3, starting transfers between devices: 21.4 us -> 14.4 us  [gathered(): return lax.all_to_all(copies, axis, 0, 0, tiled=True)]
    ppermute x1, starting transfers between devices: 0.66 us -> 4.82 us  [local(): start_turned = lax.ppermute(start_piece, ALL, turn)]
    ppermute x1, waiting for transfers between devices: 0.01 us -> 2.34 us  [local(): piece = lax.ppermute(scattered(parts, ROWS), ALL, turn)]
    ppermute x1, starting transfers between devices: 0.8 us -> 2.84 us  [local(): piece = lax.ppermute(scattered(parts, ROWS), ALL, turn)]
    all_to_all x2, blocking collectives: 36 us -> 34.1 us  [scattered(): return jnp.sum(lax.all_to_all(parts, axis, 0, 0, tiled=True), axis=0)]
    add x1, other arithmetic: 1.94 us -> 0.06 us  [local(): parts = jnp.concatenate([keep + got, small], axis=1)]
    ppermute x1, waiting for transfers between devices: 0.01 us -> 1.87 us  [local(): start_turned = lax.ppermute(start_piece, ALL, turn)]
  transfers between devices with their start and end apart: 11 -> 11, of which waited for: 8 -> 9; matrix products, arithmetic and copies ran while one was open for 1% -> 1% of each run, Pallas kernels for 12% -> 13%
where the time goes in v3:
time: 173 us; the launch traced here: 172 us
  blocking collectives  53.1 us (31%)
  Pallas kernels  42.5 us (25%)
  starting transfers between devices  39.6 us (23%)
  waiting for transfers between devices  24.9 us (14%)
  local copies, waits for them, and re-layouts  7.19 us (4%)
  other arithmetic  3.87 us (2%)
    all_to_all x2, blocking collectives, scattered(): return jnp.sum(lax.all_to_all(parts, axis, 0, 0, tiled=True), axis=0)  34.1 us
    pallas_call x5, Pallas kernels, kernel(): pl.pallas_call(body, out_shape=[jax.ShapeDtypeStruct(s, f32) for s in sha...  22.9 us
    all_to_all x1, blocking collectives, gathered(): return lax.all_to_all(copies, axis, 0, 0, tiled=True)  19 us
    all_to_all x3, starting transfers between devices, gathered(): return lax.all_to_all(copies, axis, 0, 0, tiled=True)  14.4 us
    ppermute x5, starting transfers between devices, other_core(): return lax.ppermute(value, CORE, SWAP)  13.8 us
    all_to_all x1, waiting for transfers between devices, scattered(): return jnp.sum(lax.all_to_all(parts, axis, 0, 0, tiled=True), axis=0)  11.6 us
    pallas_call x1, Pallas kernels, image_of_start(): pl.pallas_call(first_product, out_shape=[shape, shape], in_specs=[SMEM, V...  5.44 us
    pallas_call x1, Pallas kernels, basis_of(): pl.pallas_call(basis_rows, out_shape=jax.ShapeDtypeStruct((2 * half, mix....  5.4 us
  transfers between devices with their start and end apart: 11, of which 9 were waited for; matrix products, arithmetic and copies ran while one was open for 1% of the time, Pallas kernels for 13%

profile of v3, /device:TPU:1, one launch (start us, length us, event | category | flops | bytes accessed | tf_op | source)
XLA Modules:
  0.0 172.1 jit_solution(16271842280831892312)
XLA Ops:
  0.6 0.7 dynamic-slice_bitcast_fusion
  1.3 0.6 pad_add_fusion.place
  2.0 3.2 %shard_map.58 = f32[8,128,128]{2,1,0:T(8,128)} custom-call(s32[11]{0:T(128)} %pad_add_fusion.place, s32[128]{0:T(128)} %seeds.1, s32[1,128]{1,0:T(1,128)} %bitcast.10, f32[2048,1024]{1,0:T(8,128)} %covariance.5), custom_call_target="tpu_custom_call" | custom-call | tf_op jit(solution)/shard_map/pallas_call | solution.py:250
  5.1 17.8 %all_to_all.35 = f32[8,128,128]{2,1,0:T(8,128)S(1)} all-to-all(f32[8,128,128]{2,1,0:T(8,128)} %shard_map.58), channel_id=1, replica_groups=mesh['row'=8,'chip'=8,'core'=2] {'row'}, dimensions={0} | all-to-all | bytes 1048576 | tf_op jit(solution)/shard_map/all_to_all | solution.py:491
  23.0 0.0 copy-start.4
  23.0 0.0 copy-start.5
  23.0 0.1 copy.6
  23.1 0.8 broadcast_in_dim.12
  23.9 3.5 %all-to-all-start.1 = ((f32[8,128,128]{2,1,0:T(8,128)}), f32[8,128,128]{2,1,0:T(8,128)S(1)}, u32[]{:S(2)}, u32[]{:S(2)}) async-start(f32[8,128,128]{2,1,0:T(8,128)} %broadcast_in_dim.12), calls=%async_computation.1 | async-start | bytes 1048576 | tf_op jit(solution)/shard_map/all_to_all | solution.py:496
  27.4 4.8 %collective-permute-start = (f32[128,128]{0,1:T(8,128)S(1)}, f32[128,128]{0,1:T(8,128)S(1)}, u32[]{:S(2)}, u32[]{:S(2)}) collective-permute-start(f32[128,128]{0,1:T(8,128)S(1)} %bitcast.14), channel_id=1, source_target_pairs={{0,4},{1,5},{2,30},{3,31},{4,34},{5,35},{6,56},{7,57},{8,74},{9,75... | collective-permute-start | bytes 196616 | tf_op jit(solution)/shard_map/ppermute | solution.py:524
  32.3 1.9 %collective-permute-done = f32[128,128]{0,1:T(8,128)S(1)} collective-permute-done((f32[128,128]{0,1:T(8,128)S(1)}, f32[128,128]{0,1:T(8,128)S(1)}, u32[]{:S(2)}, u32[]{:S(2)}) %collective-permute-start) | collective-permute-done | bytes 65568 | tf_op jit(solution)/shard_map/ppermute | solution.py:524
  34.1 1.9 %all-to-all-done.1 = f32[8,128,128]{2,1,0:T(8,128)S(1)} async-done(((f32[8,128,128]{2,1,0:T(8,128)}), f32[8,128,128]{2,1,0:T(8,128)S(1)}, u32[]{:S(2)}, u32[]{:S(2)}) %all-to-all-start.1) | async-done | bytes 524320 | tf_op jit(solution)/shard_map/all_to_all | solution.py:496
  36.0 0.0 copy-done.4
  36.0 0.0 copy-done.5
  36.0 5.4 %shard_map.59 = (f32[8,128,128]{2,1,0:T(8,128)S(1)}, f32[8,128,128]{2,1,0:T(8,128)S(1)}) custom-call(s32[11]{0:T(128)S(1)} %copy-done.4, s32[1,128]{1,0:T(1,128)S(1)} %bitcast.11, f32[2048,1024]{1,0:T(8,128)} %covariance.5, f32[1024,128]{1,0:T(8,128)S(1)} %bitcast.8), custom_call_target="tpu_custom_call" | custom-call | tf_op jit(solution)/shard_map/pallas_call | solution.py:309
  41.5 6.4 %collective-permute-start.1 = (f32[8,128,128]{2,1,0:T(8,128)S(1)}, f32[8,128,128]{2,1,0:T(8,128)S(1)}, u32[]{:S(2)}, u32[]{:S(2)}) collective-permute-start(f32[8,128,128]{2,1,0:T(8,128)S(1)} %get-tuple-element.20), channel_id=1, source_target_pairs={{0,1},{1,0},{2,3},{3,2},{4,5},{5,4},{6,7},{7,6},{8,9},{9,8},{10,11... | collective-permute-start | bytes 1572872 | tf_op jit(solution)/shard_map/ppermute | solution.py:500
  47.8 1.1 shard_map.60
  48.9 0.5 collective-permute-done.1
  49.4 0.1 add.15
  49.4 0.9 pad_maximum_fusion
  50.3 3.8 %all-to-all-start.2 = ((f32[8,160,128]{2,1,0:T(8,128)}), f32[8,160,128]{2,1,0:T(8,128)S(1)}, u32[]{:S(2)}, u32[]{:S(2)}) async-start(f32[8,160,128]{2,1,0:T(8,128)} %pad_maximum_fusion), calls=%async_computation.2 | async-start | bytes 1310720 | tf_op jit(solution)/shard_map/all_to_all | solution.py:491
  54.1 0.1 copy.7
  54.2 11.6 %all-to-all-done.2 = f32[8,160,128]{2,1,0:T(8,128)S(1)} async-done(((f32[8,160,128]{2,1,0:T(8,128)}), f32[8,160,128]{2,1,0:T(8,128)S(1)}, u32[]{:S(2)}, u32[]{:S(2)}) %all-to-all-start.2) | async-done | bytes 655392 | tf_op jit(solution)/shard_map/all_to_all | solution.py:491
  65.8 0.1 broadcast_in_dim.13
  65.9 19.0 %all_to_all.36.mine = f32[8,288,128]{2,1,0:T(8,128)S(1)} all-to-all(f32[8,288,128]{2,1,0:T(8,128)S(1)} %broadcast_in_dim.13), channel_id=1, replica_groups=mesh['row'=8,'chip'=8,'core'=2] {'chip'}, dimensions={0} | all-to-all | bytes 2359296 | tf_op jit(solution)/shard_map/all_to_all | solution.py:496
  84.9 1.4 collective-permute-start.2
  86.4 1.0 shard_map.61.grams
  87.4 1.4 collective-permute-done.2.theirs
  88.9 4.5 %shard_map.62 = (f32[8,160,128]{2,1,0:T(8,128)S(1)}, f32[256,128]{1,0:T(8,128)S(1)}) custom-call(s32[11]{0:T(128)S(1)} %copy-done.4, f32[2048,1024]{1,0:T(8,128)} %covariance.5, f32[8,288,128]{2,1,0:T(8,128)S(1)} %all_to_all.36.mine, f32[8,288,128]{2,1,0:T(8,128)S(1)} %collective-permute-done.2.theirs, f32[256,128]{1,0:T(8,128)S(1)} %shard_map.61.grams), custom_call_target="tpu_custom_call" | custom-call | tf_op jit(solution)/shard_map/pallas_call | solution.py:415
  93.4 16.2 %all_to_all.37 = f32[8,160,128]{2,1,0:T(8,128)} all-to-all(f32[8,160,128]{2,1,0:T(8,128)S(1)} %get-tuple-element.22), channel_id=1, replica_groups=mesh['row'=8,'chip'=8,'core'=2] {'row'}, dimensions={0} | all-to-all | bytes 1310720 | tf_op jit(solution)/shard_map/all_to_all | solution.py:491
  109.6 1.1 reduce_sum.38
  110.8 2.8 %collective-permute-start.3 = (f32[160,128]{1,0:T(8,128)S(1)}, f32[160,128]{1,0:T(8,128)S(1)}, u32[]{:S(2)}, u32[]{:S(2)}) collective-permute-start(f32[160,128]{1,0:T(8,128)S(1)} %reduce_sum.38), channel_id=1, source_target_pairs={{0,4},{1,5},{2,30},{3,31},{4,34},{5,35},{6,56},{7,57},{8,74},{9,75... | collective-permute-start | bytes 245768 | tf_op jit(solution)/shard_map/ppermute | solution.py:535
  113.6 2.3 %collective-permute-done.3 = f32[160,128]{1,0:T(8,128)S(1)} collective-permute-done((f32[160,128]{1,0:T(8,128)S(1)}, f32[160,128]{1,0:T(8,128)S(1)}, u32[]{:S(2)}, u32[]{:S(2)}) %collective-permute-start.3) | collective-permute-done | bytes 81952 | tf_op jit(solution)/shard_map/ppermute | solution.py:535
  116.0 0.9 broadcast_in_dim.14
  116.8 6.8 %all-to-all-start.5 = ((f32[8,160,128]{2,1,0:T(8,128)}), f32[8,160,128]{2,1,0:T(8,128)S(1)}, u32[]{:S(2)}, u32[]{:S(2)}) async-start(f32[8,160,128]{2,1,0:T(8,128)} %broadcast_in_dim.14), calls=%async_computation.5 | async-start | bytes 1310720 | tf_op jit(solution)/shard_map/all_to_all | solution.py:496
  123.6 4.5 %shard_map.63.inv0 = f32[128,128]{1,0:T(8,128)S(1)} custom-call(f32[256,128]{1,0:T(8,128)S(1)} %get-tuple-element.23.g00.start), custom_call_target="tpu_custom_call" | custom-call | tf_op jit(solution)/shard_map/pallas_call | solution.py:198
  128.2 0.0 copy-start.2
  128.2 0.6 copy-done.2
  128.8 3.4 %all-to-all-done.5.following.mine_next = f32[8,160,128]{2,1,0:T(8,128)S(1)} async-done(((f32[8,160,128]{2,1,0:T(8,128)}), f32[8,160,128]{2,1,0:T(8,128)S(1)}, u32[]{:S(2)}, u32[]{:S(2)}) %all-to-all-start.5) | async-done | bytes 655392 | tf_op jit(solution)/shard_map/all_to_all | solution.py:496
  132.2 1.0 shard_map.64
  133.2 4.2 %collective-permute-start.5 = (f32[384,128]{1,0:T(8,128)S(1)}, f32[384,128]{1,0:T(8,128)S(1)}, u32[]{:S(2)}, u32[]{:S(2)}) collective-permute-start(f32[384,128]{1,0:T(8,128)S(1)} %get-tuple-element.26), channel_id=1, source_target_pairs={{0,1},{1,0},{2,3},{3,2},{4,5},{5,4},{6,7},{7,6},{8,9},{9,8},{10,11... | collective-permute-start | bytes 589832 | tf_op jit(solution)/shard_map/ppermute | solution.py:500
  137.4 1.1 collective-permute-done.5.got
  138.5 0.8 broadcast_in_dim.15
  139.3 4.1 %all-to-all-start.6 = ((f32[8,128,128]{2,1,0:T(8,128)}), f32[8,128,128]{2,1,0:T(8,128)}, u32[]{:S(2)}, u32[]{:S(2)}) async-start(f32[8,128,128]{2,1,0:T(8,128)} %broadcast_in_dim.15), calls=%async_computation.6 | async-start | bytes 1048576 | tf_op jit(solution)/shard_map/all_to_all | solution.py:496
  143.5 0.6 collective-permute-start.4
  144.1 0.0 copy-start.3
  144.1 0.8 copy-done.3
  144.9 8.2 %shard_map.65.refs_0_ = f32[2176,128]{1,0:T(8,128)S(1)} custom-call(f32[256,128]{1,0:T(8,128)S(1)} %get-tuple-element.23.g00.start, f32[128,128]{1,0:T(8,128)S(1)} %copy-done.3, f32[384,128]{1,0:T(8,128)S(1)} %get-tuple-element.25.keep, f32[384,128]{1,0:T(8,128)S(1)} %collective-permute-done.5.got), custom_call_target="tpu_custom_call" | custom-call | tf_op jit(solution)/shard_map/pallas_call | solution.py:198
  153.1 0.0 copy-start
  153.1 1.0 copy-done
  154.1 0.0 all-to-all-done.6
  154.1 1.1 reduce_sum.39
  155.2 1.1 collective-permute-start.6
  156.3 0.9 collective-permute-done.6
  157.2 0.0 copy-start.1
  157.3 1.2 copy-done.1
  158.5 8.2 %shard_map.66 = (f32[384,384]{1,0:T(8,128)S(1)}, f32[384,256]{1,0:T(8,128)}, f32[384,256]{1,0:T(8,128)}) custom-call(f32[2176,128]{1,0:T(8,128)S(1)} %copy-done.1, f32[128,128]{1,0:T(8,128)S(1)} %get-tuple-element.34.refs_1_, f32[128,128]{1,0:T(8,128)S(1)} %get-tuple-element.33.refs_2_), custom_call_target="tpu_custom_call" | custom-call | tf_op jit(solution)/shard_map/pallas_call | solution.py:198
  166.7 0.0 collective-permute-done.4.theirs_next
  166.7 5.4 %shard_map.67 = f32[2048,384]{1,0:T(8,128)} custom-call(s32[11]{0:T(128)S(1)} %copy-done.4, f32[8,288,128]{2,1,0:T(8,128)S(1)} %all_to_all.36.mine, f32[8,160,128]{2,1,0:T(8,128)S(1)} %all-to-all-done.5.following.mine_next, f32[8,288,128]{2,1,0:T(8,128)S(1)} %collective-permute-done.2.theirs, f32[8,160,128]{2,1,0:T(8,128)} %collective-permute-done.4.theirs_next, ...), custom_call_target="tpu_custom_call" | custom-call | tf_op jit(solution)/shard_map/pallas_call | solution.py:473
  (5 shorter events, 0.1 us)
Async XLA Ops:
  23.0 13.0 %copy-start.4 = (s32[11]{0:T(128)S(1)}, s32[11]{0:T(128)}, u32[]{:S(2)}) copy-start(s32[11]{0:T(128)} %pad_add_fusion.place) | copy-start | bytes 136
  23.0 13.0 %copy-start.5 = (s32[128]{0:T(128)S(1)}, s32[128]{0:T(128)}, u32[]{:S(2)}) copy-start(s32[128]{0:T(128)} %seeds.1) | copy-start | bytes 1540
  23.9 12.1 %all-to-all-start.1 = ((f32[8,128,128]{2,1,0:T(8,128)}), f32[8,128,128]{2,1,0:T(8,128)S(1)}, u32[]{:S(2)}, u32[]{:S(2)}) async-start(f32[8,128,128]{2,1,0:T(8,128)} %broadcast_in_dim.12), calls=%async_computation.1 | async-start | bytes 1048576 | tf_op jit(solution)/shard_map/all_to_all | solution.py:496
  27.4 6.7 %collective-permute-start = (f32[128,128]{0,1:T(8,128)S(1)}, f32[128,128]{0,1:T(8,128)S(1)}, u32[]{:S(2)}, u32[]{:S(2)}) collective-permute-start(f32[128,128]{0,1:T(8,128)S(1)} %bitcast.14), channel_id=1, source_target_pairs={{0,4},{1,5},{2,30},{3,31},{4,34},{5,35},{6,56},{7,57},{8,74},{9,75... | collective-permute-start | bytes 196616 | tf_op jit(solution)/shard_map/ppermute | solution.py:524
  41.5 7.9 %collective-permute-start.1 = (f32[8,128,128]{2,1,0:T(8,128)S(1)}, f32[8,128,128]{2,1,0:T(8,128)S(1)}, u32[]{:S(2)}, u32[]{:S(2)}) collective-permute-start(f32[8,128,128]{2,1,0:T(8,128)S(1)} %get-tuple-element.20), channel_id=1, source_target_pairs={{0,1},{1,0},{2,3},{3,2},{4,5},{5,4},{6,7},{7,6},{8,9},{9,8},{10,11... | collective-permute-start | bytes 1572872 | tf_op jit(solution)/shard_map/ppermute | solution.py:500
  50.3 15.4 %all-to-all-start.2 = ((f32[8,160,128]{2,1,0:T(8,128)}), f32[8,160,128]{2,1,0:T(8,128)S(1)}, u32[]{:S(2)}, u32[]{:S(2)}) async-start(f32[8,160,128]{2,1,0:T(8,128)} %pad_maximum_fusion), calls=%async_computation.2 | async-start | bytes 1310720 | tf_op jit(solution)/shard_map/all_to_all | solution.py:491
  84.9 3.9 %collective-permute-start.2 = (f32[8,288,128]{2,1,0:T(8,128)S(1)}, f32[8,288,128]{2,1,0:T(8,128)S(1)}, u32[]{:S(2)}, u32[]{:S(2)}) collective-permute-start(f32[8,288,128]{2,1,0:T(8,128)S(1)} %all_to_all.36.mine), channel_id=1, source_target_pairs={{0,1},{1,0},{2,3},{3,2},{4,5},{5,4},{6,7},{7,6},{8,9},{9,8},{10,11... | collective-permute-start | bytes 3538952 | tf_op jit(solution)/shard_map/ppermute | solution.py:500
  110.8 5.2 %collective-permute-start.3 = (f32[160,128]{1,0:T(8,128)S(1)}, f32[160,128]{1,0:T(8,128)S(1)}, u32[]{:S(2)}, u32[]{:S(2)}) collective-permute-start(f32[160,128]{1,0:T(8,128)S(1)} %reduce_sum.38), channel_id=1, source_target_pairs={{0,4},{1,5},{2,30},{3,31},{4,34},{5,35},{6,56},{7,57},{8,74},{9,75... | collective-permute-start | bytes 245768 | tf_op jit(solution)/shard_map/ppermute | solution.py:535
  116.8 15.3 %all-to-all-start.5 = ((f32[8,160,128]{2,1,0:T(8,128)}), f32[8,160,128]{2,1,0:T(8,128)S(1)}, u32[]{:S(2)}, u32[]{:S(2)}) async-start(f32[8,160,128]{2,1,0:T(8,128)} %broadcast_in_dim.14), calls=%async_computation.5 | async-start | bytes 1310720 | tf_op jit(solution)/shard_map/all_to_all | solution.py:496
  128.2 0.6 copy-start.2
  133.2 5.3 %collective-permute-start.5 = (f32[384,128]{1,0:T(8,128)S(1)}, f32[384,128]{1,0:T(8,128)S(1)}, u32[]{:S(2)}, u32[]{:S(2)}) collective-permute-start(f32[384,128]{1,0:T(8,128)S(1)} %get-tuple-element.26), channel_id=1, source_target_pairs={{0,1},{1,0},{2,3},{3,2},{4,5},{5,4},{6,7},{7,6},{8,9},{9,8},{10,11... | collective-permute-start | bytes 589832 | tf_op jit(solution)/shard_map/ppermute | solution.py:500
  139.3 14.8 %all-to-all-start.6 = ((f32[8,128,128]{2,1,0:T(8,128)}), f32[8,128,128]{2,1,0:T(8,128)}, u32[]{:S(2)}, u32[]{:S(2)}) async-start(f32[8,128,128]{2,1,0:T(8,128)} %broadcast_in_dim.15), calls=%async_computation.6 | async-start | bytes 1048576 | tf_op jit(solution)/shard_map/all_to_all | solution.py:496
  143.5 23.2 %collective-permute-start.4 = (f32[8,160,128]{2,1,0:T(8,128)S(1)}, f32[8,160,128]{2,1,0:T(8,128)}, u32[]{:S(2)}, u32[]{:S(2)}) collective-permute-start(f32[8,160,128]{2,1,0:T(8,128)S(1)} %all-to-all-done.5.following.mine_next), channel_id=1, source_target_pairs={{0,1},{1,0},{2,3},{3,2},{4,5},{5,4},{6,7},{7,6},{8,9},{9,8},{10,11... | collective-permute-start | bytes 1966088 | tf_op jit(solution)/shard_map/ppermute | solution.py:500
  144.1 0.8 copy-start.3
  153.1 1.0 copy-start
  155.2 2.0 %collective-permute-start.6 = (f32[128,128]{1,0:T(8,128)S(1)}, f32[128,128]{1,0:T(8,128)S(1)}, u32[]{:S(2)}, u32[]{:S(2)}) collective-permute-start(f32[128,128]{1,0:T(8,128)S(1)} %reduce_sum.39), channel_id=1, source_target_pairs={{0,1},{1,0},{2,3},{3,2},{4,5},{5,4},{6,7},{7,6},{8,9},{9,8},{10,11... | collective-permute-start | bytes 196616 | tf_op jit(solution)/shard_map/ppermute | solution.py:500
  157.2 1.3 copy-start.1

commit v4 on v3

--- a/solution.py
+++ b/solution.py
@@ -109,7 +109,7 @@
 
 
 def turned_blocks(ref, place, start, count, parts):
-    return jnp.concatenate([ref[place[3 + p], start : start + count, :] for p in parts])
+    return jnp.concatenate([ref[place[3 + place[0] * ref.shape[0] + p], start : start + count, :] for p in parts])
 
 
 def first_factor(g00, inverse, work, upper):
@@ -150,18 +150,18 @@
 PACK = 17
 
 
-def last(scale, pack, g12, g22, mix, projection, first_pass, work, upper2, inv2):
-    first, full, upper1, _, c1_top, c1_low, m00, m01, m11, a02, a00, a01, a11, li0, first0, part1, s1 = (
+def last(scale, pack, totals, mix, projection, first_pass, work, upper2, inv2):
+    first, full, upper1, _, _, c1_low, m00, m01, m11, a02, a00, a01, a11, li0, first0, part1, s1 = (
         pack[i * W : (i + 1) * W, :] for i in range(PACK)
     )
     i1 = pack[3 * W : 6 * W, :]
     c1 = i1[W:]
-    a12 = g12[...]
+    a12, a22 = unpacked(totals[...])
     gram = jnp.concatenate(
         [
             jnp.concatenate([a00, a01, a02], axis=1),
             jnp.concatenate([a01.T, a11, a12], axis=1),
-            jnp.concatenate([a02.T, a12.T, g22[...]], axis=1),
+            jnp.concatenate([a02.T, a12, a22], axis=1),
         ]
     )
     h = jnp.concatenate([first0, part1 + tn(c1_low, s1 + nn(a12, c1_low))])
@@ -351,31 +351,46 @@
     return both[:, :W] + both[:, W:] + mm(low, right[0])
 
 
-def step_grams(place, mine, out):
-    parts = mine.shape[0]
-    step, start = blocks_of(mine, 0, W), turned_blocks(mine, place, W + 2 * W // parts, W, range(parts))
-    out[:W, :] = cross(start, step)
+def step_grams(mine, start, out):
+    step = blocks_of(mine, 0, W)
+    out[:W, :] = cross(start[...], step)
     out[W:, :] = cross(step, step)
 
 
-def next_grams(place, mine, following, keep, send):
+def corner():
+    return lax.broadcasted_iota(jnp.int32, (W, W), 0), lax.broadcasted_iota(jnp.int32, (W, W), 1)
+
+
+SPARE = 8
+
+
+def next_grams(place, mine, following, out):
     parts = mine.shape[0]
     bit = W // parts
     step = blocks_of(mine, 0, W)
     then, g01, g11 = (
         turned_blocks(following, place, s, n, range(parts)) for s, n in ((0, W), (W, bit), (W + bit, bit))
     )
-    first = place[1] == 0
     g12, g22 = cross(step, then), cross(then, then)
-    for out in (keep, send):
-        out[:W, :] = g01
-        out[W : 2 * W, :] = g11
-    keep[2 * W :, :] = jnp.where(first, g12, g22)
-    send[2 * W :, :] = jnp.where(first, g22, g12)
+    i, j = corner()
+    out[:W, :] = g01
+    out[W : 2 * W, :] = g11
+    out[2 * W : 3 * W, :] = jnp.where(j >= i, g22, g12)
+    diagonal = jnp.sum(jnp.where(i == j, g12, 0.0), axis=0, keepdims=True)
+    out[3 * W :, :] = jnp.broadcast_to(diagonal, (SPARE, W))
+
+
+def unpacked(totals):
+    total = jnp.sum(totals, axis=0)
+    body = total[:W]
+    i, j = corner()
+    lower = jnp.where(j < i, body, 0.0)
+    g12 = lower + lower.T + jnp.where(i == j, total[W : W + 1], 0.0)
+    return g12, jnp.where(j >= i, body, 0.0) + jnp.where(j > i, body, 0.0).T
 
 
 def second_product(place, covariance, mine, theirs, grams, out, small, buffer, sems, total):
-    height, breadth = covariance.shape
+    height, _ = covariance.shape
     half = height // 2
     tall = height // CHUNKS
     copies = chunks_of(covariance, buffer, sems)
@@ -425,12 +440,11 @@
     )(place, covariance, mine, theirs, grams)
 
 
-def basis_rows(place, mine, mine_next, theirs, theirs_next, mix, out, wide, tip):
+def basis_rows(place, mine, mine_start, mine_next, theirs, theirs_start, theirs_next, mix, out, wide, tip):
     step = pl.program_id(0)
     count = pl.num_programs(0) // 2
     tall = out.shape[0]
     parts = tall // W
-    bit = 2 * W // mine.shape[0]
 
     @pl.when(step == 0)
     def _():
@@ -441,11 +455,11 @@
         tip[:, :W] = high
         tip[:, W:] = low
 
-    def rows(pair, following, part):
+    def rows(pair, start, following, part):
         order = [part + p for p in range(parts)]
         left = jnp.concatenate(
             [
-                turned_blocks(pair, place, W + bit, W, order),
+                start[pl.ds(pl.multiple_of(part * W, tall), tall), :],
                 pair[pl.ds(part, parts), :W, :].reshape(tall, W),
                 turned_blocks(following, place, 0, W, order),
             ],
@@ -459,14 +473,14 @@
 
     @pl.when(step < count)
     def _():
-        rows(mine, mine_next, step * parts)
+        rows(mine, mine_start, mine_next, step * parts)
 
     @pl.when(step >= count)
     def _():
-        rows(theirs, theirs_next, (step - count) * parts)
-
-
-def basis_of(place, mine, mine_next, theirs, theirs_next, mix):
+        rows(theirs, theirs_start, theirs_next, (step - count) * parts)
+
+
+def basis_of(place, mine, mine_start, mine_next, theirs, theirs_start, theirs_next, mix):
     half = mine.shape[0] * W
     tall = 512
     count = half // tall
@@ -476,7 +490,7 @@
         grid_spec=pltpu.PrefetchScalarGridSpec(
             num_scalar_prefetch=1,
             grid=(2 * count,),
-            in_specs=[VMEM] * 5,
+            in_specs=[VMEM] * 7,
             out_specs=pl.BlockSpec(
                 (tall, mix.shape[1]),
                 lambda i, c: (jnp.where(i < count, i + c[1] * count, i - count + (1 - c[1]) * count), 0),
@@ -484,7 +498,7 @@
             scratch_shapes=[pltpu.VMEM((2 * W, 4 * W), bf16), pltpu.VMEM((3 * W, 2 * W), bf16)],
         ),
         compiler_params=room(24),
-    )(place, mine, mine_next, theirs, theirs_next, mix)
+    )(place, mine, mine_start, mine_next, theirs, theirs_start, theirs_next, mix)
 
 
 def scattered(parts, axis):
@@ -516,36 +530,33 @@
     row, chip, core = (lax.axis_index(a) for a in ALL)
     order = height * rows
     square = (width, width)
-    first = core == 0
     turn = turned(rows, chips, cores)
-    slots = lax.dynamic_index_in_dim(jnp.array(SLOTS, jnp.int32), row, 0, keepdims=False)
+    slots = jnp.array(SLOTS, jnp.int32).reshape(-1)
     place = jnp.concatenate([jnp.stack([row, core, chip * cores + core]).astype(jnp.int32), slots])
     start_piece = scattered(picked_rows(place, seed_index, covariance, rows), ROWS).T
-    start_turned = lax.ppermute(start_piece, ALL, turn)
     start = gathered(start_piece, ROWS).reshape(breadth, width)
-    start, start_turned = lax.optimization_barrier((start, start_turned))
+    mine_start = lax.ppermute(start, ALL, turn)
     keep, send = image_of_start(place, seed_index, covariance, start)
     got = other_core(send)
     small = grams_of_start(place, seed_index, start, chips)
     parts = jnp.concatenate([keep + got, small], axis=1)
-    mine = gathered(jnp.concatenate([scattered(parts, CHIP), start_turned]), CHIP)
+    step = scattered(parts, CHIP)
+    mine = gathered(step, CHIP)
     theirs = other_core(mine)
-    (grams,) = kernel(step_grams, [(2 * width, width)], [], place, mine)
+    (grams,) = kernel(step_grams, [(2 * width, width)], [], mine, mine_start)
     parts, zero_grams = image_of_step(place, covariance, mine, theirs, grams)
     piece = lax.ppermute(scattered(parts, ROWS), ALL, turn)
     (inv0,) = kernel(first_factor, [square], [(width, 2 * width), square], zero_grams)
     mine_next, inv0 = lax.optimization_barrier((gathered(piece, CHIP), inv0))
-    keep, send = kernel(next_grams, [(3 * width, width)] * 2, [], place, mine, mine_next)
-    got = other_core(send)
+    (keep,) = kernel(next_grams, [(3 * width + SPARE, width)], [], place, mine, mine_next)
+    got = other_core(keep)
+    totals = gathered(keep[2 * width :] + got[2 * width :], ROWS)
     theirs_next = other_core(mine_next)
-    totals = gathered(keep[2 * width :] + got[2 * width :], ROWS)
+    theirs_start = other_core(mine_start)
     (pack,) = kernel(
         middle, [(PACK * width, width)], [(width, 2 * width), square, square], zero_grams, inv0, keep, got
     )
     totals, pack = lax.optimization_barrier((totals, pack))
-    total = jnp.sum(totals, axis=0)
-    rest_total = other_core(total)
-    g12, g22 = jnp.where(first, total, rest_total), jnp.where(first, rest_total, total)
     scale = float(order) ** 0.5
 
     def last_step(*refs):
@@ -556,16 +567,16 @@
         [(3 * width, 3 * width), (3 * width, 2 * width), (3 * width, 2 * width)],
         [(width, 2 * width), square, square],
         pack,
-        g12,
-        g22,
-    )
-    basis = basis_of(place, mine, mine_next, theirs, theirs_next, mix)
+        totals,
+    )
+    basis = basis_of(place, mine, mine_start, mine_next, theirs, theirs_start, theirs_next, mix)
     return basis, projection, first_pass
 
 
 def solution(mesh):
     rows, cols = mesh.devices.shape
     fine = Mesh(mesh.devices.reshape(rows, cols // 2, 2), ALL)
+
     return jax.shard_map(
         local,
         mesh=fine,

time: 173 us -> 197 us (1.14)
  blocking collectives: 53.1 us -> 71.9 us
  waiting for transfers between devices: 24.9 us -> 40.3 us
  starting transfers between devices: 39.6 us -> 34.5 us
  local copies, waits for them, and re-layouts: 7.19 us -> 2.84 us
  other arithmetic: 3.87 us -> 1.53 us
  Pallas kernels: 42.5 us -> 44.5 us
    ppermute x1, waiting for transfers between devices: 1.87 us -> 32.4 us  [local(): mine_start = lax.ppermute(start, ALL, turn)]
    all_to_all x2 -> x3, blocking collectives: 34.1 us -> 47.5 us  [scattered(): return jnp.sum(lax.all_to_all(parts, axis, 0, 0, tiled=True), axis=0)]
    all_to_all x1 -> x0, waiting for transfers between devices: 11.6 us -> none  [scattered(): return jnp.sum(lax.all_to_all(parts, axis, 0, 0, tiled=True), axis=0)]
    all_to_all x1 -> x2, blocking collectives: 19 us -> 24.4 us  [gathered(): return lax.all_to_all(copies, axis, 0, 0, tiled=True)]
    all_to_all x1 -> x0, starting transfers between devices: 3.77 us -> none  [scattered(): return jnp.sum(lax.all_to_all(parts, axis, 0, 0, tiled=True), axis=0)]
    ppermute x5, waiting for transfers between devices: 3.87 us -> 1.04 us  [other_core(): return lax.ppermute(value, CORE, SWAP)]
    ppermute x1, starting transfers between devices: 2.84 us -> 5.63 us  [local(): piece = lax.ppermute(scattered(parts, ROWS), ALL, turn)]
    unnamed x12 -> x8, local copies, waits for them, and re-layouts: 3.7 us -> 0.94 us
  transfers between devices with their start and end apart: 11 -> 9, of which waited for: 9 -> 6; matrix products, arithmetic and copies ran while one was open for 1% -> 0% of each run, Pallas kernels for 13% -> 13%
where the time goes in v4:
time: 197 us; the launch traced here: 196 us
  blocking collectives  71.9 us (36%)
  Pallas kernels  44.5 us (23%)
  waiting for transfers between devices  40.3 us (20%)
  starting transfers between devices  34.5 us (18%)
  local copies, waits for them, and re-layouts  2.84 us (1%)
    all_to_all x3, blocking collectives, scattered(): return jnp.sum(lax.all_to_all(parts, axis, 0, 0, tiled=True), axis=0)  47.5 us
    ppermute x1, waiting for transfers between devices, local(): mine_start = lax.ppermute(start, ALL, turn)  32.4 us
    pallas_call x5, Pallas kernels, kernel(): pl.pallas_call(body, out_shape=[jax.ShapeDtypeStruct(s, f32) for s in sha...  24.6 us
    all_to_all x2, blocking collectives, gathered(): return lax.all_to_all(copies, axis, 0, 0, tiled=True)  24.4 us
    all_to_all x2, starting transfers between devices, gathered(): return lax.all_to_all(copies, axis, 0, 0, tiled=True)  14.5 us
    ppermute x5, starting transfers between devices, other_core(): return lax.ppermute(value, CORE, SWAP)  11.6 us
    pallas_call x1, Pallas kernels, basis_of(): pl.pallas_call(basis_rows, out_shape=jax.ShapeDtypeStruct((2 * half, mix....  5.74 us
    ppermute x1, starting transfers between devices, local(): piece = lax.ppermute(scattered(parts, ROWS), ALL, turn)  5.63 us
  transfers between devices with their start and end apart: 9, of which 6 were waited for; matrix products, arithmetic and copies ran while one was open for 0% of the time, Pallas kernels for 13%

profile of v4, /device:TPU:1, one launch (start us, length us, event | category | flops | bytes accessed | tf_op | source)
XLA Modules:
  0.0 196.3 jit_solution(6026090682604353383)
XLA Ops:
  0.6 1.3 pad_add_fusion.place
  1.9 3.2 %shard_map.58 = f32[8,128,128]{2,1,0:T(8,128)} custom-call(s32[67]{0:T(128)} %pad_add_fusion.place, s32[128]{0:T(128)} %seeds.1, s32[1,128]{1,0:T(1,128)} %bitcast.9, f32[2048,1024]{1,0:T(8,128)} %covariance.5), custom_call_target="tpu_custom_call" | custom-call | tf_op jit(solution)/shard_map/pallas_call | solution.py:250
  5.1 0.0 copy-start.2
  5.1 0.0 copy-start.3
  5.1 17.7 %all_to_all.35 = f32[8,128,128]{2,1,0:T(8,128)S(1)} all-to-all(f32[8,128,128]{2,1,0:T(8,128)} %shard_map.58), channel_id=1, replica_groups=mesh['row'=8,'chip'=8,'core'=2] {'row'}, dimensions={0} | all-to-all | bytes 1048576 | tf_op jit(solution)/shard_map/all_to_all | solution.py:505
  22.9 0.1 copy.6
  23.0 12.1 %all_to_all.36 = f32[8,128,128]{2,1,0:T(8,128)S(1)} all-to-all(f32[8,128,128]{2,1,0:T(8,128)S(1)} %broadcast_in_dim.12), channel_id=1, replica_groups=mesh['row'=8,'chip'=8,'core'=2] {'row'}, dimensions={0} | all-to-all | bytes 1048576 | tf_op jit(solution)/shard_map/all_to_all | solution.py:510
  35.1 0.0 copy-done.2
  35.1 0.0 copy-done.3
  35.1 5.4 %shard_map.59 = (f32[8,128,128]{2,1,0:T(8,128)S(1)}, f32[8,128,128]{2,1,0:T(8,128)S(1)}) custom-call(s32[67]{0:T(128)S(1)} %copy-done.2, s32[1,128]{1,0:T(1,128)S(1)} %bitcast.10, f32[2048,1024]{1,0:T(8,128)} %covariance.5, f32[1024,128]{1,0:T(8,128)S(1)} %bitcast.6), custom_call_target="tpu_custom_call" | custom-call | tf_op jit(solution)/shard_map/pallas_call | solution.py:309
  40.6 3.5 %collective-permute-start = (f32[8,128,128]{2,1,0:T(8,128)S(1)}, f32[8,128,128]{2,1,0:T(8,128)S(1)}, u32[]{:S(2)}, u32[]{:S(2)}) collective-permute-start(f32[8,128,128]{2,1,0:T(8,128)S(1)} %get-tuple-element.15), channel_id=1, source_target_pairs={{0,1},{1,0},{2,3},{3,2},{4,5},{5,4},{6,7},{7,6},{8,9},{9,8},{10,11... | collective-permute-start | bytes 1572872 | tf_op jit(solution)/shard_map/ppermute | solution.py:514
  44.1 1.1 shard_map.60
  45.2 0.5 collective-permute-done
  45.6 0.1 add.10
  45.8 15.7 %all_to_all.37 = f32[8,160,128]{2,1,0:T(8,128)S(1)} all-to-all(f32[8,160,128]{2,1,0:T(8,128)S(1)} %pad_maximum_fusion), channel_id=1, replica_groups=mesh['row'=8,'chip'=8,'core'=2] {'chip'}, dimensions={0} | all-to-all | bytes 1310720 | tf_op jit(solution)/shard_map/all_to_all | solution.py:505
  61.6 12.3 %all_to_all.38.mine = f32[8,160,128]{2,1,0:T(8,128)S(1)} all-to-all(f32[8,160,128]{2,1,0:T(8,128)S(1)} %broadcast_in_dim.13), channel_id=1, replica_groups=mesh['row'=8,'chip'=8,'core'=2] {'chip'}, dimensions={0} | all-to-all | bytes 1310720 | tf_op jit(solution)/shard_map/all_to_all | solution.py:510
  73.8 2.6 %collective-permute-start.2 = (f32[8,160,128]{2,1,0:T(8,128)S(1)}, f32[8,160,128]{2,1,0:T(8,128)S(1)}, u32[]{:S(2)}, u32[]{:S(2)}) collective-permute-start(f32[8,160,128]{2,1,0:T(8,128)S(1)} %all_to_all.38.mine), channel_id=1, source_target_pairs={{0,1},{1,0},{2,3},{3,2},{4,5},{5,4},{6,7},{7,6},{8,9},{9,8},{10,11... | collective-permute-start | bytes 1966088 | tf_op jit(solution)/shard_map/ppermute | solution.py:514
  76.4 2.7 %collective-permute-start.1 = (f32[1024,128]{1,0:T(8,128)S(1)}, f32[1024,128]{1,0:T(8,128)}, u32[]{:S(2)}, u32[]{:S(2)}) collective-permute-start(f32[1024,128]{1,0:T(8,128)S(1)} %bitcast.8), channel_id=1, source_target_pairs={{0,4},{1,5},{2,30},{3,31},{4,34},{5,35},{6,56},{7,57},{8,74},{9,75... | collective-permute-start | bytes 1572872 | tf_op jit(solution)/shard_map/ppermute | solution.py:538
  79.2 32.4 %collective-permute-done.1.start.mine_start = f32[1024,128]{1,0:T(8,128)} collective-permute-done((f32[1024,128]{1,0:T(8,128)S(1)}, f32[1024,128]{1,0:T(8,128)}, u32[]{:S(2)}, u32[]{:S(2)}) %collective-permute-start.1) | collective-permute-done | bytes 524320 | tf_op jit(solution)/shard_map/ppermute | solution.py:538
  111.6 1.5 shard_map.61.grams
  113.1 0.0 collective-permute-done.2.theirs
  113.1 4.5 %shard_map.62 = (f32[8,160,128]{2,1,0:T(8,128)S(1)}, f32[256,128]{1,0:T(8,128)S(1)}) custom-call(s32[67]{0:T(128)S(1)} %copy-done.2, f32[2048,1024]{1,0:T(8,128)} %covariance.5, f32[8,160,128]{2,1,0:T(8,128)S(1)} %all_to_all.38.mine, f32[8,160,128]{2,1,0:T(8,128)S(1)} %collective-permute-done.2.theirs, f32[256,128]{1,0:T(8,128)S(1)} %shard_map.61.grams), custom_call_target="tpu_custom_call" | custom-call | tf_op jit(solution)/shard_map/pallas_call | solution.py:430
  117.7 14.1 %all_to_all.39 = f32[8,160,128]{2,1,0:T(8,128)S(1)} all-to-all(f32[8,160,128]{2,1,0:T(8,128)S(1)} %get-tuple-element.16), channel_id=1, replica_groups=mesh['row'=8,'chip'=8,'core'=2] {'row'}, dimensions={0} | all-to-all | bytes 1310720 | tf_op jit(solution)/shard_map/all_to_all | solution.py:505
  131.8 5.6 %collective-permute-start.3 = (f32[160,128]{1,0:T(8,128)S(1)}, f32[160,128]{1,0:T(8,128)S(1)}, u32[]{:S(2)}, u32[]{:S(2)}) collective-permute-start(f32[160,128]{1,0:T(8,128)S(1)} %reduce_sum.29), channel_id=1, source_target_pairs={{0,4},{1,5},{2,30},{3,31},{4,34},{5,35},{6,56},{7,57},{8,74},{9,75... | collective-permute-start | bytes 245768 | tf_op jit(solution)/shard_map/ppermute | solution.py:548
  137.4 1.5 collective-permute-done.3
  138.9 0.9 broadcast_in_dim.14
  139.8 10.2 %all-to-all-start.5 = ((f32[8,160,128]{2,1,0:T(8,128)}), f32[8,160,128]{2,1,0:T(8,128)S(1)}, u32[]{:S(2)}, u32[]{:S(2)}) async-start(f32[8,160,128]{2,1,0:T(8,128)} %broadcast_in_dim.14), calls=%async_computation.5 | async-start | bytes 1310720 | tf_op jit(solution)/shard_map/all_to_all | solution.py:510
  149.9 4.5 %shard_map.63.inv0 = f32[128,128]{1,0:T(8,128)S(1)} custom-call(f32[256,128]{1,0:T(8,128)S(1)} %get-tuple-element.17.g00.start), custom_call_target="tpu_custom_call" | custom-call | tf_op jit(solution)/shard_map/pallas_call | solution.py:198
  154.4 3.8 %all-to-all-done.5.following.mine_next = f32[8,160,128]{2,1,0:T(8,128)S(1)} async-done(((f32[8,160,128]{2,1,0:T(8,128)}), f32[8,160,128]{2,1,0:T(8,128)S(1)}, u32[]{:S(2)}, u32[]{:S(2)}) %all-to-all-start.5) | async-done | bytes 655392 | tf_op jit(solution)/shard_map/all_to_all | solution.py:510
  158.3 1.0 shard_map.64.keep
  159.3 5.0 %collective-permute-start.6 = (f32[392,128]{1,0:T(8,128)S(1)}, f32[392,128]{1,0:T(8,128)S(1)}, u32[]{:S(2)}, u32[]{:S(2)}) collective-permute-start(f32[392,128]{1,0:T(8,128)S(1)} %shard_map.64.keep), channel_id=1, source_target_pairs={{0,1},{1,0},{2,3},{3,2},{4,5},{5,4},{6,7},{7,6},{8,9},{9,8},{10,11... | collective-permute-start | bytes 602120 | tf_op jit(solution)/shard_map/ppermute | solution.py:514
  164.3 0.1 collective-permute-start.4
  164.4 0.4 collective-permute-start.5
  164.8 0.6 collective-permute-done.6.got
  165.4 0.0 copy-start
  165.4 0.9 broadcast_in_dim.15
  166.2 0.0 copy-done
  166.2 4.4 %all-to-all-start.6 = ((f32[8,136,128]{2,1,0:T(8,128)}), f32[8,136,128]{2,1,0:T(8,128)}, u32[]{:S(2)}, u32[]{:S(2)}) async-start(f32[8,136,128]{2,1,0:T(8,128)} %broadcast_in_dim.15), calls=%async_computation.6 | async-start | bytes 1114112 | tf_op jit(solution)/shard_map/all_to_all | solution.py:510
  170.6 0.0 copy-start.1
  170.6 0.9 copy-done.1
  171.6 8.2 %shard_map.65.refs_0_ = f32[2176,128]{1,0:T(8,128)S(1)} custom-call(f32[256,128]{1,0:T(8,128)S(1)} %get-tuple-element.17.g00.start, f32[128,128]{1,0:T(8,128)S(1)} %shard_map.63.inv0, f32[392,128]{1,0:T(8,128)S(1)} %shard_map.64.keep, f32[392,128]{1,0:T(8,128)S(1)} %copy-done.1), custom_call_target="tpu_custom_call" | custom-call | tf_op jit(solution)/shard_map/pallas_call | solution.py:198
  179.7 1.5 all-to-all-done.6.refs_1_
  181.3 9.3 %shard_map.66 = (f32[384,384]{1,0:T(8,128)S(1)}, f32[384,256]{1,0:T(8,128)}, f32[384,256]{1,0:T(8,128)}) custom-call(f32[2176,128]{1,0:T(8,128)S(1)} %shard_map.65.refs_0_, f32[8,136,128]{2,1,0:T(8,128)} %all-to-all-done.6.refs_1_), custom_call_target="tpu_custom_call" | custom-call | tf_op jit(solution)/shard_map/pallas_call | solution.py:198
  190.6 0.0 collective-permute-done.4.theirs_start
  190.6 0.0 collective-permute-done.5.theirs_next
  190.6 5.7 %shard_map.67 = f32[2048,384]{1,0:T(8,128)} custom-call(s32[67]{0:T(128)S(1)} %copy-done.2, f32[8,160,128]{2,1,0:T(8,128)S(1)} %all_to_all.38.mine, f32[1024,128]{1,0:T(8,128)} %collective-permute-done.1.start.mine_start, f32[8,160,128]{2,1,0:T(8,128)S(1)} %all-to-all-done.5.following.mine_next, f32[8,160,128]{2,1,0:T(8,128)S(1)} %collective-permute-done.2.theirs, ...), custom_call_target="tpu_custom_call" | custom-call | tf_op jit(solution)/shard_map/pallas_call | solution.py:487
  (7 shorter events, 0.2 us)
Async XLA Ops:
  5.1 30.0 %copy-start.2 = (s32[67]{0:T(128)S(1)}, s32[67]{0:T(128)}, u32[]{:S(2)}) copy-start(s32[67]{0:T(128)} %pad_add_fusion.place) | copy-start | bytes 808
  5.1 30.0 %copy-start.3 = (s32[128]{0:T(128)S(1)}, s32[128]{0:T(128)}, u32[]{:S(2)}) copy-start(s32[128]{0:T(128)} %seeds.1) | copy-start | bytes 1540
  40.6 5.1 %collective-permute-start = (f32[8,128,128]{2,1,0:T(8,128)S(1)}, f32[8,128,128]{2,1,0:T(8,128)S(1)}, u32[]{:S(2)}, u32[]{:S(2)}) collective-permute-start(f32[8,128,128]{2,1,0:T(8,128)S(1)} %get-tuple-element.15), channel_id=1, source_target_pairs={{0,1},{1,0},{2,3},{3,2},{4,5},{5,4},{6,7},{7,6},{8,9},{9,8},{10,11... | collective-permute-start | bytes 1572872 | tf_op jit(solution)/shard_map/ppermute | solution.py:514
  73.8 39.3 %collective-permute-start.2 = (f32[8,160,128]{2,1,0:T(8,128)S(1)}, f32[8,160,128]{2,1,0:T(8,128)S(1)}, u32[]{:S(2)}, u32[]{:S(2)}) collective-permute-start(f32[8,160,128]{2,1,0:T(8,128)S(1)} %all_to_all.38.mine), channel_id=1, source_target_pairs={{0,1},{1,0},{2,3},{3,2},{4,5},{5,4},{6,7},{7,6},{8,9},{9,8},{10,11... | collective-permute-start | bytes 1966088 | tf_op jit(solution)/shard_map/ppermute | solution.py:514
  76.4 35.1 %collective-permute-start.1 = (f32[1024,128]{1,0:T(8,128)S(1)}, f32[1024,128]{1,0:T(8,128)}, u32[]{:S(2)}, u32[]{:S(2)}) collective-permute-start(f32[1024,128]{1,0:T(8,128)S(1)} %bitcast.8), channel_id=1, source_target_pairs={{0,4},{1,5},{2,30},{3,31},{4,34},{5,35},{6,56},{7,57},{8,74},{9,75... | collective-permute-start | bytes 1572872 | tf_op jit(solution)/shard_map/ppermute | solution.py:538
  131.8 7.1 %collective-permute-start.3 = (f32[160,128]{1,0:T(8,128)S(1)}, f32[160,128]{1,0:T(8,128)S(1)}, u32[]{:S(2)}, u32[]{:S(2)}) collective-permute-start(f32[160,128]{1,0:T(8,128)S(1)} %reduce_sum.29), channel_id=1, source_target_pairs={{0,4},{1,5},{2,30},{3,31},{4,34},{5,35},{6,56},{7,57},{8,74},{9,75... | collective-permute-start | bytes 245768 | tf_op jit(solution)/shard_map/ppermute | solution.py:548
  139.8 18.5 %all-to-all-start.5 = ((f32[8,160,128]{2,1,0:T(8,128)}), f32[8,160,128]{2,1,0:T(8,128)S(1)}, u32[]{:S(2)}, u32[]{:S(2)}) async-start(f32[8,160,128]{2,1,0:T(8,128)} %broadcast_in_dim.14), calls=%async_computation.5 | async-start | bytes 1310720 | tf_op jit(solution)/shard_map/all_to_all | solution.py:510
  159.3 6.0 %collective-permute-start.6 = (f32[392,128]{1,0:T(8,128)S(1)}, f32[392,128]{1,0:T(8,128)S(1)}, u32[]{:S(2)}, u32[]{:S(2)}) collective-permute-start(f32[392,128]{1,0:T(8,128)S(1)} %shard_map.64.keep), channel_id=1, source_target_pairs={{0,1},{1,0},{2,3},{3,2},{4,5},{5,4},{6,7},{7,6},{8,9},{9,8},{10,11... | collective-permute-start | bytes 602120 | tf_op jit(solution)/shard_map/ppermute | solution.py:514
  164.3 26.3 %collective-permute-start.4 = (f32[1024,128]{1,0:T(8,128)}, f32[1024,128]{1,0:T(8,128)}, u32[]{:S(2)}, u32[]{:S(2)}) collective-permute-start(f32[1024,128]{1,0:T(8,128)} %collective-permute-done.1.start.mine_start), channel_id=1, source_target_pairs={{0,1},{1,0},{2,3},{3,2},{4,5},{5,4},{6,7},{7,6},{8,9},{9,8},{10,11... | collective-permute-start | bytes 1572872 | tf_op jit(solution)/shard_map/ppermute | solution.py:514
  164.4 26.2 %collective-permute-start.5 = (f32[8,160,128]{2,1,0:T(8,128)S(1)}, f32[8,160,128]{2,1,0:T(8,128)}, u32[]{:S(2)}, u32[]{:S(2)}) collective-permute-start(f32[8,160,128]{2,1,0:T(8,128)S(1)} %all-to-all-done.5.following.mine_next), channel_id=1, source_target_pairs={{0,1},{1,0},{2,3},{3,2},{4,5},{5,4},{6,7},{7,6},{8,9},{9,8},{10,11... | collective-permute-start | bytes 1966088 | tf_op jit(solution)/shard_map/ppermute | solution.py:514
  165.4 0.9 copy-start
  166.2 15.0 %all-to-all-start.6 = ((f32[8,136,128]{2,1,0:T(8,128)}), f32[8,136,128]{2,1,0:T(8,128)}, u32[]{:S(2)}, u32[]{:S(2)}) async-start(f32[8,136,128]{2,1,0:T(8,128)} %broadcast_in_dim.15), calls=%async_computation.6 | async-start | bytes 1114112 | tf_op jit(solution)/shard_map/all_to_all | solution.py:510
  170.6 0.9 copy-start.1

commit v5 on v4

--- a/solution.py
+++ b/solution.py
@@ -63,45 +63,56 @@
 BAND = 16
 
 
-def factor(gram, work, upper, inverse):
+def factor(gram):
     sub = lax.broadcasted_iota(jnp.int32, (BAND, W), 0)
     lane = lax.broadcasted_iota(jnp.int32, (BAND, W), 1)
-    work[:, :W] = gram
-    work[:, W:] = (
-        lax.broadcasted_iota(jnp.int32, (W, W), 0) == lax.broadcasted_iota(jnp.int32, (W, W), 1)
-    ).astype(f32)
-
-    def step(j, carry):
-        base = pl.multiple_of(j * BAND, BAND)
-        left = work[pl.ds(base, BAND), :W]
-        right = work[pl.ds(base, BAND), W:]
-        turned = pltpu.roll(left, (W - base) % W, 1)
-        cols = [jnp.broadcast_to(turned[:, k : k + 1], (BAND, W)) for k in range(BAND)]
+    eye = lax.broadcasted_iota(jnp.int32, (W, W), 0) == lax.broadcasted_iota(jnp.int32, (W, W), 1)
+    rest = jnp.concatenate([gram, eye.astype(f32)], axis=1)
+    now, rest = rest[:BAND], rest[BAND:]
+    upper, inverse = [], []
+    for base in range(0, W, BAND):
+        left, right = now[:, :W], now[:, W:]
+        cols = [jnp.broadcast_to(left[:, base + k : base + k + 1], (BAND, W)) for k in range(BAND)]
         scale = jnp.zeros((BAND, W), f32)
-        for k in range(BAND):
+        for k in range(0, BAND, 2):
             top = k // 8 * 8
-
-            def line(v):
-                return jnp.broadcast_to(v[k : k + 1, :], (BAND - top, W))
+            here = sub[top:]
+
+            def line(x, i):
+                return jnp.broadcast_to(x[i : i + 1, :], (BAND - top, W))
 
             def below(old, new):
                 return new if top == 0 else jnp.concatenate([old[:top], new])
 
-            root = lax.rsqrt(line(cols[k]))
-            weight = jnp.where(sub[top:] > k, cols[k][top:] * (root * root), 0.0)
-            scale = below(scale, jnp.where(sub[top:] == k, root, scale[top:]))
-            for m in range(k + 1, BAND):
-                cols[m] = below(cols[m], cols[m][top:] - weight * line(cols[m]))
-            left = below(left, left[top:] - weight * line(left))
-            right = below(right, right[top:] - weight * line(right))
+            c, d = cols[k][top:], cols[k + 1][top:]
+            p, q, r = line(cols[k], k), line(cols[k + 1], k), line(cols[k + 1], k + 1)
+            det = p * r - q * q
+            inv_p = 1.0 / p
+            inv = 1.0 / det
+            later = here > k + 1
+            u = jnp.where(later, (c * r - d * q) * inv, jnp.where(here == k + 1, q * inv_p, 0.0))
+            v = jnp.where(later, (d * p - c * q) * inv, 0.0)
+            last_scale = jnp.where(here == k + 1, lax.rsqrt(det * inv_p), scale[top:])
+            scale = below(scale, jnp.where(here == k, lax.rsqrt(p), last_scale))
+
+            def update(x):
+                return below(x, x[top:] - u * line(x, k) - v * line(x, k + 1))
+
+            for m in range(k + 2, BAND):
+                cols[m] = update(cols[m])
+            left = update(left)
+            right = update(right)
         left = jnp.where(lane >= base + sub, left * scale, 0.0)
         right = right * scale
-        upper[pl.ds(base, BAND), :] = left
-        inverse[pl.ds(base, BAND), :] = right
-        work[...] = work[...] - outer(left, jnp.concatenate([left, right], axis=1))
-        return carry
-
-    lax.fori_loop(0, W // BAND, step, 0)
+        upper.append(left)
+        inverse.append(right)
+        end = base + BAND
+        if end < W:
+            panel = jnp.concatenate([left, right], axis=1)
+            now = rest[:BAND] - outer(left[:, end : end + BAND], panel)
+            if end + BAND < W:
+                rest = rest[BAND:] - outer(left[:, end + BAND :], panel)
+    return jnp.concatenate(upper), jnp.concatenate(inverse)
 
 
 def blocks_of(ref, start, count):
@@ -112,11 +123,11 @@
     return jnp.concatenate([ref[place[3 + place[0] * ref.shape[0] + p], start : start + count, :] for p in parts])
 
 
-def first_factor(g00, inverse, work, upper):
-    factor(g00[:W, :], work, upper, inverse)
-
-
-def middle(start, inv0, keep, got, pack, work, upper1, inv1):
+def first_factor(g00, inverse):
+    inverse[...] = factor(g00[:W, :])[1]
+
+
+def middle(start, inv0, keep, got, pack, stage, sems):
     g00, cee = start[:W, :], start[W:, :]
     li0 = inv0[...]
     g01, g11 = (keep[i * W : (i + 1) * W, :] + got[i * W : (i + 1) * W, :] for i in range(2))
@@ -127,36 +138,49 @@
     h = nn(li0, nn(side, jnp.concatenate([u, x0])))
     m00 = nn(li0, nt(g00, li0))
     h_full = h + (h - nn(m00, h))
+    g02 = g11 + tn(cee, g01)
+    for i, block in enumerate([h, h_full, m00, g02, g00, g01, g11, li0]):
+        stage[i * W : (i + 1) * W, :] = block
+    pack_copy(stage, pack, sems, 0).start()
     comb = jnp.concatenate([u - nn(x0, h_full), x0])
     y = nn(gram, comb)
-    factor(tn(comb, y), work, upper1, inv1)
-    li1 = inv1[...]
+    upper1, li1 = factor(tn(comb, y))
     c1 = nt(comb, li1)
     y1 = nt(y, li1)
     m01 = nn(li0, y1[:W])
-    g02 = g11 + tn(cee, g01)
     i1 = jnp.concatenate([nn(cee, c1[:W]), c1])
     s0 = nn(jnp.concatenate([side, g02], axis=1), i1)
     s1 = nn(gram[W:], i1[: 2 * W])
-    blocks = (
-        [h, h_full, upper1[...], i1[:W], i1[W : 2 * W], i1[2 * W :]]
-        + [m00, m01, tn(c1, y1), g02, g00, g01, g11, li0]
-        + [nn(li0, s0), tn(c1[:W], s0), s1]
+    late = [upper1, i1[:W], i1[W : 2 * W], i1[2 * W :], m01, tn(c1, y1), nn(li0, s0), tn(c1[:W], s0), s1]
+    for i, block in enumerate(late):
+        stage[EARLY + i * W : EARLY + (i + 1) * W, :] = block
+    second = pack_copy(stage, pack, sems, 1)
+    second.start()
+    pack_copy(stage, pack, sems, 0).wait()
+    second.wait()
+
+
+EARLY = 8 * W
+PACK = 17 * W
+
+
+def pack_copy(source, target, sems, late):
+    lines = pl.ds(EARLY, PACK - EARLY) if late else pl.ds(0, EARLY)
+    return pltpu.make_async_copy(source.at[lines, :], target.at[lines, :], sems.at[late])
+
+
+def last(scale, packed, totals, mix, projection, first_pass, pack, sems):
+    copies = [pack_copy(packed, pack, sems, i) for i in range(2)]
+    for copy in copies:
+        copy.start()
+    a12, a22 = unpacked(totals[...])
+    for copy in copies:
+        copy.wait()
+    first, full, m00, a02, a00, a01, a11, li0, upper1, _, c1_top, c1_low, m01, m11, first0, part1, s1 = (
+        pack[i * W : (i + 1) * W, :] for i in range(PACK // W)
     )
-    for i, block in enumerate(blocks):
-        pack[i * W : (i + 1) * W, :] = block
-
-
-PACK = 17
-
-
-def last(scale, pack, totals, mix, projection, first_pass, work, upper2, inv2):
-    first, full, upper1, _, _, c1_low, m00, m01, m11, a02, a00, a01, a11, li0, first0, part1, s1 = (
-        pack[i * W : (i + 1) * W, :] for i in range(PACK)
-    )
-    i1 = pack[3 * W : 6 * W, :]
+    i1 = pack[EARLY + W : EARLY + 4 * W, :]
     c1 = i1[W:]
-    a12, a22 = unpacked(totals[...])
     gram = jnp.concatenate(
         [
             jnp.concatenate([a00, a01, a02], axis=1),
@@ -170,15 +194,15 @@
     zero = jnp.zeros((W, W), f32)
     places = jnp.concatenate([jnp.concatenate([li0.T, zero]), c1], axis=1)
     comb = jnp.concatenate([i1[: 2 * W] - nn(places, h_full), i1[2 * W :]])
-    factor(tn(comb, nn(gram, comb)), work, upper2, inv2)
+    upper2, li2 = factor(tn(comb, nn(gram, comb)))
     mix[: 2 * W, : 2 * W] = places * scale
     mix[2 * W :, : 2 * W] = jnp.zeros((W, 2 * W), f32)
-    mix[:, 2 * W :] = nt(comb, inv2[...]) * scale
+    mix[:, 2 * W :] = nt(comb, li2) * scale
     projection[:W, :W] = full
     projection[W : 2 * W, :W] = upper1
     projection[2 * W :, :W] = zero
     projection[: 2 * W, W:] = h_full
-    projection[2 * W :, W:] = upper2[...]
+    projection[2 * W :, W:] = upper2
     first_pass[:W, :W] = first
     first_pass[W:, :W] = jnp.zeros((2 * W, W), f32)
     first_pass[: 2 * W, W:] = h
@@ -194,13 +218,12 @@
     return pltpu.CompilerParams(vmem_limit_bytes=mib * 2**20)
 
 
-def kernel(body, shapes, scratch, *args):
+def kernel(body, shapes, *args):
     return pl.pallas_call(
         body,
         out_shape=[jax.ShapeDtypeStruct(s, f32) for s in shapes],
         in_specs=[VMEM if a.dtype == f32 else SMEM for a in args],
         out_specs=[VMEM] * len(shapes),
-        scratch_shapes=[pltpu.VMEM(s, f32) for s in scratch],
         compiler_params=room(16),
     )(*args)
 
@@ -351,9 +374,10 @@
     return both[:, :W] + both[:, W:] + mm(low, right[0])
 
 
-def step_grams(mine, start, out):
-    step = blocks_of(mine, 0, W)
-    out[:W, :] = cross(start[...], step)
+def step_grams(place, mine, out):
+    parts = mine.shape[0]
+    step, start = blocks_of(mine, 0, W), turned_blocks(mine, place, W + 2 * W // parts, W, range(parts))
+    out[:W, :] = cross(start, step)
     out[W:, :] = cross(step, step)
 
 
@@ -390,7 +414,7 @@
 
 
 def second_product(place, covariance, mine, theirs, grams, out, small, buffer, sems, total):
-    height, _ = covariance.shape
+    height, breadth = covariance.shape
     half = height // 2
     tall = height // CHUNKS
     copies = chunks_of(covariance, buffer, sems)
@@ -440,65 +464,51 @@
     )(place, covariance, mine, theirs, grams)
 
 
-def basis_rows(place, mine, mine_start, mine_next, theirs, theirs_start, theirs_next, mix, out, wide, tip):
-    step = pl.program_id(0)
-    count = pl.num_programs(0) // 2
-    tall = out.shape[0]
-    parts = tall // W
-
-    @pl.when(step == 0)
-    def _():
-        high, low = halves(mix[: 2 * W, : 2 * W])
-        wide[:, : 2 * W] = high
-        wide[:, 2 * W :] = low
-        high, low = halves(mix[:, 2 * W :])
-        tip[:, :W] = high
-        tip[:, W:] = low
-
-    def rows(pair, start, following, part):
-        order = [part + p for p in range(parts)]
+def basis_rows(place, mine, mine_next, theirs, theirs_next, mix, out, stage, sems):
+    parts = mine.shape[0]
+    bit = 2 * W // parts
+    count, tall, _ = stage.shape
+    half = count * tall // 2
+    high, low = halves(mix[: 2 * W, : 2 * W])
+    tip_high, tip_low = halves(mix[:, 2 * W :])
+    tip = jnp.concatenate([tip_high, tip_low], axis=1)
+    copies = []
+    for i in range(count):
+        line = i * tall % half
+        pair, following, side = (mine, mine_next, place[1]) if i * tall < half else (theirs, theirs_next, 1 - place[1])
+        order = range(line // W, (line + tall) // W)
         left = jnp.concatenate(
             [
-                start[pl.ds(pl.multiple_of(part * W, tall), tall), :],
-                pair[pl.ds(part, parts), :W, :].reshape(tall, W),
+                turned_blocks(pair, place, W + bit, W, order),
+                pair[line // W : (line + tall) // W, :W, :].reshape(tall, W),
                 turned_blocks(following, place, 0, W, order),
             ],
             axis=1,
         )
-        high, low = halves(left)
-        h2, l2 = high[:, : 2 * W], low[:, : 2 * W]
-        out[:, : 2 * W] = mm(h2, wide[:, : 2 * W]) + mm(h2, wide[:, 2 * W :]) + mm(l2, wide[:, : 2 * W])
-        both = mm(high, tip[...])
-        out[:, 2 * W :] = both[:, :W] + both[:, W:] + mm(low, tip[:, :W])
-
-    @pl.when(step < count)
-    def _():
-        rows(mine, mine_start, mine_next, step * parts)
-
-    @pl.when(step >= count)
-    def _():
-        rows(theirs, theirs_start, theirs_next, (step - count) * parts)
-
-
-def basis_of(place, mine, mine_start, mine_next, theirs, theirs_start, theirs_next, mix):
-    half = mine.shape[0] * W
-    tall = 512
-    count = half // tall
+        l_high, l_low = halves(left)
+        h2, l2 = l_high[:, : 2 * W], l_low[:, : 2 * W]
+        stage[i, :, : 2 * W] = mm(h2, high) + mm(h2, low) + mm(l2, high)
+        both = mm(l_high, tip)
+        stage[i, :, 2 * W :] = both[:, :W] + both[:, W:] + mm(l_low, tip_high)
+        rows = pl.ds(pl.multiple_of(side * half + line, tall), tall)
+        copies.append(pltpu.make_async_copy(stage.at[i], out.at[rows, :], sems.at[i]))
+        copies[-1].start()
+    for copy in copies:
+        copy.wait()
+
+
+def basis_of(place, mine, mine_next, theirs, theirs_next, mix):
+    height = 2 * mine.shape[0] * W
+    tall = 256
+    breadth = mix.shape[1]
     return pl.pallas_call(
         basis_rows,
-        out_shape=jax.ShapeDtypeStruct((2 * half, mix.shape[1]), f32),
-        grid_spec=pltpu.PrefetchScalarGridSpec(
-            num_scalar_prefetch=1,
-            grid=(2 * count,),
-            in_specs=[VMEM] * 7,
-            out_specs=pl.BlockSpec(
-                (tall, mix.shape[1]),
-                lambda i, c: (jnp.where(i < count, i + c[1] * count, i - count + (1 - c[1]) * count), 0),
-            ),
-            scratch_shapes=[pltpu.VMEM((2 * W, 4 * W), bf16), pltpu.VMEM((3 * W, 2 * W), bf16)],
-        ),
+        out_shape=jax.ShapeDtypeStruct((height, breadth), f32),
+        in_specs=[SMEM] + [VMEM] * 5,
+        out_specs=HBM,
+        scratch_shapes=[pltpu.VMEM((height // tall, tall, breadth), f32), pltpu.SemaphoreType.DMA((height // tall,))],
         compiler_params=room(24),
-    )(place, mine, mine_start, mine_next, theirs, theirs_start, theirs_next, mix)
+    )(place, mine, mine_next, theirs, theirs_next, mix)
 
 
 def scattered(parts, axis):
@@ -534,49 +544,55 @@
     slots = jnp.array(SLOTS, jnp.int32).reshape(-1)
     place = jnp.concatenate([jnp.stack([row, core, chip * cores + core]).astype(jnp.int32), slots])
     start_piece = scattered(picked_rows(place, seed_index, covariance, rows), ROWS).T
+    start_turned = lax.ppermute(start_piece, ALL, turn)
     start = gathered(start_piece, ROWS).reshape(breadth, width)
-    mine_start = lax.ppermute(start, ALL, turn)
+    start, start_turned = lax.optimization_barrier((start, start_turned))
     keep, send = image_of_start(place, seed_index, covariance, start)
     got = other_core(send)
     small = grams_of_start(place, seed_index, start, chips)
     parts = jnp.concatenate([keep + got, small], axis=1)
-    step = scattered(parts, CHIP)
-    mine = gathered(step, CHIP)
+    mine = gathered(jnp.concatenate([scattered(parts, CHIP), start_turned]), CHIP)
     theirs = other_core(mine)
-    (grams,) = kernel(step_grams, [(2 * width, width)], [], mine, mine_start)
+    (grams,) = kernel(step_grams, [(2 * width, width)], place, mine)
     parts, zero_grams = image_of_step(place, covariance, mine, theirs, grams)
     piece = lax.ppermute(scattered(parts, ROWS), ALL, turn)
-    (inv0,) = kernel(first_factor, [square], [(width, 2 * width), square], zero_grams)
+    (inv0,) = kernel(first_factor, [square], zero_grams)
     mine_next, inv0 = lax.optimization_barrier((gathered(piece, CHIP), inv0))
-    (keep,) = kernel(next_grams, [(3 * width + SPARE, width)], [], place, mine, mine_next)
+    (keep,) = kernel(next_grams, [(3 * width + SPARE, width)], place, mine, mine_next)
     got = other_core(keep)
     totals = gathered(keep[2 * width :] + got[2 * width :], ROWS)
     theirs_next = other_core(mine_next)
-    theirs_start = other_core(mine_start)
-    (pack,) = kernel(
-        middle, [(PACK * width, width)], [(width, 2 * width), square, square], zero_grams, inv0, keep, got
-    )
+    stage = [pltpu.VMEM((PACK, width), f32), pltpu.SemaphoreType.DMA((2,))]
+    pack = pl.pallas_call(
+        middle,
+        out_shape=jax.ShapeDtypeStruct((PACK, width), f32),
+        in_specs=[VMEM] * 4,
+        out_specs=HBM,
+        scratch_shapes=stage,
+        compiler_params=room(60),
+    )(zero_grams, inv0, keep, got)
     totals, pack = lax.optimization_barrier((totals, pack))
     scale = float(order) ** 0.5
 
     def last_step(*refs):
         last(f32(scale), *refs)
 
-    mix, projection, first_pass = kernel(
+    shapes = [(3 * width, 3 * width), (3 * width, 2 * width), (3 * width, 2 * width)]
+    mix, projection, first_pass = pl.pallas_call(
         last_step,
-        [(3 * width, 3 * width), (3 * width, 2 * width), (3 * width, 2 * width)],
-        [(width, 2 * width), square, square],
-        pack,
-        totals,
-    )
-    basis = basis_of(place, mine, mine_start, mine_next, theirs, theirs_start, theirs_next, mix)
+        out_shape=[jax.ShapeDtypeStruct(s, f32) for s in shapes],
+        in_specs=[HBM, VMEM],
+        out_specs=[VMEM] * 3,
+        scratch_shapes=stage,
+        compiler_params=room(52),
+    )(pack, totals)
+    basis = basis_of(place, mine, mine_next, theirs, theirs_next, mix)
     return basis, projection, first_pass
 
 
 def solution(mesh):
     rows, cols = mesh.devices.shape
     fine = Mesh(mesh.devices.reshape(rows, cols // 2, 2), ALL)
-
     return jax.shard_map(
         local,
         mesh=fine,

time: 197 us -> 169 us (0.86)
  blocking collectives: 71.9 us -> 53.2 us
  waiting for transfers between devices: 40.3 us -> 26.2 us
  starting transfers between devices: 34.5 us -> 38.2 us
    ppermute x1, waiting for transfers between devices: 32.4 us -> 1.87 us  [local(): start_turned = lax.ppermute(start_piece, ALL, turn)]
    pallas_call x5 -> x3, Pallas kernels: 24.6 us -> 5.85 us  [kernel(): pl.pallas_call(body, out_shape=[jax.ShapeDtypeStruct(s, f32) for s in sha...]
    pallas_call x1 -> x3, Pallas kernels: 5.74 us -> 22.9 us  [the longest x1 9.75 us: local(): pl.pallas_call(last_step, out_shape=[jax.ShapeDtypeStruct(s, f32) for s i...]
    all_to_all x3 -> x2, blocking collectives: 47.5 us -> 34.2 us  [scattered(): return jnp.sum(lax.all_to_all(parts, axis, 0, 0, tiled=True), axis=0)]
    all_to_all x0 -> x1, waiting for transfers between devices: none -> 11.6 us  [scattered(): return jnp.sum(lax.all_to_all(parts, axis, 0, 0, tiled=True), axis=0)]
    all_to_all x2 -> x1, blocking collectives: 24.4 us -> 19 us  [gathered(): return lax.all_to_all(copies, axis, 0, 0, tiled=True)]
    all_to_all x0 -> x1, starting transfers between devices: none -> 3.77 us  [scattered(): return jnp.sum(lax.all_to_all(parts, axis, 0, 0, tiled=True), axis=0)]
    ppermute x1, starting transfers between devices: 5.63 us -> 2.84 us  [local(): piece = lax.ppermute(scattered(parts, ROWS), ALL, turn)]
  transfers between devices with their start and end apart: 9 -> 10, of which waited for: 6 -> 9; matrix products, arithmetic and copies ran while one was open for 0% -> 1% of each run, Pallas kernels for 13% -> 15%
where the time goes in v5:
time: 169 us; the launch traced here: 168 us
  blocking collectives  53.2 us (31%)
  Pallas kernels  42.9 us (25%)
  starting transfers between devices  38.2 us (23%)
  waiting for transfers between devices  26.2 us (16%)
  local copies, waits for them, and re-layouts  3.49 us (2%)
  other arithmetic  3.44 us (2%)
    all_to_all x2, blocking collectives, scattered(): return jnp.sum(lax.all_to_all(parts, axis, 0, 0, tiled=True), axis=0)  34.2 us
    all_to_all x1, blocking collectives, gathered(): return lax.all_to_all(copies, axis, 0, 0, tiled=True)  19 us
    all_to_all x3, starting transfers between devices, gathered(): return lax.all_to_all(copies, axis, 0, 0, tiled=True)  14.7 us
    ppermute x4, starting transfers between devices, other_core(): return lax.ppermute(value, CORE, SWAP)  12.1 us
    all_to_all x1, waiting for transfers between devices, scattered(): return jnp.sum(lax.all_to_all(parts, axis, 0, 0, tiled=True), axis=0)  11.6 us
    pallas_call x1, Pallas kernels, local(): pl.pallas_call(last_step, out_shape=[jax.ShapeDtypeStruct(s, f32) for s i...  9.75 us
    pallas_call x1, Pallas kernels, local(): pl.pallas_call(middle, out_shape=jax.ShapeDtypeStruct((PACK, width), f32)...  9.25 us
    all_to_all x3, waiting for transfers between devices, gathered(): return lax.all_to_all(copies, axis, 0, 0, tiled=True)  7.53 us
  transfers between devices with their start and end apart: 10, of which 9 were waited for; matrix products, arithmetic and copies ran while one was open for 1% of the time, Pallas kernels for 15%

profile of v5, /device:TPU:1, one launch (start us, length us, event | category | flops | bytes accessed | tf_op | source)
XLA Modules:
  0.0 168.4 jit_solution(8630291336273055331)
XLA Ops:
  0.6 1.3 pad_add_fusion.place
  1.9 3.1 %shard_map.58 = f32[8,128,128]{2,1,0:T(8,128)} custom-call(s32[67]{0:T(128)} %pad_add_fusion.place, s32[128]{0:T(128)} %seeds.1, s32[1,128]{1,0:T(1,128)} %bitcast.8, f32[2048,1024]{1,0:T(8,128)} %covariance.5), custom_call_target="tpu_custom_call" | custom-call | tf_op jit(solution)/shard_map/pallas_call | solution.py:273
  5.1 17.9 %all_to_all.35 = f32[8,128,128]{2,1,0:T(8,128)S(1)} all-to-all(f32[8,128,128]{2,1,0:T(8,128)} %shard_map.58), channel_id=1, replica_groups=mesh['row'=8,'chip'=8,'core'=2] {'row'}, dimensions={0} | all-to-all | bytes 1048576 | tf_op jit(solution)/shard_map/all_to_all | solution.py:515
  23.0 0.0 copy-start.3
  23.0 0.0 copy-start.4
  23.0 0.1 copy.6
  23.1 0.8 broadcast_in_dim.12
  23.9 3.5 %all-to-all-start.1 = ((f32[8,128,128]{2,1,0:T(8,128)}), f32[8,128,128]{2,1,0:T(8,128)S(1)}, u32[]{:S(2)}, u32[]{:S(2)}) async-start(f32[8,128,128]{2,1,0:T(8,128)} %broadcast_in_dim.12), calls=%async_computation.1 | async-start | bytes 1048576 | tf_op jit(solution)/shard_map/all_to_all | solution.py:520
  27.5 4.8 %collective-permute-start = (f32[128,128]{0,1:T(8,128)S(1)}, f32[128,128]{0,1:T(8,128)S(1)}, u32[]{:S(2)}, u32[]{:S(2)}) collective-permute-start(f32[128,128]{0,1:T(8,128)S(1)} %bitcast.12), channel_id=1, source_target_pairs={{0,4},{1,5},{2,30},{3,31},{4,34},{5,35},{6,56},{7,57},{8,74},{9,75... | collective-permute-start | bytes 196616 | tf_op jit(solution)/shard_map/ppermute | solution.py:547
  32.3 1.9 %collective-permute-done = f32[128,128]{0,1:T(8,128)S(1)} collective-permute-done((f32[128,128]{0,1:T(8,128)S(1)}, f32[128,128]{0,1:T(8,128)S(1)}, u32[]{:S(2)}, u32[]{:S(2)}) %collective-permute-start) | collective-permute-done | bytes 65568 | tf_op jit(solution)/shard_map/ppermute | solution.py:547
  34.2 1.9 %all-to-all-done.1 = f32[8,128,128]{2,1,0:T(8,128)S(1)} async-done(((f32[8,128,128]{2,1,0:T(8,128)}), f32[8,128,128]{2,1,0:T(8,128)S(1)}, u32[]{:S(2)}, u32[]{:S(2)}) %all-to-all-start.1) | async-done | bytes 524320 | tf_op jit(solution)/shard_map/all_to_all | solution.py:520
  36.0 0.0 copy-done.3
  36.0 0.0 copy-done.4
  36.0 5.4 %shard_map.59 = (f32[8,128,128]{2,1,0:T(8,128)S(1)}, f32[8,128,128]{2,1,0:T(8,128)S(1)}) custom-call(s32[67]{0:T(128)S(1)} %copy-done.3, s32[1,128]{1,0:T(1,128)S(1)} %bitcast.9, f32[2048,1024]{1,0:T(8,128)} %covariance.5, f32[1024,128]{1,0:T(8,128)S(1)} %bitcast.6), custom_call_target="tpu_custom_call" | custom-call | tf_op jit(solution)/shard_map/pallas_call | solution.py:332
  41.5 6.4 %collective-permute-start.1 = (f32[8,128,128]{2,1,0:T(8,128)S(1)}, f32[8,128,128]{2,1,0:T(8,128)S(1)}, u32[]{:S(2)}, u32[]{:S(2)}) collective-permute-start(f32[8,128,128]{2,1,0:T(8,128)S(1)} %get-tuple-element.18), channel_id=1, source_target_pairs={{0,1},{1,0},{2,3},{3,2},{4,5},{5,4},{6,7},{7,6},{8,9},{9,8},{10,11... | collective-permute-start | bytes 1572872 | tf_op jit(solution)/shard_map/ppermute | solution.py:524
  47.9 1.1 shard_map.60
  48.9 0.5 collective-permute-done.1
  49.4 0.1 add.10
  49.5 0.9 pad_maximum_fusion
  50.3 3.8 %all-to-all-start.2 = ((f32[8,160,128]{2,1,0:T(8,128)}), f32[8,160,128]{2,1,0:T(8,128)S(1)}, u32[]{:S(2)}, u32[]{:S(2)}) async-start(f32[8,160,128]{2,1,0:T(8,128)} %pad_maximum_fusion), calls=%async_computation.2 | async-start | bytes 1310720 | tf_op jit(solution)/shard_map/all_to_all | solution.py:515
  54.1 0.1 copy.7
  54.2 11.6 %all-to-all-done.2 = f32[8,160,128]{2,1,0:T(8,128)S(1)} async-done(((f32[8,160,128]{2,1,0:T(8,128)}), f32[8,160,128]{2,1,0:T(8,128)S(1)}, u32[]{:S(2)}, u32[]{:S(2)}) %all-to-all-start.2) | async-done | bytes 655392 | tf_op jit(solution)/shard_map/all_to_all | solution.py:515
  65.8 0.1 broadcast_in_dim.13
  65.9 19.0 %all_to_all.36.mine = f32[8,288,128]{2,1,0:T(8,128)S(1)} all-to-all(f32[8,288,128]{2,1,0:T(8,128)S(1)} %broadcast_in_dim.13), channel_id=1, replica_groups=mesh['row'=8,'chip'=8,'core'=2] {'chip'}, dimensions={0} | all-to-all | bytes 2359296 | tf_op jit(solution)/shard_map/all_to_all | solution.py:520
  85.0 1.4 collective-permute-start.2
  86.4 1.0 shard_map.61.grams
  87.5 1.4 collective-permute-done.2.theirs
  88.9 4.5 %shard_map.62 = (f32[8,160,128]{2,1,0:T(8,128)S(1)}, f32[256,128]{1,0:T(8,128)S(1)}) custom-call(s32[67]{0:T(128)S(1)} %copy-done.3, f32[2048,1024]{1,0:T(8,128)} %covariance.5, f32[8,288,128]{2,1,0:T(8,128)S(1)} %all_to_all.36.mine, f32[8,288,128]{2,1,0:T(8,128)S(1)} %collective-permute-done.2.theirs, f32[256,128]{1,0:T(8,128)S(1)} %shard_map.61.grams), custom_call_target="tpu_custom_call" | custom-call | tf_op jit(solution)/shard_map/pallas_call | solution.py:454
  93.4 0.0 copy-start.1
  93.4 16.3 %all_to_all.37 = f32[8,160,128]{2,1,0:T(8,128)} all-to-all(f32[8,160,128]{2,1,0:T(8,128)S(1)} %get-tuple-element.20), channel_id=1, replica_groups=mesh['row'=8,'chip'=8,'core'=2] {'row'}, dimensions={0} | all-to-all | bytes 1310720 | tf_op jit(solution)/shard_map/all_to_all | solution.py:515
  109.7 1.1 reduce_sum.29
  110.8 2.8 %collective-permute-start.3 = (f32[160,128]{1,0:T(8,128)S(1)}, f32[160,128]{1,0:T(8,128)S(1)}, u32[]{:S(2)}, u32[]{:S(2)}) collective-permute-start(f32[160,128]{1,0:T(8,128)S(1)} %reduce_sum.29), channel_id=1, source_target_pairs={{0,4},{1,5},{2,30},{3,31},{4,34},{5,35},{6,56},{7,57},{8,74},{9,75... | collective-permute-start | bytes 245768 | tf_op jit(solution)/shard_map/ppermute | solution.py:558
  113.7 2.3 %collective-permute-done.3 = f32[160,128]{1,0:T(8,128)S(1)} collective-permute-done((f32[160,128]{1,0:T(8,128)S(1)}, f32[160,128]{1,0:T(8,128)S(1)}, u32[]{:S(2)}, u32[]{:S(2)}) %collective-permute-start.3) | collective-permute-done | bytes 81952 | tf_op jit(solution)/shard_map/ppermute | solution.py:558
  116.0 0.9 broadcast_in_dim.14
  116.9 6.8 %all-to-all-start.5 = ((f32[8,160,128]{2,1,0:T(8,128)}), f32[8,160,128]{2,1,0:T(8,128)S(1)}, u32[]{:S(2)}, u32[]{:S(2)}) async-start(f32[8,160,128]{2,1,0:T(8,128)} %broadcast_in_dim.14), calls=%async_computation.5 | async-start | bytes 1310720 | tf_op jit(solution)/shard_map/all_to_all | solution.py:520
  123.7 0.0 copy-done.1
  123.7 3.8 %shard_map.63.inv0 = f32[128,128]{1,0:T(8,128)S(1)} custom-call(f32[256,128]{1,0:T(8,128)S(1)} %get-tuple-element.21.g00.start), custom_call_target="tpu_custom_call" | custom-call | tf_op jit(solution)/shard_map/pallas_call | solution.py:222
  127.4 0.0 copy-start.2
  127.5 0.6 copy-done.2
  128.1 4.1 %all-to-all-done.5.following.mine_next = f32[8,160,128]{2,1,0:T(8,128)S(1)} async-done(((f32[8,160,128]{2,1,0:T(8,128)}), f32[8,160,128]{2,1,0:T(8,128)S(1)}, u32[]{:S(2)}, u32[]{:S(2)}) %all-to-all-start.5) | async-done | bytes 655392 | tf_op jit(solution)/shard_map/all_to_all | solution.py:520
  132.2 1.0 shard_map.64.keep
  133.3 0.0 copy-start
  133.3 4.2 %collective-permute-start.5 = (f32[392,128]{1,0:T(8,128)S(1)}, f32[392,128]{1,0:T(8,128)S(1)}, u32[]{:S(2)}, u32[]{:S(2)}) collective-permute-start(f32[392,128]{1,0:T(8,128)S(1)} %shard_map.64.keep), channel_id=1, source_target_pairs={{0,1},{1,0},{2,3},{3,2},{4,5},{5,4},{6,7},{7,6},{8,9},{9,8},{10,11... | collective-permute-start | bytes 602120 | tf_op jit(solution)/shard_map/ppermute | solution.py:524
  137.4 0.1 collective-permute-start.4
  137.5 1.0 collective-permute-done.5.got
  138.5 0.0 copy-start.5
  138.5 0.9 broadcast_in_dim.15
  139.4 4.4 %all-to-all-start.6 = ((f32[8,136,128]{2,1,0:T(8,128)}), f32[8,136,128]{2,1,0:T(8,128)}, u32[]{:S(2)}, u32[]{:S(2)}) async-start(f32[8,136,128]{2,1,0:T(8,128)} %broadcast_in_dim.15), calls=%async_computation.6 | async-start | bytes 1114112 | tf_op jit(solution)/shard_map/all_to_all | solution.py:520
  143.8 0.0 copy-done
  143.8 0.0 copy-done.5
  143.8 9.2 %shard_map.65.refs_0_ = f32[2176,128]{1,0:T(8,128)} custom-call(f32[256,128]{1,0:T(8,128)} %copy-done.1, f32[128,128]{1,0:T(8,128)} %copy-done.2, f32[392,128]{1,0:T(8,128)} %copy-done, f32[392,128]{1,0:T(8,128)} %copy-done.5), custom_call_target="tpu_custom_call" | custom-call | tf_op jit(solution)/shard_map/pallas_call | solution.py:566
  153.1 1.5 all-to-all-done.6.refs_1_
  154.6 9.8 %shard_map.66 = (f32[384,384]{1,0:T(8,128)S(1)}, f32[384,256]{1,0:T(8,128)}, f32[384,256]{1,0:T(8,128)}) custom-call(f32[2176,128]{1,0:T(8,128)} %shard_map.65.refs_0_, f32[8,136,128]{2,1,0:T(8,128)} %all-to-all-done.6.refs_1_), custom_call_target="tpu_custom_call" | custom-call | tf_op jit(solution)/shard_map/pallas_call | solution.py:581
  164.4 0.0 collective-permute-done.4.theirs_next
  164.4 3.9 %shard_map.67 = f32[2048,384]{1,0:T(8,128)} custom-call(s32[67]{0:T(128)S(1)} %copy-done.3, f32[8,288,128]{2,1,0:T(8,128)S(1)} %all_to_all.36.mine, f32[8,160,128]{2,1,0:T(8,128)S(1)} %all-to-all-done.5.following.mine_next, f32[8,288,128]{2,1,0:T(8,128)S(1)} %collective-permute-done.2.theirs, f32[8,160,128]{2,1,0:T(8,128)} %collective-permute-done.4.theirs_next, ...), custom_call_target="tpu_custom_call" | custom-call | tf_op jit(solution)/shard_map/pallas_call | solution.py:504
  (4 shorter events, 0.1 us)
Async XLA Ops:
  23.0 13.0 %copy-start.3 = (s32[67]{0:T(128)S(1)}, s32[67]{0:T(128)}, u32[]{:S(2)}) copy-start(s32[67]{0:T(128)} %pad_add_fusion.place) | copy-start | bytes 808
  23.0 13.0 %copy-start.4 = (s32[128]{0:T(128)S(1)}, s32[128]{0:T(128)}, u32[]{:S(2)}) copy-start(s32[128]{0:T(128)} %seeds.1) | copy-start | bytes 1540
  23.9 12.1 %all-to-all-start.1 = ((f32[8,128,128]{2,1,0:T(8,128)}), f32[8,128,128]{2,1,0:T(8,128)S(1)}, u32[]{:S(2)}, u32[]{:S(2)}) async-start(f32[8,128,128]{2,1,0:T(8,128)} %broadcast_in_dim.12), calls=%async_computation.1 | async-start | bytes 1048576 | tf_op jit(solution)/shard_map/all_to_all | solution.py:520
  27.5 6.7 %collective-permute-start = (f32[128,128]{0,1:T(8,128)S(1)}, f32[128,128]{0,1:T(8,128)S(1)}, u32[]{:S(2)}, u32[]{:S(2)}) collective-permute-start(f32[128,128]{0,1:T(8,128)S(1)} %bitcast.12), channel_id=1, source_target_pairs={{0,4},{1,5},{2,30},{3,31},{4,34},{5,35},{6,56},{7,57},{8,74},{9,75... | collective-permute-start | bytes 196616 | tf_op jit(solution)/shard_map/ppermute | solution.py:547
  41.5 7.9 %collective-permute-start.1 = (f32[8,128,128]{2,1,0:T(8,128)S(1)}, f32[8,128,128]{2,1,0:T(8,128)S(1)}, u32[]{:S(2)}, u32[]{:S(2)}) collective-permute-start(f32[8,128,128]{2,1,0:T(8,128)S(1)} %get-tuple-element.18), channel_id=1, source_target_pairs={{0,1},{1,0},{2,3},{3,2},{4,5},{5,4},{6,7},{7,6},{8,9},{9,8},{10,11... | collective-permute-start | bytes 1572872 | tf_op jit(solution)/shard_map/ppermute | solution.py:524
  50.3 15.4 %all-to-all-start.2 = ((f32[8,160,128]{2,1,0:T(8,128)}), f32[8,160,128]{2,1,0:T(8,128)S(1)}, u32[]{:S(2)}, u32[]{:S(2)}) async-start(f32[8,160,128]{2,1,0:T(8,128)} %pad_maximum_fusion), calls=%async_computation.2 | async-start | bytes 1310720 | tf_op jit(solution)/shard_map/all_to_all | solution.py:515
  85.0 3.9 %collective-permute-start.2 = (f32[8,288,128]{2,1,0:T(8,128)S(1)}, f32[8,288,128]{2,1,0:T(8,128)S(1)}, u32[]{:S(2)}, u32[]{:S(2)}) collective-permute-start(f32[8,288,128]{2,1,0:T(8,128)S(1)} %all_to_all.36.mine), channel_id=1, source_target_pairs={{0,1},{1,0},{2,3},{3,2},{4,5},{5,4},{6,7},{7,6},{8,9},{9,8},{10,11... | collective-permute-start | bytes 3538952 | tf_op jit(solution)/shard_map/ppermute | solution.py:524
  93.4 30.3 %copy-start.1 = (f32[256,128]{1,0:T(8,128)}, f32[256,128]{1,0:T(8,128)S(1)}, u32[]{:S(2)}) copy-start(f32[256,128]{1,0:T(8,128)S(1)} %get-tuple-element.21.g00.start) | copy-start | bytes 393220
  110.8 5.2 %collective-permute-start.3 = (f32[160,128]{1,0:T(8,128)S(1)}, f32[160,128]{1,0:T(8,128)S(1)}, u32[]{:S(2)}, u32[]{:S(2)}) collective-permute-start(f32[160,128]{1,0:T(8,128)S(1)} %reduce_sum.29), channel_id=1, source_target_pairs={{0,4},{1,5},{2,30},{3,31},{4,34},{5,35},{6,56},{7,57},{8,74},{9,75... | collective-permute-start | bytes 245768 | tf_op jit(solution)/shard_map/ppermute | solution.py:558
  116.9 15.3 %all-to-all-start.5 = ((f32[8,160,128]{2,1,0:T(8,128)}), f32[8,160,128]{2,1,0:T(8,128)S(1)}, u32[]{:S(2)}, u32[]{:S(2)}) async-start(f32[8,160,128]{2,1,0:T(8,128)} %broadcast_in_dim.14), calls=%async_computation.5 | async-start | bytes 1310720 | tf_op jit(solution)/shard_map/all_to_all | solution.py:520
  127.4 0.6 copy-start.2
  133.3 10.5 %copy-start = (f32[392,128]{1,0:T(8,128)}, f32[392,128]{1,0:T(8,128)S(1)}, u32[]{:S(2)}) copy-start(f32[392,128]{1,0:T(8,128)S(1)} %shard_map.64.keep) | copy-start | bytes 602116
  133.3 5.2 %collective-permute-start.5 = (f32[392,128]{1,0:T(8,128)S(1)}, f32[392,128]{1,0:T(8,128)S(1)}, u32[]{:S(2)}, u32[]{:S(2)}) collective-permute-start(f32[392,128]{1,0:T(8,128)S(1)} %shard_map.64.keep), channel_id=1, source_target_pairs={{0,1},{1,0},{2,3},{3,2},{4,5},{5,4},{6,7},{7,6},{8,9},{9,8},{10,11... | collective-permute-start | bytes 602120 | tf_op jit(solution)/shard_map/ppermute | solution.py:524
  137.4 26.9 %collective-permute-start.4 = (f32[8,160,128]{2,1,0:T(8,128)S(1)}, f32[8,160,128]{2,1,0:T(8,128)}, u32[]{:S(2)}, u32[]{:S(2)}) collective-permute-start(f32[8,160,128]{2,1,0:T(8,128)S(1)} %all-to-all-done.5.following.mine_next), channel_id=1, source_target_pairs={{0,1},{1,0},{2,3},{3,2},{4,5},{5,4},{6,7},{7,6},{8,9},{9,8},{10,11... | collective-permute-start | bytes 1966088 | tf_op jit(solution)/shard_map/ppermute | solution.py:524
  138.5 5.3 %copy-start.5 = (f32[392,128]{1,0:T(8,128)}, f32[392,128]{1,0:T(8,128)S(1)}, u32[]{:S(2)}) copy-start(f32[392,128]{1,0:T(8,128)S(1)} %collective-permute-done.5.got) | copy-start | bytes 602116
  139.4 15.2 %all-to-all-start.6 = ((f32[8,136,128]{2,1,0:T(8,128)}), f32[8,136,128]{2,1,0:T(8,128)}, u32[]{:S(2)}, u32[]{:S(2)}) async-start(f32[8,136,128]{2,1,0:T(8,128)} %broadcast_in_dim.15), calls=%async_computation.6 | async-start | bytes 1114112 | tf_op jit(solution)/shard_map/all_to_all | solution.py:520

commit v6 on v5

--- a/solution.py
+++ b/solution.py
@@ -11,14 +11,26 @@
 ALL = (ROWS, CHIP, CORE)
 SWAP = [(0, 1), (1, 0)]
 SLOTS = (
-    (2, 6, 0, 5, 1, 4, 3, 7),
-    (7, 1, 4, 3, 5, 2, 6, 0),
-    (1, 5, 0, 4, 3, 7, 2, 6),
-    (4, 2, 5, 1, 6, 0, 7, 3),
-    (5, 0, 7, 1, 6, 2, 4, 3),
-    (1, 4, 0, 6, 3, 5, 2, 7),
-    (4, 3, 7, 2, 6, 1, 5, 0),
-    (2, 4, 3, 6, 0, 7, 1, 5),
+    (
+        (2, 6, 3, 5, 0, 4, 1, 7),
+        (7, 3, 6, 2, 5, 1, 4, 0),
+        (3, 5, 0, 4, 1, 7, 2, 6),
+        (4, 0, 5, 1, 6, 2, 7, 3),
+        (4, 0, 7, 3, 6, 2, 5, 1),
+        (1, 5, 2, 6, 3, 7, 0, 4),
+        (7, 3, 6, 2, 5, 1, 4, 0),
+        (2, 4, 3, 7, 0, 6, 1, 5),
+    ),
+    (
+        (2, 6, 1, 7, 0, 4, 3, 5),
+        (7, 3, 4, 0, 5, 1, 6, 2),
+        (3, 7, 0, 4, 1, 5, 2, 6),
+        (6, 0, 5, 1, 4, 2, 7, 3),
+        (4, 0, 7, 1, 6, 2, 5, 3),
+        (1, 5, 0, 6, 3, 7, 2, 4),
+        (7, 3, 6, 2, 5, 1, 4, 0),
+        (2, 4, 3, 7, 0, 6, 1, 5),
+    ),
 )
 W = 128
 f32 = jnp.float32
@@ -119,24 +131,28 @@
     return ref[:, start : start + count, :].reshape(ref.shape[0] * count, W)
 
 
-def turned_blocks(ref, place, start, count, parts):
-    return jnp.concatenate([ref[place[3 + place[0] * ref.shape[0] + p], start : start + count, :] for p in parts])
-
-
-def first_factor(g00, inverse):
-    inverse[...] = factor(g00[:W, :])[1]
-
-
-def middle(start, inv0, keep, got, pack, stage, sems):
+def turned_blocks(ref, place, table, start, count, parts, core):
+    first = (core * ref.shape[0] + place[0]) * ref.shape[0]
+    return jnp.concatenate([ref[table[first + p], start : start + count, :] for p in parts])
+
+
+def first_factor(start, out):
     g00, cee = start[:W, :], start[W:, :]
-    li0 = inv0[...]
+    li0 = factor(g00)[1]
+    u = nt(cee, li0)
+    side = nn(li0, g00)
+    for i, block in enumerate([li0, u, nn(side, u), nt(side, li0)]):
+        out[i * W : (i + 1) * W, :] = block
+
+
+def middle(start, ready, keep, got, pack, stage, sems):
+    g00, cee = start[:W, :], start[W:, :]
+    li0, u, h0, m00 = (ready[i * W : (i + 1) * W, :] for i in range(4))
     g01, g11 = (keep[i * W : (i + 1) * W, :] + got[i * W : (i + 1) * W, :] for i in range(2))
     x0 = li0.T
-    u = nt(cee, li0)
     side = jnp.concatenate([g00, g01], axis=1)
     gram = jnp.concatenate([side, jnp.concatenate([g01.T, g11], axis=1)])
-    h = nn(li0, nn(side, jnp.concatenate([u, x0])))
-    m00 = nn(li0, nt(g00, li0))
+    h = h0 + nt(nn(li0, g01), li0)
     h_full = h + (h - nn(m00, h))
     g02 = g11 + tn(cee, g01)
     for i, block in enumerate([h, h_full, m00, g02, g00, g01, g11, li0]):
@@ -374,9 +390,10 @@
     return both[:, :W] + both[:, W:] + mm(low, right[0])
 
 
-def step_grams(place, mine, out):
+def step_grams(place, table, mine, out):
     parts = mine.shape[0]
-    step, start = blocks_of(mine, 0, W), turned_blocks(mine, place, W + 2 * W // parts, W, range(parts))
+    step = blocks_of(mine, 0, W)
+    start = turned_blocks(mine, place, table, W + 2 * W // parts, W, range(parts), place[1])
     out[:W, :] = cross(start, step)
     out[W:, :] = cross(step, step)
 
@@ -388,12 +405,13 @@
 SPARE = 8
 
 
-def next_grams(place, mine, following, out):
+def next_grams(place, table, mine, following, out):
     parts = mine.shape[0]
     bit = W // parts
     step = blocks_of(mine, 0, W)
     then, g01, g11 = (
-        turned_blocks(following, place, s, n, range(parts)) for s, n in ((0, W), (W, bit), (W + bit, bit))
+        turned_blocks(following, place, table, s, n, range(parts), place[1])
+        for s, n in ((0, W), (W, bit), (W + bit, bit))
     )
     g12, g22 = cross(step, then), cross(then, then)
     i, j = corner()
@@ -464,7 +482,7 @@
     )(place, covariance, mine, theirs, grams)
 
 
-def basis_rows(place, mine, mine_next, theirs, theirs_next, mix, out, stage, sems):
+def basis_rows(place, table, mine, mine_next, theirs, theirs_next, mix, out, stage, sems):
     parts = mine.shape[0]
     bit = 2 * W // parts
     count, tall, _ = stage.shape
@@ -479,9 +497,9 @@
         order = range(line // W, (line + tall) // W)
         left = jnp.concatenate(
             [
-                turned_blocks(pair, place, W + bit, W, order),
+                turned_blocks(pair, place, table, W + bit, W, order, side),
                 pair[line // W : (line + tall) // W, :W, :].reshape(tall, W),
-                turned_blocks(following, place, 0, W, order),
+                turned_blocks(following, place, table, 0, W, order, side),
             ],
             axis=1,
         )
@@ -497,18 +515,18 @@
         copy.wait()
 
 
-def basis_of(place, mine, mine_next, theirs, theirs_next, mix):
+def basis_of(place, table, mine, mine_next, theirs, theirs_next, mix):
     height = 2 * mine.shape[0] * W
     tall = 256
     breadth = mix.shape[1]
     return pl.pallas_call(
         basis_rows,
         out_shape=jax.ShapeDtypeStruct((height, breadth), f32),
-        in_specs=[SMEM] + [VMEM] * 5,
+        in_specs=[SMEM] * 2 + [VMEM] * 5,
         out_specs=HBM,
         scratch_shapes=[pltpu.VMEM((height // tall, tall, breadth), f32), pltpu.SemaphoreType.DMA((height // tall,))],
         compiler_params=room(24),
-    )(place, mine, mine_next, theirs, theirs_next, mix)
+    )(place, table, mine, mine_next, theirs, theirs_next, mix)
 
 
 def scattered(parts, axis):
@@ -526,7 +544,7 @@
 
 def turned(rows, chips, cores):
     return [
-        ((r * chips + a) * cores + b, (a * chips + SLOTS[a][r]) * cores + b)
+        ((r * chips + a) * cores + b, (a * chips + SLOTS[b][a][r]) * cores + b)
         for r in range(rows)
         for a in range(chips)
         for b in range(cores)
@@ -539,10 +557,9 @@
     rows, chips, cores = (lax.axis_size(a) for a in ALL)
     row, chip, core = (lax.axis_index(a) for a in ALL)
     order = height * rows
-    square = (width, width)
     turn = turned(rows, chips, cores)
-    slots = jnp.array(SLOTS, jnp.int32).reshape(-1)
-    place = jnp.concatenate([jnp.stack([row, core, chip * cores + core]).astype(jnp.int32), slots])
+    table = jnp.array(SLOTS, jnp.int32).reshape(-1)
+    place = jnp.stack([row, core, chip * cores + core]).astype(jnp.int32)
     start_piece = scattered(picked_rows(place, seed_index, covariance, rows), ROWS).T
     start_turned = lax.ppermute(start_piece, ALL, turn)
     start = gathered(start_piece, ROWS).reshape(breadth, width)
@@ -553,12 +570,12 @@
     parts = jnp.concatenate([keep + got, small], axis=1)
     mine = gathered(jnp.concatenate([scattered(parts, CHIP), start_turned]), CHIP)
     theirs = other_core(mine)
-    (grams,) = kernel(step_grams, [(2 * width, width)], place, mine)
+    (grams,) = kernel(step_grams, [(2 * width, width)], place, table, mine)
     parts, zero_grams = image_of_step(place, covariance, mine, theirs, grams)
     piece = lax.ppermute(scattered(parts, ROWS), ALL, turn)
-    (inv0,) = kernel(first_factor, [square], zero_grams)
-    mine_next, inv0 = lax.optimization_barrier((gathered(piece, CHIP), inv0))
-    (keep,) = kernel(next_grams, [(3 * width + SPARE, width)], place, mine, mine_next)
+    (ready,) = kernel(first_factor, [(4 * width, width)], zero_grams)
+    mine_next, ready = lax.optimization_barrier((gathered(piece, CHIP), ready))
+    (keep,) = kernel(next_grams, [(3 * width + SPARE, width)], place, table, mine, mine_next)
     got = other_core(keep)
     totals = gathered(keep[2 * width :] + got[2 * width :], ROWS)
     theirs_next = other_core(mine_next)
@@ -570,7 +587,7 @@
         out_specs=HBM,
         scratch_shapes=stage,
         compiler_params=room(60),
-    )(zero_grams, inv0, keep, got)
+    )(zero_grams, ready, keep, got)
     totals, pack = lax.optimization_barrier((totals, pack))
     scale = float(order) ** 0.5
 
@@ -586,7 +603,7 @@
         scratch_shapes=stage,
         compiler_params=room(52),
     )(pack, totals)
-    basis = basis_of(place, mine, mine_next, theirs, theirs_next, mix)
+    basis = basis_of(place, table, mine, mine_next, theirs, theirs_next, mix)
     return basis, projection, first_pass
 
 

time: 169 us -> 166 us (0.982)
  starting transfers between devices: 38.2 us -> 32.4 us
  waiting for transfers between devices: 26.2 us -> 29.3 us
    ppermute x1, waiting for transfers between devices: 1.87 us -> 5.51 us  [local(): start_turned = lax.ppermute(start_piece, ALL, turn)]
    all_to_all x3, waiting for transfers between devices: 7.53 us -> 5.5 us  [gathered(): return lax.all_to_all(copies, axis, 0, 0, tiled=True)]
    ppermute x1, starting transfers between devices: 2.84 us -> 1 us  [local(): piece = lax.ppermute(scattered(parts, ROWS), ALL, turn)]
    ppermute x1, starting transfers between devices: 4.82 us -> 2.98 us  [local(): start_turned = lax.ppermute(start_piece, ALL, turn)]
    all_to_all x3, starting transfers between devices: 14.7 us -> 12.9 us  [gathered(): return lax.all_to_all(copies, axis, 0, 0, tiled=True)]
where the time goes in v6:
time: 166 us; the launch traced here: 165 us
  blocking collectives  52.8 us (32%)
  Pallas kernels  43.2 us (26%)
  starting transfers between devices  32.4 us (20%)
  waiting for transfers between devices  29.3 us (18%)
  local copies, waits for them, and re-layouts  3.56 us (2%)
  other arithmetic  2.81 us (2%)
    all_to_all x2, blocking collectives, scattered(): return jnp.sum(lax.all_to_all(parts, axis, 0, 0, tiled=True), axis=0)  33.7 us
    all_to_all x1, blocking collectives, gathered(): return lax.all_to_all(copies, axis, 0, 0, tiled=True)  19 us
    all_to_all x3, starting transfers between devices, gathered(): return lax.all_to_all(copies, axis, 0, 0, tiled=True)  12.9 us
    ppermute x4, starting transfers between devices, other_core(): return lax.ppermute(value, CORE, SWAP)  11.8 us
    all_to_all x1, waiting for transfers between devices, scattered(): return jnp.sum(lax.all_to_all(parts, axis, 0, 0, tiled=True), axis=0)  11.6 us
    pallas_call x1, Pallas kernels, local(): pl.pallas_call(last_step, out_shape=[jax.ShapeDtypeStruct(s, f32) for s i...  9.75 us
    pallas_call x1, Pallas kernels, local(): pl.pallas_call(middle, out_shape=jax.ShapeDtypeStruct((PACK, width), f32)...  8.78 us
    pallas_call x3, Pallas kernels, kernel(): pl.pallas_call(body, out_shape=[jax.ShapeDtypeStruct(s, f32) for s in sha...  6.5 us
  transfers between devices with their start and end apart: 10, of which 9 were waited for; matrix products, arithmetic and copies ran while one was open for 1% of the time, Pallas kernels for 15%

profile of v6, /device:TPU:1, one launch (start us, length us, event | category | flops | bytes accessed | tf_op | source)
XLA Modules:
  0.0 165.0 jit_solution(16492408692386955106)
XLA Ops:
  0.6 0.6 pad_add_fusion.place
  1.3 3.2 %shard_map.58 = f32[8,128,128]{2,1,0:T(8,128)} custom-call(s32[3]{0:T(128)} %pad_add_fusion.place, s32[128]{0:T(128)} %seeds.1, s32[1,128]{1,0:T(1,128)} %bitcast.8, f32[2048,1024]{1,0:T(8,128)} %covariance.5), custom_call_target="tpu_custom_call" | custom-call | tf_op jit(solution)/shard_map/pallas_call | solution.py:289
  4.5 17.9 %all_to_all.35 = f32[8,128,128]{2,1,0:T(8,128)S(1)} all-to-all(f32[8,128,128]{2,1,0:T(8,128)} %shard_map.58), channel_id=1, replica_groups=mesh['row'=8,'chip'=8,'core'=2] {'row'}, dimensions={0} | all-to-all | bytes 1048576 | tf_op jit(solution)/shard_map/all_to_all | solution.py:533
  22.4 0.0 copy-start.3
  22.4 0.0 copy-start.4
  22.4 0.1 copy.6
  22.5 0.8 broadcast_in_dim.12
  23.4 3.5 %all-to-all-start.1 = ((f32[8,128,128]{2,1,0:T(8,128)}), f32[8,128,128]{2,1,0:T(8,128)S(1)}, u32[]{:S(2)}, u32[]{:S(2)}) async-start(f32[8,128,128]{2,1,0:T(8,128)} %broadcast_in_dim.12), calls=%async_computation.1 | async-start | bytes 1048576 | tf_op jit(solution)/shard_map/all_to_all | solution.py:538
  26.9 3.0 %collective-permute-start = (f32[128,128]{0,1:T(8,128)S(1)}, f32[128,128]{0,1:T(8,128)S(1)}, u32[]{:S(2)}, u32[]{:S(2)}) collective-permute-start(f32[128,128]{0,1:T(8,128)S(1)} %bitcast.12), channel_id=1, source_target_pairs={{0,4},{1,5},{2,30},{3,31},{4,38},{5,39},{6,56},{7,61},{8,72},{9,73... | collective-permute-start | bytes 196616 | tf_op jit(solution)/shard_map/ppermute | solution.py:564
  29.8 5.5 %collective-permute-done = f32[128,128]{0,1:T(8,128)S(1)} collective-permute-done((f32[128,128]{0,1:T(8,128)S(1)}, f32[128,128]{0,1:T(8,128)S(1)}, u32[]{:S(2)}, u32[]{:S(2)}) %collective-permute-start) | collective-permute-done | bytes 65568 | tf_op jit(solution)/shard_map/ppermute | solution.py:564
  35.3 0.1 all-to-all-done.1
  35.4 0.0 copy-done.3
  35.4 0.0 copy-done.4
  35.4 5.4 %shard_map.59 = (f32[8,128,128]{2,1,0:T(8,128)S(1)}, f32[8,128,128]{2,1,0:T(8,128)S(1)}) custom-call(s32[3]{0:T(128)S(1)} %copy-done.3, s32[1,128]{1,0:T(1,128)S(1)} %bitcast.9, f32[2048,1024]{1,0:T(8,128)} %covariance.5, f32[1024,128]{1,0:T(8,128)S(1)} %bitcast.6), custom_call_target="tpu_custom_call" | custom-call | tf_op jit(solution)/shard_map/pallas_call | solution.py:348
  40.9 6.1 %collective-permute-start.1 = (f32[8,128,128]{2,1,0:T(8,128)S(1)}, f32[8,128,128]{2,1,0:T(8,128)S(1)}, u32[]{:S(2)}, u32[]{:S(2)}) collective-permute-start(f32[8,128,128]{2,1,0:T(8,128)S(1)} %get-tuple-element.18), channel_id=1, source_target_pairs={{0,1},{1,0},{2,3},{3,2},{4,5},{5,4},{6,7},{7,6},{8,9},{9,8},{10,11... | collective-permute-start | bytes 1572872 | tf_op jit(solution)/shard_map/ppermute | solution.py:542
  47.0 1.1 shard_map.60
  48.0 0.5 collective-permute-done.1
  48.5 0.1 add.10
  48.6 0.9 pad_maximum_fusion
  49.4 3.8 %all-to-all-start.2 = ((f32[8,160,128]{2,1,0:T(8,128)}), f32[8,160,128]{2,1,0:T(8,128)S(1)}, u32[]{:S(2)}, u32[]{:S(2)}) async-start(f32[8,160,128]{2,1,0:T(8,128)} %pad_maximum_fusion), calls=%async_computation.2 | async-start | bytes 1310720 | tf_op jit(solution)/shard_map/all_to_all | solution.py:533
  53.2 0.1 copy.7
  53.3 11.6 %all-to-all-done.2 = f32[8,160,128]{2,1,0:T(8,128)S(1)} async-done(((f32[8,160,128]{2,1,0:T(8,128)}), f32[8,160,128]{2,1,0:T(8,128)S(1)}, u32[]{:S(2)}, u32[]{:S(2)}) %all-to-all-start.2) | async-done | bytes 655392 | tf_op jit(solution)/shard_map/all_to_all | solution.py:533
  64.9 0.1 broadcast_in_dim.13
  65.0 0.0 copy-start.5
  65.0 19.0 %all_to_all.36.mine = f32[8,288,128]{2,1,0:T(8,128)S(1)} all-to-all(f32[8,288,128]{2,1,0:T(8,128)S(1)} %broadcast_in_dim.13), channel_id=1, replica_groups=mesh['row'=8,'chip'=8,'core'=2] {'chip'}, dimensions={0} | all-to-all | bytes 2359296 | tf_op jit(solution)/shard_map/all_to_all | solution.py:538
  84.1 1.4 collective-permute-start.2
  85.5 0.0 copy-done.5
  85.5 1.1 shard_map.61.grams
  86.6 1.4 collective-permute-done.2.theirs
  88.0 4.5 %shard_map.62 = (f32[8,160,128]{2,1,0:T(8,128)S(1)}, f32[256,128]{1,0:T(8,128)S(1)}) custom-call(s32[3]{0:T(128)S(1)} %copy-done.3, f32[2048,1024]{1,0:T(8,128)} %covariance.5, f32[8,288,128]{2,1,0:T(8,128)S(1)} %all_to_all.36.mine, f32[8,288,128]{2,1,0:T(8,128)S(1)} %collective-permute-done.2.theirs, f32[256,128]{1,0:T(8,128)S(1)} %shard_map.61.grams), custom_call_target="tpu_custom_call" | custom-call | tf_op jit(solution)/shard_map/pallas_call | solution.py:472
  92.5 0.0 copy-start.2
  92.5 15.8 %all_to_all.37 = f32[8,160,128]{2,1,0:T(8,128)} all-to-all(f32[8,160,128]{2,1,0:T(8,128)S(1)} %get-tuple-element.20), channel_id=1, replica_groups=mesh['row'=8,'chip'=8,'core'=2] {'row'}, dimensions={0} | all-to-all | bytes 1310720 | tf_op jit(solution)/shard_map/all_to_all | solution.py:533
  108.4 1.1 reduce_sum.29
  109.5 1.0 collective-permute-start.3
  110.5 3.9 %collective-permute-done.3 = f32[160,128]{1,0:T(8,128)S(1)} collective-permute-done((f32[160,128]{1,0:T(8,128)S(1)}, f32[160,128]{1,0:T(8,128)S(1)}, u32[]{:S(2)}, u32[]{:S(2)}) %collective-permute-start.3) | collective-permute-done | bytes 81952 | tf_op jit(solution)/shard_map/ppermute | solution.py:575
  114.4 0.9 broadcast_in_dim.14
  115.3 5.2 %all-to-all-start.5 = ((f32[8,160,128]{2,1,0:T(8,128)}), f32[8,160,128]{2,1,0:T(8,128)S(1)}, u32[]{:S(2)}, u32[]{:S(2)}) async-start(f32[8,160,128]{2,1,0:T(8,128)} %broadcast_in_dim.14), calls=%async_computation.5 | async-start | bytes 1310720 | tf_op jit(solution)/shard_map/all_to_all | solution.py:538
  120.5 0.0 copy-done.2
  120.5 4.4 %shard_map.63.ready = f32[512,128]{1,0:T(8,128)S(1)} custom-call(f32[256,128]{1,0:T(8,128)S(1)} %get-tuple-element.21.start), custom_call_target="tpu_custom_call" | custom-call | tf_op jit(solution)/shard_map/pallas_call | solution.py:238
  124.9 0.0 copy-start.1
  124.9 0.7 copy-done.1
  125.6 3.4 %all-to-all-done.5.following.mine_next = f32[8,160,128]{2,1,0:T(8,128)S(1)} async-done(((f32[8,160,128]{2,1,0:T(8,128)}), f32[8,160,128]{2,1,0:T(8,128)S(1)}, u32[]{:S(2)}, u32[]{:S(2)}) %all-to-all-start.5) | async-done | bytes 655392 | tf_op jit(solution)/shard_map/all_to_all | solution.py:538
  129.0 1.0 shard_map.64.keep
  130.0 0.0 copy-start
  130.1 4.1 %collective-permute-start.5 = (f32[392,128]{1,0:T(8,128)S(1)}, f32[392,128]{1,0:T(8,128)S(1)}, u32[]{:S(2)}, u32[]{:S(2)}) collective-permute-start(f32[392,128]{1,0:T(8,128)S(1)} %shard_map.64.keep), channel_id=1, source_target_pairs={{0,1},{1,0},{2,3},{3,2},{4,5},{5,4},{6,7},{7,6},{8,9},{9,8},{10,11... | collective-permute-start | bytes 602120 | tf_op jit(solution)/shard_map/ppermute | solution.py:542
  134.2 0.1 collective-permute-start.4
  134.3 1.0 collective-permute-done.5.got
  135.3 0.0 copy-start.6
  135.3 0.9 broadcast_in_dim.15
  136.1 4.2 %all-to-all-start.6 = ((f32[8,136,128]{2,1,0:T(8,128)}), f32[8,136,128]{2,1,0:T(8,128)}, u32[]{:S(2)}, u32[]{:S(2)}) async-start(f32[8,136,128]{2,1,0:T(8,128)} %broadcast_in_dim.15), calls=%async_computation.6 | async-start | bytes 1114112 | tf_op jit(solution)/shard_map/all_to_all | solution.py:538
  140.3 0.0 copy-done
  140.4 0.0 copy-done.6
  140.4 8.8 %shard_map.65.refs_0_ = f32[2176,128]{1,0:T(8,128)} custom-call(f32[256,128]{1,0:T(8,128)} %copy-done.2, f32[512,128]{1,0:T(8,128)} %copy-done.1, f32[392,128]{1,0:T(8,128)} %copy-done, f32[392,128]{1,0:T(8,128)} %copy-done.6), custom_call_target="tpu_custom_call" | custom-call | tf_op jit(solution)/shard_map/pallas_call | solution.py:583
  149.2 2.0 %all-to-all-done.6.refs_1_ = f32[8,136,128]{2,1,0:T(8,128)} async-done(((f32[8,136,128]{2,1,0:T(8,128)}), f32[8,136,128]{2,1,0:T(8,128)}, u32[]{:S(2)}, u32[]{:S(2)}) %all-to-all-start.6) | async-done | bytes 557088 | tf_op jit(solution)/shard_map/all_to_all | solution.py:538
  151.2 9.8 %shard_map.66 = (f32[384,384]{1,0:T(8,128)S(1)}, f32[384,256]{1,0:T(8,128)}, f32[384,256]{1,0:T(8,128)}) custom-call(f32[2176,128]{1,0:T(8,128)} %shard_map.65.refs_0_, f32[8,136,128]{2,1,0:T(8,128)} %all-to-all-done.6.refs_1_), custom_call_target="tpu_custom_call" | custom-call | tf_op jit(solution)/shard_map/pallas_call | solution.py:598
  160.9 0.0 collective-permute-done.4.theirs_next
  160.9 3.9 %shard_map.67 = f32[2048,384]{1,0:T(8,128)} custom-call(s32[3]{0:T(128)S(1)} %copy-done.3, s32[128]{0:T(128)S(1)} %copy-done.5, f32[8,288,128]{2,1,0:T(8,128)S(1)} %all_to_all.36.mine, f32[8,160,128]{2,1,0:T(8,128)S(1)} %all-to-all-done.5.following.mine_next, f32[8,288,128]{2,1,0:T(8,128)S(1)} %collective-permute-done.2.theirs, ...), custom_call_target="tpu_custom_call" | custom-call | tf_op jit(solution)/shard_map/pallas_call | solution.py:522
  (4 shorter events, 0.1 us)
Async XLA Ops:
  22.4 13.0 %copy-start.3 = (s32[3]{0:T(128)S(1)}, s32[3]{0:T(128)}, u32[]{:S(2)}) copy-start(s32[3]{0:T(128)} %pad_add_fusion.place) | copy-start | bytes 40
  22.4 13.0 %copy-start.4 = (s32[128]{0:T(128)S(1)}, s32[128]{0:T(128)}, u32[]{:S(2)}) copy-start(s32[128]{0:T(128)} %seeds.1) | copy-start | bytes 1540
  23.4 12.1 %all-to-all-start.1 = ((f32[8,128,128]{2,1,0:T(8,128)}), f32[8,128,128]{2,1,0:T(8,128)S(1)}, u32[]{:S(2)}, u32[]{:S(2)}) async-start(f32[8,128,128]{2,1,0:T(8,128)} %broadcast_in_dim.12), calls=%async_computation.1 | async-start | bytes 1048576 | tf_op jit(solution)/shard_map/all_to_all | solution.py:538
  26.9 8.5 %collective-permute-start = (f32[128,128]{0,1:T(8,128)S(1)}, f32[128,128]{0,1:T(8,128)S(1)}, u32[]{:S(2)}, u32[]{:S(2)}) collective-permute-start(f32[128,128]{0,1:T(8,128)S(1)} %bitcast.12), channel_id=1, source_target_pairs={{0,4},{1,5},{2,30},{3,31},{4,38},{5,39},{6,56},{7,61},{8,72},{9,73... | collective-permute-start | bytes 196616 | tf_op jit(solution)/shard_map/ppermute | solution.py:564
  40.9 7.6 %collective-permute-start.1 = (f32[8,128,128]{2,1,0:T(8,128)S(1)}, f32[8,128,128]{2,1,0:T(8,128)S(1)}, u32[]{:S(2)}, u32[]{:S(2)}) collective-permute-start(f32[8,128,128]{2,1,0:T(8,128)S(1)} %get-tuple-element.18), channel_id=1, source_target_pairs={{0,1},{1,0},{2,3},{3,2},{4,5},{5,4},{6,7},{7,6},{8,9},{9,8},{10,11... | collective-permute-start | bytes 1572872 | tf_op jit(solution)/shard_map/ppermute | solution.py:542
  49.4 15.4 %all-to-all-start.2 = ((f32[8,160,128]{2,1,0:T(8,128)}), f32[8,160,128]{2,1,0:T(8,128)S(1)}, u32[]{:S(2)}, u32[]{:S(2)}) async-start(f32[8,160,128]{2,1,0:T(8,128)} %pad_maximum_fusion), calls=%async_computation.2 | async-start | bytes 1310720 | tf_op jit(solution)/shard_map/all_to_all | solution.py:533
  65.0 20.5 %copy-start.5 = (s32[128]{0:T(128)S(1)}, s32[128]{0:T(128)}, u32[]{:S(2)}) copy-start(s32[128]{0:T(128)} %constant.19.table) | copy-start | bytes 1540
  84.1 3.9 %collective-permute-start.2 = (f32[8,288,128]{2,1,0:T(8,128)S(1)}, f32[8,288,128]{2,1,0:T(8,128)S(1)}, u32[]{:S(2)}, u32[]{:S(2)}) collective-permute-start(f32[8,288,128]{2,1,0:T(8,128)S(1)} %all_to_all.36.mine), channel_id=1, source_target_pairs={{0,1},{1,0},{2,3},{3,2},{4,5},{5,4},{6,7},{7,6},{8,9},{9,8},{10,11... | collective-permute-start | bytes 3538952 | tf_op jit(solution)/shard_map/ppermute | solution.py:542
  92.5 27.9 %copy-start.2 = (f32[256,128]{1,0:T(8,128)}, f32[256,128]{1,0:T(8,128)S(1)}, u32[]{:S(2)}) copy-start(f32[256,128]{1,0:T(8,128)S(1)} %get-tuple-element.21.start) | copy-start | bytes 393220
  109.5 4.9 %collective-permute-start.3 = (f32[160,128]{1,0:T(8,128)S(1)}, f32[160,128]{1,0:T(8,128)S(1)}, u32[]{:S(2)}, u32[]{:S(2)}) collective-permute-start(f32[160,128]{1,0:T(8,128)S(1)} %reduce_sum.29), channel_id=1, source_target_pairs={{0,4},{1,5},{2,30},{3,31},{4,38},{5,39},{6,56},{7,61},{8,72},{9,73... | collective-permute-start | bytes 245768 | tf_op jit(solution)/shard_map/ppermute | solution.py:575
  115.3 13.7 %all-to-all-start.5 = ((f32[8,160,128]{2,1,0:T(8,128)}), f32[8,160,128]{2,1,0:T(8,128)S(1)}, u32[]{:S(2)}, u32[]{:S(2)}) async-start(f32[8,160,128]{2,1,0:T(8,128)} %broadcast_in_dim.14), calls=%async_computation.5 | async-start | bytes 1310720 | tf_op jit(solution)/shard_map/all_to_all | solution.py:538
  124.9 0.7 copy-start.1
  130.0 10.3 %copy-start = (f32[392,128]{1,0:T(8,128)}, f32[392,128]{1,0:T(8,128)S(1)}, u32[]{:S(2)}) copy-start(f32[392,128]{1,0:T(8,128)S(1)} %shard_map.64.keep) | copy-start | bytes 602116
  130.1 5.2 %collective-permute-start.5 = (f32[392,128]{1,0:T(8,128)S(1)}, f32[392,128]{1,0:T(8,128)S(1)}, u32[]{:S(2)}, u32[]{:S(2)}) collective-permute-start(f32[392,128]{1,0:T(8,128)S(1)} %shard_map.64.keep), channel_id=1, source_target_pairs={{0,1},{1,0},{2,3},{3,2},{4,5},{5,4},{6,7},{7,6},{8,9},{9,8},{10,11... | collective-permute-start | bytes 602120 | tf_op jit(solution)/shard_map/ppermute | solution.py:542
  134.2 26.7 %collective-permute-start.4 = (f32[8,160,128]{2,1,0:T(8,128)S(1)}, f32[8,160,128]{2,1,0:T(8,128)}, u32[]{:S(2)}, u32[]{:S(2)}) collective-permute-start(f32[8,160,128]{2,1,0:T(8,128)S(1)} %all-to-all-done.5.following.mine_next), channel_id=1, source_target_pairs={{0,1},{1,0},{2,3},{3,2},{4,5},{5,4},{6,7},{7,6},{8,9},{9,8},{10,11... | collective-permute-start | bytes 1966088 | tf_op jit(solution)/shard_map/ppermute | solution.py:542
  135.3 5.1 %copy-start.6 = (f32[392,128]{1,0:T(8,128)}, f32[392,128]{1,0:T(8,128)S(1)}, u32[]{:S(2)}) copy-start(f32[392,128]{1,0:T(8,128)S(1)} %collective-permute-done.5.got) | copy-start | bytes 602116
  136.1 15.0 %all-to-all-start.6 = ((f32[8,136,128]{2,1,0:T(8,128)}), f32[8,136,128]{2,1,0:T(8,128)}, u32[]{:S(2)}, u32[]{:S(2)}) async-start(f32[8,136,128]{2,1,0:T(8,128)} %broadcast_in_dim.15), calls=%async_computation.6 | async-start | bytes 1114112 | tf_op jit(solution)/shard_map/all_to_all | solution.py:538

commit v7 on v6

--- a/solution.py
+++ b/solution.py
@@ -155,7 +155,7 @@
     h = h0 + nt(nn(li0, g01), li0)
     h_full = h + (h - nn(m00, h))
     g02 = g11 + tn(cee, g01)
-    for i, block in enumerate([h, h_full, m00, g02, g00, g01, g11, li0]):
+    for i, block in enumerate([h, h_full, m00, g02, li0]):
         stage[i * W : (i + 1) * W, :] = block
     pack_copy(stage, pack, sems, 0).start()
     comb = jnp.concatenate([u - nn(x0, h_full), x0])
@@ -168,6 +168,7 @@
     s0 = nn(jnp.concatenate([side, g02], axis=1), i1)
     s1 = nn(gram[W:], i1[: 2 * W])
     late = [upper1, i1[:W], i1[W : 2 * W], i1[2 * W :], m01, tn(c1, y1), nn(li0, s0), tn(c1[:W], s0), s1]
+    late.append(tn(i1[:W], s0))
     for i, block in enumerate(late):
         stage[EARLY + i * W : EARLY + (i + 1) * W, :] = block
     second = pack_copy(stage, pack, sems, 1)
@@ -176,8 +177,8 @@
     second.wait()
 
 
-EARLY = 8 * W
-PACK = 17 * W
+EARLY = 5 * W
+PACK = 15 * W
 
 
 def pack_copy(source, target, sems, late):
@@ -192,25 +193,22 @@
     a12, a22 = unpacked(totals[...])
     for copy in copies:
         copy.wait()
-    first, full, m00, a02, a00, a01, a11, li0, upper1, _, c1_top, c1_low, m01, m11, first0, part1, s1 = (
+    first, full, m00, a02, li0, upper1, _, c1_top, c1_low, m01, m11, first0, part1, s1, square = (
         pack[i * W : (i + 1) * W, :] for i in range(PACK // W)
     )
     i1 = pack[EARLY + W : EARLY + 4 * W, :]
     c1 = i1[W:]
-    gram = jnp.concatenate(
-        [
-            jnp.concatenate([a00, a01, a02], axis=1),
-            jnp.concatenate([a01.T, a11, a12], axis=1),
-            jnp.concatenate([a02.T, a12, a22], axis=1),
-        ]
-    )
-    h = jnp.concatenate([first0, part1 + tn(c1_low, s1 + nn(a12, c1_low))])
+    s1 = s1 + nn(a12, c1_low)
+    s2 = nn(jnp.concatenate([a02.T, a12, a22], axis=1), i1)
+    square = square + tn(c1, jnp.concatenate([s1, s2]))
+    h = jnp.concatenate([first0, part1 + tn(c1_low, s1)])
     gram_p = jnp.concatenate([jnp.concatenate([m00, m01], axis=1), jnp.concatenate([m01.T, m11], axis=1)])
     h_full = h + (h - nn(gram_p, h))
+    inner = tn(h, h_full)
+    upper2, li2 = factor(square - inner - inner.T + tn(h_full, nn(gram_p, h_full)))
     zero = jnp.zeros((W, W), f32)
     places = jnp.concatenate([jnp.concatenate([li0.T, zero]), c1], axis=1)
     comb = jnp.concatenate([i1[: 2 * W] - nn(places, h_full), i1[2 * W :]])
-    upper2, li2 = factor(tn(comb, nn(gram, comb)))
     mix[: 2 * W, : 2 * W] = places * scale
     mix[2 * W :, : 2 * W] = jnp.zeros((W, 2 * W), f32)
     mix[:, 2 * W :] = nt(comb, li2) * scale
@@ -292,6 +290,7 @@
         in_specs=[SMEM, SMEM, VMEM, HBM],
         out_specs=VMEM,
         scratch_shapes=[pltpu.VMEM((count, covariance.shape[1]), f32), pltpu.SemaphoreType.DMA],
+        compiler_params=room(50),
     )(place, seeds, seeds.reshape(1, count), covariance)
 
 

time: 166 us -> 164 us (0.988)
  no operation moved by 1% of the time
where the time goes in v7:
time: 164 us
  blocking collectives  52.4 us (32%)
  Pallas kernels  42.1 us (26%)
  starting transfers between devices  32.4 us (20%)
  waiting for transfers between devices  29.3 us (18%)
  local copies, waits for them, and re-layouts  4.21 us (3%)
  other arithmetic  2.23 us (1%)
    all_to_all x2, blocking collectives, scattered(): return jnp.sum(lax.all_to_all(parts, axis, 0, 0, tiled=True), axis=0)  33.4 us
    all_to_all x1, blocking collectives, gathered(): return lax.all_to_all(copies, axis, 0, 0, tiled=True)  19 us
    all_to_all x3, starting transfers between devices, gathered(): return lax.all_to_all(copies, axis, 0, 0, tiled=True)  12.9 us
    ppermute x4, starting transfers between devices, other_core(): return lax.ppermute(value, CORE, SWAP)  11.8 us
    all_to_all x1, waiting for transfers between devices, scattered(): return jnp.sum(lax.all_to_all(parts, axis, 0, 0, tiled=True), axis=0)  11.6 us
    pallas_call x1, Pallas kernels, local(): pl.pallas_call(last_step, out_shape=[jax.ShapeDtypeStruct(s, f32) for s i...  9.58 us
    pallas_call x1, Pallas kernels, local(): pl.pallas_call(middle, out_shape=jax.ShapeDtypeStruct((PACK, width), f32)...  8.84 us
    pallas_call x3, Pallas kernels, kernel(): pl.pallas_call(body, out_shape=[jax.ShapeDtypeStruct(s, f32) for s in sha...  6.5 us
  transfers between devices with their start and end apart: 10, of which 9 were waited for; matrix products, arithmetic and copies ran while one was open for 1% of the time, Pallas kernels for 15%

profile of v7, /device:TPU:1, one launch (start us, length us, event | category | flops | bytes accessed | tf_op | source)
XLA Modules:
  0.0 163.6 jit_solution(4522860264893470065)
XLA Ops:
  0.6 0.1 pad_add_fusion.place
  0.7 0.0 copy-start.3
  0.7 0.7 copy-done.3
  1.4 2.2 %shard_map.58 = f32[8,128,128]{2,1,0:T(8,128)S(1)} custom-call(s32[3]{0:T(128)S(1)} %pad_add_fusion.place, s32[128]{0:T(128)S(1)} %copy-done.3, s32[1,128]{1,0:T(1,128)S(1)} %bitcast.8, f32[2048,1024]{1,0:T(8,128)} %covariance.5), custom_call_target="tpu_custom_call" | custom-call | tf_op jit(solution)/shard_map/pallas_call | solution.py:287
  3.6 17.6 %all_to_all.35 = f32[8,128,128]{2,1,0:T(8,128)S(1)} all-to-all(f32[8,128,128]{2,1,0:T(8,128)S(1)} %shard_map.58), channel_id=1, replica_groups=mesh['row'=8,'chip'=8,'core'=2] {'row'}, dimensions={0} | all-to-all | bytes 1048576 | tf_op jit(solution)/shard_map/all_to_all | solution.py:532
  21.2 0.0 copy-start.4
  21.2 0.1 copy.6
  21.3 0.8 broadcast_in_dim.12
  22.1 3.5 %all-to-all-start.1 = ((f32[8,128,128]{2,1,0:T(8,128)}), f32[8,128,128]{2,1,0:T(8,128)S(1)}, u32[]{:S(2)}, u32[]{:S(2)}) async-start(f32[8,128,128]{2,1,0:T(8,128)} %broadcast_in_dim.12), calls=%async_computation.1 | async-start | bytes 1048576 | tf_op jit(solution)/shard_map/all_to_all | solution.py:537
  25.6 3.0 %collective-permute-start = (f32[128,128]{0,1:T(8,128)S(1)}, f32[128,128]{0,1:T(8,128)S(1)}, u32[]{:S(2)}, u32[]{:S(2)}) collective-permute-start(f32[128,128]{0,1:T(8,128)S(1)} %bitcast.12), channel_id=1, source_target_pairs={{0,4},{1,5},{2,30},{3,31},{4,38},{5,39},{6,56},{7,61},{8,72},{9,73... | collective-permute-start | bytes 196616 | tf_op jit(solution)/shard_map/ppermute | solution.py:563
  28.6 5.5 %collective-permute-done = f32[128,128]{0,1:T(8,128)S(1)} collective-permute-done((f32[128,128]{0,1:T(8,128)S(1)}, f32[128,128]{0,1:T(8,128)S(1)}, u32[]{:S(2)}, u32[]{:S(2)}) %collective-permute-start) | collective-permute-done | bytes 65568 | tf_op jit(solution)/shard_map/ppermute | solution.py:563
  34.1 0.1 all-to-all-done.1
  34.2 0.0 copy-done.4
  34.2 5.4 %shard_map.59 = (f32[8,128,128]{2,1,0:T(8,128)S(1)}, f32[8,128,128]{2,1,0:T(8,128)S(1)}) custom-call(s32[3]{0:T(128)S(1)} %pad_add_fusion.place, s32[1,128]{1,0:T(1,128)S(1)} %bitcast.9, f32[2048,1024]{1,0:T(8,128)} %covariance.5, f32[1024,128]{1,0:T(8,128)S(1)} %bitcast.6), custom_call_target="tpu_custom_call" | custom-call | tf_op jit(solution)/shard_map/pallas_call | solution.py:347
  39.7 6.1 %collective-permute-start.1 = (f32[8,128,128]{2,1,0:T(8,128)S(1)}, f32[8,128,128]{2,1,0:T(8,128)S(1)}, u32[]{:S(2)}, u32[]{:S(2)}) collective-permute-start(f32[8,128,128]{2,1,0:T(8,128)S(1)} %get-tuple-element.18), channel_id=1, source_target_pairs={{0,1},{1,0},{2,3},{3,2},{4,5},{5,4},{6,7},{7,6},{8,9},{9,8},{10,11... | collective-permute-start | bytes 1572872 | tf_op jit(solution)/shard_map/ppermute | solution.py:541
  45.8 1.1 shard_map.60
  46.8 0.5 collective-permute-done.1
  47.3 0.1 add.10
  47.4 0.9 pad_maximum_fusion
  48.2 3.8 %all-to-all-start.2 = ((f32[8,160,128]{2,1,0:T(8,128)}), f32[8,160,128]{2,1,0:T(8,128)S(1)}, u32[]{:S(2)}, u32[]{:S(2)}) async-start(f32[8,160,128]{2,1,0:T(8,128)} %pad_maximum_fusion), calls=%async_computation.2 | async-start | bytes 1310720 | tf_op jit(solution)/shard_map/all_to_all | solution.py:532
  52.0 0.1 copy.7
  52.1 11.6 %all-to-all-done.2 = f32[8,160,128]{2,1,0:T(8,128)S(1)} async-done(((f32[8,160,128]{2,1,0:T(8,128)}), f32[8,160,128]{2,1,0:T(8,128)S(1)}, u32[]{:S(2)}, u32[]{:S(2)}) %all-to-all-start.2) | async-done | bytes 655392 | tf_op jit(solution)/shard_map/all_to_all | solution.py:532
  63.7 0.1 broadcast_in_dim.13
  63.8 0.0 copy-start.5
  63.8 19.0 %all_to_all.36.mine = f32[8,288,128]{2,1,0:T(8,128)S(1)} all-to-all(f32[8,288,128]{2,1,0:T(8,128)S(1)} %broadcast_in_dim.13), channel_id=1, replica_groups=mesh['row'=8,'chip'=8,'core'=2] {'chip'}, dimensions={0} | all-to-all | bytes 2359296 | tf_op jit(solution)/shard_map/all_to_all | solution.py:537
  82.9 1.4 collective-permute-start.2
  84.3 0.0 copy-done.5
  84.3 1.1 shard_map.61.grams
  85.4 1.4 collective-permute-done.2.theirs
  86.8 4.5 %shard_map.62 = (f32[8,160,128]{2,1,0:T(8,128)S(1)}, f32[256,128]{1,0:T(8,128)S(1)}) custom-call(s32[3]{0:T(128)S(1)} %pad_add_fusion.place, f32[2048,1024]{1,0:T(8,128)} %covariance.5, f32[8,288,128]{2,1,0:T(8,128)S(1)} %all_to_all.36.mine, f32[8,288,128]{2,1,0:T(8,128)S(1)} %collective-permute-done.2.theirs, f32[256,128]{1,0:T(8,128)S(1)} %shard_map.61.grams), custom_call_target="tpu_custom_call" | custom-call | tf_op jit(solution)/shard_map/pallas_call | solution.py:471
  91.3 0.0 copy-start.2
  91.3 15.8 %all_to_all.37 = f32[8,160,128]{2,1,0:T(8,128)} all-to-all(f32[8,160,128]{2,1,0:T(8,128)S(1)} %get-tuple-element.20), channel_id=1, replica_groups=mesh['row'=8,'chip'=8,'core'=2] {'row'}, dimensions={0} | all-to-all | bytes 1310720 | tf_op jit(solution)/shard_map/all_to_all | solution.py:532
  107.2 1.1 reduce_sum.29
  108.3 1.0 collective-permute-start.3
  109.3 3.9 %collective-permute-done.3 = f32[160,128]{1,0:T(8,128)S(1)} collective-permute-done((f32[160,128]{1,0:T(8,128)S(1)}, f32[160,128]{1,0:T(8,128)S(1)}, u32[]{:S(2)}, u32[]{:S(2)}) %collective-permute-start.3) | collective-permute-done | bytes 81952 | tf_op jit(solution)/shard_map/ppermute | solution.py:574
  113.2 0.9 broadcast_in_dim.14
  114.1 5.2 %all-to-all-start.5 = ((f32[8,160,128]{2,1,0:T(8,128)}), f32[8,160,128]{2,1,0:T(8,128)S(1)}, u32[]{:S(2)}, u32[]{:S(2)}) async-start(f32[8,160,128]{2,1,0:T(8,128)} %broadcast_in_dim.14), calls=%async_computation.5 | async-start | bytes 1310720 | tf_op jit(solution)/shard_map/all_to_all | solution.py:537
  119.3 0.0 copy-done.2
  119.3 4.4 %shard_map.63.ready = f32[512,128]{1,0:T(8,128)S(1)} custom-call(f32[256,128]{1,0:T(8,128)S(1)} %get-tuple-element.21.start), custom_call_target="tpu_custom_call" | custom-call | tf_op jit(solution)/shard_map/pallas_call | solution.py:236
  123.7 0.0 copy-start.1
  123.7 0.7 copy-done.1
  124.4 3.4 %all-to-all-done.5.following.mine_next = f32[8,160,128]{2,1,0:T(8,128)S(1)} async-done(((f32[8,160,128]{2,1,0:T(8,128)}), f32[8,160,128]{2,1,0:T(8,128)S(1)}, u32[]{:S(2)}, u32[]{:S(2)}) %all-to-all-start.5) | async-done | bytes 655392 | tf_op jit(solution)/shard_map/all_to_all | solution.py:537
  127.8 1.0 shard_map.64.keep
  128.8 0.0 copy-start
  128.9 4.1 %collective-permute-start.5 = (f32[392,128]{1,0:T(8,128)S(1)}, f32[392,128]{1,0:T(8,128)S(1)}, u32[]{:S(2)}, u32[]{:S(2)}) collective-permute-start(f32[392,128]{1,0:T(8,128)S(1)} %shard_map.64.keep), channel_id=1, source_target_pairs={{0,1},{1,0},{2,3},{3,2},{4,5},{5,4},{6,7},{7,6},{8,9},{9,8},{10,11... | collective-permute-start | bytes 602120 | tf_op jit(solution)/shard_map/ppermute | solution.py:541
  133.0 0.1 collective-permute-start.4
  133.1 1.0 collective-permute-done.5.got
  134.1 0.0 copy-start.6
  134.1 0.9 broadcast_in_dim.15
  134.9 4.2 %all-to-all-start.6 = ((f32[8,136,128]{2,1,0:T(8,128)}), f32[8,136,128]{2,1,0:T(8,128)}, u32[]{:S(2)}, u32[]{:S(2)}) async-start(f32[8,136,128]{2,1,0:T(8,128)} %broadcast_in_dim.15), calls=%async_computation.6 | async-start | bytes 1114112 | tf_op jit(solution)/shard_map/all_to_all | solution.py:537
  139.1 0.0 copy-done
  139.2 0.0 copy-done.6
  139.2 8.8 %shard_map.65.refs_0_ = f32[1920,128]{1,0:T(8,128)} custom-call(f32[256,128]{1,0:T(8,128)} %copy-done.2, f32[512,128]{1,0:T(8,128)} %copy-done.1, f32[392,128]{1,0:T(8,128)} %copy-done, f32[392,128]{1,0:T(8,128)} %copy-done.6), custom_call_target="tpu_custom_call" | custom-call | tf_op jit(solution)/shard_map/pallas_call | solution.py:582
  148.0 1.9 %all-to-all-done.6.refs_1_ = f32[8,136,128]{2,1,0:T(8,128)} async-done(((f32[8,136,128]{2,1,0:T(8,128)}), f32[8,136,128]{2,1,0:T(8,128)}, u32[]{:S(2)}, u32[]{:S(2)}) %all-to-all-start.6) | async-done | bytes 557088 | tf_op jit(solution)/shard_map/all_to_all | solution.py:537
  150.0 9.6 %shard_map.66 = (f32[384,384]{1,0:T(8,128)S(1)}, f32[384,256]{1,0:T(8,128)}, f32[384,256]{1,0:T(8,128)}) custom-call(f32[1920,128]{1,0:T(8,128)} %shard_map.65.refs_0_, f32[8,136,128]{2,1,0:T(8,128)} %all-to-all-done.6.refs_1_), custom_call_target="tpu_custom_call" | custom-call | tf_op jit(solution)/shard_map/pallas_call | solution.py:597
  159.5 0.0 collective-permute-done.4.theirs_next
  159.6 3.9 %shard_map.67 = f32[2048,384]{1,0:T(8,128)} custom-call(s32[3]{0:T(128)S(1)} %pad_add_fusion.place, s32[128]{0:T(128)S(1)} %copy-done.5, f32[8,288,128]{2,1,0:T(8,128)S(1)} %all_to_all.36.mine, f32[8,160,128]{2,1,0:T(8,128)S(1)} %all-to-all-done.5.following.mine_next, f32[8,288,128]{2,1,0:T(8,128)S(1)} %collective-permute-done.2.theirs, ...), custom_call_target="tpu_custom_call" | custom-call | tf_op jit(solution)/shard_map/pallas_call | solution.py:521
  (4 shorter events, 0.1 us)
Async XLA Ops:
  0.7 0.7 copy-start.3
  21.2 13.0 %copy-start.4 = (s32[128]{0:T(128)S(1)}, s32[128]{0:T(128)}, u32[]{:S(2)}) copy-start(s32[128]{0:T(128)} %seeds.1) | copy-start | bytes 1540
  22.1 12.1 %all-to-all-start.1 = ((f32[8,128,128]{2,1,0:T(8,128)}), f32[8,128,128]{2,1,0:T(8,128)S(1)}, u32[]{:S(2)}, u32[]{:S(2)}) async-start(f32[8,128,128]{2,1,0:T(8,128)} %broadcast_in_dim.12), calls=%async_computation.1 | async-start | bytes 1048576 | tf_op jit(solution)/shard_map/all_to_all | solution.py:537
  25.6 8.5 %collective-permute-start = (f32[128,128]{0,1:T(8,128)S(1)}, f32[128,128]{0,1:T(8,128)S(1)}, u32[]{:S(2)}, u32[]{:S(2)}) collective-permute-start(f32[128,128]{0,1:T(8,128)S(1)} %bitcast.12), channel_id=1, source_target_pairs={{0,4},{1,5},{2,30},{3,31},{4,38},{5,39},{6,56},{7,61},{8,72},{9,73... | collective-permute-start | bytes 196616 | tf_op jit(solution)/shard_map/ppermute | solution.py:563
  39.7 7.6 %collective-permute-start.1 = (f32[8,128,128]{2,1,0:T(8,128)S(1)}, f32[8,128,128]{2,1,0:T(8,128)S(1)}, u32[]{:S(2)}, u32[]{:S(2)}) collective-permute-start(f32[8,128,128]{2,1,0:T(8,128)S(1)} %get-tuple-element.18), channel_id=1, source_target_pairs={{0,1},{1,0},{2,3},{3,2},{4,5},{5,4},{6,7},{7,6},{8,9},{9,8},{10,11... | collective-permute-start | bytes 1572872 | tf_op jit(solution)/shard_map/ppermute | solution.py:541
  48.2 15.4 %all-to-all-start.2 = ((f32[8,160,128]{2,1,0:T(8,128)}), f32[8,160,128]{2,1,0:T(8,128)S(1)}, u32[]{:S(2)}, u32[]{:S(2)}) async-start(f32[8,160,128]{2,1,0:T(8,128)} %pad_maximum_fusion), calls=%async_computation.2 | async-start | bytes 1310720 | tf_op jit(solution)/shard_map/all_to_all | solution.py:532
  63.8 20.5 %copy-start.5 = (s32[128]{0:T(128)S(1)}, s32[128]{0:T(128)}, u32[]{:S(2)}) copy-start(s32[128]{0:T(128)} %constant.19.table) | copy-start | bytes 1540
  82.9 3.9 %collective-permute-start.2 = (f32[8,288,128]{2,1,0:T(8,128)S(1)}, f32[8,288,128]{2,1,0:T(8,128)S(1)}, u32[]{:S(2)}, u32[]{:S(2)}) collective-permute-start(f32[8,288,128]{2,1,0:T(8,128)S(1)} %all_to_all.36.mine), channel_id=1, source_target_pairs={{0,1},{1,0},{2,3},{3,2},{4,5},{5,4},{6,7},{7,6},{8,9},{9,8},{10,11... | collective-permute-start | bytes 3538952 | tf_op jit(solution)/shard_map/ppermute | solution.py:541
  91.3 27.9 %copy-start.2 = (f32[256,128]{1,0:T(8,128)}, f32[256,128]{1,0:T(8,128)S(1)}, u32[]{:S(2)}) copy-start(f32[256,128]{1,0:T(8,128)S(1)} %get-tuple-element.21.start) | copy-start | bytes 393220
  108.3 4.9 %collective-permute-start.3 = (f32[160,128]{1,0:T(8,128)S(1)}, f32[160,128]{1,0:T(8,128)S(1)}, u32[]{:S(2)}, u32[]{:S(2)}) collective-permute-start(f32[160,128]{1,0:T(8,128)S(1)} %reduce_sum.29), channel_id=1, source_target_pairs={{0,4},{1,5},{2,30},{3,31},{4,38},{5,39},{6,56},{7,61},{8,72},{9,73... | collective-permute-start | bytes 245768 | tf_op jit(solution)/shard_map/ppermute | solution.py:574
  114.1 13.7 %all-to-all-start.5 = ((f32[8,160,128]{2,1,0:T(8,128)}), f32[8,160,128]{2,1,0:T(8,128)S(1)}, u32[]{:S(2)}, u32[]{:S(2)}) async-start(f32[8,160,128]{2,1,0:T(8,128)} %broadcast_in_dim.14), calls=%async_computation.5 | async-start | bytes 1310720 | tf_op jit(solution)/shard_map/all_to_all | solution.py:537
  123.7 0.7 copy-start.1
  128.8 10.3 %copy-start = (f32[392,128]{1,0:T(8,128)}, f32[392,128]{1,0:T(8,128)S(1)}, u32[]{:S(2)}) copy-start(f32[392,128]{1,0:T(8,128)S(1)} %shard_map.64.keep) | copy-start | bytes 602116
  128.9 5.2 %collective-permute-start.5 = (f32[392,128]{1,0:T(8,128)S(1)}, f32[392,128]{1,0:T(8,128)S(1)}, u32[]{:S(2)}, u32[]{:S(2)}) collective-permute-start(f32[392,128]{1,0:T(8,128)S(1)} %shard_map.64.keep), channel_id=1, source_target_pairs={{0,1},{1,0},{2,3},{3,2},{4,5},{5,4},{6,7},{7,6},{8,9},{9,8},{10,11... | collective-permute-start | bytes 602120 | tf_op jit(solution)/shard_map/ppermute | solution.py:541
  133.0 26.6 %collective-permute-start.4 = (f32[8,160,128]{2,1,0:T(8,128)S(1)}, f32[8,160,128]{2,1,0:T(8,128)}, u32[]{:S(2)}, u32[]{:S(2)}) collective-permute-start(f32[8,160,128]{2,1,0:T(8,128)S(1)} %all-to-all-done.5.following.mine_next), channel_id=1, source_target_pairs={{0,1},{1,0},{2,3},{3,2},{4,5},{5,4},{6,7},{7,6},{8,9},{9,8},{10,11... | collective-permute-start | bytes 1966088 | tf_op jit(solution)/shard_map/ppermute | solution.py:541
  134.1 5.1 %copy-start.6 = (f32[392,128]{1,0:T(8,128)}, f32[392,128]{1,0:T(8,128)S(1)}, u32[]{:S(2)}) copy-start(f32[392,128]{1,0:T(8,128)S(1)} %collective-permute-done.5.got) | copy-start | bytes 602116
  134.9 15.0 %all-to-all-start.6 = ((f32[8,136,128]{2,1,0:T(8,128)}), f32[8,136,128]{2,1,0:T(8,128)}, u32[]{:S(2)}, u32[]{:S(2)}) async-start(f32[8,136,128]{2,1,0:T(8,128)} %broadcast_in_dim.15), calls=%async_computation.6 | async-start | bytes 1114112 | tf_op jit(solution)/shard_map/all_to_all | solution.py:537

commit v8 on v7

--- a/solution.py
+++ b/solution.py
@@ -161,14 +161,15 @@
     comb = jnp.concatenate([u - nn(x0, h_full), x0])
     y = nn(gram, comb)
     upper1, li1 = factor(tn(comb, y))
-    c1 = nt(comb, li1)
-    y1 = nt(y, li1)
+    scaled = nt(jnp.concatenate([comb, y]), li1)
+    c1, y1 = scaled[: 2 * W], scaled[2 * W :]
     m01 = nn(li0, y1[:W])
     i1 = jnp.concatenate([nn(cee, c1[:W]), c1])
     s0 = nn(jnp.concatenate([side, g02], axis=1), i1)
     s1 = nn(gram[W:], i1[: 2 * W])
-    late = [upper1, i1[:W], i1[W : 2 * W], i1[2 * W :], m01, tn(c1, y1), nn(li0, s0), tn(c1[:W], s0), s1]
-    late.append(tn(i1[:W], s0))
+    crossed = nn(jnp.concatenate([li0, c1[:W].T, i1[:W].T]), s0)
+    late = [upper1, i1[:W], i1[W : 2 * W], i1[2 * W :], m01, tn(c1, y1), crossed[:W], crossed[W : 2 * W], s1]
+    late.append(crossed[2 * W :])
     for i, block in enumerate(late):
         stage[EARLY + i * W : EARLY + (i + 1) * W, :] = block
     second = pack_copy(stage, pack, sems, 1)
@@ -186,11 +187,14 @@
     return pltpu.make_async_copy(source.at[lines, :], target.at[lines, :], sems.at[late])
 
 
-def last(scale, packed, totals, mix, projection, first_pass, pack, sems):
+def last(scale, packed, totals, mix, projection, first_pass, pack, sems, parts, total_sem):
     copies = [pack_copy(packed, pack, sems, i) for i in range(2)]
+    summands = pltpu.make_async_copy(totals, parts, total_sem)
+    summands.start()
     for copy in copies:
         copy.start()
-    a12, a22 = unpacked(totals[...])
+    summands.wait()
+    a12, a22 = unpacked(parts[...])
     for copy in copies:
         copy.wait()
     first, full, m00, a02, li0, upper1, _, c1_top, c1_low, m01, m11, first0, part1, s1, square = (
@@ -597,9 +601,9 @@
     mix, projection, first_pass = pl.pallas_call(
         last_step,
         out_shape=[jax.ShapeDtypeStruct(s, f32) for s in shapes],
-        in_specs=[HBM, VMEM],
+        in_specs=[HBM, HBM],
         out_specs=[VMEM] * 3,
-        scratch_shapes=stage,
+        scratch_shapes=stage + [pltpu.VMEM(totals.shape, f32), pltpu.SemaphoreType.DMA],
         compiler_params=room(52),
     )(pack, totals)
     basis = basis_of(place, table, mine, mine_next, theirs, theirs_next, mix)

time: 164 us -> 164 us (level)
  no operation moved by 1% of the time
where the time goes in v8:
time: 164 us; the launch traced here: 163 us
  blocking collectives  52.6 us (32%)
  Pallas kernels  41.5 us (25%)
  starting transfers between devices  32.4 us (20%)
  waiting for transfers between devices  28.9 us (18%)
  local copies, waits for them, and re-layouts  4.21 us (3%)
  other arithmetic  2.23 us (1%)
    all_to_all x2, blocking collectives, scattered(): return jnp.sum(lax.all_to_all(parts, axis, 0, 0, tiled=True), axis=0)  33.6 us
    all_to_all x1, blocking collectives, gathered(): return lax.all_to_all(copies, axis, 0, 0, tiled=True)  19 us
    all_to_all x3, starting transfers between devices, gathered(): return lax.all_to_all(copies, axis, 0, 0, tiled=True)  12.9 us
    ppermute x4, starting transfers between devices, other_core(): return lax.ppermute(value, CORE, SWAP)  11.8 us
    all_to_all x1, waiting for transfers between devices, scattered(): return jnp.sum(lax.all_to_all(parts, axis, 0, 0, tiled=True), axis=0)  11.6 us
    pallas_call x1, Pallas kernels, local(): pl.pallas_call(middle, out_shape=jax.ShapeDtypeStruct((PACK, width), f32)...  9.19 us
    pallas_call x1, Pallas kernels, local(): pl.pallas_call(last_step, out_shape=[jax.ShapeDtypeStruct(s, f32) for s i...  8.7 us
    pallas_call x3, Pallas kernels, kernel(): pl.pallas_call(body, out_shape=[jax.ShapeDtypeStruct(s, f32) for s in sha...  6.5 us
  transfers between devices with their start and end apart: 10, of which 9 were waited for; matrix products, arithmetic and copies ran while one was open for 1% of the time, Pallas kernels for 15%

profile of v8, /device:TPU:1, one launch (start us, length us, event | category | flops | bytes accessed | tf_op | source)
XLA Modules:
  0.0 162.9 jit_solution(13197645470298008660)
XLA Ops:
  0.6 0.1 pad_add_fusion.place
  0.7 0.0 copy-start.3
  0.7 0.7 copy-done.3
  1.4 2.2 %shard_map.58 = f32[8,128,128]{2,1,0:T(8,128)S(1)} custom-call(s32[3]{0:T(128)S(1)} %pad_add_fusion.place, s32[128]{0:T(128)S(1)} %copy-done.3, s32[1,128]{1,0:T(1,128)S(1)} %bitcast.8, f32[2048,1024]{1,0:T(8,128)} %covariance.5), custom_call_target="tpu_custom_call" | custom-call | tf_op jit(solution)/shard_map/pallas_call | solution.py:291
  3.5 17.8 %all_to_all.35 = f32[8,128,128]{2,1,0:T(8,128)S(1)} all-to-all(f32[8,128,128]{2,1,0:T(8,128)S(1)} %shard_map.58), channel_id=1, replica_groups=mesh['row'=8,'chip'=8,'core'=2] {'row'}, dimensions={0} | all-to-all | bytes 1048576 | tf_op jit(solution)/shard_map/all_to_all | solution.py:536
  21.3 0.0 copy-start.4
  21.3 0.1 copy.6
  21.4 0.8 broadcast_in_dim.12
  22.3 3.5 %all-to-all-start.1 = ((f32[8,128,128]{2,1,0:T(8,128)}), f32[8,128,128]{2,1,0:T(8,128)S(1)}, u32[]{:S(2)}, u32[]{:S(2)}) async-start(f32[8,128,128]{2,1,0:T(8,128)} %broadcast_in_dim.12), calls=%async_computation.1 | async-start | bytes 1048576 | tf_op jit(solution)/shard_map/all_to_all | solution.py:541
  25.8 3.0 %collective-permute-start = (f32[128,128]{0,1:T(8,128)S(1)}, f32[128,128]{0,1:T(8,128)S(1)}, u32[]{:S(2)}, u32[]{:S(2)}) collective-permute-start(f32[128,128]{0,1:T(8,128)S(1)} %bitcast.12), channel_id=1, source_target_pairs={{0,4},{1,5},{2,30},{3,31},{4,38},{5,39},{6,56},{7,61},{8,72},{9,73... | collective-permute-start | bytes 196616 | tf_op jit(solution)/shard_map/ppermute | solution.py:567
  28.8 5.5 %collective-permute-done = f32[128,128]{0,1:T(8,128)S(1)} collective-permute-done((f32[128,128]{0,1:T(8,128)S(1)}, f32[128,128]{0,1:T(8,128)S(1)}, u32[]{:S(2)}, u32[]{:S(2)}) %collective-permute-start) | collective-permute-done | bytes 65568 | tf_op jit(solution)/shard_map/ppermute | solution.py:567
  34.3 0.1 all-to-all-done.1
  34.3 0.0 copy-done.4
  34.3 5.4 %shard_map.59 = (f32[8,128,128]{2,1,0:T(8,128)S(1)}, f32[8,128,128]{2,1,0:T(8,128)S(1)}) custom-call(s32[3]{0:T(128)S(1)} %pad_add_fusion.place, s32[1,128]{1,0:T(1,128)S(1)} %bitcast.9, f32[2048,1024]{1,0:T(8,128)} %covariance.5, f32[1024,128]{1,0:T(8,128)S(1)} %bitcast.6), custom_call_target="tpu_custom_call" | custom-call | tf_op jit(solution)/shard_map/pallas_call | solution.py:351
  39.8 6.1 %collective-permute-start.1 = (f32[8,128,128]{2,1,0:T(8,128)S(1)}, f32[8,128,128]{2,1,0:T(8,128)S(1)}, u32[]{:S(2)}, u32[]{:S(2)}) collective-permute-start(f32[8,128,128]{2,1,0:T(8,128)S(1)} %get-tuple-element.18), channel_id=1, source_target_pairs={{0,1},{1,0},{2,3},{3,2},{4,5},{5,4},{6,7},{7,6},{8,9},{9,8},{10,11... | collective-permute-start | bytes 1572872 | tf_op jit(solution)/shard_map/ppermute | solution.py:545
  45.9 1.1 shard_map.60
  47.0 0.5 collective-permute-done.1
  47.4 0.1 add.10
  47.5 0.9 pad_maximum_fusion
  48.4 3.8 %all-to-all-start.2 = ((f32[8,160,128]{2,1,0:T(8,128)}), f32[8,160,128]{2,1,0:T(8,128)S(1)}, u32[]{:S(2)}, u32[]{:S(2)}) async-start(f32[8,160,128]{2,1,0:T(8,128)} %pad_maximum_fusion), calls=%async_computation.2 | async-start | bytes 1310720 | tf_op jit(solution)/shard_map/all_to_all | solution.py:536
  52.1 0.1 copy.7
  52.2 11.6 %all-to-all-done.2 = f32[8,160,128]{2,1,0:T(8,128)S(1)} async-done(((f32[8,160,128]{2,1,0:T(8,128)}), f32[8,160,128]{2,1,0:T(8,128)S(1)}, u32[]{:S(2)}, u32[]{:S(2)}) %all-to-all-start.2) | async-done | bytes 655392 | tf_op jit(solution)/shard_map/all_to_all | solution.py:536
  63.9 0.1 broadcast_in_dim.13
  63.9 0.0 copy-start.5
  64.0 19.0 %all_to_all.36.mine = f32[8,288,128]{2,1,0:T(8,128)S(1)} all-to-all(f32[8,288,128]{2,1,0:T(8,128)S(1)} %broadcast_in_dim.13), channel_id=1, replica_groups=mesh['row'=8,'chip'=8,'core'=2] {'chip'}, dimensions={0} | all-to-all | bytes 2359296 | tf_op jit(solution)/shard_map/all_to_all | solution.py:541
  83.0 1.4 collective-permute-start.2
  84.5 0.0 copy-done.5
  84.5 1.1 shard_map.61.grams
  85.5 1.4 collective-permute-done.2.theirs
  86.9 4.5 %shard_map.62 = (f32[8,160,128]{2,1,0:T(8,128)S(1)}, f32[256,128]{1,0:T(8,128)S(1)}) custom-call(s32[3]{0:T(128)S(1)} %pad_add_fusion.place, f32[2048,1024]{1,0:T(8,128)} %covariance.5, f32[8,288,128]{2,1,0:T(8,128)S(1)} %all_to_all.36.mine, f32[8,288,128]{2,1,0:T(8,128)S(1)} %collective-permute-done.2.theirs, f32[256,128]{1,0:T(8,128)S(1)} %shard_map.61.grams), custom_call_target="tpu_custom_call" | custom-call | tf_op jit(solution)/shard_map/pallas_call | solution.py:475
  91.5 0.0 copy-start.2
  91.5 15.8 %all_to_all.37 = f32[8,160,128]{2,1,0:T(8,128)} all-to-all(f32[8,160,128]{2,1,0:T(8,128)S(1)} %get-tuple-element.20), channel_id=1, replica_groups=mesh['row'=8,'chip'=8,'core'=2] {'row'}, dimensions={0} | all-to-all | bytes 1310720 | tf_op jit(solution)/shard_map/all_to_all | solution.py:536
  107.3 1.1 reduce_sum.29
  108.4 1.0 collective-permute-start.3
  109.4 3.9 %collective-permute-done.3 = f32[160,128]{1,0:T(8,128)S(1)} collective-permute-done((f32[160,128]{1,0:T(8,128)S(1)}, f32[160,128]{1,0:T(8,128)S(1)}, u32[]{:S(2)}, u32[]{:S(2)}) %collective-permute-start.3) | collective-permute-done | bytes 81952 | tf_op jit(solution)/shard_map/ppermute | solution.py:578
  113.3 0.9 broadcast_in_dim.14
  114.2 5.2 %all-to-all-start.5 = ((f32[8,160,128]{2,1,0:T(8,128)}), f32[8,160,128]{2,1,0:T(8,128)S(1)}, u32[]{:S(2)}, u32[]{:S(2)}) async-start(f32[8,160,128]{2,1,0:T(8,128)} %broadcast_in_dim.14), calls=%async_computation.5 | async-start | bytes 1310720 | tf_op jit(solution)/shard_map/all_to_all | solution.py:541
  119.4 0.0 copy-done.2
  119.4 4.4 %shard_map.63.ready = f32[512,128]{1,0:T(8,128)S(1)} custom-call(f32[256,128]{1,0:T(8,128)S(1)} %get-tuple-element.21.start), custom_call_target="tpu_custom_call" | custom-call | tf_op jit(solution)/shard_map/pallas_call | solution.py:240
  123.8 0.0 copy-start.1
  123.8 0.7 copy-done.1
  124.5 3.4 %all-to-all-done.5.following.mine_next = f32[8,160,128]{2,1,0:T(8,128)S(1)} async-done(((f32[8,160,128]{2,1,0:T(8,128)}), f32[8,160,128]{2,1,0:T(8,128)S(1)}, u32[]{:S(2)}, u32[]{:S(2)}) %all-to-all-start.5) | async-done | bytes 655392 | tf_op jit(solution)/shard_map/all_to_all | solution.py:541
  127.9 1.0 shard_map.64.keep
  129.0 0.0 copy-start
  129.0 4.1 %collective-permute-start.5 = (f32[392,128]{1,0:T(8,128)S(1)}, f32[392,128]{1,0:T(8,128)S(1)}, u32[]{:S(2)}, u32[]{:S(2)}) collective-permute-start(f32[392,128]{1,0:T(8,128)S(1)} %shard_map.64.keep), channel_id=1, source_target_pairs={{0,1},{1,0},{2,3},{3,2},{4,5},{5,4},{6,7},{7,6},{8,9},{9,8},{10,11... | collective-permute-start | bytes 602120 | tf_op jit(solution)/shard_map/ppermute | solution.py:545
  133.1 0.1 collective-permute-start.4
  133.2 1.0 collective-permute-done.5.got
  134.2 0.0 copy-start.6
  134.2 0.9 broadcast_in_dim.15
  135.1 4.2 %all-to-all-start.6 = ((f32[8,136,128]{2,1,0:T(8,128)}), f32[8,136,128]{2,1,0:T(8,128)}, u32[]{:S(2)}, u32[]{:S(2)}) async-start(f32[8,136,128]{2,1,0:T(8,128)} %broadcast_in_dim.15), calls=%async_computation.6 | async-start | bytes 1114112 | tf_op jit(solution)/shard_map/all_to_all | solution.py:541
  139.3 0.0 copy-done
  139.3 0.0 copy-done.6
  139.3 9.2 %shard_map.65.refs_0_ = f32[1920,128]{1,0:T(8,128)} custom-call(f32[256,128]{1,0:T(8,128)} %copy-done.2, f32[512,128]{1,0:T(8,128)} %copy-done.1, f32[392,128]{1,0:T(8,128)} %copy-done, f32[392,128]{1,0:T(8,128)} %copy-done.6), custom_call_target="tpu_custom_call" | custom-call | tf_op jit(solution)/shard_map/pallas_call | solution.py:586
  148.5 1.6 all-to-all-done.6.refs_1_
  150.1 8.7 %shard_map.66 = (f32[384,384]{1,0:T(8,128)S(1)}, f32[384,256]{1,0:T(8,128)}, f32[384,256]{1,0:T(8,128)}) custom-call(f32[1920,128]{1,0:T(8,128)} %shard_map.65.refs_0_, f32[8,136,128]{2,1,0:T(8,128)} %all-to-all-done.6.refs_1_), custom_call_target="tpu_custom_call" | custom-call | tf_op jit(solution)/shard_map/pallas_call | solution.py:601
  158.8 0.0 collective-permute-done.4.theirs_next
  158.8 3.9 %shard_map.67 = f32[2048,384]{1,0:T(8,128)} custom-call(s32[3]{0:T(128)S(1)} %pad_add_fusion.place, s32[128]{0:T(128)S(1)} %copy-done.5, f32[8,288,128]{2,1,0:T(8,128)S(1)} %all_to_all.36.mine, f32[8,160,128]{2,1,0:T(8,128)S(1)} %all-to-all-done.5.following.mine_next, f32[8,288,128]{2,1,0:T(8,128)S(1)} %collective-permute-done.2.theirs, ...), custom_call_target="tpu_custom_call" | custom-call | tf_op jit(solution)/shard_map/pallas_call | solution.py:525
  (4 shorter events, 0.1 us)
Async XLA Ops:
  0.7 0.7 copy-start.3
  21.3 13.0 %copy-start.4 = (s32[128]{0:T(128)S(1)}, s32[128]{0:T(128)}, u32[]{:S(2)}) copy-start(s32[128]{0:T(128)} %seeds.1) | copy-start | bytes 1540
  22.3 12.1 %all-to-all-start.1 = ((f32[8,128,128]{2,1,0:T(8,128)}), f32[8,128,128]{2,1,0:T(8,128)S(1)}, u32[]{:S(2)}, u32[]{:S(2)}) async-start(f32[8,128,128]{2,1,0:T(8,128)} %broadcast_in_dim.12), calls=%async_computation.1 | async-start | bytes 1048576 | tf_op jit(solution)/shard_map/all_to_all | solution.py:541
  25.8 8.5 %collective-permute-start = (f32[128,128]{0,1:T(8,128)S(1)}, f32[128,128]{0,1:T(8,128)S(1)}, u32[]{:S(2)}, u32[]{:S(2)}) collective-permute-start(f32[128,128]{0,1:T(8,128)S(1)} %bitcast.12), channel_id=1, source_target_pairs={{0,4},{1,5},{2,30},{3,31},{4,38},{5,39},{6,56},{7,61},{8,72},{9,73... | collective-permute-start | bytes 196616 | tf_op jit(solution)/shard_map/ppermute | solution.py:567
  39.8 7.6 %collective-permute-start.1 = (f32[8,128,128]{2,1,0:T(8,128)S(1)}, f32[8,128,128]{2,1,0:T(8,128)S(1)}, u32[]{:S(2)}, u32[]{:S(2)}) collective-permute-start(f32[8,128,128]{2,1,0:T(8,128)S(1)} %get-tuple-element.18), channel_id=1, source_target_pairs={{0,1},{1,0},{2,3},{3,2},{4,5},{5,4},{6,7},{7,6},{8,9},{9,8},{10,11... | collective-permute-start | bytes 1572872 | tf_op jit(solution)/shard_map/ppermute | solution.py:545
  48.4 15.4 %all-to-all-start.2 = ((f32[8,160,128]{2,1,0:T(8,128)}), f32[8,160,128]{2,1,0:T(8,128)S(1)}, u32[]{:S(2)}, u32[]{:S(2)}) async-start(f32[8,160,128]{2,1,0:T(8,128)} %pad_maximum_fusion), calls=%async_computation.2 | async-start | bytes 1310720 | tf_op jit(solution)/shard_map/all_to_all | solution.py:536
  63.9 20.5 %copy-start.5 = (s32[128]{0:T(128)S(1)}, s32[128]{0:T(128)}, u32[]{:S(2)}) copy-start(s32[128]{0:T(128)} %constant.19.table) | copy-start | bytes 1540
  83.0 3.9 %collective-permute-start.2 = (f32[8,288,128]{2,1,0:T(8,128)S(1)}, f32[8,288,128]{2,1,0:T(8,128)S(1)}, u32[]{:S(2)}, u32[]{:S(2)}) collective-permute-start(f32[8,288,128]{2,1,0:T(8,128)S(1)} %all_to_all.36.mine), channel_id=1, source_target_pairs={{0,1},{1,0},{2,3},{3,2},{4,5},{5,4},{6,7},{7,6},{8,9},{9,8},{10,11... | collective-permute-start | bytes 3538952 | tf_op jit(solution)/shard_map/ppermute | solution.py:545
  91.5 27.9 %copy-start.2 = (f32[256,128]{1,0:T(8,128)}, f32[256,128]{1,0:T(8,128)S(1)}, u32[]{:S(2)}) copy-start(f32[256,128]{1,0:T(8,128)S(1)} %get-tuple-element.21.start) | copy-start | bytes 393220
  108.4 4.9 %collective-permute-start.3 = (f32[160,128]{1,0:T(8,128)S(1)}, f32[160,128]{1,0:T(8,128)S(1)}, u32[]{:S(2)}, u32[]{:S(2)}) collective-permute-start(f32[160,128]{1,0:T(8,128)S(1)} %reduce_sum.29), channel_id=1, source_target_pairs={{0,4},{1,5},{2,30},{3,31},{4,38},{5,39},{6,56},{7,61},{8,72},{9,73... | collective-permute-start | bytes 245768 | tf_op jit(solution)/shard_map/ppermute | solution.py:578
  114.2 13.7 %all-to-all-start.5 = ((f32[8,160,128]{2,1,0:T(8,128)}), f32[8,160,128]{2,1,0:T(8,128)S(1)}, u32[]{:S(2)}, u32[]{:S(2)}) async-start(f32[8,160,128]{2,1,0:T(8,128)} %broadcast_in_dim.14), calls=%async_computation.5 | async-start | bytes 1310720 | tf_op jit(solution)/shard_map/all_to_all | solution.py:541
  123.8 0.7 copy-start.1
  129.0 10.3 %copy-start = (f32[392,128]{1,0:T(8,128)}, f32[392,128]{1,0:T(8,128)S(1)}, u32[]{:S(2)}) copy-start(f32[392,128]{1,0:T(8,128)S(1)} %shard_map.64.keep) | copy-start | bytes 602116
  129.0 5.2 %collective-permute-start.5 = (f32[392,128]{1,0:T(8,128)S(1)}, f32[392,128]{1,0:T(8,128)S(1)}, u32[]{:S(2)}, u32[]{:S(2)}) collective-permute-start(f32[392,128]{1,0:T(8,128)S(1)} %shard_map.64.keep), channel_id=1, source_target_pairs={{0,1},{1,0},{2,3},{3,2},{4,5},{5,4},{6,7},{7,6},{8,9},{9,8},{10,11... | collective-permute-start | bytes 602120 | tf_op jit(solution)/shard_map/ppermute | solution.py:545
  133.1 25.7 %collective-permute-start.4 = (f32[8,160,128]{2,1,0:T(8,128)S(1)}, f32[8,160,128]{2,1,0:T(8,128)}, u32[]{:S(2)}, u32[]{:S(2)}) collective-permute-start(f32[8,160,128]{2,1,0:T(8,128)S(1)} %all-to-all-done.5.following.mine_next), channel_id=1, source_target_pairs={{0,1},{1,0},{2,3},{3,2},{4,5},{5,4},{6,7},{7,6},{8,9},{9,8},{10,11... | collective-permute-start | bytes 1966088 | tf_op jit(solution)/shard_map/ppermute | solution.py:545
  134.2 5.1 %copy-start.6 = (f32[392,128]{1,0:T(8,128)}, f32[392,128]{1,0:T(8,128)S(1)}, u32[]{:S(2)}) copy-start(f32[392,128]{1,0:T(8,128)S(1)} %collective-permute-done.5.got) | copy-start | bytes 602116
  135.1 15.0 %all-to-all-start.6 = ((f32[8,136,128]{2,1,0:T(8,128)}), f32[8,136,128]{2,1,0:T(8,128)}, u32[]{:S(2)}, u32[]{:S(2)}) async-start(f32[8,136,128]{2,1,0:T(8,128)} %broadcast_in_dim.15), calls=%async_computation.6 | async-start | bytes 1114112 | tf_op jit(solution)/shard_map/all_to_all | solution.py:541

commit v9 on v8

--- a/solution.py
+++ b/solution.py
@@ -161,15 +161,14 @@
     comb = jnp.concatenate([u - nn(x0, h_full), x0])
     y = nn(gram, comb)
     upper1, li1 = factor(tn(comb, y))
-    scaled = nt(jnp.concatenate([comb, y]), li1)
-    c1, y1 = scaled[: 2 * W], scaled[2 * W :]
+    c1 = nt(comb, li1)
+    y1 = nt(y, li1)
     m01 = nn(li0, y1[:W])
     i1 = jnp.concatenate([nn(cee, c1[:W]), c1])
     s0 = nn(jnp.concatenate([side, g02], axis=1), i1)
     s1 = nn(gram[W:], i1[: 2 * W])
-    crossed = nn(jnp.concatenate([li0, c1[:W].T, i1[:W].T]), s0)
-    late = [upper1, i1[:W], i1[W : 2 * W], i1[2 * W :], m01, tn(c1, y1), crossed[:W], crossed[W : 2 * W], s1]
-    late.append(crossed[2 * W :])
+    late = [upper1, i1[:W], i1[W : 2 * W], i1[2 * W :], m01, tn(c1, y1), nn(li0, s0), tn(c1[:W], s0), s1]
+    late.append(tn(i1[:W], s0))
     for i, block in enumerate(late):
         stage[EARLY + i * W : EARLY + (i + 1) * W, :] = block
     second = pack_copy(stage, pack, sems, 1)
@@ -301,33 +300,60 @@
 CHUNKS = 8
 
 
-def chunks_of(covariance, buffer, sems):
+def hold_rows(covariance, out, sem):
+    tall = out.shape[0]
+    copy = pltpu.make_async_copy(covariance.at[pl.ds(covariance.shape[0] - tall, tall), :], out, sem)
+    copy.start()
+    copy.wait()
+
+
+def held_rows(covariance, chunks):
+    height, breadth = covariance.shape
+    return pl.pallas_call(
+        hold_rows,
+        out_shape=pltpu.VMEM((height // CHUNKS * chunks, breadth), f32),
+        in_specs=[HBM],
+        out_specs=VMEM,
+        scratch_shapes=[pltpu.SemaphoreType.DMA],
+        compiler_params=room(57),
+    )(covariance)
+
+
+def chunks_of(covariance, held, buffer, sems):
     tall = covariance.shape[0] // CHUNKS
-    return [
-        pltpu.make_async_copy(covariance.at[pl.ds(i * tall, tall), :], buffer.at[i], sems.at[i]) for i in range(CHUNKS)
+    streamed = buffer.shape[0]
+    copies = [
+        pltpu.make_async_copy(covariance.at[pl.ds(i * tall, tall), :], buffer.at[i], sems.at[i]) for i in range(streamed)
     ]
-
-
-def chunk_scratch(covariance):
+    for copy in copies:
+        copy.start()
+    chunks = [(streamed + i, lambda i=i: held[i * tall : (i + 1) * tall, :]) for i in range(CHUNKS - streamed)]
+
+    def arrived(i):
+        copies[i].wait()
+        return buffer[i]
+
+    return chunks + [(i, lambda i=i: arrived(i)) for i in range(streamed)]
+
+
+def chunk_scratch(covariance, held):
     height, breadth = covariance.shape
-    return [pltpu.VMEM((CHUNKS, height // CHUNKS, breadth), f32), pltpu.SemaphoreType.DMA((CHUNKS,))]
-
-
-def first_product(place, lanes, covariance, start, keep, send, buffer, sems):
+    streamed = CHUNKS - held.shape[0] * CHUNKS // height
+    return [pltpu.VMEM((streamed, height // CHUNKS, breadth), f32), pltpu.SemaphoreType.DMA((streamed,))]
+
+
+def first_product(place, lanes, covariance, held, start, keep, send, buffer, sems):
     height, breadth = covariance.shape
     half = height // 2
     tall = height // CHUNKS
-    copies = chunks_of(covariance, buffer, sems)
-    for copy in copies:
-        copy.start()
+    chunks = chunks_of(covariance, held, buffer, sems)
     lines = lax.broadcasted_iota(jnp.int32, (breadth, W), 0) + place[2] * breadth
     hot = jnp.where(lines == lanes[...], 1.0, 0.0)
     hit = jnp.max(hot, axis=1, keepdims=True) > 0
     weights = jnp.concatenate(halves(jnp.where(hit, 0.0, start[...])), axis=1)
     first = place[1] == 0
-    for i, copy in enumerate(copies):
-        copy.wait()
-        high, low = halves(buffer[i])
+    for i, read in chunks:
+        high, low = halves(read())
         both = mm(high, weights)
         value = both[:, :W] + both[:, W:] + mm(low, weights[:, :W])
         mine = first if i * tall < half else jnp.logical_not(first)
@@ -345,17 +371,17 @@
             store(send)
 
 
-def image_of_start(place, seeds, covariance, start):
+def image_of_start(place, seeds, covariance, held, start):
     height = covariance.shape[0]
     shape = jax.ShapeDtypeStruct((height // 2 // W, W, W), f32)
     return pl.pallas_call(
         first_product,
         out_shape=[shape, shape],
-        in_specs=[SMEM, VMEM, HBM, VMEM],
+        in_specs=[SMEM, VMEM, HBM, VMEM, VMEM],
         out_specs=[VMEM] * 2,
-        scratch_shapes=chunk_scratch(covariance),
+        scratch_shapes=chunk_scratch(covariance, held),
         compiler_params=room(50),
-    )(place, seeds.reshape(1, W), covariance, start)
+    )(place, seeds.reshape(1, W), covariance, held, start)
 
 
 def start_grams(place, lanes, start, out):
@@ -434,13 +460,11 @@
     return g12, jnp.where(j >= i, body, 0.0) + jnp.where(j > i, body, 0.0).T
 
 
-def second_product(place, covariance, mine, theirs, grams, out, small, buffer, sems, total):
+def second_product(place, covariance, held, mine, theirs, grams, out, small, buffer, sems, total):
     height, breadth = covariance.shape
     half = height // 2
     tall = height // CHUNKS
-    copies = chunks_of(covariance, buffer, sems)
-    for copy in copies:
-        copy.start()
+    chunks = chunks_of(covariance, held, buffer, sems)
     first = place[1] == 0
     parts = out.shape[0]
     bit = W // parts
@@ -450,18 +474,17 @@
     for i in range(2):
         lines = W + i * bit
         small[i * W : (i + 1) * W, :] = blocks_of(mine, lines, bit) + blocks_of(theirs, lines, bit)
-    for i, copy in enumerate(copies):
+    for i, read in chunks:
         lines = slice(i * tall % half // W, (i * tall % half + tall) // W)
         own, other = (mine, theirs) if i * tall < half else (theirs, mine)
         block = jnp.where(first, own[lines, :W, :], other[lines, :W, :]).reshape(tall, W)
         v_high, v_low = halves(block.T)
-        copy.wait()
-        high, low = halves(buffer[i])
+        high, low = halves(read())
         both = mm(jnp.concatenate([v_high, v_low]), high)
         value = both[:W] + both[W:] + mm(v_high, low)
-        if i == 0:
+        if i == chunks[0][0]:
             total[...] = value
-        elif i + 1 < CHUNKS:
+        elif i != chunks[-1][0]:
             total[...] += value
         else:
             value += total[...]
@@ -469,7 +492,7 @@
                 out[p, :W, :] = value[:, p * W : (p + 1) * W].T
 
 
-def image_of_step(place, covariance, mine, theirs, grams):
+def image_of_step(place, covariance, held, mine, theirs, grams):
     breadth = covariance.shape[1]
     parts = breadth // W
     return pl.pallas_call(
@@ -478,11 +501,11 @@
             jax.ShapeDtypeStruct((parts, W + 2 * (W // parts), W), f32),
             jax.ShapeDtypeStruct((2 * W, W), f32),
         ],
-        in_specs=[SMEM, HBM] + [VMEM] * 3,
+        in_specs=[SMEM, HBM] + [VMEM] * 4,
         out_specs=[VMEM] * 2,
-        scratch_shapes=chunk_scratch(covariance) + [pltpu.VMEM((W, breadth), f32)],
+        scratch_shapes=chunk_scratch(covariance, held) + [pltpu.VMEM((W, breadth), f32)],
         compiler_params=room(50),
-    )(place, covariance, mine, theirs, grams)
+    )(place, covariance, held, mine, theirs, grams)
 
 
 def basis_rows(place, table, mine, mine_next, theirs, theirs_next, mix, out, stage, sems):
@@ -564,17 +587,22 @@
     table = jnp.array(SLOTS, jnp.int32).reshape(-1)
     place = jnp.stack([row, core, chip * cores + core]).astype(jnp.int32)
     start_piece = scattered(picked_rows(place, seed_index, covariance, rows), ROWS).T
+    block, start_piece = lax.optimization_barrier((covariance, start_piece))
+    held = held_rows(block, 2)
     start_turned = lax.ppermute(start_piece, ALL, turn)
     start = gathered(start_piece, ROWS).reshape(breadth, width)
-    start, start_turned = lax.optimization_barrier((start, start_turned))
-    keep, send = image_of_start(place, seed_index, covariance, start)
+    start, start_turned, held = lax.optimization_barrier((start, start_turned, held))
+    keep, send = image_of_start(place, seed_index, covariance, held, start)
     got = other_core(send)
     small = grams_of_start(place, seed_index, start, chips)
     parts = jnp.concatenate([keep + got, small], axis=1)
-    mine = gathered(jnp.concatenate([scattered(parts, CHIP), start_turned]), CHIP)
+    block, parts = lax.optimization_barrier((covariance, parts))
+    held = held_rows(block, 1)
+    step, held = lax.optimization_barrier((lax.all_to_all(parts, CHIP, 0, 0, tiled=True), held))
+    mine = gathered(jnp.concatenate([jnp.sum(step, axis=0), start_turned]), CHIP)
     theirs = other_core(mine)
     (grams,) = kernel(step_grams, [(2 * width, width)], place, table, mine)
-    parts, zero_grams = image_of_step(place, covariance, mine, theirs, grams)
+    parts, zero_grams = image_of_step(place, covariance, held, mine, theirs, grams)
     piece = lax.ppermute(scattered(parts, ROWS), ALL, turn)
     (ready,) = kernel(first_factor, [(4 * width, width)], zero_grams)
     mine_next, ready = lax.optimization_barrier((gathered(piece, CHIP), ready))

time: 164 us -> 163 us (level)
  waiting for transfers between devices: 28.9 us -> 25.4 us
  Pallas kernels: 41.5 us -> 43.7 us
  local copies, waits for them, and re-layouts: 4.21 us -> 6.23 us
    pallas_call x0 -> x2, Pallas kernels: none -> 2.84 us  [held_rows(): pl.pallas_call(hold_rows, out_shape=pltpu.VMEM((height // CHUNKS * chunks...]
    all_to_all x1, waiting for transfers between devices: 11.6 us -> 9.33 us  [local(): lax.all_to_all(parts, CHIP, 0, 0, tiled=True)]
    unnamed x14 -> x22, local copies, waits for them, and re-layouts: 1.38 us -> 3.37 us
  transfers between devices with their start and end apart: 10 -> 10, of which waited for: 9 -> 9; matrix products, arithmetic and copies ran while one was open for 1% -> 1% of each run, Pallas kernels for 15% -> 17%
where the time goes in v9:
time: 163 us; the launch traced here: 162 us
  blocking collectives  52.5 us (32%)
  Pallas kernels  43.7 us (27%)
  starting transfers between devices  32.5 us (20%)
  waiting for transfers between devices  25.4 us (16%)
  local copies, waits for them, and re-layouts  6.23 us (4%)
    all_to_all x2, blocking collectives, scattered(): return jnp.sum(lax.all_to_all(parts, axis, 0, 0, tiled=True), axis=0)  33.3 us
    all_to_all x1, blocking collectives, gathered(): return lax.all_to_all(copies, axis, 0, 0, tiled=True)  19.2 us
    all_to_all x3, starting transfers between devices, gathered(): return lax.all_to_all(copies, axis, 0, 0, tiled=True)  13 us
    ppermute x4, starting transfers between devices, other_core(): return lax.ppermute(value, CORE, SWAP)  11.7 us
    all_to_all x1, waiting for transfers between devices, local(): lax.all_to_all(parts, CHIP, 0, 0, tiled=True)  9.33 us
    pallas_call x1, Pallas kernels, local(): pl.pallas_call(middle, out_shape=jax.ShapeDtypeStruct((PACK, width), f32)...  8.88 us
    pallas_call x1, Pallas kernels, local(): pl.pallas_call(last_step, out_shape=[jax.ShapeDtypeStruct(s, f32) for s i...  8.7 us
    pallas_call x3, Pallas kernels, kernel(): pl.pallas_call(body, out_shape=[jax.ShapeDtypeStruct(s, f32) for s in sha...  6.49 us
  transfers between devices with their start and end apart: 10, of which 9 were waited for; matrix products, arithmetic and copies ran while one was open for 1% of the time, Pallas kernels for 17%

profile of v9, /device:TPU:1, one launch (start us, length us, event | category | flops | bytes accessed | tf_op | source)
XLA Modules:
  0.0 162.5 jit_solution(10722101067641691922)
XLA Ops:
  0.6 0.1 pad_add_fusion.place
  0.7 0.0 copy-start.7
  0.7 0.7 copy-done.7
  1.4 2.2 %shard_map.58 = f32[8,128,128]{2,1,0:T(8,128)S(1)} custom-call(s32[3]{0:T(128)S(1)} %pad_add_fusion.place, s32[128]{0:T(128)S(1)} %copy-done.7, s32[1,128]{1,0:T(1,128)S(1)} %bitcast.8, f32[2048,1024]{1,0:T(8,128)} %covariance.7), custom_call_target="tpu_custom_call" | custom-call | tf_op jit(solution)/shard_map/pallas_call | solution.py:290
  3.6 17.6 %all_to_all.35 = f32[8,128,128]{2,1,0:T(8,128)S(1)} all-to-all(f32[8,128,128]{2,1,0:T(8,128)S(1)} %shard_map.58), channel_id=1, replica_groups=mesh['row'=8,'chip'=8,'core'=2] {'row'}, dimensions={0} | all-to-all | bytes 1048576 | tf_op jit(solution)/shard_map/all_to_all | solution.py:559
  21.3 0.1 copy.6
  21.4 0.8 broadcast_in_dim.12
  22.2 3.5 %all-to-all-start.1 = ((f32[8,128,128]{2,1,0:T(8,128)}), f32[8,128,128]{2,1,0:T(8,128)S(1)}, u32[]{:S(2)}, u32[]{:S(2)}) async-start(f32[8,128,128]{2,1,0:T(8,128)} %broadcast_in_dim.12), calls=%async_computation.1 | async-start | bytes 1048576 | tf_op jit(solution)/shard_map/all_to_all | solution.py:564
  25.7 0.0 copy-start.8
  25.7 3.0 %collective-permute-start = (f32[128,128]{0,1:T(8,128)S(1)}, f32[128,128]{0,1:T(8,128)S(1)}, u32[]{:S(2)}, u32[]{:S(2)}) collective-permute-start(f32[128,128]{0,1:T(8,128)S(1)} %bitcast.12), channel_id=1, source_target_pairs={{0,4},{1,5},{2,30},{3,31},{4,38},{5,39},{6,56},{7,61},{8,72},{9,73... | collective-permute-start | bytes 196616 | tf_op jit(solution)/shard_map/ppermute | solution.py:592
  28.7 1.6 shard_map.59.held
  30.3 3.9 %collective-permute-done = f32[128,128]{0,1:T(8,128)S(1)} collective-permute-done((f32[128,128]{0,1:T(8,128)S(1)}, f32[128,128]{0,1:T(8,128)S(1)}, u32[]{:S(2)}, u32[]{:S(2)}) %collective-permute-start) | collective-permute-done | bytes 65568 | tf_op jit(solution)/shard_map/ppermute | solution.py:592
  34.2 0.1 all-to-all-done.1
  34.3 0.0 copy-done.8
  34.3 4.5 %shard_map.60 = (f32[8,128,128]{2,1,0:T(8,128)S(1)}, f32[8,128,128]{2,1,0:T(8,128)S(1)}) custom-call(s32[3]{0:T(128)S(1)} %pad_add_fusion.place, s32[1,128]{1,0:T(1,128)S(1)} %bitcast.9, f32[2048,1024]{1,0:T(8,128)} %covariance.7, f32[512,1024]{1,0:T(8,128)S(1)} %shard_map.59.held, f32[1024,128]{1,0:T(8,128)S(1)} %bitcast.6), custom_call_target="tpu_custom_call" | custom-call | tf_op jit(solution)/shard_map/pallas_call | solution.py:377
  38.8 6.1 %collective-permute-start.1 = (f32[8,128,128]{2,1,0:T(8,128)S(1)}, f32[8,128,128]{2,1,0:T(8,128)S(1)}, u32[]{:S(2)}, u32[]{:S(2)}) collective-permute-start(f32[8,128,128]{2,1,0:T(8,128)S(1)} %get-tuple-element.28), channel_id=1, source_target_pairs={{0,1},{1,0},{2,3},{3,2},{4,5},{5,4},{6,7},{7,6},{8,9},{9,8},{10,11... | collective-permute-start | bytes 1572872 | tf_op jit(solution)/shard_map/ppermute | solution.py:568
  44.9 1.1 shard_map.61
  46.0 0.5 collective-permute-done.1
  46.4 0.1 add.10
  46.5 0.9 pad_maximum_fusion
  47.4 3.8 %all-to-all-start.2 = ((f32[8,160,128]{2,1,0:T(8,128)}), f32[8,160,128]{2,1,0:T(8,128)S(1)}, u32[]{:S(2)}, u32[]{:S(2)}) async-start(f32[8,160,128]{2,1,0:T(8,128)} %pad_maximum_fusion), calls=%async_computation.2 | async-start | bytes 1310720 | tf_op jit(solution)/shard_map/all_to_all | solution.py:601
  51.1 0.1 copy.7
  51.2 1.2 shard_map.62.held
  52.5 0.0 copy-start.2
  52.5 1.0 copy-done.2
  53.5 9.3 %all-to-all-done.2 = f32[8,160,128]{2,1,0:T(8,128)S(1)} async-done(((f32[8,160,128]{2,1,0:T(8,128)}), f32[8,160,128]{2,1,0:T(8,128)S(1)}, u32[]{:S(2)}, u32[]{:S(2)}) %all-to-all-start.2) | async-done | bytes 655392 | tf_op jit(solution)/shard_map/all_to_all | solution.py:601
  62.8 0.0 copy-start.9
  62.9 0.1 broadcast_in_dim.13
  63.0 0.0 copy-start.3
  63.0 19.2 %all_to_all.36.mine = f32[8,288,128]{2,1,0:T(8,128)S(1)} all-to-all(f32[8,288,128]{2,1,0:T(8,128)S(1)} %broadcast_in_dim.13), channel_id=1, replica_groups=mesh['row'=8,'chip'=8,'core'=2] {'chip'}, dimensions={0} | all-to-all | bytes 2359296 | tf_op jit(solution)/shard_map/all_to_all | solution.py:564
  82.2 1.4 collective-permute-start.2
  83.6 0.0 copy-done.9
  83.6 1.1 shard_map.63.grams
  84.7 1.4 collective-permute-done.2.theirs
  86.1 0.0 copy-start
  86.1 1.0 copy-done
  87.1 0.0 copy-done.3
  87.1 5.0 %shard_map.64 = (f32[8,160,128]{2,1,0:T(8,128)S(1)}, f32[256,128]{1,0:T(8,128)S(1)}) custom-call(s32[3]{0:T(128)S(1)} %pad_add_fusion.place, f32[2048,1024]{1,0:T(8,128)} %covariance.7, f32[256,1024]{1,0:T(8,128)S(1)} %copy-done.3, f32[8,288,128]{2,1,0:T(8,128)S(1)} %all_to_all.36.mine, f32[8,288,128]{2,1,0:T(8,128)} %copy-done, f32[256,128]{1,0:T(8,128)S(1)} %shard_map.63.grams), custom_call_target="tpu_custom_call" | custom-call | tf_op jit(solution)/shard_map/pallas_call | solution.py:498
  92.1 0.0 copy-start.6
  92.1 15.7 %all_to_all.37 = f32[8,160,128]{2,1,0:T(8,128)S(1)} all-to-all(f32[8,160,128]{2,1,0:T(8,128)S(1)} %get-tuple-element.34), channel_id=1, replica_groups=mesh['row'=8,'chip'=8,'core'=2] {'row'}, dimensions={0} | all-to-all | bytes 1310720 | tf_op jit(solution)/shard_map/all_to_all | solution.py:559
  107.8 1.0 collective-permute-start.3
  108.8 3.9 %collective-permute-done.3 = f32[160,128]{1,0:T(8,128)S(1)} collective-permute-done((f32[160,128]{1,0:T(8,128)S(1)}, f32[160,128]{1,0:T(8,128)S(1)}, u32[]{:S(2)}, u32[]{:S(2)}) %collective-permute-start.3) | collective-permute-done | bytes 81952 | tf_op jit(solution)/shard_map/ppermute | solution.py:606
  112.7 0.9 broadcast_in_dim.14
  113.6 5.2 %all-to-all-start.5 = ((f32[8,160,128]{2,1,0:T(8,128)}), f32[8,160,128]{2,1,0:T(8,128)S(1)}, u32[]{:S(2)}, u32[]{:S(2)}) async-start(f32[8,160,128]{2,1,0:T(8,128)} %broadcast_in_dim.14), calls=%async_computation.5 | async-start | bytes 1310720 | tf_op jit(solution)/shard_map/all_to_all | solution.py:564
  118.8 4.4 %shard_map.65.ready = f32[512,128]{1,0:T(8,128)S(1)} custom-call(f32[256,128]{1,0:T(8,128)S(1)} %get-tuple-element.35.start), custom_call_target="tpu_custom_call" | custom-call | tf_op jit(solution)/shard_map/pallas_call | solution.py:239
  123.2 0.0 copy-done.6
  123.2 0.0 copy-start.5
  123.2 0.7 copy-done.5
  123.9 3.4 %all-to-all-done.5.following.mine_next = f32[8,160,128]{2,1,0:T(8,128)S(1)} async-done(((f32[8,160,128]{2,1,0:T(8,128)}), f32[8,160,128]{2,1,0:T(8,128)S(1)}, u32[]{:S(2)}, u32[]{:S(2)}) %all-to-all-start.5) | async-done | bytes 655392 | tf_op jit(solution)/shard_map/all_to_all | solution.py:564
  127.4 1.0 shard_map.66.keep
  128.4 0.0 copy-start.4
  128.4 4.1 %collective-permute-start.5 = (f32[392,128]{1,0:T(8,128)S(1)}, f32[392,128]{1,0:T(8,128)S(1)}, u32[]{:S(2)}, u32[]{:S(2)}) collective-permute-start(f32[392,128]{1,0:T(8,128)S(1)} %shard_map.66.keep), channel_id=1, source_target_pairs={{0,1},{1,0},{2,3},{3,2},{4,5},{5,4},{6,7},{7,6},{8,9},{9,8},{10,11... | collective-permute-start | bytes 602120 | tf_op jit(solution)/shard_map/ppermute | solution.py:568
  132.5 0.1 collective-permute-start.4
  132.6 1.0 collective-permute-done.5.got
  133.6 0.9 broadcast_in_dim.15
  134.5 4.3 %all-to-all-start.6 = ((f32[8,136,128]{2,1,0:T(8,128)}), f32[8,136,128]{2,1,0:T(8,128)}, u32[]{:S(2)}, u32[]{:S(2)}) async-start(f32[8,136,128]{2,1,0:T(8,128)} %broadcast_in_dim.15), calls=%async_computation.6 | async-start | bytes 1114112 | tf_op jit(solution)/shard_map/all_to_all | solution.py:564
  138.8 0.0 copy-done.4
  138.9 0.0 copy-done.10
  138.9 8.9 %shard_map.67.refs_0_ = f32[1920,128]{1,0:T(8,128)} custom-call(f32[256,128]{1,0:T(8,128)} %copy-done.6, f32[512,128]{1,0:T(8,128)} %copy-done.5, f32[392,128]{1,0:T(8,128)} %copy-done.4, f32[392,128]{1,0:T(8,128)} %copy-done.10), custom_call_target="tpu_custom_call" | custom-call | tf_op jit(solution)/shard_map/pallas_call | solution.py:614
  147.8 1.9 %all-to-all-done.6.refs_1_ = f32[8,136,128]{2,1,0:T(8,128)} async-done(((f32[8,136,128]{2,1,0:T(8,128)}), f32[8,136,128]{2,1,0:T(8,128)}, u32[]{:S(2)}, u32[]{:S(2)}) %all-to-all-start.6) | async-done | bytes 557088 | tf_op jit(solution)/shard_map/all_to_all | solution.py:564
  149.7 8.7 %shard_map.68 = (f32[384,384]{1,0:T(8,128)S(1)}, f32[384,256]{1,0:T(8,128)}, f32[384,256]{1,0:T(8,128)}) custom-call(f32[1920,128]{1,0:T(8,128)} %shard_map.67.refs_0_, f32[8,136,128]{2,1,0:T(8,128)} %all-to-all-done.6.refs_1_), custom_call_target="tpu_custom_call" | custom-call | tf_op jit(solution)/shard_map/pallas_call | solution.py:629
  158.4 0.0 collective-permute-done.4.theirs_next
  158.4 0.0 copy-done.1
  158.4 3.9 %shard_map.69 = f32[2048,384]{1,0:T(8,128)} custom-call(s32[3]{0:T(128)S(1)} %pad_add_fusion.place, s32[128]{0:T(128)S(1)} %copy-done.9, f32[8,288,128]{2,1,0:T(8,128)S(1)} %all_to_all.36.mine, f32[8,160,128]{2,1,0:T(8,128)S(1)} %all-to-all-done.5.following.mine_next, f32[8,288,128]{2,1,0:T(8,128)S(1)} %copy-done.1, ...), custom_call_target="tpu_custom_call" | custom-call | tf_op jit(solution)/shard_map/pallas_call | solution.py:548
  (7 shorter events, 0.1 us)
Async XLA Ops:
  0.7 0.7 copy-start.7
  22.2 12.1 %all-to-all-start.1 = ((f32[8,128,128]{2,1,0:T(8,128)}), f32[8,128,128]{2,1,0:T(8,128)S(1)}, u32[]{:S(2)}, u32[]{:S(2)}) async-start(f32[8,128,128]{2,1,0:T(8,128)} %broadcast_in_dim.12), calls=%async_computation.1 | async-start | bytes 1048576 | tf_op jit(solution)/shard_map/all_to_all | solution.py:564
  25.7 8.6 %copy-start.8 = (s32[128]{0:T(128)S(1)}, s32[128]{0:T(128)}, u32[]{:S(2)}) copy-start(s32[128]{0:T(128)} %seeds.1) | copy-start | bytes 1540
  25.7 8.5 %collective-permute-start = (f32[128,128]{0,1:T(8,128)S(1)}, f32[128,128]{0,1:T(8,128)S(1)}, u32[]{:S(2)}, u32[]{:S(2)}) collective-permute-start(f32[128,128]{0,1:T(8,128)S(1)} %bitcast.12), channel_id=1, source_target_pairs={{0,4},{1,5},{2,30},{3,31},{4,38},{5,39},{6,56},{7,61},{8,72},{9,73... | collective-permute-start | bytes 196616 | tf_op jit(solution)/shard_map/ppermute | solution.py:592
  38.8 7.6 %collective-permute-start.1 = (f32[8,128,128]{2,1,0:T(8,128)S(1)}, f32[8,128,128]{2,1,0:T(8,128)S(1)}, u32[]{:S(2)}, u32[]{:S(2)}) collective-permute-start(f32[8,128,128]{2,1,0:T(8,128)S(1)} %get-tuple-element.28), channel_id=1, source_target_pairs={{0,1},{1,0},{2,3},{3,2},{4,5},{5,4},{6,7},{7,6},{8,9},{9,8},{10,11... | collective-permute-start | bytes 1572872 | tf_op jit(solution)/shard_map/ppermute | solution.py:568
  47.4 15.4 %all-to-all-start.2 = ((f32[8,160,128]{2,1,0:T(8,128)}), f32[8,160,128]{2,1,0:T(8,128)S(1)}, u32[]{:S(2)}, u32[]{:S(2)}) async-start(f32[8,160,128]{2,1,0:T(8,128)} %pad_maximum_fusion), calls=%async_computation.2 | async-start | bytes 1310720 | tf_op jit(solution)/shard_map/all_to_all | solution.py:601
  52.5 1.0 copy-start.2
  62.8 20.8 %copy-start.9 = (s32[128]{0:T(128)S(1)}, s32[128]{0:T(128)}, u32[]{:S(2)}) copy-start(s32[128]{0:T(128)} %constant.19.table) | copy-start | bytes 1540
  63.0 24.1 %copy-start.3 = (f32[256,1024]{1,0:T(8,128)S(1)}, f32[256,1024]{1,0:T(8,128)}, u32[]{:S(2)}) copy-start(f32[256,1024]{1,0:T(8,128)} %copy-done.2) | copy-start | bytes 3145732
  82.2 3.9 %collective-permute-start.2 = (f32[8,288,128]{2,1,0:T(8,128)S(1)}, f32[8,288,128]{2,1,0:T(8,128)S(1)}, u32[]{:S(2)}, u32[]{:S(2)}) collective-permute-start(f32[8,288,128]{2,1,0:T(8,128)S(1)} %all_to_all.36.mine), channel_id=1, source_target_pairs={{0,1},{1,0},{2,3},{3,2},{4,5},{5,4},{6,7},{7,6},{8,9},{9,8},{10,11... | collective-permute-start | bytes 3538952 | tf_op jit(solution)/shard_map/ppermute | solution.py:568
  86.1 1.0 copy-start
  92.1 31.2 %copy-start.6 = (f32[256,128]{1,0:T(8,128)}, f32[256,128]{1,0:T(8,128)S(1)}, u32[]{:S(2)}) copy-start(f32[256,128]{1,0:T(8,128)S(1)} %get-tuple-element.35.start) | copy-start | bytes 393220
  107.8 4.9 %collective-permute-start.3 = (f32[160,128]{1,0:T(8,128)S(1)}, f32[160,128]{1,0:T(8,128)S(1)}, u32[]{:S(2)}, u32[]{:S(2)}) collective-permute-start(f32[160,128]{1,0:T(8,128)S(1)} %reduce_sum.29), channel_id=1, source_target_pairs={{0,4},{1,5},{2,30},{3,31},{4,38},{5,39},{6,56},{7,61},{8,72},{9,73... | collective-permute-start | bytes 245768 | tf_op jit(solution)/shard_map/ppermute | solution.py:606
  113.6 13.7 %all-to-all-start.5 = ((f32[8,160,128]{2,1,0:T(8,128)}), f32[8,160,128]{2,1,0:T(8,128)S(1)}, u32[]{:S(2)}, u32[]{:S(2)}) async-start(f32[8,160,128]{2,1,0:T(8,128)} %broadcast_in_dim.14), calls=%async_computation.5 | async-start | bytes 1310720 | tf_op jit(solution)/shard_map/all_to_all | solution.py:564
  123.2 0.7 copy-start.5
  128.4 10.4 %copy-start.4 = (f32[392,128]{1,0:T(8,128)}, f32[392,128]{1,0:T(8,128)S(1)}, u32[]{:S(2)}) copy-start(f32[392,128]{1,0:T(8,128)S(1)} %shard_map.66.keep) | copy-start | bytes 602116
  128.4 5.2 %collective-permute-start.5 = (f32[392,128]{1,0:T(8,128)S(1)}, f32[392,128]{1,0:T(8,128)S(1)}, u32[]{:S(2)}, u32[]{:S(2)}) collective-permute-start(f32[392,128]{1,0:T(8,128)S(1)} %shard_map.66.keep), channel_id=1, source_target_pairs={{0,1},{1,0},{2,3},{3,2},{4,5},{5,4},{6,7},{7,6},{8,9},{9,8},{10,11... | collective-permute-start | bytes 602120 | tf_op jit(solution)/shard_map/ppermute | solution.py:568
  132.5 25.8 %collective-permute-start.4 = (f32[8,160,128]{2,1,0:T(8,128)S(1)}, f32[8,160,128]{2,1,0:T(8,128)}, u32[]{:S(2)}, u32[]{:S(2)}) collective-permute-start(f32[8,160,128]{2,1,0:T(8,128)S(1)} %all-to-all-done.5.following.mine_next), channel_id=1, source_target_pairs={{0,1},{1,0},{2,3},{3,2},{4,5},{5,4},{6,7},{7,6},{8,9},{9,8},{10,11... | collective-permute-start | bytes 1966088 | tf_op jit(solution)/shard_map/ppermute | solution.py:568
  133.6 5.2 %copy-start.10 = (f32[392,128]{1,0:T(8,128)}, f32[392,128]{1,0:T(8,128)S(1)}, u32[]{:S(2)}) copy-start(f32[392,128]{1,0:T(8,128)S(1)} %collective-permute-done.5.got) | copy-start | bytes 602116
  134.5 23.9 %copy-start.1 = (f32[8,288,128]{2,1,0:T(8,128)S(1)}, f32[8,288,128]{2,1,0:T(8,128)}, u32[]{:S(2)}) copy-start(f32[8,288,128]{2,1,0:T(8,128)} %copy-done) | copy-start | bytes 3538948
  134.5 15.2 %all-to-all-start.6 = ((f32[8,136,128]{2,1,0:T(8,128)}), f32[8,136,128]{2,1,0:T(8,128)}, u32[]{:S(2)}, u32[]{:S(2)}) async-start(f32[8,136,128]{2,1,0:T(8,128)} %broadcast_in_dim.15), calls=%async_computation.6 | async-start | bytes 1114112 | tf_op jit(solution)/shard_map/all_to_all | solution.py:564

commit v10 on v9

--- a/solution.py
+++ b/solution.py
@@ -338,7 +338,7 @@
 
 def chunk_scratch(covariance, held):
     height, breadth = covariance.shape
-    streamed = CHUNKS - held.shape[0] * CHUNKS // height
+    streamed = CHUNKS - held * CHUNKS // height
     return [pltpu.VMEM((streamed, height // CHUNKS, breadth), f32), pltpu.SemaphoreType.DMA((streamed,))]
 
 
@@ -379,7 +379,7 @@
         out_shape=[shape, shape],
         in_specs=[SMEM, VMEM, HBM, VMEM, VMEM],
         out_specs=[VMEM] * 2,
-        scratch_shapes=chunk_scratch(covariance, held),
+        scratch_shapes=chunk_scratch(covariance, held.shape[0]),
         compiler_params=room(50),
     )(place, seeds.reshape(1, W), covariance, held, start)
 
@@ -419,6 +419,10 @@
     return both[:, :W] + both[:, W:] + mm(low, right[0])
 
 
+def fold(parts, out):
+    out[...] = jnp.sum(parts[...], axis=0)
+
+
 def step_grams(place, table, mine, out):
     parts = mine.shape[0]
     step = blocks_of(mine, 0, W)
@@ -460,11 +464,11 @@
     return g12, jnp.where(j >= i, body, 0.0) + jnp.where(j > i, body, 0.0).T
 
 
-def second_product(place, covariance, held, mine, theirs, grams, out, small, buffer, sems, total):
+def second_product(place, covariance, mine, theirs, grams, out, small, buffer, sems, total):
     height, breadth = covariance.shape
     half = height // 2
     tall = height // CHUNKS
-    chunks = chunks_of(covariance, held, buffer, sems)
+    chunks = chunks_of(covariance, None, buffer, sems)
     first = place[1] == 0
     parts = out.shape[0]
     bit = W // parts
@@ -492,7 +496,7 @@
                 out[p, :W, :] = value[:, p * W : (p + 1) * W].T
 
 
-def image_of_step(place, covariance, held, mine, theirs, grams):
+def image_of_step(place, covariance, mine, theirs, grams):
     breadth = covariance.shape[1]
     parts = breadth // W
     return pl.pallas_call(
@@ -501,11 +505,11 @@
             jax.ShapeDtypeStruct((parts, W + 2 * (W // parts), W), f32),
             jax.ShapeDtypeStruct((2 * W, W), f32),
         ],
-        in_specs=[SMEM, HBM] + [VMEM] * 4,
+        in_specs=[SMEM, HBM] + [VMEM] * 3,
         out_specs=[VMEM] * 2,
-        scratch_shapes=chunk_scratch(covariance, held) + [pltpu.VMEM((W, breadth), f32)],
+        scratch_shapes=chunk_scratch(covariance, 0) + [pltpu.VMEM((W, breadth), f32)],
         compiler_params=room(50),
-    )(place, covariance, held, mine, theirs, grams)
+    )(place, covariance, mine, theirs, grams)
 
 
 def basis_rows(place, table, mine, mine_next, theirs, theirs_next, mix, out, stage, sems):
@@ -596,14 +600,12 @@
     got = other_core(send)
     small = grams_of_start(place, seed_index, start, chips)
     parts = jnp.concatenate([keep + got, small], axis=1)
-    block, parts = lax.optimization_barrier((covariance, parts))
-    held = held_rows(block, 1)
-    step, held = lax.optimization_barrier((lax.all_to_all(parts, CHIP, 0, 0, tiled=True), held))
-    mine = gathered(jnp.concatenate([jnp.sum(step, axis=0), start_turned]), CHIP)
+    mine = gathered(jnp.concatenate([scattered(parts, CHIP), start_turned]), CHIP)
     theirs = other_core(mine)
     (grams,) = kernel(step_grams, [(2 * width, width)], place, table, mine)
-    parts, zero_grams = image_of_step(place, covariance, held, mine, theirs, grams)
-    piece = lax.ppermute(scattered(parts, ROWS), ALL, turn)
+    parts, zero_grams = image_of_step(place, covariance, mine, theirs, grams)
+    (piece,) = kernel(fold, [parts.shape[1:]], lax.all_to_all(parts, ROWS, 0, 0, tiled=True))
+    piece = lax.ppermute(piece, ALL, turn)
     (ready,) = kernel(first_factor, [(4 * width, width)], zero_grams)
     mine_next, ready = lax.optimization_barrier((gathered(piece, CHIP), ready))
     (keep,) = kernel(next_grams, [(3 * width + SPARE, width)], place, table, mine, mine_next)

time: 163 us -> 161 us (0.988)
  waiting for transfers between devices: 25.4 us -> 27.6 us
  local copies, waits for them, and re-layouts: 6.23 us -> 4.22 us
  Pallas kernels: 43.7 us -> 42 us
    all_to_all x0 -> x1, blocking collectives: none -> 15.7 us  [local(): lax.all_to_all(parts, ROWS, 0, 0, tiled=True)]
    all_to_all x2 -> x1, blocking collectives: 33.3 us -> 17.6 us  [scattered(): return jnp.sum(lax.all_to_all(parts, axis, 0, 0, tiled=True), axis=0)]
    all_to_all x1, waiting for transfers between devices: 9.33 us -> 11.6 us  [scattered(): return jnp.sum(lax.all_to_all(parts, axis, 0, 0, tiled=True), axis=0)]
    unnamed x22 -> x14, local copies, waits for them, and re-layouts: 3.37 us -> 1.38 us
    pallas_call x3 -> x4, Pallas kernels: 6.49 us -> 6.53 us  [kernel(): pl.pallas_call(body, out_shape=[jax.ShapeDtypeStruct(s, f32) for s in sha...]
  transfers between devices with their start and end apart: 10 -> 10, of which waited for: 9 -> 9; matrix products, arithmetic and copies ran while one was open for 1% -> 1% of each run, Pallas kernels for 17% -> 16%
where the time goes in v10:
time: 161 us
  blocking collectives  52.4 us (33%)
  Pallas kernels  42 us (26%)
  starting transfers between devices  32.4 us (20%)
  waiting for transfers between devices  27.6 us (17%)
  local copies, waits for them, and re-layouts  4.22 us (3%)
    all_to_all x1, blocking collectives, gathered(): return lax.all_to_all(copies, axis, 0, 0, tiled=True)  19 us
    all_to_all x1, blocking collectives, scattered(): return jnp.sum(lax.all_to_all(parts, axis, 0, 0, tiled=True), axis=0)  17.6 us
    all_to_all x1, blocking collectives, local(): lax.all_to_all(parts, ROWS, 0, 0, tiled=True)  15.7 us
    all_to_all x3, starting transfers between devices, gathered(): return lax.all_to_all(copies, axis, 0, 0, tiled=True)  12.9 us
    ppermute x4, starting transfers between devices, other_core(): return lax.ppermute(value, CORE, SWAP)  11.7 us
    all_to_all x1, waiting for transfers between devices, scattered(): return jnp.sum(lax.all_to_all(parts, axis, 0, 0, tiled=True), axis=0)  11.6 us
    pallas_call x1, Pallas kernels, local(): pl.pallas_call(middle, out_shape=jax.ShapeDtypeStruct((PACK, width), f32)...  8.84 us
    pallas_call x1, Pallas kernels, local(): pl.pallas_call(last_step, out_shape=[jax.ShapeDtypeStruct(s, f32) for s i...  8.7 us
  transfers between devices with their start and end apart: 10, of which 9 were waited for; matrix products, arithmetic and copies ran while one was open for 1% of the time, Pallas kernels for 16%

profile of v10, /device:TPU:1, one launch (start us, length us, event | category | flops | bytes accessed | tf_op | source)
XLA Modules:
  0.0 160.7 jit_solution(446300523959473433)
XLA Ops:
  0.6 0.1 pad_add_fusion.place
  0.7 0.0 copy-start.3
  0.7 0.7 copy-done.3
  1.4 2.2 %shard_map.58 = f32[8,128,128]{2,1,0:T(8,128)S(1)} custom-call(s32[3]{0:T(128)S(1)} %pad_add_fusion.place, s32[128]{0:T(128)S(1)} %copy-done.3, s32[1,128]{1,0:T(1,128)S(1)} %bitcast.8, f32[2048,1024]{1,0:T(8,128)} %covariance.6), custom_call_target="tpu_custom_call" | custom-call | tf_op jit(solution)/shard_map/pallas_call | solution.py:290
  3.6 17.6 %all_to_all.35 = f32[8,128,128]{2,1,0:T(8,128)S(1)} all-to-all(f32[8,128,128]{2,1,0:T(8,128)S(1)} %shard_map.58), channel_id=1, replica_groups=mesh['row'=8,'chip'=8,'core'=2] {'row'}, dimensions={0} | all-to-all | bytes 1048576 | tf_op jit(solution)/shard_map/all_to_all | solution.py:563
  21.3 0.1 copy.6
  21.3 0.8 broadcast_in_dim.12
  22.2 3.5 %all-to-all-start.1 = ((f32[8,128,128]{2,1,0:T(8,128)}), f32[8,128,128]{2,1,0:T(8,128)S(1)}, u32[]{:S(2)}, u32[]{:S(2)}) async-start(f32[8,128,128]{2,1,0:T(8,128)} %broadcast_in_dim.12), calls=%async_computation.1 | async-start | bytes 1048576 | tf_op jit(solution)/shard_map/all_to_all | solution.py:568
  25.7 0.0 copy-start.4
  25.7 3.0 %collective-permute-start = (f32[128,128]{0,1:T(8,128)S(1)}, f32[128,128]{0,1:T(8,128)S(1)}, u32[]{:S(2)}, u32[]{:S(2)}) collective-permute-start(f32[128,128]{0,1:T(8,128)S(1)} %bitcast.12), channel_id=1, source_target_pairs={{0,4},{1,5},{2,30},{3,31},{4,38},{5,39},{6,56},{7,61},{8,72},{9,73... | collective-permute-start | bytes 196616 | tf_op jit(solution)/shard_map/ppermute | solution.py:596
  28.7 1.6 shard_map.59.held
  30.3 3.9 %collective-permute-done = f32[128,128]{0,1:T(8,128)S(1)} collective-permute-done((f32[128,128]{0,1:T(8,128)S(1)}, f32[128,128]{0,1:T(8,128)S(1)}, u32[]{:S(2)}, u32[]{:S(2)}) %collective-permute-start) | collective-permute-done | bytes 65568 | tf_op jit(solution)/shard_map/ppermute | solution.py:596
  34.2 0.1 all-to-all-done.1
  34.3 0.0 copy-done.4
  34.3 4.5 %shard_map.60 = (f32[8,128,128]{2,1,0:T(8,128)S(1)}, f32[8,128,128]{2,1,0:T(8,128)S(1)}) custom-call(s32[3]{0:T(128)S(1)} %pad_add_fusion.place, s32[1,128]{1,0:T(1,128)S(1)} %bitcast.9, f32[2048,1024]{1,0:T(8,128)} %covariance.6, f32[512,1024]{1,0:T(8,128)S(1)} %shard_map.59.held, f32[1024,128]{1,0:T(8,128)S(1)} %bitcast.6), custom_call_target="tpu_custom_call" | custom-call | tf_op jit(solution)/shard_map/pallas_call | solution.py:377
  38.8 6.1 %collective-permute-start.1 = (f32[8,128,128]{2,1,0:T(8,128)S(1)}, f32[8,128,128]{2,1,0:T(8,128)S(1)}, u32[]{:S(2)}, u32[]{:S(2)}) collective-permute-start(f32[8,128,128]{2,1,0:T(8,128)S(1)} %get-tuple-element.24), channel_id=1, source_target_pairs={{0,1},{1,0},{2,3},{3,2},{4,5},{5,4},{6,7},{7,6},{8,9},{9,8},{10,11... | collective-permute-start | bytes 1572872 | tf_op jit(solution)/shard_map/ppermute | solution.py:572
  44.9 1.1 shard_map.61
  45.9 0.5 collective-permute-done.1
  46.4 0.1 add.10
  46.5 0.9 pad_maximum_fusion
  47.4 3.8 %all-to-all-start.2 = ((f32[8,160,128]{2,1,0:T(8,128)}), f32[8,160,128]{2,1,0:T(8,128)S(1)}, u32[]{:S(2)}, u32[]{:S(2)}) async-start(f32[8,160,128]{2,1,0:T(8,128)} %pad_maximum_fusion), calls=%async_computation.2 | async-start | bytes 1310720 | tf_op jit(solution)/shard_map/all_to_all | solution.py:563
  51.1 0.1 copy.7
  51.2 11.6 %all-to-all-done.2 = f32[8,160,128]{2,1,0:T(8,128)S(1)} async-done(((f32[8,160,128]{2,1,0:T(8,128)}), f32[8,160,128]{2,1,0:T(8,128)S(1)}, u32[]{:S(2)}, u32[]{:S(2)}) %all-to-all-start.2) | async-done | bytes 655392 | tf_op jit(solution)/shard_map/all_to_all | solution.py:563
  62.8 0.0 copy-start.5
  62.9 0.1 broadcast_in_dim.13
  62.9 19.0 %all_to_all.36.mine = f32[8,288,128]{2,1,0:T(8,128)S(1)} all-to-all(f32[8,288,128]{2,1,0:T(8,128)S(1)} %broadcast_in_dim.13), channel_id=1, replica_groups=mesh['row'=8,'chip'=8,'core'=2] {'chip'}, dimensions={0} | all-to-all | bytes 2359296 | tf_op jit(solution)/shard_map/all_to_all | solution.py:568
  82.0 1.4 collective-permute-start.2
  83.4 0.0 copy-done.5
  83.4 1.1 shard_map.62.grams
  84.5 1.4 collective-permute-done.2.theirs
  85.9 4.5 %shard_map.63 = (f32[8,160,128]{2,1,0:T(8,128)S(1)}, f32[256,128]{1,0:T(8,128)S(1)}) custom-call(s32[3]{0:T(128)S(1)} %pad_add_fusion.place, f32[2048,1024]{1,0:T(8,128)} %covariance.6, f32[8,288,128]{2,1,0:T(8,128)S(1)} %all_to_all.36.mine, f32[8,288,128]{2,1,0:T(8,128)S(1)} %collective-permute-done.2.theirs, f32[256,128]{1,0:T(8,128)S(1)} %shard_map.62.grams), custom_call_target="tpu_custom_call" | custom-call | tf_op jit(solution)/shard_map/pallas_call | solution.py:502
  90.4 0.0 copy-start.2
  90.5 15.7 %all_to_all.37.parts = f32[8,160,128]{2,1,0:T(8,128)S(1)} all-to-all(f32[8,160,128]{2,1,0:T(8,128)S(1)} %get-tuple-element.26), channel_id=1, replica_groups=mesh['row'=8,'chip'=8,'core'=2] {'row'}, dimensions={0} | all-to-all | bytes 1310720 | tf_op jit(solution)/shard_map/all_to_all | solution.py:607
  106.2 1.0 collective-permute-start.3
  107.2 3.9 %collective-permute-done.3 = f32[160,128]{1,0:T(8,128)S(1)} collective-permute-done((f32[160,128]{1,0:T(8,128)S(1)}, f32[160,128]{1,0:T(8,128)S(1)}, u32[]{:S(2)}, u32[]{:S(2)}) %collective-permute-start.3) | collective-permute-done | bytes 81952 | tf_op jit(solution)/shard_map/ppermute | solution.py:608
  111.1 0.9 broadcast_in_dim.14
  112.0 5.2 %all-to-all-start.5 = ((f32[8,160,128]{2,1,0:T(8,128)}), f32[8,160,128]{2,1,0:T(8,128)S(1)}, u32[]{:S(2)}, u32[]{:S(2)}) async-start(f32[8,160,128]{2,1,0:T(8,128)} %broadcast_in_dim.14), calls=%async_computation.5 | async-start | bytes 1310720 | tf_op jit(solution)/shard_map/all_to_all | solution.py:568
  117.2 4.4 %shard_map.65.ready = f32[512,128]{1,0:T(8,128)S(1)} custom-call(f32[256,128]{1,0:T(8,128)S(1)} %get-tuple-element.27.start), custom_call_target="tpu_custom_call" | custom-call | tf_op jit(solution)/shard_map/pallas_call | solution.py:239
  121.6 0.0 copy-done.2
  121.6 0.0 copy-start.1
  121.6 0.7 copy-done.1
  122.3 3.4 %all-to-all-done.5.following.mine_next = f32[8,160,128]{2,1,0:T(8,128)S(1)} async-done(((f32[8,160,128]{2,1,0:T(8,128)}), f32[8,160,128]{2,1,0:T(8,128)S(1)}, u32[]{:S(2)}, u32[]{:S(2)}) %all-to-all-start.5) | async-done | bytes 655392 | tf_op jit(solution)/shard_map/all_to_all | solution.py:568
  125.7 1.0 shard_map.66.keep
  126.8 0.0 copy-start
  126.8 4.1 %collective-permute-start.5 = (f32[392,128]{1,0:T(8,128)S(1)}, f32[392,128]{1,0:T(8,128)S(1)}, u32[]{:S(2)}, u32[]{:S(2)}) collective-permute-start(f32[392,128]{1,0:T(8,128)S(1)} %shard_map.66.keep), channel_id=1, source_target_pairs={{0,1},{1,0},{2,3},{3,2},{4,5},{5,4},{6,7},{7,6},{8,9},{9,8},{10,11... | collective-permute-start | bytes 602120 | tf_op jit(solution)/shard_map/ppermute | solution.py:572
  130.9 0.1 collective-permute-start.4
  131.0 1.0 collective-permute-done.5.got
  132.0 0.0 copy-start.6
  132.0 0.9 broadcast_in_dim.15
  132.9 4.2 %all-to-all-start.6 = ((f32[8,136,128]{2,1,0:T(8,128)}), f32[8,136,128]{2,1,0:T(8,128)}, u32[]{:S(2)}, u32[]{:S(2)}) async-start(f32[8,136,128]{2,1,0:T(8,128)} %broadcast_in_dim.15), calls=%async_computation.6 | async-start | bytes 1114112 | tf_op jit(solution)/shard_map/all_to_all | solution.py:568
  137.0 0.0 copy-done
  137.1 0.0 copy-done.6
  137.1 8.8 %shard_map.67.refs_0_ = f32[1920,128]{1,0:T(8,128)} custom-call(f32[256,128]{1,0:T(8,128)} %copy-done.2, f32[512,128]{1,0:T(8,128)} %copy-done.1, f32[392,128]{1,0:T(8,128)} %copy-done, f32[392,128]{1,0:T(8,128)} %copy-done.6), custom_call_target="tpu_custom_call" | custom-call | tf_op jit(solution)/shard_map/pallas_call | solution.py:616
  145.9 1.9 %all-to-all-done.6.refs_1_ = f32[8,136,128]{2,1,0:T(8,128)} async-done(((f32[8,136,128]{2,1,0:T(8,128)}), f32[8,136,128]{2,1,0:T(8,128)}, u32[]{:S(2)}, u32[]{:S(2)}) %all-to-all-start.6) | async-done | bytes 557088 | tf_op jit(solution)/shard_map/all_to_all | solution.py:568
  147.9 8.7 %shard_map.68 = (f32[384,384]{1,0:T(8,128)S(1)}, f32[384,256]{1,0:T(8,128)}, f32[384,256]{1,0:T(8,128)}) custom-call(f32[1920,128]{1,0:T(8,128)} %shard_map.67.refs_0_, f32[8,136,128]{2,1,0:T(8,128)} %all-to-all-done.6.refs_1_), custom_call_target="tpu_custom_call" | custom-call | tf_op jit(solution)/shard_map/pallas_call | solution.py:631
  156.6 0.0 collective-permute-done.4.theirs_next
  156.6 3.9 %shard_map.69 = f32[2048,384]{1,0:T(8,128)} custom-call(s32[3]{0:T(128)S(1)} %pad_add_fusion.place, s32[128]{0:T(128)S(1)} %copy-done.5, f32[8,288,128]{2,1,0:T(8,128)S(1)} %all_to_all.36.mine, f32[8,160,128]{2,1,0:T(8,128)S(1)} %all-to-all-done.5.following.mine_next, f32[8,288,128]{2,1,0:T(8,128)S(1)} %collective-permute-done.2.theirs, ...), custom_call_target="tpu_custom_call" | custom-call | tf_op jit(solution)/shard_map/pallas_call | solution.py:552
  (5 shorter events, 0.1 us)
Async XLA Ops:
  0.7 0.7 copy-start.3
  22.2 12.1 %all-to-all-start.1 = ((f32[8,128,128]{2,1,0:T(8,128)}), f32[8,128,128]{2,1,0:T(8,128)S(1)}, u32[]{:S(2)}, u32[]{:S(2)}) async-start(f32[8,128,128]{2,1,0:T(8,128)} %broadcast_in_dim.12), calls=%async_computation.1 | async-start | bytes 1048576 | tf_op jit(solution)/shard_map/all_to_all | solution.py:568
  25.7 8.6 %copy-start.4 = (s32[128]{0:T(128)S(1)}, s32[128]{0:T(128)}, u32[]{:S(2)}) copy-start(s32[128]{0:T(128)} %seeds.1) | copy-start | bytes 1540
  25.7 8.5 %collective-permute-start = (f32[128,128]{0,1:T(8,128)S(1)}, f32[128,128]{0,1:T(8,128)S(1)}, u32[]{:S(2)}, u32[]{:S(2)}) collective-permute-start(f32[128,128]{0,1:T(8,128)S(1)} %bitcast.12), channel_id=1, source_target_pairs={{0,4},{1,5},{2,30},{3,31},{4,38},{5,39},{6,56},{7,61},{8,72},{9,73... | collective-permute-start | bytes 196616 | tf_op jit(solution)/shard_map/ppermute | solution.py:596
  38.8 7.6 %collective-permute-start.1 = (f32[8,128,128]{2,1,0:T(8,128)S(1)}, f32[8,128,128]{2,1,0:T(8,128)S(1)}, u32[]{:S(2)}, u32[]{:S(2)}) collective-permute-start(f32[8,128,128]{2,1,0:T(8,128)S(1)} %get-tuple-element.24), channel_id=1, source_target_pairs={{0,1},{1,0},{2,3},{3,2},{4,5},{5,4},{6,7},{7,6},{8,9},{9,8},{10,11... | collective-permute-start | bytes 1572872 | tf_op jit(solution)/shard_map/ppermute | solution.py:572
  47.4 15.4 %all-to-all-start.2 = ((f32[8,160,128]{2,1,0:T(8,128)}), f32[8,160,128]{2,1,0:T(8,128)S(1)}, u32[]{:S(2)}, u32[]{:S(2)}) async-start(f32[8,160,128]{2,1,0:T(8,128)} %pad_maximum_fusion), calls=%async_computation.2 | async-start | bytes 1310720 | tf_op jit(solution)/shard_map/all_to_all | solution.py:563
  62.8 20.6 %copy-start.5 = (s32[128]{0:T(128)S(1)}, s32[128]{0:T(128)}, u32[]{:S(2)}) copy-start(s32[128]{0:T(128)} %constant.19.table) | copy-start | bytes 1540
  82.0 3.9 %collective-permute-start.2 = (f32[8,288,128]{2,1,0:T(8,128)S(1)}, f32[8,288,128]{2,1,0:T(8,128)S(1)}, u32[]{:S(2)}, u32[]{:S(2)}) collective-permute-start(f32[8,288,128]{2,1,0:T(8,128)S(1)} %all_to_all.36.mine), channel_id=1, source_target_pairs={{0,1},{1,0},{2,3},{3,2},{4,5},{5,4},{6,7},{7,6},{8,9},{9,8},{10,11... | collective-permute-start | bytes 3538952 | tf_op jit(solution)/shard_map/ppermute | solution.py:572
  90.4 31.2 %copy-start.2 = (f32[256,128]{1,0:T(8,128)}, f32[256,128]{1,0:T(8,128)S(1)}, u32[]{:S(2)}) copy-start(f32[256,128]{1,0:T(8,128)S(1)} %get-tuple-element.27.start) | copy-start | bytes 393220
  106.2 4.9 %collective-permute-start.3 = (f32[160,128]{1,0:T(8,128)S(1)}, f32[160,128]{1,0:T(8,128)S(1)}, u32[]{:S(2)}, u32[]{:S(2)}) collective-permute-start(f32[160,128]{1,0:T(8,128)S(1)} %shard_map.64), channel_id=1, source_target_pairs={{0,4},{1,5},{2,30},{3,31},{4,38},{5,39},{6,56},{7,61},{8,72},{9,73... | collective-permute-start | bytes 245768 | tf_op jit(solution)/shard_map/ppermute | solution.py:608
  112.0 13.7 %all-to-all-start.5 = ((f32[8,160,128]{2,1,0:T(8,128)}), f32[8,160,128]{2,1,0:T(8,128)S(1)}, u32[]{:S(2)}, u32[]{:S(2)}) async-start(f32[8,160,128]{2,1,0:T(8,128)} %broadcast_in_dim.14), calls=%async_computation.5 | async-start | bytes 1310720 | tf_op jit(solution)/shard_map/all_to_all | solution.py:568
  121.6 0.7 copy-start.1
  126.8 10.3 %copy-start = (f32[392,128]{1,0:T(8,128)}, f32[392,128]{1,0:T(8,128)S(1)}, u32[]{:S(2)}) copy-start(f32[392,128]{1,0:T(8,128)S(1)} %shard_map.66.keep) | copy-start | bytes 602116
  126.8 5.2 %collective-permute-start.5 = (f32[392,128]{1,0:T(8,128)S(1)}, f32[392,128]{1,0:T(8,128)S(1)}, u32[]{:S(2)}, u32[]{:S(2)}) collective-permute-start(f32[392,128]{1,0:T(8,128)S(1)} %shard_map.66.keep), channel_id=1, source_target_pairs={{0,1},{1,0},{2,3},{3,2},{4,5},{5,4},{6,7},{7,6},{8,9},{9,8},{10,11... | collective-permute-start | bytes 602120 | tf_op jit(solution)/shard_map/ppermute | solution.py:572
  130.9 25.7 %collective-permute-start.4 = (f32[8,160,128]{2,1,0:T(8,128)S(1)}, f32[8,160,128]{2,1,0:T(8,128)}, u32[]{:S(2)}, u32[]{:S(2)}) collective-permute-start(f32[8,160,128]{2,1,0:T(8,128)S(1)} %all-to-all-done.5.following.mine_next), channel_id=1, source_target_pairs={{0,1},{1,0},{2,3},{3,2},{4,5},{5,4},{6,7},{7,6},{8,9},{9,8},{10,11... | collective-permute-start | bytes 1966088 | tf_op jit(solution)/shard_map/ppermute | solution.py:572
  132.0 5.1 %copy-start.6 = (f32[392,128]{1,0:T(8,128)}, f32[392,128]{1,0:T(8,128)S(1)}, u32[]{:S(2)}) copy-start(f32[392,128]{1,0:T(8,128)S(1)} %collective-permute-done.5.got) | copy-start | bytes 602116
  132.9 15.0 %all-to-all-start.6 = ((f32[8,136,128]{2,1,0:T(8,128)}), f32[8,136,128]{2,1,0:T(8,128)}, u32[]{:S(2)}, u32[]{:S(2)}) async-start(f32[8,136,128]{2,1,0:T(8,128)} %broadcast_in_dim.15), calls=%async_computation.6 | async-start | bytes 1114112 | tf_op jit(solution)/shard_map/all_to_all | solution.py:568

commit v11 on v10

--- a/solution.py
+++ b/solution.py
@@ -423,6 +423,10 @@
     out[...] = jnp.sum(parts[...], axis=0)
 
 
+def fold_turned(parts, out):
+    out[...] = jnp.sum(parts[...], axis=0).T
+
+
 def step_grams(place, table, mine, out):
     parts = mine.shape[0]
     step = blocks_of(mine, 0, W)
@@ -512,7 +516,11 @@
     )(place, covariance, mine, theirs, grams)
 
 
-def basis_rows(place, table, mine, mine_next, theirs, theirs_next, mix, out, stage, sems):
+def basis_rows(place, table, mine, mine_next, theirs, theirs_next, mix, *refs):
+    small_in, (out, *small_out), (stage, sems, small_sems) = refs[:2], refs[2:5], refs[5:]
+    copies = [pltpu.make_async_copy(a, b, small_sems.at[i]) for i, (a, b) in enumerate(zip(small_in, small_out))]
+    for copy in copies:
+        copy.start()
     parts = mine.shape[0]
     bit = 2 * W // parts
     count, tall, _ = stage.shape
@@ -520,7 +528,6 @@
     high, low = halves(mix[: 2 * W, : 2 * W])
     tip_high, tip_low = halves(mix[:, 2 * W :])
     tip = jnp.concatenate([tip_high, tip_low], axis=1)
-    copies = []
     for i in range(count):
         line = i * tall % half
         pair, following, side = (mine, mine_next, place[1]) if i * tall < half else (theirs, theirs_next, 1 - place[1])
@@ -545,18 +552,22 @@
         copy.wait()
 
 
-def basis_of(place, table, mine, mine_next, theirs, theirs_next, mix):
+def basis_of(place, table, mine, mine_next, theirs, theirs_next, mix, *small):
     height = 2 * mine.shape[0] * W
     tall = 256
     breadth = mix.shape[1]
     return pl.pallas_call(
         basis_rows,
-        out_shape=jax.ShapeDtypeStruct((height, breadth), f32),
-        in_specs=[SMEM] * 2 + [VMEM] * 5,
-        out_specs=HBM,
-        scratch_shapes=[pltpu.VMEM((height // tall, tall, breadth), f32), pltpu.SemaphoreType.DMA((height // tall,))],
+        out_shape=[jax.ShapeDtypeStruct(s, f32) for s in ((height, breadth), *(a.shape for a in small))],
+        in_specs=[SMEM] * 2 + [VMEM] * 7,
+        out_specs=[HBM] * 3,
+        scratch_shapes=[
+            pltpu.VMEM((height // tall, tall, breadth), f32),
+            pltpu.SemaphoreType.DMA((height // tall,)),
+            pltpu.SemaphoreType.DMA((2,)),
+        ],
         compiler_params=room(24),
-    )(place, table, mine, mine_next, theirs, theirs_next, mix)
+    )(place, table, mine, mine_next, theirs, theirs_next, mix, *small)
 
 
 def scattered(parts, axis):
@@ -590,7 +601,8 @@
     turn = turned(rows, chips, cores)
     table = jnp.array(SLOTS, jnp.int32).reshape(-1)
     place = jnp.stack([row, core, chip * cores + core]).astype(jnp.int32)
-    start_piece = scattered(picked_rows(place, seed_index, covariance, rows), ROWS).T
+    picked = picked_rows(place, seed_index, covariance, rows)
+    (start_piece,) = kernel(fold_turned, [(breadth // rows, width)], lax.all_to_all(picked, ROWS, 0, 0, tiled=True))
     block, start_piece = lax.optimization_barrier((covariance, start_piece))
     held = held_rows(block, 2)
     start_turned = lax.ppermute(start_piece, ALL, turn)
@@ -636,8 +648,7 @@
         scratch_shapes=stage + [pltpu.VMEM(totals.shape, f32), pltpu.SemaphoreType.DMA],
         compiler_params=room(52),
     )(pack, totals)
-    basis = basis_of(place, table, mine, mine_next, theirs, theirs_next, mix)
-    return basis, projection, first_pass
+    return tuple(basis_of(place, table, mine, mine_next, theirs, theirs_next, mix, projection, first_pass))
 
 
 def solution(mesh):

time: 161 us -> 159 us (0.988)
  blocking collectives: 52.4 us -> 66.2 us
  waiting for transfers between devices: 27.6 us -> 16.2 us
  starting transfers between devices: 32.4 us -> 29.6 us
    all_to_all x0 -> x1, blocking collectives: none -> 17.7 us  [local(): lax.all_to_all(picked, ROWS, 0, 0, tiled=True)]
    all_to_all x1 -> x0, waiting for transfers between devices: 11.6 us -> none  [scattered(): return jnp.sum(lax.all_to_all(parts, axis, 0, 0, tiled=True), axis=0)]
    all_to_all x1 -> x0, starting transfers between devices: 3.77 us -> none  [scattered(): return jnp.sum(lax.all_to_all(parts, axis, 0, 0, tiled=True), axis=0)]
    all_to_all x1, blocking collectives: 17.6 us -> 14.8 us  [scattered(): return jnp.sum(lax.all_to_all(parts, axis, 0, 0, tiled=True), axis=0)]
    pallas_call x4 -> x5, Pallas kernels: 6.53 us -> 6.62 us  [kernel(): pl.pallas_call(body, out_shape=[jax.ShapeDtypeStruct(s, f32) for s in sha...]
  transfers between devices with their start and end apart: 10 -> 9, of which waited for: 9 -> 8; matrix products, arithmetic and copies ran while one was open for 1% -> 1% of each run, Pallas kernels for 16% -> 16%
where the time goes in v11:
time: 159 us
  blocking collectives  66.2 us (42%)
  Pallas kernels  41.5 us (26%)
  starting transfers between devices  29.6 us (19%)
  waiting for transfers between devices  16.2 us (10%)
  local copies, waits for them, and re-layouts  4.04 us (3%)
    all_to_all x1, blocking collectives, gathered(): return lax.all_to_all(copies, axis, 0, 0, tiled=True)  17.9 us
    all_to_all x1, blocking collectives, local(): lax.all_to_all(picked, ROWS, 0, 0, tiled=True)  17.7 us
    all_to_all x1, blocking collectives, local(): lax.all_to_all(parts, ROWS, 0, 0, tiled=True)  15.7 us
    all_to_all x1, blocking collectives, scattered(): return jnp.sum(lax.all_to_all(parts, axis, 0, 0, tiled=True), axis=0)  14.8 us
    all_to_all x3, starting transfers between devices, gathered(): return lax.all_to_all(copies, axis, 0, 0, tiled=True)  13 us
    ppermute x4, starting transfers between devices, other_core(): return lax.ppermute(value, CORE, SWAP)  12.8 us
    pallas_call x1, Pallas kernels, local(): pl.pallas_call(middle, out_shape=jax.ShapeDtypeStruct((PACK, width), f32)...  8.84 us
    pallas_call x1, Pallas kernels, local(): pl.pallas_call(last_step, out_shape=[jax.ShapeDtypeStruct(s, f32) for s i...  7.99 us
  transfers between devices with their start and end apart: 9, of which 8 were waited for; matrix products, arithmetic and copies ran while one was open for 1% of the time, Pallas kernels for 16%

profile of v11, /device:TPU:1, one launch (start us, length us, event | category | flops | bytes accessed | tf_op | source)
XLA Modules:
  0.0 158.8 jit_solution(5508442738817553315)
XLA Ops:
  0.6 0.1 pad_add_fusion.place
  0.7 0.0 copy-start.3
  0.7 0.7 copy-done.3
  1.4 2.2 %shard_map.58 = f32[8,128,128]{2,1,0:T(8,128)S(1)} custom-call(s32[3]{0:T(128)S(1)} %pad_add_fusion.place, s32[128]{0:T(128)S(1)} %copy-done.3, s32[1,128]{1,0:T(1,128)S(1)} %bitcast.7, f32[2048,1024]{1,0:T(8,128)} %covariance.6), custom_call_target="tpu_custom_call" | custom-call | tf_op jit(solution)/shard_map/pallas_call | solution.py:290
  3.6 17.7 %all_to_all.35.parts = f32[8,128,128]{2,1,0:T(8,128)S(1)} all-to-all(f32[8,128,128]{2,1,0:T(8,128)S(1)} %shard_map.58), channel_id=1, replica_groups=mesh['row'=8,'chip'=8,'core'=2] {'row'}, dimensions={0} | all-to-all | bytes 1048576 | tf_op jit(solution)/shard_map/all_to_all | solution.py:605
  21.3 0.1 shard_map.59
  21.4 0.8 broadcast_in_dim.12
  22.2 3.5 %all-to-all-start.1 = ((f32[8,128,128]{2,1,0:T(8,128)}), f32[8,128,128]{2,1,0:T(8,128)S(1)}, u32[]{:S(2)}, u32[]{:S(2)}) async-start(f32[8,128,128]{2,1,0:T(8,128)} %broadcast_in_dim.12), calls=%async_computation.1 | async-start | bytes 1048576 | tf_op jit(solution)/shard_map/all_to_all | solution.py:579
  25.7 0.0 copy-start.4
  25.7 3.0 %collective-permute-start = (f32[128,128]{1,0:T(8,128)S(1)}, f32[128,128]{1,0:T(8,128)S(1)}, u32[]{:S(2)}, u32[]{:S(2)}) collective-permute-start(f32[128,128]{1,0:T(8,128)S(1)} %shard_map.59), channel_id=1, source_target_pairs={{0,4},{1,5},{2,30},{3,31},{4,38},{5,39},{6,56},{7,61},{8,72},{9,73... | collective-permute-start | bytes 196616 | tf_op jit(solution)/shard_map/ppermute | solution.py:608
  28.7 1.6 %shard_map.60.held = f32[512,1024]{1,0:T(8,128)S(1)} custom-call(f32[2048,1024]{1,0:T(8,128)} %covariance.6), custom_call_target="tpu_custom_call" | custom-call | tf_op jit(solution)/shard_map/pallas_call | solution.py:312
  30.3 3.9 %collective-permute-done = f32[128,128]{1,0:T(8,128)S(1)} collective-permute-done((f32[128,128]{1,0:T(8,128)S(1)}, f32[128,128]{1,0:T(8,128)S(1)}, u32[]{:S(2)}, u32[]{:S(2)}) %collective-permute-start) | collective-permute-done | bytes 65568 | tf_op jit(solution)/shard_map/ppermute | solution.py:608
  34.2 0.1 all-to-all-done.1
  34.3 0.0 copy-done.4
  34.3 4.5 %shard_map.61 = (f32[8,128,128]{2,1,0:T(8,128)S(1)}, f32[8,128,128]{2,1,0:T(8,128)S(1)}) custom-call(s32[3]{0:T(128)S(1)} %pad_add_fusion.place, s32[1,128]{1,0:T(1,128)S(1)} %bitcast.8, f32[2048,1024]{1,0:T(8,128)} %covariance.6, f32[512,1024]{1,0:T(8,128)S(1)} %shard_map.60.held, f32[1024,128]{1,0:T(8,128)S(1)} %bitcast.5), custom_call_target="tpu_custom_call" | custom-call | tf_op jit(solution)/shard_map/pallas_call | solution.py:377
  38.9 6.1 %collective-permute-start.1 = (f32[8,128,128]{2,1,0:T(8,128)S(1)}, f32[8,128,128]{2,1,0:T(8,128)S(1)}, u32[]{:S(2)}, u32[]{:S(2)}) collective-permute-start(f32[8,128,128]{2,1,0:T(8,128)S(1)} %get-tuple-element.24), channel_id=1, source_target_pairs={{0,1},{1,0},{2,3},{3,2},{4,5},{5,4},{6,7},{7,6},{8,9},{9,8},{10,11... | collective-permute-start | bytes 1572872 | tf_op jit(solution)/shard_map/ppermute | solution.py:583
  44.9 1.1 shard_map.62
  46.0 0.5 collective-permute-done.1
  46.5 0.1 add.10
  46.6 14.8 %all_to_all.36 = f32[8,160,128]{2,1,0:T(8,128)S(1)} all-to-all(f32[8,160,128]{2,1,0:T(8,128)S(1)} %pad_maximum_fusion), channel_id=1, replica_groups=mesh['row'=8,'chip'=8,'core'=2] {'chip'}, dimensions={0} | all-to-all | bytes 1310720 | tf_op jit(solution)/shard_map/all_to_all | solution.py:574
  61.5 0.0 copy-start.5
  61.5 0.1 broadcast_in_dim.13
  61.6 17.9 %all_to_all.37.mine = f32[8,288,128]{2,1,0:T(8,128)S(1)} all-to-all(f32[8,288,128]{2,1,0:T(8,128)S(1)} %broadcast_in_dim.13), channel_id=1, replica_groups=mesh['row'=8,'chip'=8,'core'=2] {'chip'}, dimensions={0} | all-to-all | bytes 2359296 | tf_op jit(solution)/shard_map/all_to_all | solution.py:579
  79.5 2.6 %collective-permute-start.2 = (f32[8,288,128]{2,1,0:T(8,128)S(1)}, f32[8,288,128]{2,1,0:T(8,128)S(1)}, u32[]{:S(2)}, u32[]{:S(2)}) collective-permute-start(f32[8,288,128]{2,1,0:T(8,128)S(1)} %all_to_all.37.mine), channel_id=1, source_target_pairs={{0,1},{1,0},{2,3},{3,2},{4,5},{5,4},{6,7},{7,6},{8,9},{9,8},{10,11... | collective-permute-start | bytes 3538952 | tf_op jit(solution)/shard_map/ppermute | solution.py:583
  82.1 0.0 copy-done.5
  82.1 1.1 shard_map.63.grams
  83.1 1.4 collective-permute-done.2.theirs
  84.5 4.5 %shard_map.64 = (f32[8,160,128]{2,1,0:T(8,128)S(1)}, f32[256,128]{1,0:T(8,128)S(1)}) custom-call(s32[3]{0:T(128)S(1)} %pad_add_fusion.place, f32[2048,1024]{1,0:T(8,128)} %covariance.6, f32[8,288,128]{2,1,0:T(8,128)S(1)} %all_to_all.37.mine, f32[8,288,128]{2,1,0:T(8,128)S(1)} %collective-permute-done.2.theirs, f32[256,128]{1,0:T(8,128)S(1)} %shard_map.63.grams), custom_call_target="tpu_custom_call" | custom-call | tf_op jit(solution)/shard_map/pallas_call | solution.py:506
  89.1 0.0 copy-start.2
  89.1 15.7 %all_to_all.38.parts = f32[8,160,128]{2,1,0:T(8,128)S(1)} all-to-all(f32[8,160,128]{2,1,0:T(8,128)S(1)} %get-tuple-element.26), channel_id=1, replica_groups=mesh['row'=8,'chip'=8,'core'=2] {'row'}, dimensions={0} | all-to-all | bytes 1310720 | tf_op jit(solution)/shard_map/all_to_all | solution.py:619
  104.8 0.9 collective-permute-start.3
  105.7 4.0 %collective-permute-done.3 = f32[160,128]{1,0:T(8,128)S(1)} collective-permute-done((f32[160,128]{1,0:T(8,128)S(1)}, f32[160,128]{1,0:T(8,128)S(1)}, u32[]{:S(2)}, u32[]{:S(2)}) %collective-permute-start.3) | collective-permute-done | bytes 81952 | tf_op jit(solution)/shard_map/ppermute | solution.py:620
  109.7 0.9 broadcast_in_dim.14
  110.6 5.3 %all-to-all-start.5 = ((f32[8,160,128]{2,1,0:T(8,128)}), f32[8,160,128]{2,1,0:T(8,128)S(1)}, u32[]{:S(2)}, u32[]{:S(2)}) async-start(f32[8,160,128]{2,1,0:T(8,128)} %broadcast_in_dim.14), calls=%async_computation.5 | async-start | bytes 1310720 | tf_op jit(solution)/shard_map/all_to_all | solution.py:579
  115.9 4.4 %shard_map.66.ready = f32[512,128]{1,0:T(8,128)S(1)} custom-call(f32[256,128]{1,0:T(8,128)S(1)} %get-tuple-element.27.start), custom_call_target="tpu_custom_call" | custom-call | tf_op jit(solution)/shard_map/pallas_call | solution.py:239
  120.3 0.0 copy-done.2
  120.3 0.0 copy-start.1
  120.3 0.7 copy-done.1
  121.0 3.4 %all-to-all-done.5.following.mine_next = f32[8,160,128]{2,1,0:T(8,128)S(1)} async-done(((f32[8,160,128]{2,1,0:T(8,128)}), f32[8,160,128]{2,1,0:T(8,128)S(1)}, u32[]{:S(2)}, u32[]{:S(2)}) %all-to-all-start.5) | async-done | bytes 655392 | tf_op jit(solution)/shard_map/all_to_all | solution.py:579
  124.4 1.0 shard_map.67.keep
  125.5 0.0 copy-start
  125.5 4.0 %collective-permute-start.5 = (f32[392,128]{1,0:T(8,128)S(1)}, f32[392,128]{1,0:T(8,128)S(1)}, u32[]{:S(2)}, u32[]{:S(2)}) collective-permute-start(f32[392,128]{1,0:T(8,128)S(1)} %shard_map.67.keep), channel_id=1, source_target_pairs={{0,1},{1,0},{2,3},{3,2},{4,5},{5,4},{6,7},{7,6},{8,9},{9,8},{10,11... | collective-permute-start | bytes 602120 | tf_op jit(solution)/shard_map/ppermute | solution.py:583
  129.5 0.1 collective-permute-start.4
  129.6 1.0 collective-permute-done.5.got
  130.6 0.0 copy-start.6
  130.6 0.9 broadcast_in_dim.15
  131.5 4.2 %all-to-all-start.6 = ((f32[8,136,128]{2,1,0:T(8,128)}), f32[8,136,128]{2,1,0:T(8,128)}, u32[]{:S(2)}, u32[]{:S(2)}) async-start(f32[8,136,128]{2,1,0:T(8,128)} %broadcast_in_dim.15), calls=%async_computation.6 | async-start | bytes 1114112 | tf_op jit(solution)/shard_map/all_to_all | solution.py:579
  135.7 0.0 copy-done
  135.7 0.0 copy-done.6
  135.7 8.8 %shard_map.68.refs_0_ = f32[1920,128]{1,0:T(8,128)} custom-call(f32[256,128]{1,0:T(8,128)} %copy-done.2, f32[512,128]{1,0:T(8,128)} %copy-done.1, f32[392,128]{1,0:T(8,128)} %copy-done, f32[392,128]{1,0:T(8,128)} %copy-done.6), custom_call_target="tpu_custom_call" | custom-call | tf_op jit(solution)/shard_map/pallas_call | solution.py:628
  144.5 1.9 %all-to-all-done.6.refs_1_ = f32[8,136,128]{2,1,0:T(8,128)} async-done(((f32[8,136,128]{2,1,0:T(8,128)}), f32[8,136,128]{2,1,0:T(8,128)}, u32[]{:S(2)}, u32[]{:S(2)}) %all-to-all-start.6) | async-done | bytes 557088 | tf_op jit(solution)/shard_map/all_to_all | solution.py:579
  146.5 8.0 %shard_map.69 = (f32[384,384]{1,0:T(8,128)S(1)}, f32[384,256]{1,0:T(8,128)S(1)}, f32[384,256]{1,0:T(8,128)S(1)}) custom-call(f32[1920,128]{1,0:T(8,128)} %shard_map.68.refs_0_, f32[8,136,128]{2,1,0:T(8,128)} %all-to-all-done.6.refs_1_), custom_call_target="tpu_custom_call" | custom-call | tf_op jit(solution)/shard_map/pallas_call | solution.py:643
  154.5 0.0 collective-permute-done.4.theirs_next
  154.5 4.1 %shard_map.70 = (f32[2048,384]{1,0:T(8,128)}, f32[384,256]{1,0:T(8,128)}, f32[384,256]{1,0:T(8,128)}) custom-call(s32[3]{0:T(128)S(1)} %pad_add_fusion.place, s32[128]{0:T(128)S(1)} %copy-done.5, f32[8,288,128]{2,1,0:T(8,128)S(1)} %all_to_all.37.mine, f32[8,160,128]{2,1,0:T(8,128)S(1)} %all-to-all-done.5.following.mine_next, ...), custom_call_target="tpu_custom_call" | custom-call | tf_op jit(solution)/shard_map/pallas_call | solution.py:559
  (5 shorter events, 0.1 us)
Async XLA Ops:
  0.7 0.7 copy-start.3
  22.2 12.1 %all-to-all-start.1 = ((f32[8,128,128]{2,1,0:T(8,128)}), f32[8,128,128]{2,1,0:T(8,128)S(1)}, u32[]{:S(2)}, u32[]{:S(2)}) async-start(f32[8,128,128]{2,1,0:T(8,128)} %broadcast_in_dim.12), calls=%async_computation.1 | async-start | bytes 1048576 | tf_op jit(solution)/shard_map/all_to_all | solution.py:579
  25.7 8.6 %copy-start.4 = (s32[128]{0:T(128)S(1)}, s32[128]{0:T(128)}, u32[]{:S(2)}) copy-start(s32[128]{0:T(128)} %seeds.1) | copy-start | bytes 1540
  25.7 8.5 %collective-permute-start = (f32[128,128]{1,0:T(8,128)S(1)}, f32[128,128]{1,0:T(8,128)S(1)}, u32[]{:S(2)}, u32[]{:S(2)}) collective-permute-start(f32[128,128]{1,0:T(8,128)S(1)} %shard_map.59), channel_id=1, source_target_pairs={{0,4},{1,5},{2,30},{3,31},{4,38},{5,39},{6,56},{7,61},{8,72},{9,73... | collective-permute-start | bytes 196616 | tf_op jit(solution)/shard_map/ppermute | solution.py:608
  38.9 7.6 %collective-permute-start.1 = (f32[8,128,128]{2,1,0:T(8,128)S(1)}, f32[8,128,128]{2,1,0:T(8,128)S(1)}, u32[]{:S(2)}, u32[]{:S(2)}) collective-permute-start(f32[8,128,128]{2,1,0:T(8,128)S(1)} %get-tuple-element.24), channel_id=1, source_target_pairs={{0,1},{1,0},{2,3},{3,2},{4,5},{5,4},{6,7},{7,6},{8,9},{9,8},{10,11... | collective-permute-start | bytes 1572872 | tf_op jit(solution)/shard_map/ppermute | solution.py:583
  61.5 20.6 %copy-start.5 = (s32[128]{0:T(128)S(1)}, s32[128]{0:T(128)}, u32[]{:S(2)}) copy-start(s32[128]{0:T(128)} %constant.19.table) | copy-start | bytes 1540
  79.5 5.1 %collective-permute-start.2 = (f32[8,288,128]{2,1,0:T(8,128)S(1)}, f32[8,288,128]{2,1,0:T(8,128)S(1)}, u32[]{:S(2)}, u32[]{:S(2)}) collective-permute-start(f32[8,288,128]{2,1,0:T(8,128)S(1)} %all_to_all.37.mine), channel_id=1, source_target_pairs={{0,1},{1,0},{2,3},{3,2},{4,5},{5,4},{6,7},{7,6},{8,9},{9,8},{10,11... | collective-permute-start | bytes 3538952 | tf_op jit(solution)/shard_map/ppermute | solution.py:583
  89.1 31.2 %copy-start.2 = (f32[256,128]{1,0:T(8,128)}, f32[256,128]{1,0:T(8,128)S(1)}, u32[]{:S(2)}) copy-start(f32[256,128]{1,0:T(8,128)S(1)} %get-tuple-element.27.start) | copy-start | bytes 393220
  104.8 4.9 %collective-permute-start.3 = (f32[160,128]{1,0:T(8,128)S(1)}, f32[160,128]{1,0:T(8,128)S(1)}, u32[]{:S(2)}, u32[]{:S(2)}) collective-permute-start(f32[160,128]{1,0:T(8,128)S(1)} %shard_map.65), channel_id=1, source_target_pairs={{0,4},{1,5},{2,30},{3,31},{4,38},{5,39},{6,56},{7,61},{8,72},{9,73... | collective-permute-start | bytes 245768 | tf_op jit(solution)/shard_map/ppermute | solution.py:620
  110.6 13.8 %all-to-all-start.5 = ((f32[8,160,128]{2,1,0:T(8,128)}), f32[8,160,128]{2,1,0:T(8,128)S(1)}, u32[]{:S(2)}, u32[]{:S(2)}) async-start(f32[8,160,128]{2,1,0:T(8,128)} %broadcast_in_dim.14), calls=%async_computation.5 | async-start | bytes 1310720 | tf_op jit(solution)/shard_map/all_to_all | solution.py:579
  120.3 0.7 copy-start.1
  125.5 10.2 %copy-start = (f32[392,128]{1,0:T(8,128)}, f32[392,128]{1,0:T(8,128)S(1)}, u32[]{:S(2)}) copy-start(f32[392,128]{1,0:T(8,128)S(1)} %shard_map.67.keep) | copy-start | bytes 602116
  125.5 5.1 %collective-permute-start.5 = (f32[392,128]{1,0:T(8,128)S(1)}, f32[392,128]{1,0:T(8,128)S(1)}, u32[]{:S(2)}, u32[]{:S(2)}) collective-permute-start(f32[392,128]{1,0:T(8,128)S(1)} %shard_map.67.keep), channel_id=1, source_target_pairs={{0,1},{1,0},{2,3},{3,2},{4,5},{5,4},{6,7},{7,6},{8,9},{9,8},{10,11... | collective-permute-start | bytes 602120 | tf_op jit(solution)/shard_map/ppermute | solution.py:583
  129.5 25.0 %collective-permute-start.4 = (f32[8,160,128]{2,1,0:T(8,128)S(1)}, f32[8,160,128]{2,1,0:T(8,128)}, u32[]{:S(2)}, u32[]{:S(2)}) collective-permute-start(f32[8,160,128]{2,1,0:T(8,128)S(1)} %all-to-all-done.5.following.mine_next), channel_id=1, source_target_pairs={{0,1},{1,0},{2,3},{3,2},{4,5},{5,4},{6,7},{7,6},{8,9},{9,8},{10,11... | collective-permute-start | bytes 1966088 | tf_op jit(solution)/shard_map/ppermute | solution.py:583
  130.6 5.1 %copy-start.6 = (f32[392,128]{1,0:T(8,128)}, f32[392,128]{1,0:T(8,128)S(1)}, u32[]{:S(2)}) copy-start(f32[392,128]{1,0:T(8,128)S(1)} %collective-permute-done.5.got) | copy-start | bytes 602116
  131.5 15.0 %all-to-all-start.6 = ((f32[8,136,128]{2,1,0:T(8,128)}), f32[8,136,128]{2,1,0:T(8,128)}, u32[]{:S(2)}, u32[]{:S(2)}) async-start(f32[8,136,128]{2,1,0:T(8,128)} %broadcast_in_dim.15), calls=%async_computation.6 | async-start | bytes 1114112 | tf_op jit(solution)/shard_map/all_to_all | solution.py:579

commit v12 on v11

--- a/solution.py
+++ b/solution.py
@@ -196,7 +196,7 @@
     a12, a22 = unpacked(parts[...])
     for copy in copies:
         copy.wait()
-    first, full, m00, a02, li0, upper1, _, c1_top, c1_low, m01, m11, first0, part1, s1, square = (
+    first, full, m00, a02, li0, upper1, _, _, c1_low, m01, m11, first0, part1, s1, square = (
         pack[i * W : (i + 1) * W, :] for i in range(PACK // W)
     )
     i1 = pack[EARLY + W : EARLY + 4 * W, :]
@@ -469,7 +469,7 @@
 
 
 def second_product(place, covariance, mine, theirs, grams, out, small, buffer, sems, total):
-    height, breadth = covariance.shape
+    height, _ = covariance.shape
     half = height // 2
     tall = height // CHUNKS
     chunks = chunks_of(covariance, None, buffer, sems)
@@ -605,11 +605,12 @@
     (start_piece,) = kernel(fold_turned, [(breadth // rows, width)], lax.all_to_all(picked, ROWS, 0, 0, tiled=True))
     block, start_piece = lax.optimization_barrier((covariance, start_piece))
     held = held_rows(block, 2)
+    start = gathered(start_piece, ROWS).reshape(breadth, width)
+    start, held = lax.optimization_barrier((start, held))
+    keep, send = image_of_start(place, seed_index, covariance, held, start)
+    send, start_piece = lax.optimization_barrier((send, start_piece))
+    got = other_core(send)
     start_turned = lax.ppermute(start_piece, ALL, turn)
-    start = gathered(start_piece, ROWS).reshape(breadth, width)
-    start, start_turned, held = lax.optimization_barrier((start, start_turned, held))
-    keep, send = image_of_start(place, seed_index, covariance, held, start)
-    got = other_core(send)
     small = grams_of_start(place, seed_index, start, chips)
     parts = jnp.concatenate([keep + got, small], axis=1)
     mine = gathered(jnp.concatenate([scattered(parts, CHIP), start_turned]), CHIP)
@@ -654,6 +655,7 @@
 def solution(mesh):
     rows, cols = mesh.devices.shape
     fine = Mesh(mesh.devices.reshape(rows, cols // 2, 2), ALL)
+
     return jax.shard_map(
         local,
         mesh=fine,

time: 159 us -> 161 us (1.013)
  blocking collectives: 66.2 us -> 53 us
  waiting for transfers between devices: 16.2 us -> 27.9 us
  starting transfers between devices: 29.6 us -> 31.7 us
    all_to_all x1 -> x0, blocking collectives: 14.8 us -> none  [scattered(): return jnp.sum(lax.all_to_all(parts, axis, 0, 0, tiled=True), axis=0)]
    all_to_all x0 -> x1, waiting for transfers between devices: none -> 8.69 us  [scattered(): return jnp.sum(lax.all_to_all(parts, axis, 0, 0, tiled=True), axis=0)]
    all_to_all x3, waiting for transfers between devices: 5.44 us -> 12.3 us  [gathered(): return lax.all_to_all(copies, axis, 0, 0, tiled=True)]
    all_to_all x0 -> x1, starting transfers between devices: none -> 4.65 us  [scattered(): return jnp.sum(lax.all_to_all(parts, axis, 0, 0, tiled=True), axis=0)]
    ppermute x1, waiting for transfers between devices: 3.89 us -> 0.01 us  [local(): start_turned = lax.ppermute(start_piece, ALL, turn)]
    ppermute x4, starting transfers between devices: 12.8 us -> 10.3 us  [other_core(): return lax.ppermute(value, CORE, SWAP)]
  transfers between devices with their start and end apart: 9 -> 10, of which waited for: 8 -> 8; matrix products, arithmetic and copies ran while one was open for 1% -> 1% of each run, Pallas kernels for 16% -> 16%
where the time goes in v12:
time: 161 us; the launch traced here: 160 us
  blocking collectives  53 us (33%)
  Pallas kernels  41.5 us (26%)
  starting transfers between devices  31.7 us (20%)
  waiting for transfers between devices  27.9 us (17%)
  local copies, waits for them, and re-layouts  4.03 us (3%)
    all_to_all x1, blocking collectives, gathered(): return lax.all_to_all(copies, axis, 0, 0, tiled=True)  18.8 us
    all_to_all x1, blocking collectives, local(): lax.all_to_all(picked, ROWS, 0, 0, tiled=True)  17.5 us
    all_to_all x1, blocking collectives, local(): lax.all_to_all(parts, ROWS, 0, 0, tiled=True)  16.7 us
    all_to_all x3, starting transfers between devices, gathered(): return lax.all_to_all(copies, axis, 0, 0, tiled=True)  13 us
    all_to_all x3, waiting for transfers between devices, gathered(): return lax.all_to_all(copies, axis, 0, 0, tiled=True)  12.3 us
    ppermute x4, starting transfers between devices, other_core(): return lax.ppermute(value, CORE, SWAP)  10.3 us
    pallas_call x1, Pallas kernels, local(): pl.pallas_call(middle, out_shape=jax.ShapeDtypeStruct((PACK, width), f32)...  8.84 us
    all_to_all x1, waiting for transfers between devices, scattered(): return jnp.sum(lax.all_to_all(parts, axis, 0, 0, tiled=True), axis=0)  8.69 us
  transfers between devices with their start and end apart: 10, of which 8 were waited for; matrix products, arithmetic and copies ran while one was open for 1% of the time, Pallas kernels for 16%

profile of v12, /device:TPU:1, one launch (start us, length us, event | category | flops | bytes accessed | tf_op | source)
XLA Modules:
  0.0 160.2 jit_solution(1013707080019292699)
XLA Ops:
  0.6 0.1 pad_add_fusion.place
  0.7 0.0 copy-start.3
  0.7 0.7 copy-done.3
  1.4 2.2 %shard_map.58 = f32[8,128,128]{2,1,0:T(8,128)S(1)} custom-call(s32[3]{0:T(128)S(1)} %pad_add_fusion.place, s32[128]{0:T(128)S(1)} %copy-done.3, s32[1,128]{1,0:T(1,128)S(1)} %bitcast.7, f32[2048,1024]{1,0:T(8,128)} %covariance.6), custom_call_target="tpu_custom_call" | custom-call | tf_op jit(solution)/shard_map/pallas_call | solution.py:290
  3.6 17.5 %all_to_all.35.parts = f32[8,128,128]{2,1,0:T(8,128)S(1)} all-to-all(f32[8,128,128]{2,1,0:T(8,128)S(1)} %shard_map.58), channel_id=1, replica_groups=mesh['row'=8,'chip'=8,'core'=2] {'row'}, dimensions={0} | all-to-all | bytes 1048576 | tf_op jit(solution)/shard_map/all_to_all | solution.py:605
  21.1 0.1 shard_map.59
  21.2 0.8 broadcast_in_dim.12
  22.0 3.5 %all-to-all-start.1 = ((f32[8,128,128]{2,1,0:T(8,128)}), f32[8,128,128]{2,1,0:T(8,128)S(1)}, u32[]{:S(2)}, u32[]{:S(2)}) async-start(f32[8,128,128]{2,1,0:T(8,128)} %broadcast_in_dim.12), calls=%async_computation.1 | async-start | bytes 1048576 | tf_op jit(solution)/shard_map/all_to_all | solution.py:579
  25.6 0.0 copy-start.4
  25.6 1.6 %shard_map.60.held = f32[512,1024]{1,0:T(8,128)S(1)} custom-call(f32[2048,1024]{1,0:T(8,128)} %covariance.6), custom_call_target="tpu_custom_call" | custom-call | tf_op jit(solution)/shard_map/pallas_call | solution.py:312
  27.2 6.9 %all-to-all-done.1 = f32[8,128,128]{2,1,0:T(8,128)S(1)} async-done(((f32[8,128,128]{2,1,0:T(8,128)}), f32[8,128,128]{2,1,0:T(8,128)S(1)}, u32[]{:S(2)}, u32[]{:S(2)}) %all-to-all-start.1) | async-done | bytes 524320 | tf_op jit(solution)/shard_map/all_to_all | solution.py:579
  34.1 0.0 copy-done.4
  34.1 4.5 %shard_map.61 = (f32[8,128,128]{2,1,0:T(8,128)S(1)}, f32[8,128,128]{2,1,0:T(8,128)S(1)}) custom-call(s32[3]{0:T(128)S(1)} %pad_add_fusion.place, s32[1,128]{1,0:T(1,128)S(1)} %bitcast.8, f32[2048,1024]{1,0:T(8,128)} %covariance.6, f32[512,1024]{1,0:T(8,128)S(1)} %shard_map.60.held, f32[1024,128]{1,0:T(8,128)S(1)} %bitcast.5), custom_call_target="tpu_custom_call" | custom-call | tf_op jit(solution)/shard_map/pallas_call | solution.py:377
  38.7 3.6 %collective-permute-start = (f32[8,128,128]{2,1,0:T(8,128)S(1)}, f32[8,128,128]{2,1,0:T(8,128)S(1)}, u32[]{:S(2)}, u32[]{:S(2)}) collective-permute-start(f32[8,128,128]{2,1,0:T(8,128)S(1)} %get-tuple-element.26), channel_id=1, source_target_pairs={{0,1},{1,0},{2,3},{3,2},{4,5},{5,4},{6,7},{7,6},{8,9},{9,8},{10,11... | collective-permute-start | bytes 1572872 | tf_op jit(solution)/shard_map/ppermute | solution.py:583
  42.2 1.1 shard_map.62
  43.3 0.5 collective-permute-done
  43.8 0.1 add.10
  43.8 0.9 pad_maximum_fusion
  44.7 4.6 %all-to-all-start.2 = ((f32[8,160,128]{2,1,0:T(8,128)}), f32[8,160,128]{2,1,0:T(8,128)S(1)}, u32[]{:S(2)}, u32[]{:S(2)}) async-start(f32[8,160,128]{2,1,0:T(8,128)} %pad_maximum_fusion), calls=%async_computation.2 | async-start | bytes 1310720 | tf_op jit(solution)/shard_map/all_to_all | solution.py:574
  49.4 3.0 %collective-permute-start.1 = (f32[128,128]{1,0:T(8,128)S(1)}, f32[128,128]{1,0:T(8,128)S(1)}, u32[]{:S(2)}, u32[]{:S(2)}) collective-permute-start(f32[128,128]{1,0:T(8,128)S(1)} %shard_map.59), channel_id=1, source_target_pairs={{0,4},{1,5},{2,30},{3,31},{4,38},{5,39},{6,56},{7,61},{8,72},{9,73... | collective-permute-start | bytes 196616 | tf_op jit(solution)/shard_map/ppermute | solution.py:613
  52.3 8.7 %all-to-all-done.2 = f32[8,160,128]{2,1,0:T(8,128)S(1)} async-done(((f32[8,160,128]{2,1,0:T(8,128)}), f32[8,160,128]{2,1,0:T(8,128)S(1)}, u32[]{:S(2)}, u32[]{:S(2)}) %all-to-all-start.2) | async-done | bytes 655392 | tf_op jit(solution)/shard_map/all_to_all | solution.py:574
  61.1 0.0 copy-start.5
  61.1 0.0 collective-permute-done.1
  61.1 0.1 broadcast_in_dim.13
  61.2 18.8 %all_to_all.36.mine = f32[8,288,128]{2,1,0:T(8,128)S(1)} all-to-all(f32[8,288,128]{2,1,0:T(8,128)S(1)} %broadcast_in_dim.13), channel_id=1, replica_groups=mesh['row'=8,'chip'=8,'core'=2] {'chip'}, dimensions={0} | all-to-all | bytes 2359296 | tf_op jit(solution)/shard_map/all_to_all | solution.py:579
  80.0 2.6 %collective-permute-start.2 = (f32[8,288,128]{2,1,0:T(8,128)S(1)}, f32[8,288,128]{2,1,0:T(8,128)S(1)}, u32[]{:S(2)}, u32[]{:S(2)}) collective-permute-start(f32[8,288,128]{2,1,0:T(8,128)S(1)} %all_to_all.36.mine), channel_id=1, source_target_pairs={{0,1},{1,0},{2,3},{3,2},{4,5},{5,4},{6,7},{7,6},{8,9},{9,8},{10,11... | collective-permute-start | bytes 3538952 | tf_op jit(solution)/shard_map/ppermute | solution.py:583
  82.5 0.0 copy-done.5
  82.5 1.1 shard_map.63.grams
  83.6 1.4 collective-permute-done.2.theirs
  85.0 4.5 %shard_map.64 = (f32[8,160,128]{2,1,0:T(8,128)S(1)}, f32[256,128]{1,0:T(8,128)S(1)}) custom-call(s32[3]{0:T(128)S(1)} %pad_add_fusion.place, f32[2048,1024]{1,0:T(8,128)} %covariance.6, f32[8,288,128]{2,1,0:T(8,128)S(1)} %all_to_all.36.mine, f32[8,288,128]{2,1,0:T(8,128)S(1)} %collective-permute-done.2.theirs, f32[256,128]{1,0:T(8,128)S(1)} %shard_map.63.grams), custom_call_target="tpu_custom_call" | custom-call | tf_op jit(solution)/shard_map/pallas_call | solution.py:506
  89.5 0.0 copy-start.2
  89.6 16.7 %all_to_all.37.parts = f32[8,160,128]{2,1,0:T(8,128)S(1)} all-to-all(f32[8,160,128]{2,1,0:T(8,128)S(1)} %get-tuple-element.28), channel_id=1, replica_groups=mesh['row'=8,'chip'=8,'core'=2] {'row'}, dimensions={0} | all-to-all | bytes 1310720 | tf_op jit(solution)/shard_map/all_to_all | solution.py:620
  106.3 0.9 collective-permute-start.3
  107.2 4.0 %collective-permute-done.3 = f32[160,128]{1,0:T(8,128)S(1)} collective-permute-done((f32[160,128]{1,0:T(8,128)S(1)}, f32[160,128]{1,0:T(8,128)S(1)}, u32[]{:S(2)}, u32[]{:S(2)}) %collective-permute-start.3) | collective-permute-done | bytes 81952 | tf_op jit(solution)/shard_map/ppermute | solution.py:621
  111.2 0.9 broadcast_in_dim.14
  112.0 5.3 %all-to-all-start.5 = ((f32[8,160,128]{2,1,0:T(8,128)}), f32[8,160,128]{2,1,0:T(8,128)S(1)}, u32[]{:S(2)}, u32[]{:S(2)}) async-start(f32[8,160,128]{2,1,0:T(8,128)} %broadcast_in_dim.14), calls=%async_computation.5 | async-start | bytes 1310720 | tf_op jit(solution)/shard_map/all_to_all | solution.py:579
  117.3 4.4 %shard_map.66.ready = f32[512,128]{1,0:T(8,128)S(1)} custom-call(f32[256,128]{1,0:T(8,128)S(1)} %get-tuple-element.29.start), custom_call_target="tpu_custom_call" | custom-call | tf_op jit(solution)/shard_map/pallas_call | solution.py:239
  121.7 0.0 copy-done.2
  121.7 0.0 copy-start.1
  121.8 0.7 copy-done.1
  122.5 3.4 %all-to-all-done.5.following.mine_next = f32[8,160,128]{2,1,0:T(8,128)S(1)} async-done(((f32[8,160,128]{2,1,0:T(8,128)}), f32[8,160,128]{2,1,0:T(8,128)S(1)}, u32[]{:S(2)}, u32[]{:S(2)}) %all-to-all-start.5) | async-done | bytes 655392 | tf_op jit(solution)/shard_map/all_to_all | solution.py:579
  125.9 1.0 shard_map.67.keep
  126.9 0.0 copy-start
  126.9 4.0 %collective-permute-start.5 = (f32[392,128]{1,0:T(8,128)S(1)}, f32[392,128]{1,0:T(8,128)S(1)}, u32[]{:S(2)}, u32[]{:S(2)}) collective-permute-start(f32[392,128]{1,0:T(8,128)S(1)} %shard_map.67.keep), channel_id=1, source_target_pairs={{0,1},{1,0},{2,3},{3,2},{4,5},{5,4},{6,7},{7,6},{8,9},{9,8},{10,11... | collective-permute-start | bytes 602120 | tf_op jit(solution)/shard_map/ppermute | solution.py:583
  131.0 0.1 collective-permute-start.4
  131.1 1.0 collective-permute-done.5.got
  132.0 0.0 copy-start.6
  132.1 0.9 broadcast_in_dim.15
  132.9 4.2 %all-to-all-start.6 = ((f32[8,136,128]{2,1,0:T(8,128)}), f32[8,136,128]{2,1,0:T(8,128)}, u32[]{:S(2)}, u32[]{:S(2)}) async-start(f32[8,136,128]{2,1,0:T(8,128)} %broadcast_in_dim.15), calls=%async_computation.6 | async-start | bytes 1114112 | tf_op jit(solution)/shard_map/all_to_all | solution.py:579
  137.1 0.0 copy-done
  137.1 0.0 copy-done.6
  137.1 8.8 %shard_map.68.refs_0_ = f32[1920,128]{1,0:T(8,128)} custom-call(f32[256,128]{1,0:T(8,128)} %copy-done.2, f32[512,128]{1,0:T(8,128)} %copy-done.1, f32[392,128]{1,0:T(8,128)} %copy-done, f32[392,128]{1,0:T(8,128)} %copy-done.6), custom_call_target="tpu_custom_call" | custom-call | tf_op jit(solution)/shard_map/pallas_call | solution.py:629
  146.0 1.9 %all-to-all-done.6.refs_1_ = f32[8,136,128]{2,1,0:T(8,128)} async-done(((f32[8,136,128]{2,1,0:T(8,128)}), f32[8,136,128]{2,1,0:T(8,128)}, u32[]{:S(2)}, u32[]{:S(2)}) %all-to-all-start.6) | async-done | bytes 557088 | tf_op jit(solution)/shard_map/all_to_all | solution.py:579
  147.9 8.0 %shard_map.69 = (f32[384,384]{1,0:T(8,128)S(1)}, f32[384,256]{1,0:T(8,128)S(1)}, f32[384,256]{1,0:T(8,128)S(1)}) custom-call(f32[1920,128]{1,0:T(8,128)} %shard_map.68.refs_0_, f32[8,136,128]{2,1,0:T(8,128)} %all-to-all-done.6.refs_1_), custom_call_target="tpu_custom_call" | custom-call | tf_op jit(solution)/shard_map/pallas_call | solution.py:644
  155.9 0.0 collective-permute-done.4.theirs_next
  155.9 4.1 %shard_map.70 = (f32[2048,384]{1,0:T(8,128)}, f32[384,256]{1,0:T(8,128)}, f32[384,256]{1,0:T(8,128)}) custom-call(s32[3]{0:T(128)S(1)} %pad_add_fusion.place, s32[128]{0:T(128)S(1)} %copy-done.5, f32[8,288,128]{2,1,0:T(8,128)S(1)} %all_to_all.36.mine, f32[8,160,128]{2,1,0:T(8,128)S(1)} %all-to-all-done.5.following.mine_next, ...), custom_call_target="tpu_custom_call" | custom-call | tf_op jit(solution)/shard_map/pallas_call | solution.py:559
  (4 shorter events, 0.1 us)
Async XLA Ops:
  0.7 0.7 copy-start.3
  22.0 12.1 %all-to-all-start.1 = ((f32[8,128,128]{2,1,0:T(8,128)}), f32[8,128,128]{2,1,0:T(8,128)S(1)}, u32[]{:S(2)}, u32[]{:S(2)}) async-start(f32[8,128,128]{2,1,0:T(8,128)} %broadcast_in_dim.12), calls=%async_computation.1 | async-start | bytes 1048576 | tf_op jit(solution)/shard_map/all_to_all | solution.py:579
  25.6 8.6 %copy-start.4 = (s32[128]{0:T(128)S(1)}, s32[128]{0:T(128)}, u32[]{:S(2)}) copy-start(s32[128]{0:T(128)} %seeds.1) | copy-start | bytes 1540
  38.7 5.1 %collective-permute-start = (f32[8,128,128]{2,1,0:T(8,128)S(1)}, f32[8,128,128]{2,1,0:T(8,128)S(1)}, u32[]{:S(2)}, u32[]{:S(2)}) collective-permute-start(f32[8,128,128]{2,1,0:T(8,128)S(1)} %get-tuple-element.26), channel_id=1, source_target_pairs={{0,1},{1,0},{2,3},{3,2},{4,5},{5,4},{6,7},{7,6},{8,9},{9,8},{10,11... | collective-permute-start | bytes 1572872 | tf_op jit(solution)/shard_map/ppermute | solution.py:583
  44.7 16.3 %all-to-all-start.2 = ((f32[8,160,128]{2,1,0:T(8,128)}), f32[8,160,128]{2,1,0:T(8,128)S(1)}, u32[]{:S(2)}, u32[]{:S(2)}) async-start(f32[8,160,128]{2,1,0:T(8,128)} %pad_maximum_fusion), calls=%async_computation.2 | async-start | bytes 1310720 | tf_op jit(solution)/shard_map/all_to_all | solution.py:574
  49.4 11.7 %collective-permute-start.1 = (f32[128,128]{1,0:T(8,128)S(1)}, f32[128,128]{1,0:T(8,128)S(1)}, u32[]{:S(2)}, u32[]{:S(2)}) collective-permute-start(f32[128,128]{1,0:T(8,128)S(1)} %shard_map.59), channel_id=1, source_target_pairs={{0,4},{1,5},{2,30},{3,31},{4,38},{5,39},{6,56},{7,61},{8,72},{9,73... | collective-permute-start | bytes 196616 | tf_op jit(solution)/shard_map/ppermute | solution.py:613
  61.1 21.5 %copy-start.5 = (s32[128]{0:T(128)S(1)}, s32[128]{0:T(128)}, u32[]{:S(2)}) copy-start(s32[128]{0:T(128)} %constant.19.table) | copy-start | bytes 1540
  80.0 5.0 %collective-permute-start.2 = (f32[8,288,128]{2,1,0:T(8,128)S(1)}, f32[8,288,128]{2,1,0:T(8,128)S(1)}, u32[]{:S(2)}, u32[]{:S(2)}) collective-permute-start(f32[8,288,128]{2,1,0:T(8,128)S(1)} %all_to_all.36.mine), channel_id=1, source_target_pairs={{0,1},{1,0},{2,3},{3,2},{4,5},{5,4},{6,7},{7,6},{8,9},{9,8},{10,11... | collective-permute-start | bytes 3538952 | tf_op jit(solution)/shard_map/ppermute | solution.py:583
  89.5 32.2 %copy-start.2 = (f32[256,128]{1,0:T(8,128)}, f32[256,128]{1,0:T(8,128)S(1)}, u32[]{:S(2)}) copy-start(f32[256,128]{1,0:T(8,128)S(1)} %get-tuple-element.29.start) | copy-start | bytes 393220
  106.3 4.9 %collective-permute-start.3 = (f32[160,128]{1,0:T(8,128)S(1)}, f32[160,128]{1,0:T(8,128)S(1)}, u32[]{:S(2)}, u32[]{:S(2)}) collective-permute-start(f32[160,128]{1,0:T(8,128)S(1)} %shard_map.65), channel_id=1, source_target_pairs={{0,4},{1,5},{2,30},{3,31},{4,38},{5,39},{6,56},{7,61},{8,72},{9,73... | collective-permute-start | bytes 245768 | tf_op jit(solution)/shard_map/ppermute | solution.py:621
  112.0 13.8 %all-to-all-start.5 = ((f32[8,160,128]{2,1,0:T(8,128)}), f32[8,160,128]{2,1,0:T(8,128)S(1)}, u32[]{:S(2)}, u32[]{:S(2)}) async-start(f32[8,160,128]{2,1,0:T(8,128)} %broadcast_in_dim.14), calls=%async_computation.5 | async-start | bytes 1310720 | tf_op jit(solution)/shard_map/all_to_all | solution.py:579
  121.7 0.7 copy-start.1
  126.9 10.2 %copy-start = (f32[392,128]{1,0:T(8,128)}, f32[392,128]{1,0:T(8,128)S(1)}, u32[]{:S(2)}) copy-start(f32[392,128]{1,0:T(8,128)S(1)} %shard_map.67.keep) | copy-start | bytes 602116
  126.9 5.1 %collective-permute-start.5 = (f32[392,128]{1,0:T(8,128)S(1)}, f32[392,128]{1,0:T(8,128)S(1)}, u32[]{:S(2)}, u32[]{:S(2)}) collective-permute-start(f32[392,128]{1,0:T(8,128)S(1)} %shard_map.67.keep), channel_id=1, source_target_pairs={{0,1},{1,0},{2,3},{3,2},{4,5},{5,4},{6,7},{7,6},{8,9},{9,8},{10,11... | collective-permute-start | bytes 602120 | tf_op jit(solution)/shard_map/ppermute | solution.py:583
  131.0 25.0 %collective-permute-start.4 = (f32[8,160,128]{2,1,0:T(8,128)S(1)}, f32[8,160,128]{2,1,0:T(8,128)}, u32[]{:S(2)}, u32[]{:S(2)}) collective-permute-start(f32[8,160,128]{2,1,0:T(8,128)S(1)} %all-to-all-done.5.following.mine_next), channel_id=1, source_target_pairs={{0,1},{1,0},{2,3},{3,2},{4,5},{5,4},{6,7},{7,6},{8,9},{9,8},{10,11... | collective-permute-start | bytes 1966088 | tf_op jit(solution)/shard_map/ppermute | solution.py:583
  132.0 5.1 %copy-start.6 = (f32[392,128]{1,0:T(8,128)}, f32[392,128]{1,0:T(8,128)S(1)}, u32[]{:S(2)}) copy-start(f32[392,128]{1,0:T(8,128)S(1)} %collective-permute-done.5.got) | copy-start | bytes 602116
  132.9 15.0 %all-to-all-start.6 = ((f32[8,136,128]{2,1,0:T(8,128)}), f32[8,136,128]{2,1,0:T(8,128)}, u32[]{:S(2)}, u32[]{:S(2)}) async-start(f32[8,136,128]{2,1,0:T(8,128)} %broadcast_in_dim.15), calls=%async_computation.6 | async-start | bytes 1114112 | tf_op jit(solution)/shard_map/all_to_all | solution.py:579
